TPU v7x, 8 devices: a whole 2x2x1 slice. The times are simulated.
8 devices in a mesh: rep: 2 (over y, z), dp: 4 (over x, core).
Axes of the slice: x: 2, y: 2, z: 1, core: 2. Of those that a mesh axis runs over, the one named last changes fastest.
Arguments:
- x: bfloat16 [8, 2048, 896], P(('rep', 'dp')), parts along dimension 0
- dy: bfloat16 [8, 2048, 896], P(('rep', 'dp')), parts along dimension 0
- w_gate: bfloat16 [2, 896, 4736], replicated
- w_up: bfloat16 [2, 896, 4736], replicated
- w_down: bfloat16 [2, 4736, 896], replicated
- m_w_gate: float32 [2, 896, 4736], replicated
- m_w_up: float32 [2, 896, 4736], replicated
- m_w_down: float32 [2, 4736, 896], replicated
- v_w_gate: float32 [2, 896, 4736], replicated
- v_w_up: float32 [2, 896, 4736], replicated
- v_w_down: float32 [2, 4736, 896], replicated
Outputs:
- output 1: bfloat16 [4, 896, 4736], P('rep'), parts along dimension 0
- output 2: bfloat16 [4, 896, 4736], P('rep'), parts along dimension 0
- output 3: bfloat16 [4, 4736, 896], P('rep'), parts along dimension 0
- output 4: float32 [4, 896, 4736], P('rep'), parts along dimension 0
- output 5: float32 [4, 896, 4736], P('rep'), parts along dimension 0
- output 6: float32 [4, 4736, 896], P('rep'), parts along dimension 0
- output 7: float32 [4, 896, 4736], P('rep'), parts along dimension 0
- output 8: float32 [4, 896, 4736], P('rep'), parts along dimension 0
- output 9: float32 [4, 4736, 896], P('rep'), parts along dimension 0
There are 2 independent parts. A program takes and returns all parts, laid end to end along the dimension named above; an argument that names none is the same for every part.
All inputs are finite; a program needn't handle non-finite values.
Results may differ from a plain program's by a relative error of at most 0.022.
Values are sent between devices in bfloat16 or wider.
A program may use at most 3 GiB of HBM per device.

v0:
```python
import jax
import jax.numpy as jnp
from jax import lax
from jax.sharding import PartitionSpec as P

NAMES = ("w_gate", "w_up", "w_down")


def matmul(a, w):
    return jnp.dot(a, w, preferred_element_type=jnp.float32).astype(jnp.bfloat16)


def normed(h):
    wide = h.astype(jnp.float32)
    scale = lax.rsqrt(jnp.mean(wide**2, -1, keepdims=True) + 1e-6)
    return (wide * scale).astype(jnp.bfloat16)


def layer(h, w):
    a = normed(h)
    gate = jnp.dot(a, w["w_gate"], preferred_element_type=jnp.float32)
    up = jnp.dot(a, w["w_up"], preferred_element_type=jnp.float32)
    return h + matmul((jax.nn.silu(gate) * up).astype(jnp.bfloat16), w["w_down"])


def adamw(w, m, v, g):
    m = 0.9 * m + 0.1 * g
    v = 0.95 * v + 0.05 * g * g
    step = m * lax.rsqrt(v + 1e-8) + 0.1 * w
    return (w - 0.02 * step).astype(jnp.bfloat16), m, v


def clipped(gradients, sum_of_squares, count):
    factor = jnp.minimum(1.0, 0.5 * lax.rsqrt(sum_of_squares / count + 1e-30))
    return [g * factor for g in gradients]


def solution(mesh):
    def step(x, dy, *arrays):
        weights, m, v = (arrays[i : i + 3] for i in (0, 3, 6))
        layers = weights[0].shape[0]
        h, kept = x[0], []
        for number in range(layers):
            kept.append(h)
            h = layer(h, {name: w[number] for name, w in zip(NAMES, weights, strict=True)})
        by_h, summed = dy[0], [None] * layers
        for number in reversed(range(layers)):
            _, back = jax.vjp(lambda w, h: layer(h, w), {name: w[number] for name, w in zip(NAMES, weights, strict=True)}, kept[number])
            by_w, by_h = back(by_h)
            summed[number] = [lax.psum(by_w[name], "dp") for name in NAMES]
        gradients = [jnp.stack([summed[number][i] for number in range(layers)]).astype(jnp.float32) for i in range(3)]
        gradients = clipped(gradients, sum(jnp.sum(g * g) for g in gradients), sum(g.size for g in gradients))
        new = [adamw(w.astype(jnp.float32), m, v, g) for w, m, v, g in zip(weights, m, v, gradients, strict=True)]
        return tuple(one[which] for which in range(3) for one in new)

    return jax.shard_map(
        step,
        mesh=mesh,
        in_specs=(P(("rep", "dp"), None, None),) * 2 + (P(None, None, None),) * 9,
        out_specs=(P("rep", None, None),) * 9,
        check_vma=False,
    )
```

profile of v0, /device:TPU:0, one launch (start us, length us, event | category | flops | bytes accessed | tf_op | source)
XLA Modules:
  0.0 1548.8 jit_solution(9324843520327648026)
XLA Ops:
  7.2 0.0 all-reduce.3.cloned.1.call-start
  7.2 6.1 copy.20
  13.3 2.8 fusion.74
  16.1 6.2 copy.21
  22.3 27.9 %convolution_convert_fusion.1 = bf16[2048,4736]{1,0:T(8,128)(2,1)} fusion(bf16[2,4736,896]{2,1,0:T(8,128)(2,1)} %param.15, bf16[1,2048,896]{2,1,0:T(8,128)(2,1)} %param.12), kind=kOutput, calls=%fused_computation.61 | convolution fusion | flops 17390895104 | bytes 31555584 | tf_op jit(solution)/shard_map/transpose(jvp())/dot_general | solution.py:10
  50.2 29.2 %fusion.55 = f32[2048,4736]{1,0:T(8,128)} fusion(bf16[2,896,4736]{2,1,0:T(8,128)(2,1)} %param.13, bf16[1,2048,896]{2,1,0:T(8,128)(2,1)} %param.11, f32[2048]{0:T(1024)S(1)} %add_rsqrt_fusion), kind=kOutput, calls=%fused_computation.91 | convolution fusion | flops 17386700800 | bytes 50962432 | tf_op jit(solution)/shard_map/dot_general | solution.py:21
  79.3 0.0 copy-done.7
  79.3 42.0 %multiply_convert_fusion.1 = (bf16[2048,4736]{1,0:T(8,128)(2,1)}, f32[2048,4736]{1,0:T(8,128)}) fusion(f32[2048,4736]{1,0:T(8,128)} %fusion.55, bf16[2,896,4736]{2,1,0:T(8,128)(2,1)} %param.14, bf16[1,2048,896]{2,1,0:T(8,128)(2,1)} %param.11, f32[2048]{0:T(1024)S(1)} %add_rsqrt_fusion), kind=kOutput, calls=%fused_computation.35 | convolution fusion | flops 17444896768 | bytes 109158400 | tf_op jit(solution)/shard_map/dot_general | solution.py:22
  121.4 24.2 %fusion.78 = (f32[2048]{0:T(1024)S(1)}, bf16[2048,896]{0,1:T(8,128)(2,1)S(1)}) fusion(bf16[2048,4736]{1,0:T(8,128)(2,1)} %get-tuple-element.24, bf16[2,4736,896]{2,1,0:T(8,128)(2,1)} %param.15, bf16[1,2048,896]{1,2,0:T(8,128)(2,1)} %copy.20), kind=kOutput, calls=%fused_computation.112 | convolution fusion | flops 17390368768 | bytes 35233792 | tf_op jit(solution)/shard_map/dot_general | solution.py:10
  145.6 0.0 copy-start.2
  145.6 29.0 %fusion.42 = f32[2048,4736]{1,0:T(8,128)} fusion(bf16[2,896,4736]{2,1,0:T(8,128)(2,1)} %param.14, bf16[2048,896]{0,1:T(8,128)(2,1)S(1)} %get-tuple-element.27, f32[2048]{0:T(1024)S(1)} %fusion.98), kind=kOutput, calls=%fused_computation.78 | convolution fusion | flops 17386700800 | bytes 50962432 | tf_op jit(solution)/shard_map/jvp()/dot_general | solution.py:22
  174.6 50.2 %fusion.5 = (bf16[2048,4736]{1,0:T(8,128)(2,1)}, f32[2048,4736]{1,0:T(8,128)}) fusion(f32[2048,4736]{1,0:T(8,128)} %fusion.42, bf16[2048,4736]{1,0:T(8,128)(2,1)} %convolution_convert_fusion.1, bf16[2,896,4736]{2,1,0:T(8,128)(2,1)} %param.13, bf16[2048,896]{0,1:T(8,128)(2,1)S(1)} %get-tuple-element.27, f32[2048]{0:T(1024)S(1)} %fusion.98), kind=kOutput, calls=%fused_computation.26 | convolution fusion | flops 17503092736 | bytes 128557056 | tf_op jit(solution)/shard_map/jvp()/dot_general | solution.py:21
  224.8 30.0 %fusion.33 = bf16[2048,896]{0,1:T(8,128)(2,1)} fusion(bf16[2048,4736]{1,0:T(8,128)(2,1)} %convolution_convert_fusion.1, bf16[2,896,4736]{2,1,0:T(8,128)(2,1)} %param.14, f32[2048,4736]{1,0:T(8,128)} %get-tuple-element.29), kind=kOutput, calls=%fused_computation.57 | convolution fusion | flops 17439391744 | bytes 70352896 | tf_op jit(solution)/shard_map/transpose(jvp())/dot_general | solution.py:22
  254.7 30.2 %fusion.66 = bf16[1,896,4736]{2,1,0:T(8,128)(2,1)} fusion(bf16[2048,4736]{1,0:T(8,128)(2,1)} %convolution_convert_fusion.1, bf16[2048,896]{0,1:T(8,128)(2,1)} %copy-done.2, f32[2048]{0:T(1024)S(1)} %fusion.98, f32[2048,4736]{1,0:T(8,128)} %get-tuple-element.29), kind=kOutput, calls=%fused_computation.100 | convolution fusion | flops 17449140224 | bytes 70361088 | tf_op jit(solution)/shard_map/transpose(jvp())/dot_general | solution.py:22
  285.0 36.0 %fusion.67 = bf16[1,4736,896]{2,1,0:T(8,128)(2,1)} fusion(f32[2048,4736]{1,0:T(8,128)} %fusion.42, bf16[1,2048,896]{2,1,0:T(8,128)(2,1)} %param.12, f32[2048,4736]{1,0:T(8,128)} %get-tuple-element.29), kind=kOutput, calls=%fused_computation.101 | convolution fusion | flops 17443635200 | bytes 89751552 | tf_op jit(solution)/shard_map/transpose(jvp())/dot_general | solution.py:10
  321.0 24.6 %fusion.60 = bf16[1,896,4736]{2,1,0:T(8,128)(2,1)} fusion(bf16[2048,4736]{1,0:T(8,128)(2,1)} %get-tuple-element.28, bf16[2048,896]{0,1:T(8,128)(2,1)} %copy-done.2, f32[2048]{0:T(1024)S(1)} %fusion.98), kind=kOutput, calls=%fused_computation.96 | convolution fusion | flops 17386700800 | bytes 31563776 | tf_op jit(solution)/shard_map/transpose(jvp())/dot_general | solution.py:21
  345.6 0.0 copy-done.3
  345.6 24.7 %fusion.80 = (f32[2048]{0:T(1024)S(1)}, bf16[2048,896]{0,1:T(8,128)(2,1)S(1)}) fusion(bf16[2048,896]{0,1:T(8,128)(2,1)S(1)} %copy-done.3, bf16[2048,896]{0,1:T(8,128)(2,1)} %fusion.33, bf16[2048,4736]{1,0:T(8,128)(2,1)} %get-tuple-element.28, bf16[2,896,4736]{2,1,0:T(8,128)(2,1)} %param.13), kind=kOutput, calls=%fused_computation.114 | convolution fusion | flops 17390368768 | bytes 38903808 | tf_op jit(solution)/shard_map/transpose(jvp())/dot_general | solution.py:21
  370.4 4.9 fusion.83
  375.2 27.6 %convolution_convert_fusion = bf16[2048,4736]{1,0:T(8,128)(2,1)} fusion(bf16[2048,896]{0,1:T(8,128)(2,1)} %fusion.83, bf16[2,4736,896]{2,1,0:T(8,128)(2,1)} %param.15), kind=kOutput, calls=%fused_computation.60 | convolution fusion | flops 17390895104 | bytes 31555584 | tf_op jit(solution)/shard_map/transpose(jvp())/dot_general | solution.py:10
  402.8 0.0 copy-done.4
  402.8 26.5 %fusion.61 = bf16[1,4736,896]{2,1,0:T(8,128)(2,1)} fusion(bf16[2048,4736]{1,0:T(8,128)(2,1)} %get-tuple-element.24, bf16[2048,896]{0,1:T(8,128)(2,1)S(1)} %copy-done.4), kind=kOutput, calls=%fused_computation.97 | convolution fusion | flops 17385439232 | bytes 31555584 | tf_op jit(solution)/shard_map/transpose(jvp())/dot_general | solution.py:10
  429.3 30.4 %fusion.62 = bf16[1,896,4736]{2,1,0:T(8,128)(2,1)} fusion(bf16[2048,4736]{1,0:T(8,128)(2,1)} %convolution_convert_fusion, f32[2048,4736]{1,0:T(8,128)} %fusion.55, bf16[1,2048,896]{1,2,0:T(8,128)(2,1)} %copy.20, f32[2048]{0:T(1024)S(1)} %copy-done.8), kind=kOutput, calls=%fused_computation.98 | convolution fusion | flops 17449140224 | bytes 70361088 | tf_op jit(solution)/shard_map/transpose(jvp())/dot_general | solution.py:22
  459.7 38.2 %fusion.63 = bf16[1,896,4736]{2,1,0:T(8,128)(2,1)} fusion(f32[2048,4736]{1,0:T(8,128)} %fusion.55, f32[2048,4736]{1,0:T(8,128)} %get-tuple-element.25, bf16[2048,4736]{1,0:T(8,128)(2,1)} %convolution_convert_fusion, bf16[1,2048,896]{1,2,0:T(8,128)(2,1)} %copy.20, f32[2048]{0:T(1024)S(1)} %copy-done.8), kind=kOutput, calls=%fused_computation.99 | convolution fusion | flops 17497636864 | bytes 109158400 | tf_op jit(solution)/shard_map/transpose(jvp())/dot_general | solution.py:21
  497.8 0.0 all-reduce.3.cloned.1.call-update
  497.9 834.3 %all-reduce.3.cloned.1.call-done = (bf16[1,896,4736]{2,1,0:T(8,128)(2,1)}, bf16[1,896,4736]{2,1,0:T(8,128)(2,1)}, bf16[1,896,4736]{2,1,0:T(8,128)(2,1)}, bf16[1,...) async-done(((bf16[1,896,4736]{2,1,0:T(8,128)(2,1)}, bf16[1,896,4736]{2,1,0:T(8,128)(2,1)}, bf16[1,896,4736]{2,1,0:T(8,128)(2,1)}, ...) | async-done | bytes 50921488 | tf_op jit(solution)/shard_map/psum | solution.py:50
  1332.2 11.6 fusion.20
  1343.7 0.0 slice-done
  1343.8 9.4 fusion.21
  1354.4 11.3 fusion.22
  1366.4 58.2 %fusion.28 = (bf16[2,4736,896]{2,1,0:T(8,128)(2,1)}, f32[2,4736,896]{2,1,0:T(8,128)}, f32[2,4736,896]{2,1,0:T(8,128)}) fusion(bf16[2,4736,896]{2,1,0:T(8,128)(2,1)} %param.15, f32[]{:T(128)S(6)} %min_shard_map.3, bf16[1,4736,896]{2,1,0:T(8,128)(2,1)} %get-tuple-element.13, bf16[1,4736,896]{2,1,0:T(8,128)(2,1)} %get-tuple-element.14, ...), kind=kLoop, calls=%fused_computation.52 | loop fusion | flops 169738240 | bytes 186712064 | tf_op jit(solution)/shard_map/convert_element_type | solution.py:30
  1424.7 116.8 %fusion.19 = (bf16[2,896,4736]{2,1,0:T(8,128)(2,1)}, f32[2,896,4736]{2,1,0:T(8,128)}, f32[2,896,4736]{2,1,0:T(8,128)}, bf16[2,896,4736]{2,1,0:T(8,128)(2,1)}, f3...) fusion(bf16[2,896,4736]{2,1,0:T(8,128)(2,1)} %param.13, f32[]{:T(128)S(6)} %min_shard_map.3, ...), kind=kLoop, calls=%fused_computation.43 | loop fusion | flops 339476480 | bytes 373424128 | tf_op jit(solution)/shard_map/convert_element_type | solution.py:30
  (23 shorter events, 0.1 us)
Async XLA Ops:
  7.2 1325.0 %all-reduce.3.cloned.1.call-start = ((), (), s32[]{:S(2)}) async-start(), calls=%async_computation | async-start | bytes 101842944 | tf_op jit(solution)/shard_map/psum | solution.py:50
  16.1 63.2 %copy-start.7 = (f32[2048]{0:T(1024)}, f32[2048]{0:T(1024)S(1)}, u32[]{:S(2)}) copy-start(f32[2048]{0:T(1024)S(1)} %add_rsqrt_fusion) | copy-start | bytes 24580
  145.6 29.0 %copy-start.2 = (bf16[2048,896]{0,1:T(8,128)(2,1)}, bf16[2048,896]{0,1:T(8,128)(2,1)S(1)}, u32[]{:S(2)}) copy-start(bf16[2048,896]{0,1:T(8,128)(2,1)S(1)} %get-tuple-element.27) | copy-start | bytes 11010052
  145.6 29.0 %copy-start.5 = (f32[2048]{0:T(1024)}, f32[2048]{0:T(1024)S(1)}, u32[]{:S(2)}) copy-start(f32[2048]{0:T(1024)S(1)} %get-tuple-element.26) | copy-start | bytes 24580
  321.0 24.6 %copy-start.3 = (bf16[2048,896]{0,1:T(8,128)(2,1)S(1)}, bf16[2048,896]{0,1:T(8,128)(2,1)}, u32[]{:S(2)}) copy-start(bf16[2048,896]{0,1:T(8,128)(2,1)} %copy-done.2) | copy-start | bytes 11010052
  345.6 24.7 %copy-start.6 = (f32[2048]{0:T(1024)S(1)}, f32[2048]{0:T(1024)}, u32[]{:S(2)}) copy-start(f32[2048]{0:T(1024)} %copy-done.5) | copy-start | bytes 24580
  345.6 24.8 %copy-start.1 = (bf16[1,2048,896]{1,2,0:T(8,128)(2,1)S(1)}, bf16[1,2048,896]{1,2,0:T(8,128)(2,1)}, u32[]{:S(2)}) copy-start(bf16[1,2048,896]{1,2,0:T(8,128)(2,1)} %copy.21) | copy-start | bytes 11010052
  375.2 27.6 %copy-start.4 = (bf16[2048,896]{0,1:T(8,128)(2,1)S(1)}, bf16[2048,896]{0,1:T(8,128)(2,1)}, u32[]{:S(2)}) copy-start(bf16[2048,896]{0,1:T(8,128)(2,1)} %fusion.83) | copy-start | bytes 11010052
  402.8 26.5 %copy-start.8 = (f32[2048]{0:T(1024)S(1)}, f32[2048]{0:T(1024)}, u32[]{:S(2)}) copy-start(f32[2048]{0:T(1024)} %copy-done.7) | copy-start | bytes 24580
  1332.1 11.6 slice-start
  1332.1 11.6 copy-start
  1332.2 11.6 slice-start.1
  1332.2 11.6 slice-start.2
Sparse Core Ops, SparseCore 0:
  498.0 834.1 all-reduce.2
where the time goes:
time: 1560 us; the launch traced here: 1550 us
  waiting for transfers between devices  834 us (53%)
  matrix products  471 us (30%)
  other arithmetic  215 us (14%)
  between operations  16.6 us (1%)
    psum x1, waiting for transfers between devices, step(): summed[number] = [lax.psum(by_w[name], 'dp') for name in NAMES]  834 us
    convert_element_type x2, other arithmetic, adamw(): return ((w - 0.02 * step).astype(jnp.bfloat16), m, v)  175 us
    dot_general x5, matrix products, layer(): gate = jnp.dot(a, w['w_gate'], preferred_element_type=jnp.float32)  167 us
    dot_general x5, matrix products, layer(): up = jnp.dot(a, w['w_up'], preferred_element_type=jnp.float32)  162 us
    dot_general x5, matrix products, matmul(): jnp.dot(a, w, preferred_element_type=jnp.float32).astype(jnp.bfloat16)  142 us
    reduce_sum x3, other arithmetic, step(): jnp.sum(g * g)  32.3 us
  transfers between devices with their start and end apart: 1, of which 1 were waited for; matrix products, arithmetic and copies ran while one was open for 0% of the time, Pallas kernels for 0%

commit v1 on v0

v1 whole, which is shorter than its diff:
```python
import jax
import jax.numpy as jnp
from jax import lax
from jax.experimental import pallas as pl
from jax.experimental.pallas import tpu as pltpu
from jax.sharding import PartitionSpec as P


F32, BF16 = jnp.float32, jnp.bfloat16
PX = ((0, 2), (2, 0), (1, 3), (3, 1))
PD = ((0, 1), (1, 0), (2, 3), (3, 2))
NN, NT = ((1,), (0,)), ((1,), (1,))

LANES = 128
BLOCK = 512
ROWS = 512
SHARED_APART = False


def dot(a, b, dims):
    return lax.dot_general(a, b, (dims, ((), ())), preferred_element_type=F32)


def sigmoid(x):
    return 0.5 * jnp.tanh(0.5 * x) + 0.5


def px(a):
    return lax.ppermute(a, "dp", PX)


def pd(a):
    return lax.ppermute(a, "dp", PD)


def once(shape, index):
    return pl.BlockSpec(shape, index, pipeline_mode=pl.Buffered(1))


def params(mib=62):
    return pltpu.CompilerParams(vmem_limit_bytes=mib << 20)


def norm_scale(wide):
    return lax.rsqrt(jnp.mean(wide * wide, -1, keepdims=True) + 1e-6)


def normed(h):
    wide = h.astype(F32)
    return (wide * norm_scale(wide)).astype(BF16)


def forward_kernel(tail, x_ref, wg_ref, wu_ref, wd_ref, h_ref, a_ref, a0_ref, acc_ref):
    j, last = pl.program_id(0), pl.num_programs(0) - 1
    tokens = x_ref.shape[0]
    chunks = [pl.ds(r, ROWS) for r in range(0, tokens, ROWS)]

    @pl.when(j == 0)
    def _():
        for r in chunks:
            a0_ref[r, :] = normed(x_ref[r, :])
            acc_ref[r, :] = jnp.zeros((ROWS, acc_ref.shape[1]), F32)

    def block(width):
        hid = {}

        def up(r):
            a = a0_ref[chunks[r], :]
            g = dot(a, wg_ref[0, :, :width], NN)
            u = dot(a, wu_ref[0, :, :width], NN)
            hid[r] = (g * sigmoid(g) * u).astype(BF16)

        def down(r):
            acc_ref[chunks[r], :] += dot(hid.pop(r), wd_ref[0, :width, :], NN)

        up(0)
        for r in range(1, len(chunks)):
            up(r)
            down(r - 1)
        down(len(chunks) - 1)

    @pl.when(j < last)
    def _():
        block(wg_ref.shape[2])

    @pl.when(j == last)
    def _():
        block(tail)
        for r in chunks:
            h = (x_ref[r, :].astype(F32) + acc_ref[r, :].astype(BF16).astype(F32)).astype(BF16)
            h_ref[r, :] = h
            a_ref[r, :] = normed(h)


def forward(x, wg, wu, wd):
    tokens, d = x.shape
    ff = wg.shape[2]
    steps = pl.cdiv(ff, BLOCK)
    full = once((tokens, d), lambda j: (0, 0))
    across = pl.BlockSpec((1, d, BLOCK), lambda j: (0, 0, j))
    down = pl.BlockSpec((1, BLOCK, d), lambda j: (0, j, 0))
    return pl.pallas_call(
        lambda *refs: forward_kernel(ff - (steps - 1) * BLOCK, *refs),
        grid=(steps,),
        in_specs=[full, across, across, down],
        out_specs=[full] * 3,
        out_shape=[jax.ShapeDtypeStruct((tokens, d), BF16)] * 3,
        scratch_shapes=[pltpu.VMEM((tokens, d), F32)],
        cost_estimate=pl.CostEstimate(flops=6 * tokens * d * ff, bytes_accessed=6 * d * ff, transcendentals=tokens * ff),
        compiler_params=params(),
        name="forward",
    )(x, wg, wu, wd)


def hidden_back(g, u, dhid):
    dhid = dhid.astype(BF16).astype(F32)
    sig = sigmoid(g)
    act = g * sig
    return (dhid * u * (sig + act * (1 - sig))).astype(BF16), (dhid * act).astype(BF16), (act * u).astype(BF16)


def chain_kernel(tail, a_ref, dy_ref, h_ref, wg_ref, wu_ref, wd_ref, dh_ref, acc_ref):
    j, last = pl.program_id(0), pl.num_programs(0) - 1
    tokens = a_ref.shape[0]
    chunks = [pl.ds(r, ROWS) for r in range(0, tokens, ROWS)]

    @pl.when(j == 0)
    def _():
        for r in chunks:
            acc_ref[r, :] = jnp.zeros((ROWS, acc_ref.shape[1]), F32)

    def block(width):
        held = {}

        def there(r):
            a, dy = a_ref[chunks[r], :], dy_ref[chunks[r], :]
            g = dot(a, wg_ref[0, :, :width], NN)
            u = dot(a, wu_ref[0, :, :width], NN)
            dhid = dot(dy, wd_ref[0, :width, :], NT)
            held[r] = hidden_back(g, u, dhid)[:2]

        def back(r):
            dg, du = held.pop(r)
            acc_ref[chunks[r], :] += dot(dg, wg_ref[0, :, :width], NT) + dot(du, wu_ref[0, :, :width], NT)

        there(0)
        for r in range(1, len(chunks)):
            there(r)
            back(r - 1)
        back(len(chunks) - 1)

    @pl.when(j < last)
    def _():
        block(wg_ref.shape[2])

    @pl.when(j == last)
    def _():
        block(tail)
        for r in chunks:
            wide, da = h_ref[r, :].astype(F32), acc_ref[r, :].astype(BF16).astype(F32)
            scale = norm_scale(wide)
            back = scale * da - wide * (scale * scale * scale * jnp.mean(wide * da, -1, keepdims=True))
            dh_ref[r, :] = (dy_ref[r, :].astype(F32) + back.astype(BF16).astype(F32)).astype(BF16)


def chain(a, dy, h, wg, wu, wd):
    tokens, d = a.shape
    ff = wg.shape[2]
    steps = pl.cdiv(ff, BLOCK)
    full = once((tokens, d), lambda j: (0, 0))
    across = pl.BlockSpec((1, d, BLOCK), lambda j: (1, 0, j))
    down = pl.BlockSpec((1, BLOCK, d), lambda j: (1, j, 0))
    return pl.pallas_call(
        lambda *refs: chain_kernel(ff - (steps - 1) * BLOCK, *refs),
        grid=(steps,),
        in_specs=[full, full, full, across, across, down],
        out_specs=full,
        out_shape=jax.ShapeDtypeStruct((tokens, d), BF16),
        scratch_shapes=[pltpu.VMEM((tokens, d), F32)],
        cost_estimate=pl.CostEstimate(flops=10 * tokens * d * ff, bytes_accessed=6 * d * ff, transcendentals=tokens * ff),
        compiler_params=params(),
        name="chain",
    )(a, dy, h, wg, wu, wd)


def squares(x):
    x = x.astype(F32)
    x = x * x
    total = None
    for c in range(0, x.shape[1], LANES):
        part = jnp.sum(x[:, c : c + LANES].reshape(x.shape[0] // 8, 8, LANES), 0)
        total = part if total is None else total + part
    return total


def slices_kernel(own, me_ref, *refs):
    a_refs, dy_refs = refs[:4], refs[4:8]
    weights, outs, scratch = refs[8:14], refs[14:22], refs[22:]
    wg_ref, wu_ref, wd_ref, accg_ref, accu_ref, accd_ref, a_buf, dy_buf, sems = scratch
    i, steps = pl.program_id(0), pl.num_programs(0)
    tokens = a_refs[0].shape[0]
    each = tokens // ROWS
    me = me_ref[0]

    def fetch(step, do):
        slot = lax.rem(step, 2)
        owner, chunk = step // each, lax.rem(step, each)
        away = (owner + me) % 2 + 2 * ((owner // 2 + me // 2) % 2)
        rows = pl.ds(pl.multiple_of(chunk * ROWS, ROWS), ROWS)
        for k in range(4):

            @pl.when(away == k)
            def _():
                do(pltpu.make_async_copy(a_refs[k].at[rows, :], a_buf.at[slot], sems.at[0, slot]))
                do(pltpu.make_async_copy(dy_refs[k].at[rows, :], dy_buf.at[slot], sems.at[1, slot]))

    @pl.when(i == 0)
    def _():
        fetch(i, lambda copy: copy.start())
        wg_ref[:, :own], wg_ref[:, own:] = weights[0][0], weights[1][0]
        wu_ref[:, :own], wu_ref[:, own:] = weights[2][0], weights[3][0]
        wd_ref[:own, :], wd_ref[own:, :] = weights[4][0], weights[5][0]
        for ref in (accg_ref, accu_ref, accd_ref):
            ref[...] = jnp.zeros_like(ref)

    @pl.when(i + 1 < steps)
    def _():
        fetch(i + 1, lambda copy: copy.start())

    slot = lax.rem(i, 2)
    pltpu.make_async_copy(a_refs[0].at[pl.ds(0, ROWS), :], a_buf.at[slot], sems.at[0, slot]).wait()
    pltpu.make_async_copy(dy_refs[0].at[pl.ds(0, ROWS), :], dy_buf.at[slot], sems.at[1, slot]).wait()
    a, dy = a_buf[slot], dy_buf[slot]
    a_t, dy_t = a.T, dy.T
    width = wg_ref.shape[1]
    blocks = [pl.ds(c, min(BLOCK, width - c)) for c in range(0, width, BLOCK)]
    held = {}

    def there(c):
        s = blocks[c]
        held[c] = hidden_back(dot(a, wg_ref[:, s], NN), dot(a, wu_ref[:, s], NN), dot(dy, wd_ref[s, :], NT))

    def back(c):
        s = blocks[c]
        dg, du, hid = held.pop(c)
        accg_ref[:, s] += dot(a_t, dg, NN)
        accu_ref[:, s] += dot(a_t, du, NN)
        accd_ref[:, s] += dot(dy_t, hid, NN)

    there(0)
    for c in range(1, len(blocks)):
        there(c)
        back(c - 1)
    back(len(blocks) - 1)

    @pl.when(i == steps - 1)
    def _():
        g_ref, u_ref, d_ref, gs_ref, us_ref, ds_ref, own_ref, shared_ref = outs
        g, u, d = accg_ref[...].astype(BF16), accu_ref[...].astype(BF16), accd_ref[...].astype(BF16)
        g_ref[...], gs_ref[...] = g[:, :own], g[:, own:]
        u_ref[...], us_ref[...] = u[:, :own], u[:, own:]
        d_ref[...], ds_ref[...] = d[:, :own].T, d[:, own:].T
        own_ref[...] = squares(g[:, :own]) + squares(u[:, :own]) + squares(d[:, :own])
        shared_ref[...] = squares(g[:, own:]) + squares(u[:, own:]) + squares(d[:, own:])


def slices(layer, own, me, a_all, dy_all, wg, wu, wd):
    tokens, d = a_all[0].shape
    ff = wg.shape[2]
    rest = ff - 4 * own
    width = own + rest
    any_ = pl.BlockSpec(memory_space=pl.ANY)
    at = lambda s: once(s, lambda i, me: (0, 0))
    sizes = [(d, own), (d, own), (own, d), (d, rest), (d, rest), (rest, d)]
    return pl.pallas_call(
        lambda *refs: slices_kernel(own, *refs),
        grid_spec=pltpu.PrefetchScalarGridSpec(
            num_scalar_prefetch=1,
            grid=(4 * tokens // ROWS,),
            in_specs=[any_] * 8
            + [
                once((1, d, own), lambda i, me: (layer, 0, me[0])),
                once((1, d, rest), lambda i, me: (layer, 0, 4 * own // rest)),
            ]
            * 2
            + [
                once((1, own, d), lambda i, me: (layer, me[0], 0)),
                once((1, rest, d), lambda i, me: (layer, 4 * own // rest, 0)),
            ],
            out_specs=[at(s) for s in sizes] + [at((8, LANES))] * 2,
            scratch_shapes=[pltpu.VMEM((d, width), BF16)] * 2
            + [pltpu.VMEM((width, d), BF16)]
            + [pltpu.VMEM((d, width), F32)] * 3
            + [pltpu.VMEM((2, ROWS, d), BF16)] * 2
            + [pltpu.SemaphoreType.DMA((2, 2))],
        ),
        out_shape=[jax.ShapeDtypeStruct(s, BF16) for s in sizes] + [jax.ShapeDtypeStruct((8, LANES), F32)] * 2,
        cost_estimate=pl.CostEstimate(
            flops=12 * 4 * tokens * d * width, bytes_accessed=16 * tokens * d, transcendentals=4 * tokens * width
        ),
        compiler_params=params(),
        name="slices",
    )(me.reshape(1), *a_all, *dy_all, wg, wg, wu, wu, wd, wd)


def adam_math(f, w, m, v, g):
    g = g.astype(F32) * f
    m = 0.9 * m + 0.1 * g
    v = 0.95 * v + 0.05 * g * g
    w = w.astype(F32)
    return (w - 0.02 * (m * lax.rsqrt(v + 1e-8) + 0.1 * w)).astype(BF16), m, v


PARTS = 4


def adam(own, who, factor, arrays, pieces, outs):
    d = arrays[0][0].shape[1]
    table, start = [], 0
    for which, layer, slot, g in sorted(pieces, key=lambda piece: piece[0]):
        steps = 1 if slot is None and which == 2 else PARTS
        table.append((which, layer, slot, g, start, steps))
        start += steps
    total = start
    names = sorted({t[0] for t in table})

    def block_of(which):
        return (1, d // PARTS, own) if which < 2 else (1, own // PARTS, d)

    def index_of(which):
        mine = [t for t in table if t[0] == which]

        def index(i, who):
            step = jnp.clip(i, mine[0][4], mine[-1][4] + mine[-1][5] - 1)
            at, row, col = jnp.int32(0), jnp.int32(0), jnp.int32(0)
            for _, layer, slot, _, first, steps in mine:
                here = (step >= first) & (step < first + steps)
                k = 4 if slot is None else who[slot]
                part = step - first
                at = jnp.where(here, layer, at)
                row = jnp.where(here, part if which < 2 else k * PARTS + part, row)
                col = jnp.where(here, k if which < 2 else 0, col)
            return at, row, col

        return index

    in_specs, operands = [pl.BlockSpec(memory_space=pltpu.SMEM)], [factor]
    out_specs, out_shape = [], []
    for which in names:
        spec = pl.BlockSpec(block_of(which), index_of(which))
        in_specs += [spec] * 3
        out_specs += [spec] * 3
        operands += list(arrays[which])
        out_shape += [jax.ShapeDtypeStruct(arrays[which][0].shape, t) for t in (BF16, F32, F32)]
    for _, _, _, g, first, steps in table:
        size = (g.shape[0] // steps, g.shape[1])
        in_specs.append(pl.BlockSpec(size, lambda i, who, first=first, steps=steps: (jnp.clip(i - first, 0, steps - 1), 0)))
        operands.append(g)
    aliases = {}
    if outs is not None:
        for n, which in enumerate(names):
            for k in range(3):
                aliases[1 + len(operands)] = 3 * n + k
                in_specs.append(pl.BlockSpec(memory_space=pl.ANY))
                operands.append(outs[which][k])

    def kernel(who_ref, f_ref, *refs):
        ins, grads = refs[: 3 * len(names)], refs[3 * len(names) : 3 * len(names) + len(table)]
        results = refs[len(refs) - 3 * len(names) :]
        i, f = pl.program_id(0), f_ref[0]
        for (which, _, _, _, first, steps), g_ref in zip(table, grads, strict=True):
            n = names.index(which)
            w, m, v = ins[3 * n : 3 * n + 3]
            wo, mo, vo = results[3 * n : 3 * n + 3]
            rows, cols = g_ref.shape
            some = 32

            @pl.when((i >= first) & (i < first + steps))
            def _():
                def body(r, carry):
                    at = pl.ds(pl.multiple_of(r * some, some), some)
                    new = adam_math(f, w[0, at, :cols], m[0, at, :cols], v[0, at, :cols], g_ref[at, :])
                    wo[0, at, :cols], mo[0, at, :cols], vo[0, at, :cols] = new
                    return carry

                lax.fori_loop(0, rows // some, body, 0)

    elements = sum(t[3].size for t in table)
    new = pl.pallas_call(
        kernel,
        grid_spec=pltpu.PrefetchScalarGridSpec(num_scalar_prefetch=1, grid=(total,), in_specs=in_specs, out_specs=out_specs),
        out_shape=out_shape,
        input_output_aliases=aliases,
        cost_estimate=pl.CostEstimate(flops=2000 * elements, bytes_accessed=22 * elements, transcendentals=elements),
        compiler_params=params(),
    )(who, *operands)
    result = list(outs) if outs is not None else [None] * 3
    for n, which in enumerate(names):
        result[which] = tuple(new[3 * n : 3 * n + 3])
    return result


def solution(mesh):
    def step(x, dy, wg, wu, wd, mg, mu, md, vg, vu, vd):
        me = lax.axis_index("dp")
        chip, core = me // 2, me % 2
        who = jnp.stack([me, chip * 2 + 1 - core, (1 - chip) * 2 + core, (1 - chip) * 2 + 1 - core])
        x, dy = x[0], dy[0]
        ff = wg.shape[2]
        own = ff // LANES // 4 * LANES

        def send(a, perm):
            return perm(a)

        dy_x, dy_d = send(dy, px), send(dy, pd)
        h1, a1, a0 = forward(x, wg, wu, wd)
        a1_x, a1_d = send(a1, px), send(a1, pd)
        dh1 = chain(a1, dy, h1, wg, wu, wd)
        dh1, a0 = lax.optimization_barrier((dh1, a0))
        dh1_x, dh1_d = send(dh1, px), send(dh1, pd)
        a0_x, a0_d = send(a0, px), send(a0, pd)
        a1_xd, dy_xd = send(a1_x, pd), send(dy_x, pd)
        top = slices(1, own, me, [a1, a1_d, a1_x, a1_xd], [dy, dy_d, dy_x, dy_xd], wg, wu, wd)
        top, a0_x, dh1_x = lax.optimization_barrier((top, a0_x, dh1_x))
        a0_xd, dh1_xd = send(a0_x, pd), send(dh1_x, pd)
        top_x = [send(top[n], px) for n in range(3)]
        top_d = [send(top[n], pd) for n in range(3)]
        low = slices(0, own, me, [a0, a0_d, a0_x, a0_xd], [dh1, dh1_d, dh1_x, dh1_xd], wg, wu, wd)
        total = jnp.sum(top[6] + low[6]).reshape(1)
        total = total + px(total)
        low, total = lax.optimization_barrier((low, total))
        low_x = [send(low[n], px) for n in range(3)]
        low_d = [send(low[n], pd) for n in range(3)]
        total = total + pd(total) + jnp.sum(top[7] + low[7])
        count = wg.size + wu.size + wd.size
        factor = jnp.minimum(1.0, 0.5 * lax.rsqrt(total / count + 1e-30))

        top_xd = [send(top_x[n], pd) for n in range(3)]
        low_xd = [send(low_x[n], pd) for n in range(2)]
        arrays = ((wg, mg, vg), (wu, mu, vu), (wd, md, vd))

        def pieces(layer, slot, gs, names=(0, 1, 2)):
            return [(n, layer, slot, gs[n]) for n in names]

        first = pieces(1, 0, top) + pieces(1, 1, top_d) + pieces(1, 2, top_x) + pieces(0, 0, low)
        shared = pieces(1, None, top[3:6]) + pieces(0, None, low[3:6])
        if SHARED_APART:
            outs = adam(LANES, jnp.full((1,), ff // LANES - 1, jnp.int32), factor, arrays, [(n, l, 0, g) for n, l, _, g in shared], None)
        else:
            first, outs = first + shared, None
        outs = adam(own, who, factor, arrays, first, outs)
        outs = adam(own, who, factor, arrays, pieces(1, 3, top_xd) + pieces(0, 1, low_d), outs)
        outs, low_x[2] = lax.optimization_barrier((outs, low_x[2]))
        low_xd.append(send(low_x[2], pd))
        outs = adam(own, who, factor, arrays, pieces(0, 2, low_x) + pieces(0, 3, low_xd, (0, 1)), outs)
        outs = adam(own, who, factor, arrays, pieces(0, 3, low_xd, (2,)), outs)
        return tuple(outs[name][which] for which in range(3) for name in range(3))

    return jax.shard_map(
        step,
        mesh=mesh,
        in_specs=(P(("rep", "dp"), None, None),) * 2 + (P(None, None, None),) * 9,
        out_specs=(P("rep", None, None),) * 9,
        check_vma=False,
    )
```

time: 1560 us -> 955 us (0.61)
  Pallas kernels: 0 us -> 707 us
  waiting for transfers between devices: 834 us -> 201 us
  matrix products: 471 us -> 0 us
  other arithmetic: 215 us -> 3.25 us
  starting transfers between devices: 0.04 us -> 29.7 us
    psum x1 -> x0, waiting for transfers between devices: 834 us -> none  [step(): summed[number] = [lax.psum(by_w[name], 'dp') for name in NAMES]]
    pallas_call x0 -> x8, Pallas kernels: none -> 707 us  [the longest x2 281 us: slices(): pl.pallas_call(lambda *refs: slices_kernel(own, *refs), grid_spec=pltpu.P...]
    dot_general x15 -> x0, matrix products: 471 us -> none  [the longest x5 167 us: layer(): gate = jnp.dot(a, w['w_gate'], preferred_element_type=jnp.float32)]
    ppermute x0 -> x32, waiting for transfers between devices: none -> 201 us  [the longest x11 191 us: px(): return lax.ppermute(a, 'dp', PX)]
    convert_element_type x2 -> x0, other arithmetic: 175 us -> none  [adamw(): return ((w - 0.02 * step).astype(jnp.bfloat16), m, v)]
    reduce_sum x4 -> x2, other arithmetic: 35.1 us -> 2.59 us  [the longest x1 1.29 us: step(): total = jnp.sum(top[6] + low[6]).reshape(1)]
    ppermute x0 -> x32, starting transfers between devices: none -> 29.7 us  [the longest x21 15 us: pd(): return lax.ppermute(a, 'dp', PD)]
  transfers between devices with their start and end apart: 1 -> 32, of which waited for: 1 -> 9; matrix products, arithmetic and copies ran while one was open for 0% -> 0% of each run, Pallas kernels for 0% -> 66%
where the time goes in v1:
time: 955 us; the launch traced here: 945 us
  Pallas kernels  707 us (74%)
  waiting for transfers between devices  201 us (21%)
  starting transfers between devices  29.7 us (3%)
    pallas_call x2, Pallas kernels, slices(): pl.pallas_call(lambda *refs: slices_kernel(own, *refs), grid_spec=pltpu.P...  281 us
    pallas_call x4, Pallas kernels, adam(): pl.pallas_call(kernel, grid_spec=pltpu.PrefetchScalarGridSpec(num_scalar_...  227 us
    ppermute x11, waiting for transfers between devices, px(): return lax.ppermute(a, 'dp', PX)  191 us
    pallas_call x1, Pallas kernels, chain(): pl.pallas_call(lambda *refs: chain_kernel(ff - (steps - 1) * BLOCK, *refs...  125 us
    pallas_call x1, Pallas kernels, forward(): pl.pallas_call(lambda *refs: forward_kernel(ff - (steps - 1) * BLOCK, *re...  74.3 us
  transfers between devices with their start and end apart: 32, of which 9 were waited for; matrix products, arithmetic and copies ran while one was open for 0% of the time, Pallas kernels for 66%

profile of v1, /device:TPU:0, one launch (start us, length us, event | category | flops | bytes accessed | tf_op | source)
XLA Modules:
  0.0 944.7 jit_solution(9030582263163319867)
XLA Ops:
  0.6 74.3 %forward.1 = (bf16[2048,896]{1,0:T(8,128)(2,1)}, bf16[2048,896]{1,0:T(8,128)(2,1)}, bf16[2048,896]{1,0:T(8,128)(2,1)}) custom-call(bf16[2048,896]{1,0:T(8,128)(2,1)} %bitcast.8, bf16[2,896,4736]{2,1,0:T(8,128)(2,1)} %refs_0_.6, bf16[2,896,4736]{2,1,0:T(8,128)(2,1)} %refs_3_.9, bf16[2,4736,896]{2,1,0:T(8,128)(2,1)} %refs_0_.7), custom_call_target="tpu_custom_call" | custom-call | flops 52143587328 | bytes 25460736 | tf_op jit(solution)/shard_map/forward/pallas_call | solution.py:102
  74.9 3.3 collective-permute-start.2
  78.2 0.5 collective-permute-start.4
  78.8 80.0 %collective-permute-done.2.refs_3_ = bf16[2048,896]{1,0:T(8,128)(2,1)} collective-permute-done((bf16[2048,896]{1,0:T(8,128)(2,1)}, bf16[2048,896]{1,0:T(8,128)(2,1)}, u32[]{:S(2)}, u32[]{:S(2)}) %collective-permute-start.2) | collective-permute-done | bytes 3670048 | tf_op jit(solution)/shard_map/ppermute | solution.py:29
  158.7 77.8 %collective-permute-done.5.refs_7_ = bf16[2048,896]{1,0:T(8,128)(2,1)} collective-permute-done((bf16[2048,896]{1,0:T(8,128)(2,1)}, bf16[2048,896]{1,0:T(8,128)(2,1)}, u32[]{:S(2)}, u32[]{:S(2)}) %collective-permute-start.5) | collective-permute-done | bytes 3670048 | tf_op jit(solution)/shard_map/ppermute | solution.py:29
  236.5 124.9 %chain.1.refs_5_ = bf16[2048,896]{1,0:T(8,128)(2,1)} custom-call(bf16[2048,896]{1,0:T(8,128)(2,1)} %get-tuple-element.88.refs_0_.refs_1_, bf16[2048,896]{1,0:T(8,128)(2,1)} %bitcast.11, bf16[2048,896]{1,0:T(8,128)(2,1)} %get-tuple-element.89.refs_2_, bf16[2,896,4736]{2,1,0:T(8,128)(2,1)} %refs_0_.6, bf16[2,896,4736]{2,1,0:T(8,128)(2,1)} %refs_3_.9, ...), custom_call_target="tpu_custom_call" | custom-call | flops 86905978880 | bytes 25460736 | tf_op jit(solution)/shard_map/chain/pallas_call | solution.py:173
  361.4 1.8 collective-permute-start.7
  363.7 140.2 %slices.2 = (bf16[896,1152]{1,0:T(8,128)(2,1)}, bf16[896,1152]{1,0:T(8,128)(2,1)}, bf16[1152,896]{1,0:T(8,128)(2,1)}, bf16[896,128]{1,0:T(8,128)(2,1)}, bf16[896...) custom-call(s32[1]{0:T(128)} %bitcast.refs_0_, ...), custom_call_target="tpu_custom_call" | custom-call | flops 112742891520 | bytes 29360128 | tf_op jit(solution)/shard_map/slices/pallas_call | solution.py:275
  504.0 18.1 %collective-permute-done.8.refs_7_ = bf16[2048,896]{1,0:T(8,128)(2,1)} collective-permute-done((bf16[2048,896]{1,0:T(8,128)(2,1)}, bf16[2048,896]{1,0:T(8,128)(2,1)}, u32[]{:S(2)}, u32[]{:S(2)}) %collective-permute-start.8) | collective-permute-done | bytes 3670048 | tf_op jit(solution)/shard_map/ppermute | solution.py:29
  522.1 0.5 collective-permute-start.9
  522.6 1.7 collective-permute-start.18
  524.7 4.2 collective-permute-done.11.refs_8_
  528.9 1.7 collective-permute-start.24
  530.6 3.5 collective-permute-done.9.refs_4_
  534.1 140.4 %slices.3 = (bf16[896,1152]{1,0:T(8,128)(2,1)}, bf16[896,1152]{1,0:T(8,128)(2,1)}, bf16[1152,896]{1,0:T(8,128)(2,1)}, bf16[896,128]{1,0:T(8,128)(2,1)}, bf16[896...) custom-call(s32[1]{0:T(128)} %bitcast.refs_0_, ...), custom_call_target="tpu_custom_call" | custom-call | flops 112742891520 | bytes 29360128 | tf_op jit(solution)/shard_map/slices/pallas_call | solution.py:275
  674.6 1.3 add_reduce_fusion.1
  675.9 1.7 collective-permute-start.12
  677.6 1.9 collective-permute-done.12
  680.9 0.5 collective-permute-start.29
  681.5 0.5 collective-permute-start.22
  682.0 2.0 collective-permute-done.28.refs_16_
  684.0 11.4 %collective-permute-start.13 = (f32[1]{0:T(128)}, f32[1]{0:T(128)}, u32[]{:S(2)}, u32[]{:S(2)}) collective-permute-start(f32[1]{0:T(128)} %add.40), channel_id=1, source_target_pairs={{0,1},{1,0},{2,3},{3,2},{4,5},{5,4},{6,7},{7,6}} | collective-permute-start | bytes 20 | tf_op jit(solution)/shard_map/ppermute | solution.py:33
  696.0 0.7 pad_add_fusion.who_ref
  696.6 1.3 add_reduce_fusion
  699.6 1.7 collective-permute-start.30
  701.6 1.8 collective-permute-start.16
  703.4 118.5 %shard_map.178 = (bf16[2,896,4736]{2,1,0:T(8,128)(2,1)}, f32[2,896,4736]{2,1,0:T(8,128)}, f32[2,896,4736]{2,1,0:T(8,128)}, bf16[2,896,4736]{2,1,0:T(8,128)(2,1)}...) custom-call(s32[4]{0:T(128)} %pad_add_fusion.who_ref, ...), custom_call_target="tpu_custom_call" | custom-call | flops 26148864000 | bytes 287637504 | tf_op jit(solution)/shard_map/pallas_call | solution.py:389
  822.2 13.2 %collective-permute-done.16.refs_11_ = bf16[896,1152]{1,0:T(8,128)(2,1)} collective-permute-done((bf16[896,1152]{1,0:T(8,128)(2,1)}, bf16[896,1152]{1,0:T(8,128)(2,1)}, u32[]{:S(2)}, u32[]{:S(2)}) %collective-permute-start.16) | collective-permute-done | bytes 2064416 | tf_op jit(solution)/shard_map/ppermute | solution.py:29
  835.4 53.4 %shard_map.179 = (bf16[2,896,4736]{2,1,0:T(8,128)(2,1)}, f32[2,896,4736]{2,1,0:T(8,128)}, f32[2,896,4736]{2,1,0:T(8,128)}, bf16[2,896,4736]{2,1,0:T(8,128)(2,1)}...) custom-call(s32[4]{0:T(128)} %pad_add_fusion.who_ref, ...), custom_call_target="tpu_custom_call", output_to_operand_aliasing={{0}: (17, {}), {1}: (18, {}), {2}: (19, {}), {3}: (20, {}),... | custom-call | flops 12386304000 | bytes 136249344 | tf_op jit(solution)/shard_map/pallas_call | solution.py:389
  888.8 0.5 collective-permute-start.31
  889.3 44.9 %shard_map.180 = (bf16[2,896,4736]{2,1,0:T(8,128)(2,1)}, f32[2,896,4736]{2,1,0:T(8,128)}, f32[2,896,4736]{2,1,0:T(8,128)}, bf16[2,896,4736]{2,1,0:T(8,128)(2,1)}...) custom-call(s32[4]{0:T(128)} %pad_add_fusion.who_ref, ...), custom_call_target="tpu_custom_call", output_to_operand_aliasing={{0}: (16, {}), {1}: (17, {}), {2}: (18, {}), {3}: (19, {}),... | custom-call | flops 10321920000 | bytes 113541120 | tf_op jit(solution)/shard_map/pallas_call | solution.py:389
  934.2 10.1 %shard_map.181 = (bf16[2,4736,896]{2,1,0:T(8,128)(2,1)}, f32[2,4736,896]{2,1,0:T(8,128)}, f32[2,4736,896]{2,1,0:T(8,128)}) custom-call(s32[4]{0:T(128)} %pad_add_fusion.who_ref, f32[1]{0:T(128)S(6)} %min.3.f_ref, bf16[2,4736,896]{2,1,0:T(8,128)(2,1)} %refs_0_.7, f32[2,4736,896]{2,1,0:T(8,128)} %refs_1_.9, ...), custom_call_target="tpu_custom_call", output_to_operand_aliasing={{0}: (6, {}), {1}: (7, {}), {2}: (8, {})} | custom-call | flops 2064384000 | bytes 22708224 | tf_op jit(solution)/shard_map/pallas_call | solution.py:389
  (47 shorter events, 2.5 us)
Async XLA Ops:
  74.9 83.8 %collective-permute-start.2 = (bf16[2048,896]{1,0:T(8,128)(2,1)}, bf16[2048,896]{1,0:T(8,128)(2,1)}, u32[]{:S(2)}, u32[]{:S(2)}) collective-permute-start(bf16[2048,896]{1,0:T(8,128)(2,1)} %get-tuple-element.88.refs_0_.refs_1_), channel_id=1, source_target_pairs={{0,2},{2,0},{1,3},{3,1},{4,6},{6,4},{5,7},{7,5}} | collective-permute-start | bytes 11010056 | tf_op jit(solution)/shard_map/ppermute | solution.py:29
  78.2 158.3 %collective-permute-start.5 = (bf16[2048,896]{1,0:T(8,128)(2,1)}, bf16[2048,896]{1,0:T(8,128)(2,1)}, u32[]{:S(2)}, u32[]{:S(2)}) collective-permute-start(bf16[2048,896]{1,0:T(8,128)(2,1)} %bitcast.9), channel_id=1, source_target_pairs={{0,2},{2,0},{1,3},{3,1},{4,6},{6,4},{5,7},{7,5}} | collective-permute-start | bytes 11010056 | tf_op jit(solution)/shard_map/ppermute | solution.py:29
  78.2 284.9 %collective-permute-start.1 = (bf16[2048,896]{1,0:T(8,128)(2,1)}, bf16[2048,896]{1,0:T(8,128)(2,1)}, u32[]{:S(2)}, u32[]{:S(2)}) collective-permute-start(bf16[2048,896]{1,0:T(8,128)(2,1)} %get-tuple-element.88.refs_0_.refs_1_), channel_id=1, source_target_pairs={{0,1},{1,0},{2,3},{3,2},{4,5},{5,4},{6,7},{7,6}} | collective-permute-start | bytes 11010056 | tf_op jit(solution)/shard_map/ppermute | solution.py:33
  78.2 285.1 %collective-permute-start.4 = (bf16[2048,896]{1,0:T(8,128)(2,1)}, bf16[2048,896]{1,0:T(8,128)(2,1)}, u32[]{:S(2)}, u32[]{:S(2)}) collective-permute-start(bf16[2048,896]{1,0:T(8,128)(2,1)} %bitcast.10), channel_id=1, source_target_pairs={{0,1},{1,0},{2,3},{3,2},{4,5},{5,4},{6,7},{7,6}} | collective-permute-start | bytes 11010056 | tf_op jit(solution)/shard_map/ppermute | solution.py:33
  158.7 205.0 %collective-permute-start.3 = (bf16[2048,896]{1,0:T(8,128)(2,1)}, bf16[2048,896]{1,0:T(8,128)(2,1)}, u32[]{:S(2)}, u32[]{:S(2)}) collective-permute-start(bf16[2048,896]{1,0:T(8,128)(2,1)} %collective-permute-done.2.refs_3_), channel_id=1, source_target_pairs={{0,1},{1,0},{2,3},{3,2},{4,5},{5,4},{6,7},{7,6}} | collective-permute-start | bytes 11010056 | tf_op jit(solution)/shard_map/ppermute | solution.py:33
  236.5 127.2 %collective-permute-start.6 = (bf16[2048,896]{1,0:T(8,128)(2,1)}, bf16[2048,896]{1,0:T(8,128)(2,1)}, u32[]{:S(2)}, u32[]{:S(2)}) collective-permute-start(bf16[2048,896]{1,0:T(8,128)(2,1)} %collective-permute-done.5.refs_7_), channel_id=1, source_target_pairs={{0,1},{1,0},{2,3},{3,2},{4,5},{5,4},{6,7},{7,6}} | collective-permute-start | bytes 11010056 | tf_op jit(solution)/shard_map/ppermute | solution.py:33
  361.4 142.6 %collective-permute-start.7 = (bf16[2048,896]{1,0:T(8,128)(2,1)}, bf16[2048,896]{1,0:T(8,128)(2,1)}, u32[]{:S(2)}, u32[]{:S(2)}) collective-permute-start(bf16[2048,896]{1,0:T(8,128)(2,1)} %get-tuple-element.91.refs_1_), channel_id=1, source_target_pairs={{0,2},{2,0},{1,3},{3,1},{4,6},{6,4},{5,7},{7,5}} | collective-permute-start | bytes 11010056 | tf_op jit(solution)/shard_map/ppermute | solution.py:29
  363.2 161.2 %collective-permute-start = (bf16[2048,896]{1,0:T(8,128)(2,1)}, bf16[2048,896]{1,0:T(8,128)(2,1)}, u32[]{:S(2)}, u32[]{:S(2)}) collective-permute-start(bf16[2048,896]{1,0:T(8,128)(2,1)} %get-tuple-element.91.refs_1_), channel_id=1, source_target_pairs={{0,1},{1,0},{2,3},{3,2},{4,5},{5,4},{6,7},{7,6}} | collective-permute-start | bytes 11010056 | tf_op jit(solution)/shard_map/ppermute | solution.py:33
  363.4 158.7 %collective-permute-start.8 = (bf16[2048,896]{1,0:T(8,128)(2,1)}, bf16[2048,896]{1,0:T(8,128)(2,1)}, u32[]{:S(2)}, u32[]{:S(2)}) collective-permute-start(bf16[2048,896]{1,0:T(8,128)(2,1)} %chain.1.refs_5_), channel_id=1, source_target_pairs={{0,2},{2,0},{1,3},{3,1},{4,6},{6,4},{5,7},{7,5}} | collective-permute-start | bytes 11010056 | tf_op jit(solution)/shard_map/ppermute | solution.py:29
  363.7 160.7 %collective-permute-start.10 = (bf16[2048,896]{1,0:T(8,128)(2,1)}, bf16[2048,896]{1,0:T(8,128)(2,1)}, u32[]{:S(2)}, u32[]{:S(2)}) collective-permute-start(bf16[2048,896]{1,0:T(8,128)(2,1)} %chain.1.refs_5_), channel_id=1, source_target_pairs={{0,1},{1,0},{2,3},{3,2},{4,5},{5,4},{6,7},{7,6}} | collective-permute-start | bytes 11010056 | tf_op jit(solution)/shard_map/ppermute | solution.py:33
  522.1 6.8 collective-permute-start.11
  522.1 12.0 %collective-permute-start.9 = (bf16[2048,896]{1,0:T(8,128)(2,1)}, bf16[2048,896]{1,0:T(8,128)(2,1)}, u32[]{:S(2)}, u32[]{:S(2)}) collective-permute-start(bf16[2048,896]{1,0:T(8,128)(2,1)} %collective-permute-done.7.refs_3_), channel_id=1, source_target_pairs={{0,1},{1,0},{2,3},{3,2},{4,5},{5,4},{6,7},{7,6}} | collective-permute-start | bytes 11010056 | tf_op jit(solution)/shard_map/ppermute | solution.py:33
  522.6 158.2 %collective-permute-start.18 = (bf16[896,1152]{1,0:T(8,128)(2,1)}, bf16[896,1152]{1,0:T(8,128)(2,1)}, u32[]{:S(2)}, u32[]{:S(2)}) collective-permute-start(bf16[896,1152]{1,0:T(8,128)(2,1)} %get-tuple-element.117.refs_9_), channel_id=1, source_target_pairs={{0,2},{2,0},{1,3},{3,1},{4,6},{6,4},{5,7},{7,5}} | collective-permute-start | bytes 6193160 | tf_op jit(solution)/shard_map/ppermute | solution.py:29
  524.4 157.5 %collective-permute-start.27 = (bf16[896,1152]{1,0:T(8,128)(2,1)}, bf16[896,1152]{1,0:T(8,128)(2,1)}, u32[]{:S(2)}, u32[]{:S(2)}) collective-permute-start(bf16[896,1152]{1,0:T(8,128)(2,1)} %get-tuple-element.117.refs_9_), channel_id=1, source_target_pairs={{0,1},{1,0},{2,3},{3,2},{4,5},{5,4},{6,7},{7,6}} | collective-permute-start | bytes 6193160 | tf_op jit(solution)/shard_map/ppermute | solution.py:33
  524.4 157.0 %collective-permute-start.21 = (bf16[896,1152]{1,0:T(8,128)(2,1)}, bf16[896,1152]{1,0:T(8,128)(2,1)}, u32[]{:S(2)}, u32[]{:S(2)}) collective-permute-start(bf16[896,1152]{1,0:T(8,128)(2,1)} %get-tuple-element.118.refs_15_), channel_id=1, source_target_pairs={{0,2},{2,0},{1,3},{3,1},{4,6},{6,4},{5,7},{7,5}} | collective-permute-start | bytes 6193160 | tf_op jit(solution)/shard_map/ppermute | solution.py:29
  528.9 152.6 %collective-permute-start.24 = (bf16[1152,896]{1,0:T(8,128)(2,1)}, bf16[1152,896]{1,0:T(8,128)(2,1)}, u32[]{:S(2)}, u32[]{:S(2)}) collective-permute-start(bf16[1152,896]{1,0:T(8,128)(2,1)} %get-tuple-element.119.refs_21_), channel_id=1, source_target_pairs={{0,2},{2,0},{1,3},{3,1},{4,6},{6,4},{5,7},{7,5}} | collective-permute-start | bytes 6193160 | tf_op jit(solution)/shard_map/ppermute | solution.py:29
  675.9 3.7 collective-permute-start.12
  679.5 4.5 collective-permute-start.28
  680.9 18.3 %collective-permute-start.29 = (bf16[1152,896]{1,0:T(8,128)(2,1)}, bf16[1152,896]{1,0:T(8,128)(2,1)}, u32[]{:S(2)}, u32[]{:S(2)}) collective-permute-start(bf16[1152,896]{1,0:T(8,128)(2,1)} %get-tuple-element.119.refs_21_), channel_id=1, source_target_pairs={{0,1},{1,0},{2,3},{3,2},{4,5},{5,4},{6,7},{7,6}} | collective-permute-start | bytes 6193160 | tf_op jit(solution)/shard_map/ppermute | solution.py:33
  681.4 18.2 %collective-permute-start.19 = (bf16[896,1152]{1,0:T(8,128)(2,1)}, bf16[896,1152]{1,0:T(8,128)(2,1)}, u32[]{:S(2)}, u32[]{:S(2)}) collective-permute-start(bf16[896,1152]{1,0:T(8,128)(2,1)} %collective-permute-done.18.refs_11_), channel_id=1, source_target_pairs={{0,1},{1,0},{2,3},{3,2},{4,5},{5,4},{6,7},{7,6}} | collective-permute-start | bytes 6193160 | tf_op jit(solution)/shard_map/ppermute | solution.py:33
  681.5 19.9 %collective-permute-start.22 = (bf16[896,1152]{1,0:T(8,128)(2,1)}, bf16[896,1152]{1,0:T(8,128)(2,1)}, u32[]{:S(2)}, u32[]{:S(2)}) collective-permute-start(bf16[896,1152]{1,0:T(8,128)(2,1)} %collective-permute-done.21.refs_17_), channel_id=1, source_target_pairs={{0,1},{1,0},{2,3},{3,2},{4,5},{5,4},{6,7},{7,6}} | collective-permute-start | bytes 6193160 | tf_op jit(solution)/shard_map/ppermute | solution.py:33
  681.9 19.7 %collective-permute-start.25 = (bf16[1152,896]{1,0:T(8,128)(2,1)}, bf16[1152,896]{1,0:T(8,128)(2,1)}, u32[]{:S(2)}, u32[]{:S(2)}) collective-permute-start(bf16[1152,896]{1,0:T(8,128)(2,1)} %collective-permute-done.24.refs_23_), channel_id=1, source_target_pairs={{0,1},{1,0},{2,3},{3,2},{4,5},{5,4},{6,7},{7,6}} | collective-permute-start | bytes 6193160 | tf_op jit(solution)/shard_map/ppermute | solution.py:33
  684.0 11.8 %collective-permute-start.13 = (f32[1]{0:T(128)}, f32[1]{0:T(128)}, u32[]{:S(2)}, u32[]{:S(2)}) collective-permute-start(f32[1]{0:T(128)} %add.40), channel_id=1, source_target_pairs={{0,1},{1,0},{2,3},{3,2},{4,5},{5,4},{6,7},{7,6}} | collective-permute-start | bytes 20 | tf_op jit(solution)/shard_map/ppermute | solution.py:33
  695.8 5.8 collective-permute-start.20
  699.2 136.2 %collective-permute-start.26 = (bf16[1152,896]{1,0:T(8,128)(2,1)}, bf16[1152,896]{1,0:T(8,128)(2,1)}, u32[]{:S(2)}, u32[]{:S(2)}) collective-permute-start(bf16[1152,896]{1,0:T(8,128)(2,1)} %get-tuple-element.120.refs_24_), channel_id=1, source_target_pairs={{0,1},{1,0},{2,3},{3,2},{4,5},{5,4},{6,7},{7,6}} | collective-permute-start | bytes 6193160 | tf_op jit(solution)/shard_map/ppermute | solution.py:33
  699.6 189.2 %collective-permute-start.30 = (bf16[1152,896]{1,0:T(8,128)(2,1)}, bf16[1152,896]{1,0:T(8,128)(2,1)}, u32[]{:S(2)}, u32[]{:S(2)}) collective-permute-start(bf16[1152,896]{1,0:T(8,128)(2,1)} %get-tuple-element.120.refs_24_), channel_id=1, source_target_pairs={{0,2},{2,0},{1,3},{3,1},{4,6},{6,4},{5,7},{7,5}} | collective-permute-start | bytes 6193160 | tf_op jit(solution)/shard_map/ppermute | solution.py:29
  701.3 120.6 %collective-permute-start.14 = (bf16[896,1152]{1,0:T(8,128)(2,1)}, bf16[896,1152]{1,0:T(8,128)(2,1)}, u32[]{:S(2)}, u32[]{:S(2)}) collective-permute-start(bf16[896,1152]{1,0:T(8,128)(2,1)} %get-tuple-element.115.refs_12_), channel_id=1, source_target_pairs={{0,2},{2,0},{1,3},{3,1},{4,6},{6,4},{5,7},{7,5}} | collective-permute-start | bytes 6193160 | tf_op jit(solution)/shard_map/ppermute | solution.py:29
  701.6 133.7 %collective-permute-start.23 = (bf16[896,1152]{1,0:T(8,128)(2,1)}, bf16[896,1152]{1,0:T(8,128)(2,1)}, u32[]{:S(2)}, u32[]{:S(2)}) collective-permute-start(bf16[896,1152]{1,0:T(8,128)(2,1)} %get-tuple-element.116.refs_18_), channel_id=1, source_target_pairs={{0,1},{1,0},{2,3},{3,2},{4,5},{5,4},{6,7},{7,6}} | collective-permute-start | bytes 6193160 | tf_op jit(solution)/shard_map/ppermute | solution.py:33
  701.6 133.7 %collective-permute-start.16 = (bf16[896,1152]{1,0:T(8,128)(2,1)}, bf16[896,1152]{1,0:T(8,128)(2,1)}, u32[]{:S(2)}, u32[]{:S(2)}) collective-permute-start(bf16[896,1152]{1,0:T(8,128)(2,1)} %get-tuple-element.116.refs_18_), channel_id=1, source_target_pairs={{0,2},{2,0},{1,3},{3,1},{4,6},{6,4},{5,7},{7,5}} | collective-permute-start | bytes 6193160 | tf_op jit(solution)/shard_map/ppermute | solution.py:29
  821.9 67.3 %collective-permute-start.15 = (bf16[896,1152]{1,0:T(8,128)(2,1)}, bf16[896,1152]{1,0:T(8,128)(2,1)}, u32[]{:S(2)}, u32[]{:S(2)}) collective-permute-start(bf16[896,1152]{1,0:T(8,128)(2,1)} %collective-permute-done.14.refs_9_), channel_id=1, source_target_pairs={{0,1},{1,0},{2,3},{3,2},{4,5},{5,4},{6,7},{7,6}} | collective-permute-start | bytes 6193160 | tf_op jit(solution)/shard_map/ppermute | solution.py:33
  835.4 53.9 %collective-permute-start.17 = (bf16[896,1152]{1,0:T(8,128)(2,1)}, bf16[896,1152]{1,0:T(8,128)(2,1)}, u32[]{:S(2)}, u32[]{:S(2)}) collective-permute-start(bf16[896,1152]{1,0:T(8,128)(2,1)} %collective-permute-done.16.refs_11_), channel_id=1, source_target_pairs={{0,1},{1,0},{2,3},{3,2},{4,5},{5,4},{6,7},{7,6}} | collective-permute-start | bytes 6193160 | tf_op jit(solution)/shard_map/ppermute | solution.py:33
  888.8 45.3 %collective-permute-start.31 = (bf16[1152,896]{1,0:T(8,128)(2,1)}, bf16[1152,896]{1,0:T(8,128)(2,1)}, u32[]{:S(2)}, u32[]{:S(2)}) collective-permute-start(bf16[1152,896]{1,0:T(8,128)(2,1)} %collective-permute-done.30.refs_13_), channel_id=1, source_target_pairs={{0,1},{1,0},{2,3},{3,2},{4,5},{5,4},{6,7},{7,6}} | collective-permute-start | bytes 6193160 | tf_op jit(solution)/shard_map/ppermute | solution.py:33
  (2 other events, 326.9 us)

commit v2 on v1

--- a/solution.py
+++ b/solution.py
@@ -1,5 +1,6 @@
 import jax
 import jax.numpy as jnp
+import numpy as np
 from jax import lax
 from jax.experimental import pallas as pl
 from jax.experimental.pallas import tpu as pltpu
@@ -14,7 +15,6 @@
 LANES = 128
 BLOCK = 512
 ROWS = 512
-SHARED_APART = False
 
 
 def dot(a, b, dims):
@@ -311,100 +311,129 @@
     return (w - 0.02 * (m * lax.rsqrt(v + 1e-8) + 0.1 * w)).astype(BF16), m, v
 
 
-PARTS = 4
-
-
-def adam(own, who, factor, arrays, pieces, outs):
-    d = arrays[0][0].shape[1]
-    table, start = [], 0
-    for which, layer, slot, g in sorted(pieces, key=lambda piece: piece[0]):
-        steps = 1 if slot is None and which == 2 else PARTS
-        table.append((which, layer, slot, g, start, steps))
-        start += steps
-    total = start
-    names = sorted({t[0] for t in table})
-
-    def block_of(which):
-        return (1, d // PARTS, own) if which < 2 else (1, own // PARTS, d)
-
-    def index_of(which):
-        mine = [t for t in table if t[0] == which]
-
-        def index(i, who):
-            step = jnp.clip(i, mine[0][4], mine[-1][4] + mine[-1][5] - 1)
-            at, row, col = jnp.int32(0), jnp.int32(0), jnp.int32(0)
-            for _, layer, slot, _, first, steps in mine:
-                here = (step >= first) & (step < first + steps)
-                k = 4 if slot is None else who[slot]
-                part = step - first
-                at = jnp.where(here, layer, at)
-                row = jnp.where(here, part if which < 2 else k * PARTS + part, row)
-                col = jnp.where(here, k if which < 2 else 0, col)
-            return at, row, col
-
-        return index
-
-    in_specs, operands = [pl.BlockSpec(memory_space=pltpu.SMEM)], [factor]
-    out_specs, out_shape = [], []
-    for which in names:
-        spec = pl.BlockSpec(block_of(which), index_of(which))
-        in_specs += [spec] * 3
-        out_specs += [spec] * 3
-        operands += list(arrays[which])
-        out_shape += [jax.ShapeDtypeStruct(arrays[which][0].shape, t) for t in (BF16, F32, F32)]
-    for _, _, _, g, first, steps in table:
-        size = (g.shape[0] // steps, g.shape[1])
-        in_specs.append(pl.BlockSpec(size, lambda i, who, first=first, steps=steps: (jnp.clip(i - first, 0, steps - 1), 0)))
-        operands.append(g)
-    aliases = {}
-    if outs is not None:
-        for n, which in enumerate(names):
+SLOTS, AHEAD = 6, 3
+
+
+def adam(own, factor, who, arrays, pieces, outs):
+    d, _ = arrays[0][0].shape[1:]
+    shapes = ((d // 8, own), (LANES, d), (d, LANES))
+    rows = []
+    for n, (which, layer, slot, g) in enumerate(pieces):
+        kind = 1 if which == 2 else 2 if slot == 4 else 0
+        for r in range(0, g.shape[0], shapes[kind][0]):
+            rows.append((kind, which, layer, n, slot, r, *((own, 0) if which == 2 else (0, own))))
+    table = np.array(rows, np.int32).T
+    total = len(rows)
+    kinds = sorted({row[0] for row in rows})
+    n_in = 9 + len(pieces)
+
+    def kernel(table_ref, who_ref, f_ref, *refs):
+        weights, grads = refs[:9], refs[9:n_in]
+        refs = refs[n_in + (9 if outs is not None else 0) :]
+        results, scratch = refs[:9], refs[9:]
+        buffers = {kind: scratch[4 * n : 4 * n + 4] for n, kind in enumerate(kinds)}
+        sem_in, sem_out = scratch[-2:]
+        f = f_ref[0]
+
+        def place(step):
+            kind, which, layer = (table_ref[n, step] for n in range(3))
+            unit = who_ref[table_ref[4, step]]
+            row, col = table_ref[5, step] + table_ref[6, step] * unit, table_ref[7, step] * unit
+            return kind, which, lambda shape: (layer, pl.ds(pl.multiple_of(row, 16), shape[0]), pl.ds(pl.multiple_of(col, LANES), shape[1]))
+
+        def fetch(step):
+            slot = lax.rem(step, SLOTS)
+            kind, which, at = place(step)
             for k in range(3):
-                aliases[1 + len(operands)] = 3 * n + k
-                in_specs.append(pl.BlockSpec(memory_space=pl.ANY))
-                operands.append(outs[which][k])
-
-    def kernel(who_ref, f_ref, *refs):
-        ins, grads = refs[: 3 * len(names)], refs[3 * len(names) : 3 * len(names) + len(table)]
-        results = refs[len(refs) - 3 * len(names) :]
-        i, f = pl.program_id(0), f_ref[0]
-        for (which, _, _, _, first, steps), g_ref in zip(table, grads, strict=True):
-            n = names.index(which)
-            w, m, v = ins[3 * n : 3 * n + 3]
-            wo, mo, vo = results[3 * n : 3 * n + 3]
-            rows, cols = g_ref.shape
-            some = 32
-
-            @pl.when((i >= first) & (i < first + steps))
+                its = [q for q in kinds if (q == 1) == (k == 2)]
+                for q in its:
+
+                    @pl.when((which == k) & (kind == q))
+                    def _():
+                        for n in range(3):
+                            pltpu.make_async_copy(weights[3 * k + n].at[at(shapes[q])], buffers[q][n].at[slot], sem_in.at[n, slot]).start()
+
+            piece, row = table_ref[3, step], table_ref[5, step]
+            for n, (which_, _, slot_, _) in enumerate(pieces):
+                q = 1 if which_ == 2 else 2 if slot_ == 4 else 0
+
+                @pl.when(piece == n)
+                def _():
+                    rows_ = pl.ds(pl.multiple_of(row, 16), shapes[q][0])
+                    pltpu.make_async_copy(grads[n].at[rows_, :], buffers[q][3].at[slot], sem_in.at[3, slot]).start()
+
+        def stored(step, do):
+            slot = lax.rem(step, SLOTS)
+            kind, which, at = place(step)
+            for k in range(3):
+                for q in [q for q in kinds if (q == 1) == (k == 2)]:
+
+                    @pl.when((which == k) & (kind == q))
+                    def _():
+                        for n in range(3):
+                            do(pltpu.make_async_copy(buffers[q][n].at[slot], results[3 * k + n].at[at(shapes[q])], sem_out.at[n, slot]))
+
+        for step in range(min(AHEAD, total)):
+            fetch(jnp.int32(step))
+
+        def body(step, carry):
+            @pl.when(step + AHEAD < total)
             def _():
-                def body(r, carry):
-                    at = pl.ds(pl.multiple_of(r * some, some), some)
-                    new = adam_math(f, w[0, at, :cols], m[0, at, :cols], v[0, at, :cols], g_ref[at, :])
-                    wo[0, at, :cols], mo[0, at, :cols], vo[0, at, :cols] = new
-                    return carry
-
-                lax.fori_loop(0, rows // some, body, 0)
-
-    elements = sum(t[3].size for t in table)
+                @pl.when(step + AHEAD >= SLOTS)
+                def _():
+                    stored(step + AHEAD - SLOTS, lambda copy: copy.wait())
+
+                fetch(step + AHEAD)
+
+            slot = lax.rem(step, SLOTS)
+            for q in kinds:
+
+                @pl.when(table_ref[0, step] == q)
+                def _():
+                    w, m, v, g = buffers[q]
+                    for n in range(3):
+                        pltpu.make_async_copy(weights[n].at[0, pl.ds(0, shapes[q][0]), pl.ds(0, shapes[q][1])], buffers[q][n].at[slot], sem_in.at[n, slot]).wait()
+                    pltpu.make_async_copy(buffers[q][3].at[slot], buffers[q][3].at[slot], sem_in.at[3, slot]).wait()
+                    some = 16 if shapes[q][1] > d else 32 if shapes[q][1] > LANES else 128
+
+                    def part(r, carry):
+                        at = pl.ds(pl.multiple_of(r * some, some), some)
+                        new = adam_math(f, w[slot, at, :], m[slot, at, :], v[slot, at, :], g[slot, at, :])
+                        w[slot, at, :], m[slot, at, :], v[slot, at, :] = new
+                        return carry
+
+                    lax.fori_loop(0, shapes[q][0] // some, part, 0)
+
+            stored(step, lambda copy: copy.start())
+            return carry
+
+        lax.fori_loop(0, total, body, 0)
+        for step in range(max(0, total - SLOTS), total):
+            stored(jnp.int32(step), lambda copy: copy.wait())
+
+    any_ = pl.BlockSpec(memory_space=pl.ANY)
+    given = [a for three in arrays for a in three]
+    before = [a for three in outs for a in three] if outs is not None else []
+    elements = sum(piece[3].size for piece in pieces)
     new = pl.pallas_call(
         kernel,
-        grid_spec=pltpu.PrefetchScalarGridSpec(num_scalar_prefetch=1, grid=(total,), in_specs=in_specs, out_specs=out_specs),
-        out_shape=out_shape,
-        input_output_aliases=aliases,
+        in_specs=[pl.BlockSpec(memory_space=pltpu.SMEM)] * 3 + [any_] * (n_in + len(before)),
+        out_specs=[any_] * 9,
+        out_shape=[jax.ShapeDtypeStruct(a.shape, a.dtype) for a in given],
+        scratch_shapes=[pltpu.VMEM((SLOTS, *shapes[q]), t) for q in kinds for t in (BF16, F32, F32, BF16)]
+        + [pltpu.SemaphoreType.DMA((4, SLOTS)), pltpu.SemaphoreType.DMA((3, SLOTS))],
+        input_output_aliases={3 + n_in + n: n for n in range(len(before))},
         cost_estimate=pl.CostEstimate(flops=2000 * elements, bytes_accessed=22 * elements, transcendentals=elements),
         compiler_params=params(),
-    )(who, *operands)
-    result = list(outs) if outs is not None else [None] * 3
-    for n, which in enumerate(names):
-        result[which] = tuple(new[3 * n : 3 * n + 3])
-    return result
+    )(table, who, factor, *given, *(piece[3] for piece in pieces), *before)
+    return tuple(tuple(new[3 * n : 3 * n + 3]) for n in range(3))
 
 
 def solution(mesh):
     def step(x, dy, wg, wu, wd, mg, mu, md, vg, vu, vd):
         me = lax.axis_index("dp")
-        chip, core = me // 2, me % 2
-        who = jnp.stack([me, chip * 2 + 1 - core, (1 - chip) * 2 + core, (1 - chip) * 2 + 1 - core])
+        places = jnp.arange(5, dtype=jnp.int32)
+        who = jnp.where(places < 4, me ^ places, places)
         x, dy = x[0], dy[0]
         ff = wg.shape[2]
         own = ff // LANES // 4 * LANES
@@ -415,10 +444,9 @@
         dy_x, dy_d = send(dy, px), send(dy, pd)
         h1, a1, a0 = forward(x, wg, wu, wd)
         a1_x, a1_d = send(a1, px), send(a1, pd)
+        a0_x, a0_d = send(a0, px), send(a0, pd)
         dh1 = chain(a1, dy, h1, wg, wu, wd)
-        dh1, a0 = lax.optimization_barrier((dh1, a0))
         dh1_x, dh1_d = send(dh1, px), send(dh1, pd)
-        a0_x, a0_d = send(a0, px), send(a0, pd)
         a1_xd, dy_xd = send(a1_x, pd), send(dy_x, pd)
         top = slices(1, own, me, [a1, a1_d, a1_x, a1_xd], [dy, dy_d, dy_x, dy_xd], wg, wu, wd)
         top, a0_x, dh1_x = lax.optimization_barrier((top, a0_x, dh1_x))
@@ -443,17 +471,13 @@
             return [(n, layer, slot, gs[n]) for n in names]
 
         first = pieces(1, 0, top) + pieces(1, 1, top_d) + pieces(1, 2, top_x) + pieces(0, 0, low)
-        shared = pieces(1, None, top[3:6]) + pieces(0, None, low[3:6])
-        if SHARED_APART:
-            outs = adam(LANES, jnp.full((1,), ff // LANES - 1, jnp.int32), factor, arrays, [(n, l, 0, g) for n, l, _, g in shared], None)
-        else:
-            first, outs = first + shared, None
-        outs = adam(own, who, factor, arrays, first, outs)
-        outs = adam(own, who, factor, arrays, pieces(1, 3, top_xd) + pieces(0, 1, low_d), outs)
+        shared = pieces(1, 4, top[3:6]) + pieces(0, 4, low[3:6])
+        outs = adam(own, factor, who, arrays, first + shared, None)
+        outs = adam(own, factor, who, arrays, pieces(1, 3, top_xd) + pieces(0, 1, low_d), outs)
         outs, low_x[2] = lax.optimization_barrier((outs, low_x[2]))
         low_xd.append(send(low_x[2], pd))
-        outs = adam(own, who, factor, arrays, pieces(0, 2, low_x) + pieces(0, 3, low_xd, (0, 1)), outs)
-        outs = adam(own, who, factor, arrays, pieces(0, 3, low_xd, (2,)), outs)
+        outs = adam(own, factor, who, arrays, pieces(0, 2, low_x) + pieces(0, 3, low_xd, (0, 1)), outs)
+        outs = adam(own, factor, who, arrays, pieces(0, 3, low_xd, (2,)), outs)
         return tuple(outs[name][which] for which in range(3) for name in range(3))
 
     return jax.shard_map(

time: 955 us -> 942 us (0.986)
  Pallas kernels: 707 us -> 673 us
  waiting for transfers between devices: 201 us -> 223 us
    pallas_call x4, Pallas kernels: 227 us -> 194 us  [adam(): pl.pallas_call(kernel, in_specs=[pl.BlockSpec(memory_space=pltpu.SMEM)] *...]
    ppermute x11, waiting for transfers between devices: 191 us -> 213 us  [px(): return lax.ppermute(a, 'dp', PX)]
  transfers between devices with their start and end apart: 32 -> 32, of which waited for: 9 -> 9; matrix products, arithmetic and copies ran while one was open for 0% -> 0% of each run, Pallas kernels for 66% -> 63%
where the time goes in v2:
time: 942 us; the launch traced here: 933 us
  Pallas kernels  673 us (71%)
  waiting for transfers between devices  223 us (24%)
  starting transfers between devices  29.7 us (3%)
    pallas_call x2, Pallas kernels, slices(): pl.pallas_call(lambda *refs: slices_kernel(own, *refs), grid_spec=pltpu.P...  281 us
    ppermute x11, waiting for transfers between devices, px(): return lax.ppermute(a, 'dp', PX)  213 us
    pallas_call x4, Pallas kernels, adam(): pl.pallas_call(kernel, in_specs=[pl.BlockSpec(memory_space=pltpu.SMEM)] *...  194 us
    pallas_call x1, Pallas kernels, chain(): pl.pallas_call(lambda *refs: chain_kernel(ff - (steps - 1) * BLOCK, *refs...  125 us
    pallas_call x1, Pallas kernels, forward(): pl.pallas_call(lambda *refs: forward_kernel(ff - (steps - 1) * BLOCK, *re...  74.3 us
  transfers between devices with their start and end apart: 32, of which 9 were waited for; matrix products, arithmetic and copies ran while one was open for 0% of the time, Pallas kernels for 63%

profile of v2, /device:TPU:0, one launch (start us, length us, event | category | flops | bytes accessed | tf_op | source)
XLA Modules:
  0.0 933.3 jit_solution(2043390199307433591)
XLA Ops:
  0.6 74.3 %forward.1 = (bf16[2048,896]{1,0:T(8,128)(2,1)}, bf16[2048,896]{1,0:T(8,128)(2,1)}, bf16[2048,896]{1,0:T(8,128)(2,1)}) custom-call(bf16[2048,896]{1,0:T(8,128)(2,1)} %bitcast.5, bf16[2,896,4736]{2,1,0:T(8,128)(2,1)} %refs_0_.7, bf16[2,896,4736]{2,1,0:T(8,128)(2,1)} %refs_3_.11, bf16[2,4736,896]{2,1,0:T(8,128)(2,1)} %refs_6_.7), custom_call_target="tpu_custom_call" | custom-call | flops 52143587328 | bytes 25460736 | tf_op jit(solution)/shard_map/forward/pallas_call | solution.py:102
  74.9 3.3 collective-permute-start.2
  78.2 0.5 collective-permute-start.4
  78.8 80.0 %collective-permute-done.2.refs_3_ = bf16[2048,896]{1,0:T(8,128)(2,1)} collective-permute-done((bf16[2048,896]{1,0:T(8,128)(2,1)}, bf16[2048,896]{1,0:T(8,128)(2,1)}, u32[]{:S(2)}, u32[]{:S(2)}) %collective-permute-start.2) | collective-permute-done | bytes 3670048 | tf_op jit(solution)/shard_map/ppermute | solution.py:29
  158.7 77.8 %collective-permute-done.5.refs_7_ = bf16[2048,896]{1,0:T(8,128)(2,1)} collective-permute-done((bf16[2048,896]{1,0:T(8,128)(2,1)}, bf16[2048,896]{1,0:T(8,128)(2,1)}, u32[]{:S(2)}, u32[]{:S(2)}) %collective-permute-start.5) | collective-permute-done | bytes 3670048 | tf_op jit(solution)/shard_map/ppermute | solution.py:29
  236.5 124.9 %chain.1.refs_5_ = bf16[2048,896]{1,0:T(8,128)(2,1)} custom-call(bf16[2048,896]{1,0:T(8,128)(2,1)} %get-tuple-element.93.refs_1_.refs_0_, bf16[2048,896]{1,0:T(8,128)(2,1)} %bitcast.8, bf16[2048,896]{1,0:T(8,128)(2,1)} %get-tuple-element.102.refs_2_, bf16[2,896,4736]{2,1,0:T(8,128)(2,1)} %refs_0_.7, bf16[2,896,4736]{2,1,0:T(8,128)(2,1)} %refs_3_.11, ...), custom_call_target="tpu_custom_call" | custom-call | flops 86905978880 | bytes 25460736 | tf_op jit(solution)/shard_map/chain/pallas_call | solution.py:173
  361.4 1.8 collective-permute-start.8
  363.7 140.2 %slices.2 = (bf16[896,1152]{1,0:T(8,128)(2,1)}, bf16[896,1152]{1,0:T(8,128)(2,1)}, bf16[1152,896]{1,0:T(8,128)(2,1)}, bf16[896,128]{1,0:T(8,128)(2,1)}, bf16[896...) custom-call(s32[1]{0:T(128)} %bitcast.refs_0_, ...), custom_call_target="tpu_custom_call" | custom-call | flops 112742891520 | bytes 29360128 | tf_op jit(solution)/shard_map/slices/pallas_call | solution.py:275
  504.0 18.1 %collective-permute-done.7.refs_3_ = bf16[2048,896]{1,0:T(8,128)(2,1)} collective-permute-done((bf16[2048,896]{1,0:T(8,128)(2,1)}, bf16[2048,896]{1,0:T(8,128)(2,1)}, u32[]{:S(2)}, u32[]{:S(2)}) %collective-permute-start.7) | collective-permute-done | bytes 3670048 | tf_op jit(solution)/shard_map/ppermute | solution.py:29
  522.1 0.5 collective-permute-start.9
  522.6 1.7 collective-permute-start.14
  524.7 4.2 collective-permute-done.11.refs_8_
  528.9 1.7 collective-permute-start.18
  530.6 3.5 collective-permute-done.9.refs_4_
  534.1 140.4 %slices.3 = (bf16[896,1152]{1,0:T(8,128)(2,1)}, bf16[896,1152]{1,0:T(8,128)(2,1)}, bf16[1152,896]{1,0:T(8,128)(2,1)}, bf16[896,128]{1,0:T(8,128)(2,1)}, bf16[896...) custom-call(s32[1]{0:T(128)} %bitcast.refs_0_, ...), custom_call_target="tpu_custom_call" | custom-call | flops 112742891520 | bytes 29360128 | tf_op jit(solution)/shard_map/slices/pallas_call | solution.py:275
  674.6 1.3 add_reduce_fusion.1
  675.9 1.7 collective-permute-start.12
  677.6 1.9 collective-permute-done.12
  680.9 0.5 collective-permute-start.25
  681.5 0.5 collective-permute-start.17
  682.0 2.0 collective-permute-done.24.refs_13_
  684.0 11.4 %collective-permute-start.13 = (f32[1]{0:T(128)}, f32[1]{0:T(128)}, u32[]{:S(2)}, u32[]{:S(2)}) collective-permute-start(f32[1]{0:T(128)} %add.22), channel_id=1, source_target_pairs={{0,1},{1,0},{2,3},{3,2},{4,5},{5,4},{6,7},{7,6}} | collective-permute-start | bytes 20 | tf_op jit(solution)/shard_map/ppermute | solution.py:33
  696.0 0.6 compare_select_fusion.who_ref
  696.5 1.3 add_reduce_fusion
  699.5 1.7 collective-permute-start.26
  701.6 1.8 collective-permute-start.29
  703.3 96.5 %shard_map.214 = (bf16[2,896,4736]{2,1,0:T(8,128)(2,1)}, f32[2,896,4736]{2,1,0:T(8,128)}, f32[2,896,4736]{2,1,0:T(8,128)}, bf16[2,896,4736]{2,1,0:T(8,128)(2,1)}...) custom-call(s32[8,106]{1,0:T(8,128)} %constant.25.clone.table_ref, ...), custom_call_target="tpu_custom_call" | custom-call | flops 26148864000 | bytes 287637504 | tf_op jit(solution)/shard_map/pallas_call | solution.py:418
  800.0 35.3 %collective-permute-done.29.refs_10_ = bf16[896,1152]{1,0:T(8,128)(2,1)} collective-permute-done((bf16[896,1152]{1,0:T(8,128)(2,1)}, bf16[896,1152]{1,0:T(8,128)(2,1)}, u32[]{:S(2)}, u32[]{:S(2)}) %collective-permute-start.29) | collective-permute-done | bytes 2064416 | tf_op jit(solution)/shard_map/ppermute | solution.py:29
  835.3 47.1 %shard_map.215 = (bf16[2,896,4736]{2,1,0:T(8,128)(2,1)}, f32[2,896,4736]{2,1,0:T(8,128)}, f32[2,896,4736]{2,1,0:T(8,128)}, bf16[2,896,4736]{2,1,0:T(8,128)(2,1)}...) custom-call(s32[8,50]{1,0:T(8,128)} %constant.26.clone.table_ref, ...), custom_call_target="tpu_custom_call", output_to_operand_aliasing={{0}: (18, {}), {1}: (19, {}), {2}: (20, {}), {3}: (21, {}),... | custom-call | flops 12386304000 | bytes 136249344 | tf_op jit(solution)/shard_map/pallas_call | solution.py:418
  882.4 0.4 collective-permute-start.27
  882.9 39.8 %shard_map.216 = (bf16[2,896,4736]{2,1,0:T(8,128)(2,1)}, f32[2,896,4736]{2,1,0:T(8,128)}, f32[2,896,4736]{2,1,0:T(8,128)}, bf16[2,896,4736]{2,1,0:T(8,128)(2,1)}...) custom-call(s32[8,41]{1,0:T(8,128)} %constant.27.clone.table_ref, ...), custom_call_target="tpu_custom_call", output_to_operand_aliasing={{0}: (17, {}), {1}: (18, {}), {2}: (19, {}), {3}: (20, {}),... | custom-call | flops 10321920000 | bytes 113541120 | tf_op jit(solution)/shard_map/pallas_call | solution.py:418
  922.7 10.2 %shard_map.217 = (bf16[2,896,4736]{2,1,0:T(8,128)(2,1)}, f32[2,896,4736]{2,1,0:T(8,128)}, f32[2,896,4736]{2,1,0:T(8,128)}, bf16[2,896,4736]{2,1,0:T(8,128)(2,1)}...) custom-call(s32[8,9]{1,0:T(8,128)} %constant.28.clone.table_ref, ...), custom_call_target="tpu_custom_call", output_to_operand_aliasing={{0}: (13, {}), {1}: (14, {}), {2}: (15, {}), {3}: (16, {}),... | custom-call | flops 2064384000 | bytes 22708224 | tf_op jit(solution)/shard_map/pallas_call | solution.py:418
  (47 shorter events, 2.5 us)
Async XLA Ops:
  74.9 83.8 %collective-permute-start.2 = (bf16[2048,896]{1,0:T(8,128)(2,1)}, bf16[2048,896]{1,0:T(8,128)(2,1)}, u32[]{:S(2)}, u32[]{:S(2)}) collective-permute-start(bf16[2048,896]{1,0:T(8,128)(2,1)} %get-tuple-element.93.refs_1_.refs_0_), channel_id=1, source_target_pairs={{0,2},{2,0},{1,3},{3,1},{4,6},{6,4},{5,7},{7,5}} | collective-permute-start | bytes 11010056 | tf_op jit(solution)/shard_map/ppermute | solution.py:29
  78.2 158.3 %collective-permute-start.5 = (bf16[2048,896]{1,0:T(8,128)(2,1)}, bf16[2048,896]{1,0:T(8,128)(2,1)}, u32[]{:S(2)}, u32[]{:S(2)}) collective-permute-start(bf16[2048,896]{1,0:T(8,128)(2,1)} %bitcast.6), channel_id=1, source_target_pairs={{0,2},{2,0},{1,3},{3,1},{4,6},{6,4},{5,7},{7,5}} | collective-permute-start | bytes 11010056 | tf_op jit(solution)/shard_map/ppermute | solution.py:29
  78.2 284.9 %collective-permute-start.1 = (bf16[2048,896]{1,0:T(8,128)(2,1)}, bf16[2048,896]{1,0:T(8,128)(2,1)}, u32[]{:S(2)}, u32[]{:S(2)}) collective-permute-start(bf16[2048,896]{1,0:T(8,128)(2,1)} %get-tuple-element.93.refs_1_.refs_0_), channel_id=1, source_target_pairs={{0,1},{1,0},{2,3},{3,2},{4,5},{5,4},{6,7},{7,6}} | collective-permute-start | bytes 11010056 | tf_op jit(solution)/shard_map/ppermute | solution.py:33
  78.2 285.1 %collective-permute-start.4 = (bf16[2048,896]{1,0:T(8,128)(2,1)}, bf16[2048,896]{1,0:T(8,128)(2,1)}, u32[]{:S(2)}, u32[]{:S(2)}) collective-permute-start(bf16[2048,896]{1,0:T(8,128)(2,1)} %bitcast.7), channel_id=1, source_target_pairs={{0,1},{1,0},{2,3},{3,2},{4,5},{5,4},{6,7},{7,6}} | collective-permute-start | bytes 11010056 | tf_op jit(solution)/shard_map/ppermute | solution.py:33
  158.7 205.0 %collective-permute-start.3 = (bf16[2048,896]{1,0:T(8,128)(2,1)}, bf16[2048,896]{1,0:T(8,128)(2,1)}, u32[]{:S(2)}, u32[]{:S(2)}) collective-permute-start(bf16[2048,896]{1,0:T(8,128)(2,1)} %collective-permute-done.2.refs_3_), channel_id=1, source_target_pairs={{0,1},{1,0},{2,3},{3,2},{4,5},{5,4},{6,7},{7,6}} | collective-permute-start | bytes 11010056 | tf_op jit(solution)/shard_map/ppermute | solution.py:33
  236.5 127.2 %collective-permute-start.6 = (bf16[2048,896]{1,0:T(8,128)(2,1)}, bf16[2048,896]{1,0:T(8,128)(2,1)}, u32[]{:S(2)}, u32[]{:S(2)}) collective-permute-start(bf16[2048,896]{1,0:T(8,128)(2,1)} %collective-permute-done.5.refs_7_), channel_id=1, source_target_pairs={{0,1},{1,0},{2,3},{3,2},{4,5},{5,4},{6,7},{7,6}} | collective-permute-start | bytes 11010056 | tf_op jit(solution)/shard_map/ppermute | solution.py:33
  361.4 142.6 %collective-permute-start.8 = (bf16[2048,896]{1,0:T(8,128)(2,1)}, bf16[2048,896]{1,0:T(8,128)(2,1)}, u32[]{:S(2)}, u32[]{:S(2)}) collective-permute-start(bf16[2048,896]{1,0:T(8,128)(2,1)} %chain.1.refs_5_), channel_id=1, source_target_pairs={{0,2},{2,0},{1,3},{3,1},{4,6},{6,4},{5,7},{7,5}} | collective-permute-start | bytes 11010056 | tf_op jit(solution)/shard_map/ppermute | solution.py:29
  363.2 161.2 %collective-permute-start.10 = (bf16[2048,896]{1,0:T(8,128)(2,1)}, bf16[2048,896]{1,0:T(8,128)(2,1)}, u32[]{:S(2)}, u32[]{:S(2)}) collective-permute-start(bf16[2048,896]{1,0:T(8,128)(2,1)} %chain.1.refs_5_), channel_id=1, source_target_pairs={{0,1},{1,0},{2,3},{3,2},{4,5},{5,4},{6,7},{7,6}} | collective-permute-start | bytes 11010056 | tf_op jit(solution)/shard_map/ppermute | solution.py:33
  363.4 158.7 %collective-permute-start.7 = (bf16[2048,896]{1,0:T(8,128)(2,1)}, bf16[2048,896]{1,0:T(8,128)(2,1)}, u32[]{:S(2)}, u32[]{:S(2)}) collective-permute-start(bf16[2048,896]{1,0:T(8,128)(2,1)} %get-tuple-element.92.refs_1_), channel_id=1, source_target_pairs={{0,2},{2,0},{1,3},{3,1},{4,6},{6,4},{5,7},{7,5}} | collective-permute-start | bytes 11010056 | tf_op jit(solution)/shard_map/ppermute | solution.py:29
  363.7 160.7 %collective-permute-start = (bf16[2048,896]{1,0:T(8,128)(2,1)}, bf16[2048,896]{1,0:T(8,128)(2,1)}, u32[]{:S(2)}, u32[]{:S(2)}) collective-permute-start(bf16[2048,896]{1,0:T(8,128)(2,1)} %get-tuple-element.92.refs_1_), channel_id=1, source_target_pairs={{0,1},{1,0},{2,3},{3,2},{4,5},{5,4},{6,7},{7,6}} | collective-permute-start | bytes 11010056 | tf_op jit(solution)/shard_map/ppermute | solution.py:33
  522.1 6.8 collective-permute-start.11
  522.1 12.0 %collective-permute-start.9 = (bf16[2048,896]{1,0:T(8,128)(2,1)}, bf16[2048,896]{1,0:T(8,128)(2,1)}, u32[]{:S(2)}, u32[]{:S(2)}) collective-permute-start(bf16[2048,896]{1,0:T(8,128)(2,1)} %collective-permute-done.7.refs_3_), channel_id=1, source_target_pairs={{0,1},{1,0},{2,3},{3,2},{4,5},{5,4},{6,7},{7,6}} | collective-permute-start | bytes 11010056 | tf_op jit(solution)/shard_map/ppermute | solution.py:33
  522.6 158.2 %collective-permute-start.14 = (bf16[896,1152]{1,0:T(8,128)(2,1)}, bf16[896,1152]{1,0:T(8,128)(2,1)}, u32[]{:S(2)}, u32[]{:S(2)}) collective-permute-start(bf16[896,1152]{1,0:T(8,128)(2,1)} %get-tuple-element.117.refs_9_), channel_id=1, source_target_pairs={{0,2},{2,0},{1,3},{3,1},{4,6},{6,4},{5,7},{7,5}} | collective-permute-start | bytes 6193160 | tf_op jit(solution)/shard_map/ppermute | solution.py:29
  524.4 157.5 %collective-permute-start.23 = (bf16[896,1152]{1,0:T(8,128)(2,1)}, bf16[896,1152]{1,0:T(8,128)(2,1)}, u32[]{:S(2)}, u32[]{:S(2)}) collective-permute-start(bf16[896,1152]{1,0:T(8,128)(2,1)} %get-tuple-element.117.refs_9_), channel_id=1, source_target_pairs={{0,1},{1,0},{2,3},{3,2},{4,5},{5,4},{6,7},{7,6}} | collective-permute-start | bytes 6193160 | tf_op jit(solution)/shard_map/ppermute | solution.py:33
  524.4 157.0 %collective-permute-start.16 = (bf16[896,1152]{1,0:T(8,128)(2,1)}, bf16[896,1152]{1,0:T(8,128)(2,1)}, u32[]{:S(2)}, u32[]{:S(2)}) collective-permute-start(bf16[896,1152]{1,0:T(8,128)(2,1)} %get-tuple-element.118.refs_10_), channel_id=1, source_target_pairs={{0,2},{2,0},{1,3},{3,1},{4,6},{6,4},{5,7},{7,5}} | collective-permute-start | bytes 6193160 | tf_op jit(solution)/shard_map/ppermute | solution.py:29
  528.9 152.6 %collective-permute-start.18 = (bf16[1152,896]{1,0:T(8,128)(2,1)}, bf16[1152,896]{1,0:T(8,128)(2,1)}, u32[]{:S(2)}, u32[]{:S(2)}) collective-permute-start(bf16[1152,896]{1,0:T(8,128)(2,1)} %get-tuple-element.119.refs_11_), channel_id=1, source_target_pairs={{0,2},{2,0},{1,3},{3,1},{4,6},{6,4},{5,7},{7,5}} | collective-permute-start | bytes 6193160 | tf_op jit(solution)/shard_map/ppermute | solution.py:29
  675.9 3.7 collective-permute-start.12
  679.5 4.5 collective-permute-start.24
  680.9 18.2 %collective-permute-start.25 = (bf16[1152,896]{1,0:T(8,128)(2,1)}, bf16[1152,896]{1,0:T(8,128)(2,1)}, u32[]{:S(2)}, u32[]{:S(2)}) collective-permute-start(bf16[1152,896]{1,0:T(8,128)(2,1)} %get-tuple-element.119.refs_11_), channel_id=1, source_target_pairs={{0,1},{1,0},{2,3},{3,2},{4,5},{5,4},{6,7},{7,6}} | collective-permute-start | bytes 6193160 | tf_op jit(solution)/shard_map/ppermute | solution.py:33
  681.4 18.1 %collective-permute-start.15 = (bf16[896,1152]{1,0:T(8,128)(2,1)}, bf16[896,1152]{1,0:T(8,128)(2,1)}, u32[]{:S(2)}, u32[]{:S(2)}) collective-permute-start(bf16[896,1152]{1,0:T(8,128)(2,1)} %collective-permute-done.14.refs_15_), channel_id=1, source_target_pairs={{0,1},{1,0},{2,3},{3,2},{4,5},{5,4},{6,7},{7,6}} | collective-permute-start | bytes 6193160 | tf_op jit(solution)/shard_map/ppermute | solution.py:33
  681.5 19.8 %collective-permute-start.17 = (bf16[896,1152]{1,0:T(8,128)(2,1)}, bf16[896,1152]{1,0:T(8,128)(2,1)}, u32[]{:S(2)}, u32[]{:S(2)}) collective-permute-start(bf16[896,1152]{1,0:T(8,128)(2,1)} %collective-permute-done.16.refs_16_), channel_id=1, source_target_pairs={{0,1},{1,0},{2,3},{3,2},{4,5},{5,4},{6,7},{7,6}} | collective-permute-start | bytes 6193160 | tf_op jit(solution)/shard_map/ppermute | solution.py:33
  681.9 19.6 %collective-permute-start.19 = (bf16[1152,896]{1,0:T(8,128)(2,1)}, bf16[1152,896]{1,0:T(8,128)(2,1)}, u32[]{:S(2)}, u32[]{:S(2)}) collective-permute-start(bf16[1152,896]{1,0:T(8,128)(2,1)} %collective-permute-done.18.refs_17_), channel_id=1, source_target_pairs={{0,1},{1,0},{2,3},{3,2},{4,5},{5,4},{6,7},{7,6}} | collective-permute-start | bytes 6193160 | tf_op jit(solution)/shard_map/ppermute | solution.py:33
  684.0 11.8 %collective-permute-start.13 = (f32[1]{0:T(128)}, f32[1]{0:T(128)}, u32[]{:S(2)}, u32[]{:S(2)}) collective-permute-start(f32[1]{0:T(128)} %add.22), channel_id=1, source_target_pairs={{0,1},{1,0},{2,3},{3,2},{4,5},{5,4},{6,7},{7,6}} | collective-permute-start | bytes 20 | tf_op jit(solution)/shard_map/ppermute | solution.py:33
  695.8 5.7 collective-permute-start.20
  699.1 136.2 %collective-permute-start.22 = (bf16[1152,896]{1,0:T(8,128)(2,1)}, bf16[1152,896]{1,0:T(8,128)(2,1)}, u32[]{:S(2)}, u32[]{:S(2)}) collective-permute-start(bf16[1152,896]{1,0:T(8,128)(2,1)} %get-tuple-element.122.refs_20_), channel_id=1, source_target_pairs={{0,1},{1,0},{2,3},{3,2},{4,5},{5,4},{6,7},{7,6}} | collective-permute-start | bytes 6193160 | tf_op jit(solution)/shard_map/ppermute | solution.py:33
  699.5 182.9 %collective-permute-start.26 = (bf16[1152,896]{1,0:T(8,128)(2,1)}, bf16[1152,896]{1,0:T(8,128)(2,1)}, u32[]{:S(2)}, u32[]{:S(2)}) collective-permute-start(bf16[1152,896]{1,0:T(8,128)(2,1)} %get-tuple-element.122.refs_20_), channel_id=1, source_target_pairs={{0,2},{2,0},{1,3},{3,1},{4,6},{6,4},{5,7},{7,5}} | collective-permute-start | bytes 6193160 | tf_op jit(solution)/shard_map/ppermute | solution.py:29
  701.3 98.5 %collective-permute-start.28 = (bf16[896,1152]{1,0:T(8,128)(2,1)}, bf16[896,1152]{1,0:T(8,128)(2,1)}, u32[]{:S(2)}, u32[]{:S(2)}) collective-permute-start(bf16[896,1152]{1,0:T(8,128)(2,1)} %get-tuple-element.120.refs_18_), channel_id=1, source_target_pairs={{0,2},{2,0},{1,3},{3,1},{4,6},{6,4},{5,7},{7,5}} | collective-permute-start | bytes 6193160 | tf_op jit(solution)/shard_map/ppermute | solution.py:29
  701.6 133.7 %collective-permute-start.21 = (bf16[896,1152]{1,0:T(8,128)(2,1)}, bf16[896,1152]{1,0:T(8,128)(2,1)}, u32[]{:S(2)}, u32[]{:S(2)}) collective-permute-start(bf16[896,1152]{1,0:T(8,128)(2,1)} %get-tuple-element.121.refs_19_), channel_id=1, source_target_pairs={{0,1},{1,0},{2,3},{3,2},{4,5},{5,4},{6,7},{7,6}} | collective-permute-start | bytes 6193160 | tf_op jit(solution)/shard_map/ppermute | solution.py:33
  701.6 133.7 %collective-permute-start.29 = (bf16[896,1152]{1,0:T(8,128)(2,1)}, bf16[896,1152]{1,0:T(8,128)(2,1)}, u32[]{:S(2)}, u32[]{:S(2)}) collective-permute-start(bf16[896,1152]{1,0:T(8,128)(2,1)} %get-tuple-element.121.refs_19_), channel_id=1, source_target_pairs={{0,2},{2,0},{1,3},{3,1},{4,6},{6,4},{5,7},{7,5}} | collective-permute-start | bytes 6193160 | tf_op jit(solution)/shard_map/ppermute | solution.py:29
  799.8 83.1 %collective-permute-start.30 = (bf16[896,1152]{1,0:T(8,128)(2,1)}, bf16[896,1152]{1,0:T(8,128)(2,1)}, u32[]{:S(2)}, u32[]{:S(2)}) collective-permute-start(bf16[896,1152]{1,0:T(8,128)(2,1)} %collective-permute-done.28.refs_9_), channel_id=1, source_target_pairs={{0,1},{1,0},{2,3},{3,2},{4,5},{5,4},{6,7},{7,6}} | collective-permute-start | bytes 6193160 | tf_op jit(solution)/shard_map/ppermute | solution.py:33
  835.3 47.6 %collective-permute-start.31 = (bf16[896,1152]{1,0:T(8,128)(2,1)}, bf16[896,1152]{1,0:T(8,128)(2,1)}, u32[]{:S(2)}, u32[]{:S(2)}) collective-permute-start(bf16[896,1152]{1,0:T(8,128)(2,1)} %collective-permute-done.29.refs_10_), channel_id=1, source_target_pairs={{0,1},{1,0},{2,3},{3,2},{4,5},{5,4},{6,7},{7,6}} | collective-permute-start | bytes 6193160 | tf_op jit(solution)/shard_map/ppermute | solution.py:33
  882.4 40.3 %collective-permute-start.27 = (bf16[1152,896]{1,0:T(8,128)(2,1)}, bf16[1152,896]{1,0:T(8,128)(2,1)}, u32[]{:S(2)}, u32[]{:S(2)}) collective-permute-start(bf16[1152,896]{1,0:T(8,128)(2,1)} %collective-permute-done.26.refs_11_), channel_id=1, source_target_pairs={{0,1},{1,0},{2,3},{3,2},{4,5},{5,4},{6,7},{7,6}} | collective-permute-start | bytes 6193160 | tf_op jit(solution)/shard_map/ppermute | solution.py:33
  (2 other events, 326.9 us)

commit v3 on v2

--- a/solution.py
+++ b/solution.py
@@ -14,7 +14,7 @@
 
 LANES = 128
 BLOCK = 512
-ROWS = 512
+ROWS = 1024
 
 
 def dot(a, b, dims):
@@ -183,16 +183,6 @@
     )(a, dy, h, wg, wu, wd)
 
 
-def squares(x):
-    x = x.astype(F32)
-    x = x * x
-    total = None
-    for c in range(0, x.shape[1], LANES):
-        part = jnp.sum(x[:, c : c + LANES].reshape(x.shape[0] // 8, 8, LANES), 0)
-        total = part if total is None else total + part
-    return total
-
-
 def slices_kernel(own, me_ref, *refs):
     a_refs, dy_refs = refs[:4], refs[4:8]
     weights, outs, scratch = refs[8:14], refs[14:22], refs[22:]
@@ -220,8 +210,6 @@
         wg_ref[:, :own], wg_ref[:, own:] = weights[0][0], weights[1][0]
         wu_ref[:, :own], wu_ref[:, own:] = weights[2][0], weights[3][0]
         wd_ref[:own, :], wd_ref[own:, :] = weights[4][0], weights[5][0]
-        for ref in (accg_ref, accu_ref, accd_ref):
-            ref[...] = jnp.zeros_like(ref)
 
     @pl.when(i + 1 < steps)
     def _():
@@ -243,9 +231,8 @@
     def back(c):
         s = blocks[c]
         dg, du, hid = held.pop(c)
-        accg_ref[:, s] += dot(a_t, dg, NN)
-        accu_ref[:, s] += dot(a_t, du, NN)
-        accd_ref[:, s] += dot(dy_t, hid, NN)
+        for acc, left, right in ((accg_ref, a_t, dg), (accu_ref, a_t, du), (accd_ref, dy_t, hid)):
+            acc[:, s] = jnp.where(i == 0, 0.0, acc[:, s]) + dot(left, right, NN)
 
     there(0)
     for c in range(1, len(blocks)):
@@ -255,13 +242,20 @@
 
     @pl.when(i == steps - 1)
     def _():
-        g_ref, u_ref, d_ref, gs_ref, us_ref, ds_ref, own_ref, shared_ref = outs
-        g, u, d = accg_ref[...].astype(BF16), accu_ref[...].astype(BF16), accd_ref[...].astype(BF16)
-        g_ref[...], gs_ref[...] = g[:, :own], g[:, own:]
-        u_ref[...], us_ref[...] = u[:, :own], u[:, own:]
-        d_ref[...], ds_ref[...] = d[:, :own].T, d[:, own:].T
-        own_ref[...] = squares(g[:, :own]) + squares(u[:, :own]) + squares(d[:, :own])
-        shared_ref[...] = squares(g[:, own:]) + squares(u[:, own:]) + squares(d[:, own:])
+        sums = [None, None]
+        for acc, out, out_s, turned in ((accg_ref, *outs[0:4:3], False), (accu_ref, *outs[1:5:3], False), (accd_ref, *outs[2:6:3], True)):
+            for c in range(0, width, LANES):
+                part = acc[:, c : c + LANES].astype(BF16)
+                if turned:
+                    ref, at = (out, pl.ds(c, LANES)) if c < own else (out_s, pl.ds(c - own, LANES))
+                    ref[at, :] = part.T
+                else:
+                    ref, at = (out, pl.ds(c, LANES)) if c < own else (out_s, pl.ds(c - own, LANES))
+                    ref[:, at] = part
+                square = part.astype(F32)
+                square = jnp.sum((square * square).reshape(-1, 8, LANES), 0)
+                sums[c >= own] = square if sums[c >= own] is None else sums[c >= own] + square
+        outs[6][...], outs[7][...] = sums
 
 
 def slices(layer, own, me, a_all, dy_all, wg, wu, wd):
@@ -424,7 +418,7 @@
         + [pltpu.SemaphoreType.DMA((4, SLOTS)), pltpu.SemaphoreType.DMA((3, SLOTS))],
         input_output_aliases={3 + n_in + n: n for n in range(len(before))},
         cost_estimate=pl.CostEstimate(flops=2000 * elements, bytes_accessed=22 * elements, transcendentals=elements),
-        compiler_params=params(),
+        compiler_params=params(30),
     )(table, who, factor, *given, *(piece[3] for piece in pieces), *before)
     return tuple(tuple(new[3 * n : 3 * n + 3]) for n in range(3))
 
@@ -454,30 +448,28 @@
         top_x = [send(top[n], px) for n in range(3)]
         top_d = [send(top[n], pd) for n in range(3)]
         low = slices(0, own, me, [a0, a0_d, a0_x, a0_xd], [dh1, dh1_d, dh1_x, dh1_xd], wg, wu, wd)
+        top_xd = [send(top_x[n], pd) for n in range(3)]
         total = jnp.sum(top[6] + low[6]).reshape(1)
         total = total + px(total)
+        total = total + pd(total) + jnp.sum(top[7] + low[7])
         low, total = lax.optimization_barrier((low, total))
         low_x = [send(low[n], px) for n in range(3)]
         low_d = [send(low[n], pd) for n in range(3)]
-        total = total + pd(total) + jnp.sum(top[7] + low[7])
         count = wg.size + wu.size + wd.size
         factor = jnp.minimum(1.0, 0.5 * lax.rsqrt(total / count + 1e-30))
 
-        top_xd = [send(top_x[n], pd) for n in range(3)]
-        low_xd = [send(low_x[n], pd) for n in range(2)]
         arrays = ((wg, mg, vg), (wu, mu, vu), (wd, md, vd))
 
-        def pieces(layer, slot, gs, names=(0, 1, 2)):
-            return [(n, layer, slot, gs[n]) for n in names]
-
-        first = pieces(1, 0, top) + pieces(1, 1, top_d) + pieces(1, 2, top_x) + pieces(0, 0, low)
+        def pieces(layer, slot, gs):
+            return [(n, layer, slot, gs[n]) for n in range(3)]
+
+        first = pieces(1, 0, top) + pieces(1, 1, top_d) + pieces(1, 2, top_x) + pieces(1, 3, top_xd) + pieces(0, 0, low)
         shared = pieces(1, 4, top[3:6]) + pieces(0, 4, low[3:6])
         outs = adam(own, factor, who, arrays, first + shared, None)
-        outs = adam(own, factor, who, arrays, pieces(1, 3, top_xd) + pieces(0, 1, low_d), outs)
-        outs, low_x[2] = lax.optimization_barrier((outs, low_x[2]))
-        low_xd.append(send(low_x[2], pd))
-        outs = adam(own, factor, who, arrays, pieces(0, 2, low_x) + pieces(0, 3, low_xd, (0, 1)), outs)
-        outs = adam(own, factor, who, arrays, pieces(0, 3, low_xd, (2,)), outs)
+        outs, low_x = lax.optimization_barrier((outs, low_x))
+        low_xd = [send(low_x[n], pd) for n in range(3)]
+        outs = adam(own, factor, who, arrays, pieces(0, 1, low_d) + pieces(0, 2, low_x), outs)
+        outs = adam(own, factor, who, arrays, pieces(0, 3, low_xd), outs)
         return tuple(outs[name][which] for which in range(3) for name in range(3))
 
     return jax.shard_map(

time: 942 us -> 873 us (0.927)
  waiting for transfers between devices: 223 us -> 157 us
  local copies, waits for them, and re-layouts: 0.01 us -> 14.5 us
    ppermute x11, waiting for transfers between devices: 213 us -> 141 us  [px(): return lax.ppermute(a, 'dp', PX)]
    unnamed x4 -> x32, local copies, waits for them, and re-layouts: 0.01 us -> 14.5 us
    ppermute x21, starting transfers between devices: 15 us -> 4.84 us  [pd(): return lax.ppermute(a, 'dp', PD)]
    pallas_call x4 -> x3, Pallas kernels: 194 us -> 187 us  [adam(): pl.pallas_call(kernel, in_specs=[pl.BlockSpec(memory_space=pltpu.SMEM)] *...]
  transfers between devices with their start and end apart: 32 -> 32, of which waited for: 9 -> 13; matrix products, arithmetic and copies ran while one was open for 0% -> 0% of each run, Pallas kernels for 63% -> 74%
where the time goes in v3:
time: 873 us; the launch traced here: 864 us
  Pallas kernels  665 us (76%)
  waiting for transfers between devices  157 us (18%)
  starting transfers between devices  21 us (2%)
  local copies, waits for them, and re-layouts  14.5 us (2%)
    pallas_call x2, Pallas kernels, slices(): pl.pallas_call(lambda *refs: slices_kernel(own, *refs), grid_spec=pltpu.P...  275 us
    pallas_call x3, Pallas kernels, adam(): pl.pallas_call(kernel, in_specs=[pl.BlockSpec(memory_space=pltpu.SMEM)] *...  187 us
    ppermute x11, waiting for transfers between devices, px(): return lax.ppermute(a, 'dp', PX)  141 us
    pallas_call x1, Pallas kernels, chain(): pl.pallas_call(lambda *refs: chain_kernel(ff - (steps - 1) * BLOCK, *refs...  128 us
    pallas_call x1, Pallas kernels, forward(): pl.pallas_call(lambda *refs: forward_kernel(ff - (steps - 1) * BLOCK, *re...  74.2 us
  transfers between devices with their start and end apart: 32, of which 13 were waited for; matrix products, arithmetic and copies ran while one was open for 0% of the time, Pallas kernels for 74%

profile of v3, /device:TPU:0, one launch (start us, length us, event | category | flops | bytes accessed | tf_op | source)
XLA Modules:
  0.0 864.1 jit_solution(3100758326709727935)
XLA Ops:
  0.6 3.3 collective-permute-start.5
  4.0 74.2 %forward.1 = (bf16[2048,896]{1,0:T(8,128)(2,1)}, bf16[2048,896]{1,0:T(8,128)(2,1)}, bf16[2048,896]{1,0:T(8,128)(2,1)}) custom-call(bf16[2048,896]{1,0:T(8,128)(2,1)} %bitcast.5, bf16[2,896,4736]{2,1,0:T(8,128)(2,1)} %refs_0_.5, bf16[2,896,4736]{2,1,0:T(8,128)(2,1)} %refs_3_.9, bf16[2,4736,896]{2,1,0:T(8,128)(2,1)} %refs_6_.5), custom_call_target="tpu_custom_call" | custom-call | flops 52143587328 | bytes 25460736 | tf_op jit(solution)/shard_map/forward/pallas_call | solution.py:102
  78.8 5.7 collective-permute-done.5.refs_7_
  84.5 77.8 %collective-permute-done.2.refs_3_ = bf16[2048,896]{1,0:T(8,128)(2,1)} collective-permute-done((bf16[2048,896]{1,0:T(8,128)(2,1)}, bf16[2048,896]{1,0:T(8,128)(2,1)}, u32[]{:S(2)}, u32[]{:S(2)}) %collective-permute-start.2) | collective-permute-done | bytes 3670048 | tf_op jit(solution)/shard_map/ppermute | solution.py:29
  162.3 127.6 %chain.1.refs_5_ = bf16[2048,896]{1,0:T(8,128)(2,1)} custom-call(bf16[2048,896]{1,0:T(8,128)(2,1)} %get-tuple-element.85.refs_1_.refs_0_, bf16[2048,896]{1,0:T(8,128)(2,1)} %bitcast.8, bf16[2048,896]{1,0:T(8,128)(2,1)} %get-tuple-element.94.refs_2_, bf16[2,896,4736]{2,1,0:T(8,128)(2,1)} %refs_0_.5, bf16[2,896,4736]{2,1,0:T(8,128)(2,1)} %refs_3_.9, ...), custom_call_target="tpu_custom_call" | custom-call | flops 86905978880 | bytes 25460736 | tf_op jit(solution)/shard_map/chain/pallas_call | solution.py:173
  290.4 1.7 collective-permute-start.8
  292.5 137.7 %slices.2 = (bf16[896,1152]{1,0:T(8,128)(2,1)}, bf16[896,1152]{1,0:T(8,128)(2,1)}, bf16[1152,896]{1,0:T(8,128)(2,1)}, bf16[896,128]{1,0:T(8,128)(2,1)}, bf16[896...) custom-call(s32[1]{0:T(128)} %bitcast.refs_0_, ...), custom_call_target="tpu_custom_call" | custom-call | flops 112742891520 | bytes 29360128 | tf_op jit(solution)/shard_map/slices/pallas_call | solution.py:269
  430.2 20.5 %collective-permute-done.7.refs_3_ = bf16[2048,896]{1,0:T(8,128)(2,1)} collective-permute-done((bf16[2048,896]{1,0:T(8,128)(2,1)}, bf16[2048,896]{1,0:T(8,128)(2,1)}, u32[]{:S(2)}, u32[]{:S(2)}) %collective-permute-start.7) | collective-permute-done | bytes 3670048 | tf_op jit(solution)/shard_map/ppermute | solution.py:29
  451.3 1.7 collective-permute-start.17
  453.3 4.2 collective-permute-done.9.refs_4_
  457.5 1.7 collective-permute-start.19
  459.2 3.5 collective-permute-done.11.refs_8_
  462.8 137.7 %slices.3 = (bf16[896,1152]{1,0:T(8,128)(2,1)}, bf16[896,1152]{1,0:T(8,128)(2,1)}, bf16[1152,896]{1,0:T(8,128)(2,1)}, bf16[896,128]{1,0:T(8,128)(2,1)}, bf16[896...) custom-call(s32[1]{0:T(128)} %bitcast.refs_0_, ...), custom_call_target="tpu_custom_call" | custom-call | flops 112742891520 | bytes 29360128 | tf_op jit(solution)/shard_map/slices/pallas_call | solution.py:269
  600.5 1.3 add_reduce_fusion.1
  601.8 1.7 collective-permute-start.12
  603.5 2.1 collective-permute-done.12
  608.3 1.3 add_reduce_fusion
  612.5 1.7 collective-permute-start.23
  614.3 1.2 collective-permute-done.16.refs_14_
  615.6 2.8 collective-permute-done.20.refs_18_
  618.6 2.8 collective-permute-done.21.refs_19_
  621.3 1.7 collective-permute-start.24
  623.1 1.2 collective-permute-done.22.refs_20_
  625.6 34.9 %collective-permute-done.23.refs_12_ = bf16[896,1152]{1,0:T(8,128)(2,1)S(1)} collective-permute-done((bf16[896,1152]{1,0:T(8,128)(2,1)}, bf16[896,1152]{1,0:T(8,128)(2,1)S(1)}, u32[]{:S(2)}, u32[]{:S(2)}) %collective-permute-start.23) | collective-permute-done | bytes 2064416 | tf_op jit(solution)/shard_map/ppermute | solution.py:29
  660.5 1.7 collective-permute-start.25
  662.2 1.6 copy-done.1
  663.8 1.6 copy-done.2
  665.4 1.6 copy-done.3
  669.8 120.5 %shard_map.205 = (bf16[2,896,4736]{2,1,0:T(8,128)(2,1)}, f32[2,896,4736]{2,1,0:T(8,128)}, f32[2,896,4736]{2,1,0:T(8,128)}, bf16[2,896,4736]{2,1,0:T(8,128)(2,1)}...) custom-call(s32[8,131]{1,0:T(8,128)S(1)} %copy-done.10, ...), custom_call_target="tpu_custom_call" | custom-call | flops 32342016000 | bytes 355762176 | tf_op jit(solution)/shard_map/pallas_call | solution.py:412
  790.9 44.1 %shard_map.206 = (bf16[2,896,4736]{2,1,0:T(8,128)(2,1)}, f32[2,896,4736]{2,1,0:T(8,128)}, f32[2,896,4736]{2,1,0:T(8,128)}, bf16[2,896,4736]{2,1,0:T(8,128)(2,1)}...) custom-call(s32[8,50]{1,0:T(8,128)S(1)} %copy-done.12, ...), custom_call_target="tpu_custom_call", output_to_operand_aliasing={{0}: (18, {}), {1}: (19, {}), {2}: (20, {}), {3}: (21, {}),... | custom-call | flops 12386304000 | bytes 136249344 | tf_op jit(solution)/shard_map/pallas_call | solution.py:412
  835.1 5.8 copy-done
  840.9 22.7 %shard_map.207 = (bf16[2,896,4736]{2,1,0:T(8,128)(2,1)}, f32[2,896,4736]{2,1,0:T(8,128)}, f32[2,896,4736]{2,1,0:T(8,128)}, bf16[2,896,4736]{2,1,0:T(8,128)(2,1)}...) custom-call(s32[8,25]{1,0:T(8,128)S(1)} %copy-done.11, ...), custom_call_target="tpu_custom_call", output_to_operand_aliasing={{0}: (15, {}), {1}: (16, {}), {2}: (17, {}), {3}: (18, {}),... | custom-call | flops 6193152000 | bytes 68124672 | tf_op jit(solution)/shard_map/pallas_call | solution.py:412
  (74 shorter events, 10.4 us)
Async XLA Ops:
  0.6 83.8 %collective-permute-start.5 = (bf16[2048,896]{1,0:T(8,128)(2,1)}, bf16[2048,896]{1,0:T(8,128)(2,1)}, u32[]{:S(2)}, u32[]{:S(2)}) collective-permute-start(bf16[2048,896]{1,0:T(8,128)(2,1)} %bitcast.6), channel_id=1, source_target_pairs={{0,2},{2,0},{1,3},{3,1},{4,6},{6,4},{5,7},{7,5}} | collective-permute-start | bytes 11010056 | tf_op jit(solution)/shard_map/ppermute | solution.py:29
  78.2 84.1 %collective-permute-start.2 = (bf16[2048,896]{1,0:T(8,128)(2,1)}, bf16[2048,896]{1,0:T(8,128)(2,1)}, u32[]{:S(2)}, u32[]{:S(2)}) collective-permute-start(bf16[2048,896]{1,0:T(8,128)(2,1)} %get-tuple-element.85.refs_1_.refs_0_), channel_id=1, source_target_pairs={{0,2},{2,0},{1,3},{3,1},{4,6},{6,4},{5,7},{7,5}} | collective-permute-start | bytes 11010056 | tf_op jit(solution)/shard_map/ppermute | solution.py:29
  78.3 212.2 %collective-permute-start.4 = (bf16[2048,896]{1,0:T(8,128)(2,1)}, bf16[2048,896]{1,0:T(8,128)(2,1)}, u32[]{:S(2)}, u32[]{:S(2)}) collective-permute-start(bf16[2048,896]{1,0:T(8,128)(2,1)} %bitcast.7), channel_id=1, source_target_pairs={{0,1},{1,0},{2,3},{3,2},{4,5},{5,4},{6,7},{7,6}} | collective-permute-start | bytes 11010056 | tf_op jit(solution)/shard_map/ppermute | solution.py:33
  78.3 213.9 %collective-permute-start.1 = (bf16[2048,896]{1,0:T(8,128)(2,1)}, bf16[2048,896]{1,0:T(8,128)(2,1)}, u32[]{:S(2)}, u32[]{:S(2)}) collective-permute-start(bf16[2048,896]{1,0:T(8,128)(2,1)} %get-tuple-element.85.refs_1_.refs_0_), channel_id=1, source_target_pairs={{0,1},{1,0},{2,3},{3,2},{4,5},{5,4},{6,7},{7,6}} | collective-permute-start | bytes 11010056 | tf_op jit(solution)/shard_map/ppermute | solution.py:33
  84.5 208.0 %collective-permute-start.6 = (bf16[2048,896]{1,0:T(8,128)(2,1)}, bf16[2048,896]{1,0:T(8,128)(2,1)}, u32[]{:S(2)}, u32[]{:S(2)}) collective-permute-start(bf16[2048,896]{1,0:T(8,128)(2,1)} %collective-permute-done.5.refs_7_), channel_id=1, source_target_pairs={{0,1},{1,0},{2,3},{3,2},{4,5},{5,4},{6,7},{7,6}} | collective-permute-start | bytes 11010056 | tf_op jit(solution)/shard_map/ppermute | solution.py:33
  162.3 130.2 %collective-permute-start.3 = (bf16[2048,896]{1,0:T(8,128)(2,1)}, bf16[2048,896]{1,0:T(8,128)(2,1)}, u32[]{:S(2)}, u32[]{:S(2)}) collective-permute-start(bf16[2048,896]{1,0:T(8,128)(2,1)} %collective-permute-done.2.refs_3_), channel_id=1, source_target_pairs={{0,1},{1,0},{2,3},{3,2},{4,5},{5,4},{6,7},{7,6}} | collective-permute-start | bytes 11010056 | tf_op jit(solution)/shard_map/ppermute | solution.py:33
  289.9 163.1 %collective-permute-start.10 = (bf16[2048,896]{1,0:T(8,128)(2,1)}, bf16[2048,896]{1,0:T(8,128)(2,1)}, u32[]{:S(2)}, u32[]{:S(2)}) collective-permute-start(bf16[2048,896]{1,0:T(8,128)(2,1)} %chain.1.refs_5_), channel_id=1, source_target_pairs={{0,1},{1,0},{2,3},{3,2},{4,5},{5,4},{6,7},{7,6}} | collective-permute-start | bytes 11010056 | tf_op jit(solution)/shard_map/ppermute | solution.py:33
  290.4 139.8 %collective-permute-start.8 = (bf16[2048,896]{1,0:T(8,128)(2,1)}, bf16[2048,896]{1,0:T(8,128)(2,1)}, u32[]{:S(2)}, u32[]{:S(2)}) collective-permute-start(bf16[2048,896]{1,0:T(8,128)(2,1)} %chain.1.refs_5_), channel_id=1, source_target_pairs={{0,2},{2,0},{1,3},{3,1},{4,6},{6,4},{5,7},{7,5}} | collective-permute-start | bytes 11010056 | tf_op jit(solution)/shard_map/ppermute | solution.py:29
  292.2 158.5 %collective-permute-start.7 = (bf16[2048,896]{1,0:T(8,128)(2,1)}, bf16[2048,896]{1,0:T(8,128)(2,1)}, u32[]{:S(2)}, u32[]{:S(2)}) collective-permute-start(bf16[2048,896]{1,0:T(8,128)(2,1)} %get-tuple-element.84.refs_1_), channel_id=1, source_target_pairs={{0,2},{2,0},{1,3},{3,1},{4,6},{6,4},{5,7},{7,5}} | collective-permute-start | bytes 11010056 | tf_op jit(solution)/shard_map/ppermute | solution.py:29
  292.5 160.5 %collective-permute-start = (bf16[2048,896]{1,0:T(8,128)(2,1)}, bf16[2048,896]{1,0:T(8,128)(2,1)}, u32[]{:S(2)}, u32[]{:S(2)}) collective-permute-start(bf16[2048,896]{1,0:T(8,128)(2,1)} %get-tuple-element.84.refs_1_), channel_id=1, source_target_pairs={{0,1},{1,0},{2,3},{3,2},{4,5},{5,4},{6,7},{7,6}} | collective-permute-start | bytes 11010056 | tf_op jit(solution)/shard_map/ppermute | solution.py:33
  450.7 6.8 collective-permute-start.9
  450.8 12.0 %collective-permute-start.11 = (bf16[2048,896]{1,0:T(8,128)(2,1)}, bf16[2048,896]{1,0:T(8,128)(2,1)}, u32[]{:S(2)}, u32[]{:S(2)}) collective-permute-start(bf16[2048,896]{1,0:T(8,128)(2,1)} %collective-permute-done.8.refs_7_), channel_id=1, source_target_pairs={{0,1},{1,0},{2,3},{3,2},{4,5},{5,4},{6,7},{7,6}} | collective-permute-start | bytes 11010056 | tf_op jit(solution)/shard_map/ppermute | solution.py:33
  451.3 159.6 %collective-permute-start.17 = (bf16[896,1152]{1,0:T(8,128)(2,1)}, bf16[896,1152]{1,0:T(8,128)(2,1)}, u32[]{:S(2)}, u32[]{:S(2)}) collective-permute-start(bf16[896,1152]{1,0:T(8,128)(2,1)} %get-tuple-element.108.refs_9_), channel_id=1, source_target_pairs={{0,2},{2,0},{1,3},{3,1},{4,6},{6,4},{5,7},{7,5}} | collective-permute-start | bytes 6193160 | tf_op jit(solution)/shard_map/ppermute | solution.py:29
  453.0 158.3 %collective-permute-start.14 = (bf16[896,1152]{1,0:T(8,128)(2,1)}, bf16[896,1152]{1,0:T(8,128)(2,1)}, u32[]{:S(2)}, u32[]{:S(2)}) collective-permute-start(bf16[896,1152]{1,0:T(8,128)(2,1)} %get-tuple-element.108.refs_9_), channel_id=1, source_target_pairs={{0,1},{1,0},{2,3},{3,2},{4,5},{5,4},{6,7},{7,6}} | collective-permute-start | bytes 6193160 | tf_op jit(solution)/shard_map/ppermute | solution.py:33
  453.0 158.4 %collective-permute-start.18 = (bf16[896,1152]{1,0:T(8,128)(2,1)}, bf16[896,1152]{1,0:T(8,128)(2,1)}, u32[]{:S(2)}, u32[]{:S(2)}) collective-permute-start(bf16[896,1152]{1,0:T(8,128)(2,1)} %get-tuple-element.109.refs_10_), channel_id=1, source_target_pairs={{0,2},{2,0},{1,3},{3,1},{4,6},{6,4},{5,7},{7,5}} | collective-permute-start | bytes 6193160 | tf_op jit(solution)/shard_map/ppermute | solution.py:29
  457.5 154.3 %collective-permute-start.19 = (bf16[1152,896]{1,0:T(8,128)(2,1)}, bf16[1152,896]{1,0:T(8,128)(2,1)}, u32[]{:S(2)}, u32[]{:S(2)}) collective-permute-start(bf16[1152,896]{1,0:T(8,128)(2,1)} %get-tuple-element.110.refs_11_), channel_id=1, source_target_pairs={{0,2},{2,0},{1,3},{3,1},{4,6},{6,4},{5,7},{7,5}} | collective-permute-start | bytes 6193160 | tf_op jit(solution)/shard_map/ppermute | solution.py:29
  601.8 3.8 collective-permute-start.12
  606.8 1.3 collective-permute-start.13
  608.1 4.3 collective-permute-start.15
  610.9 4.5 collective-permute-start.16
  611.3 7.1 collective-permute-start.20
  611.4 9.9 %collective-permute-start.21 = (bf16[896,1152]{1,0:T(8,128)(2,1)}, bf16[896,1152]{1,0:T(8,128)(2,1)S(1)}, u32[]{:S(2)}, u32[]{:S(2)}) collective-permute-start(bf16[896,1152]{1,0:T(8,128)(2,1)} %collective-permute-done.18.refs_16_), channel_id=1, source_target_pairs={{0,1},{1,0},{2,3},{3,2},{4,5},{5,4},{6,7},{7,6}} | collective-permute-start | bytes 6193160 | tf_op jit(solution)/shard_map/ppermute | solution.py:33
  611.8 12.5 %collective-permute-start.22 = (bf16[1152,896]{1,0:T(8,128)(2,1)}, bf16[1152,896]{1,0:T(8,128)(2,1)S(1)}, u32[]{:S(2)}, u32[]{:S(2)}) collective-permute-start(bf16[1152,896]{1,0:T(8,128)(2,1)} %collective-permute-done.19.refs_17_), channel_id=1, source_target_pairs={{0,1},{1,0},{2,3},{3,2},{4,5},{5,4},{6,7},{7,6}} | collective-permute-start | bytes 6193160 | tf_op jit(solution)/shard_map/ppermute | solution.py:33
  612.5 48.0 %collective-permute-start.23 = (bf16[896,1152]{1,0:T(8,128)(2,1)}, bf16[896,1152]{1,0:T(8,128)(2,1)S(1)}, u32[]{:S(2)}, u32[]{:S(2)}) collective-permute-start(bf16[896,1152]{1,0:T(8,128)(2,1)} %get-tuple-element.111.refs_21_), channel_id=1, source_target_pairs={{0,2},{2,0},{1,3},{3,1},{4,6},{6,4},{5,7},{7,5}} | collective-permute-start | bytes 6193160 | tf_op jit(solution)/shard_map/ppermute | solution.py:29
  615.4 175.4 %collective-permute-start.29 = (bf16[896,1152]{1,0:T(8,128)(2,1)}, bf16[896,1152]{1,0:T(8,128)(2,1)S(1)}, u32[]{:S(2)}, u32[]{:S(2)}) collective-permute-start(bf16[896,1152]{1,0:T(8,128)(2,1)} %get-tuple-element.111.refs_21_), channel_id=1, source_target_pairs={{0,1},{1,0},{2,3},{3,2},{4,5},{5,4},{6,7},{7,6}} | collective-permute-start | bytes 6193160 | tf_op jit(solution)/shard_map/ppermute | solution.py:33
  618.4 172.5 %collective-permute-start.30 = (bf16[896,1152]{1,0:T(8,128)(2,1)}, bf16[896,1152]{1,0:T(8,128)(2,1)S(1)}, u32[]{:S(2)}, u32[]{:S(2)}) collective-permute-start(bf16[896,1152]{1,0:T(8,128)(2,1)} %get-tuple-element.112.refs_22_), channel_id=1, source_target_pairs={{0,1},{1,0},{2,3},{3,2},{4,5},{5,4},{6,7},{7,6}} | collective-permute-start | bytes 6193160 | tf_op jit(solution)/shard_map/ppermute | solution.py:33
  621.3 169.0 %collective-permute-start.24 = (bf16[896,1152]{1,0:T(8,128)(2,1)}, bf16[896,1152]{1,0:T(8,128)(2,1)S(1)}, u32[]{:S(2)}, u32[]{:S(2)}) collective-permute-start(bf16[896,1152]{1,0:T(8,128)(2,1)} %get-tuple-element.112.refs_22_), channel_id=1, source_target_pairs={{0,2},{2,0},{1,3},{3,1},{4,6},{6,4},{5,7},{7,5}} | collective-permute-start | bytes 6193160 | tf_op jit(solution)/shard_map/ppermute | solution.py:29
  624.3 166.6 %collective-permute-start.31 = (bf16[1152,896]{1,0:T(8,128)(2,1)}, bf16[1152,896]{1,0:T(8,128)(2,1)}, u32[]{:S(2)}, u32[]{:S(2)}) collective-permute-start(bf16[1152,896]{1,0:T(8,128)(2,1)} %get-tuple-element.113.refs_23_), channel_id=1, source_target_pairs={{0,1},{1,0},{2,3},{3,2},{4,5},{5,4},{6,7},{7,6}} | collective-permute-start | bytes 6193160 | tf_op jit(solution)/shard_map/ppermute | solution.py:33
  660.5 129.8 %collective-permute-start.25 = (bf16[1152,896]{1,0:T(8,128)(2,1)}, bf16[1152,896]{1,0:T(8,128)(2,1)S(1)}, u32[]{:S(2)}, u32[]{:S(2)}) collective-permute-start(bf16[1152,896]{1,0:T(8,128)(2,1)} %get-tuple-element.113.refs_23_), channel_id=1, source_target_pairs={{0,2},{2,0},{1,3},{3,1},{4,6},{6,4},{5,7},{7,5}} | collective-permute-start | bytes 6193160 | tf_op jit(solution)/shard_map/ppermute | solution.py:29
  790.3 44.7 %collective-permute-start.26 = (bf16[896,1152]{1,0:T(8,128)(2,1)S(1)}, bf16[896,1152]{1,0:T(8,128)(2,1)S(1)}, u32[]{:S(2)}, u32[]{:S(2)}) collective-permute-start(bf16[896,1152]{1,0:T(8,128)(2,1)S(1)} %collective-permute-done.23.refs_12_), channel_id=1, source_target_pairs={{0,1},{1,0},{2,3},{3,2},{4,5},{5,4},{6,7},{7,6}} | collective-permute-start | bytes 6193160 | tf_op jit(solution)/shard_map/ppermute | solution.py:33
  790.4 44.7 %collective-permute-start.27 = (bf16[896,1152]{1,0:T(8,128)(2,1)S(1)}, bf16[896,1152]{1,0:T(8,128)(2,1)S(1)}, u32[]{:S(2)}, u32[]{:S(2)}) collective-permute-start(bf16[896,1152]{1,0:T(8,128)(2,1)S(1)} %collective-permute-done.24.refs_13_), channel_id=1, source_target_pairs={{0,1},{1,0},{2,3},{3,2},{4,5},{5,4},{6,7},{7,6}} | collective-permute-start | bytes 6193160 | tf_op jit(solution)/shard_map/ppermute | solution.py:33
  790.9 44.2 %collective-permute-start.28 = (bf16[1152,896]{1,0:T(8,128)(2,1)S(1)}, bf16[1152,896]{1,0:T(8,128)(2,1)S(1)}, u32[]{:S(2)}, u32[]{:S(2)}) collective-permute-start(bf16[1152,896]{1,0:T(8,128)(2,1)S(1)} %collective-permute-done.25.refs_14_), channel_id=1, source_target_pairs={{0,1},{1,0},{2,3},{3,2},{4,5},{5,4},{6,7},{7,6}} | collective-permute-start | bytes 6193160 | tf_op jit(solution)/shard_map/ppermute | solution.py:33
  (16 other events, 1389.6 us)

commit v4 on v3

--- a/solution.py
+++ b/solution.py
@@ -14,7 +14,7 @@
 
 LANES = 128
 BLOCK = 512
-ROWS = 1024
+ROWS = 512
 
 
 def dot(a, b, dims):
@@ -301,8 +301,7 @@
     g = g.astype(F32) * f
     m = 0.9 * m + 0.1 * g
     v = 0.95 * v + 0.05 * g * g
-    w = w.astype(F32)
-    return (w - 0.02 * (m * lax.rsqrt(v + 1e-8) + 0.1 * w)).astype(BF16), m, v
+    return (0.998 * w.astype(F32) - 0.02 * (m * lax.rsqrt(v + 1e-8))).astype(BF16), m, v
 
 
 SLOTS, AHEAD = 6, 3
@@ -310,7 +309,7 @@
 
 def adam(own, factor, who, arrays, pieces, outs):
     d, _ = arrays[0][0].shape[1:]
-    shapes = ((d // 8, own), (LANES, d), (d, LANES))
+    shapes = ((LANES, own), (LANES, d), (d, LANES))
     rows = []
     for n, (which, layer, slot, g) in enumerate(pieces):
         kind = 1 if which == 2 else 2 if slot == 4 else 0
@@ -388,7 +387,7 @@
                     for n in range(3):
                         pltpu.make_async_copy(weights[n].at[0, pl.ds(0, shapes[q][0]), pl.ds(0, shapes[q][1])], buffers[q][n].at[slot], sem_in.at[n, slot]).wait()
                     pltpu.make_async_copy(buffers[q][3].at[slot], buffers[q][3].at[slot], sem_in.at[3, slot]).wait()
-                    some = 16 if shapes[q][1] > d else 32 if shapes[q][1] > LANES else 128
+                    some = 32 if shapes[q][1] > LANES else 224
 
                     def part(r, carry):
                         at = pl.ds(pl.multiple_of(r * some, some), some)
@@ -418,7 +417,7 @@
         + [pltpu.SemaphoreType.DMA((4, SLOTS)), pltpu.SemaphoreType.DMA((3, SLOTS))],
         input_output_aliases={3 + n_in + n: n for n in range(len(before))},
         cost_estimate=pl.CostEstimate(flops=2000 * elements, bytes_accessed=22 * elements, transcendentals=elements),
-        compiler_params=params(30),
+        compiler_params=params(),
     )(table, who, factor, *given, *(piece[3] for piece in pieces), *before)
     return tuple(tuple(new[3 * n : 3 * n + 3]) for n in range(3))
 
@@ -448,28 +447,30 @@
         top_x = [send(top[n], px) for n in range(3)]
         top_d = [send(top[n], pd) for n in range(3)]
         low = slices(0, own, me, [a0, a0_d, a0_x, a0_xd], [dh1, dh1_d, dh1_x, dh1_xd], wg, wu, wd)
-        top_xd = [send(top_x[n], pd) for n in range(3)]
         total = jnp.sum(top[6] + low[6]).reshape(1)
         total = total + px(total)
-        total = total + pd(total) + jnp.sum(top[7] + low[7])
         low, total = lax.optimization_barrier((low, total))
         low_x = [send(low[n], px) for n in range(3)]
         low_d = [send(low[n], pd) for n in range(3)]
+        total = total + pd(total) + jnp.sum(top[7] + low[7])
         count = wg.size + wu.size + wd.size
         factor = jnp.minimum(1.0, 0.5 * lax.rsqrt(total / count + 1e-30))
 
+        top_xd = [send(top_x[n], pd) for n in range(3)]
+        low_xd = [send(low_x[n], pd) for n in range(2)]
         arrays = ((wg, mg, vg), (wu, mu, vu), (wd, md, vd))
 
-        def pieces(layer, slot, gs):
-            return [(n, layer, slot, gs[n]) for n in range(3)]
-
-        first = pieces(1, 0, top) + pieces(1, 1, top_d) + pieces(1, 2, top_x) + pieces(1, 3, top_xd) + pieces(0, 0, low)
+        def pieces(layer, slot, gs, names=(0, 1, 2)):
+            return [(n, layer, slot, gs[n]) for n in names]
+
+        first = pieces(1, 0, top) + pieces(1, 1, top_d) + pieces(1, 2, top_x) + pieces(0, 0, low)
         shared = pieces(1, 4, top[3:6]) + pieces(0, 4, low[3:6])
         outs = adam(own, factor, who, arrays, first + shared, None)
-        outs, low_x = lax.optimization_barrier((outs, low_x))
-        low_xd = [send(low_x[n], pd) for n in range(3)]
-        outs = adam(own, factor, who, arrays, pieces(0, 1, low_d) + pieces(0, 2, low_x), outs)
-        outs = adam(own, factor, who, arrays, pieces(0, 3, low_xd), outs)
+        outs = adam(own, factor, who, arrays, pieces(1, 3, top_xd) + pieces(0, 1, low_d), outs)
+        outs, low_x[2] = lax.optimization_barrier((outs, low_x[2]))
+        low_xd.append(send(low_x[2], pd))
+        outs = adam(own, factor, who, arrays, pieces(0, 2, low_x) + pieces(0, 3, low_xd, (0, 1)), outs)
+        outs = adam(own, factor, who, arrays, pieces(0, 3, low_xd, (2,)), outs)
         return tuple(outs[name][which] for which in range(3) for name in range(3))
 
     return jax.shard_map(

time: 873 us -> 932 us (1.068)
  waiting for transfers between devices: 157 us -> 223 us
  local copies, waits for them, and re-layouts: 14.5 us -> 0.01 us
    ppermute x11, waiting for transfers between devices: 141 us -> 213 us  [px(): return lax.ppermute(a, 'dp', PX)]
    unnamed x32 -> x4, local copies, waits for them, and re-layouts: 14.5 us -> 0.01 us
    pallas_call x1, Pallas kernels: 128 us -> 117 us  [chain(): pl.pallas_call(lambda *refs: chain_kernel(ff - (steps - 1) * BLOCK, *refs...]
    ppermute x21, starting transfers between devices: 4.84 us -> 15.1 us  [pd(): return lax.ppermute(a, 'dp', PD)]
    pallas_call x3 -> x4, Pallas kernels: 187 us -> 192 us  [adam(): pl.pallas_call(kernel, in_specs=[pl.BlockSpec(memory_space=pltpu.SMEM)] *...]
  transfers between devices with their start and end apart: 32 -> 32, of which waited for: 13 -> 9; matrix products, arithmetic and copies ran while one was open for 0% -> 0% of each run, Pallas kernels for 74% -> 63%
where the time goes in v4:
time: 932 us; the launch traced here: 924 us
  Pallas kernels  664 us (71%)
  waiting for transfers between devices  223 us (24%)
  starting transfers between devices  30.1 us (3%)
    pallas_call x2, Pallas kernels, slices(): pl.pallas_call(lambda *refs: slices_kernel(own, *refs), grid_spec=pltpu.P...  281 us
    ppermute x11, waiting for transfers between devices, px(): return lax.ppermute(a, 'dp', PX)  213 us
    pallas_call x4, Pallas kernels, adam(): pl.pallas_call(kernel, in_specs=[pl.BlockSpec(memory_space=pltpu.SMEM)] *...  192 us
    pallas_call x1, Pallas kernels, chain(): pl.pallas_call(lambda *refs: chain_kernel(ff - (steps - 1) * BLOCK, *refs...  117 us
    pallas_call x1, Pallas kernels, forward(): pl.pallas_call(lambda *refs: forward_kernel(ff - (steps - 1) * BLOCK, *re...  74.2 us
  transfers between devices with their start and end apart: 32, of which 9 were waited for; matrix products, arithmetic and copies ran while one was open for 0% of the time, Pallas kernels for 63%

profile of v4, /device:TPU:0, one launch (start us, length us, event | category | flops | bytes accessed | tf_op | source)
XLA Modules:
  0.0 924.2 jit_solution(15556720443227276998)
XLA Ops:
  0.6 74.2 %forward.1 = (bf16[2048,896]{1,0:T(8,128)(2,1)}, bf16[2048,896]{1,0:T(8,128)(2,1)}, bf16[2048,896]{1,0:T(8,128)(2,1)}) custom-call(bf16[2048,896]{1,0:T(8,128)(2,1)} %bitcast.5, bf16[2,896,4736]{2,1,0:T(8,128)(2,1)} %refs_0_.7, bf16[2,896,4736]{2,1,0:T(8,128)(2,1)} %refs_3_.11, bf16[2,4736,896]{2,1,0:T(8,128)(2,1)} %refs_6_.7), custom_call_target="tpu_custom_call" | custom-call | flops 52143587328 | bytes 25460736 | tf_op jit(solution)/shard_map/forward/pallas_call | solution.py:102
  74.8 3.3 collective-permute-start.2
  78.2 0.5 collective-permute-start.4
  78.7 80.0 %collective-permute-done.2.refs_3_ = bf16[2048,896]{1,0:T(8,128)(2,1)} collective-permute-done((bf16[2048,896]{1,0:T(8,128)(2,1)}, bf16[2048,896]{1,0:T(8,128)(2,1)}, u32[]{:S(2)}, u32[]{:S(2)}) %collective-permute-start.2) | collective-permute-done | bytes 3670048 | tf_op jit(solution)/shard_map/ppermute | solution.py:29
  158.7 77.9 %collective-permute-done.5.refs_7_ = bf16[2048,896]{1,0:T(8,128)(2,1)} collective-permute-done((bf16[2048,896]{1,0:T(8,128)(2,1)}, bf16[2048,896]{1,0:T(8,128)(2,1)}, u32[]{:S(2)}, u32[]{:S(2)}) %collective-permute-start.5) | collective-permute-done | bytes 3670048 | tf_op jit(solution)/shard_map/ppermute | solution.py:29
  236.5 116.9 %chain.1.refs_5_ = bf16[2048,896]{1,0:T(8,128)(2,1)} custom-call(bf16[2048,896]{1,0:T(8,128)(2,1)} %get-tuple-element.93.refs_1_.refs_0_, bf16[2048,896]{1,0:T(8,128)(2,1)} %bitcast.8, bf16[2048,896]{1,0:T(8,128)(2,1)} %get-tuple-element.102.refs_2_, bf16[2,896,4736]{2,1,0:T(8,128)(2,1)} %refs_0_.7, bf16[2,896,4736]{2,1,0:T(8,128)(2,1)} %refs_3_.11, ...), custom_call_target="tpu_custom_call" | custom-call | flops 86905978880 | bytes 25460736 | tf_op jit(solution)/shard_map/chain/pallas_call | solution.py:173
  353.5 1.8 collective-permute-start.8
  355.8 140.2 %slices.2 = (bf16[896,1152]{1,0:T(8,128)(2,1)}, bf16[896,1152]{1,0:T(8,128)(2,1)}, bf16[1152,896]{1,0:T(8,128)(2,1)}, bf16[896,128]{1,0:T(8,128)(2,1)}, bf16[896...) custom-call(s32[1]{0:T(128)} %bitcast.refs_0_, ...), custom_call_target="tpu_custom_call" | custom-call | flops 112742891520 | bytes 29360128 | tf_op jit(solution)/shard_map/slices/pallas_call | solution.py:269
  496.0 18.2 %collective-permute-done.7.refs_3_ = bf16[2048,896]{1,0:T(8,128)(2,1)} collective-permute-done((bf16[2048,896]{1,0:T(8,128)(2,1)}, bf16[2048,896]{1,0:T(8,128)(2,1)}, u32[]{:S(2)}, u32[]{:S(2)}) %collective-permute-start.7) | collective-permute-done | bytes 3670048 | tf_op jit(solution)/shard_map/ppermute | solution.py:29
  514.2 0.5 collective-permute-start.9
  514.7 1.7 collective-permute-start.14
  516.8 4.2 collective-permute-done.11.refs_8_
  520.9 1.7 collective-permute-start.18
  522.7 3.5 collective-permute-done.9.refs_4_
  526.2 140.4 %slices.3 = (bf16[896,1152]{1,0:T(8,128)(2,1)}, bf16[896,1152]{1,0:T(8,128)(2,1)}, bf16[1152,896]{1,0:T(8,128)(2,1)}, bf16[896,128]{1,0:T(8,128)(2,1)}, bf16[896...) custom-call(s32[1]{0:T(128)} %bitcast.refs_0_, ...), custom_call_target="tpu_custom_call" | custom-call | flops 112742891520 | bytes 29360128 | tf_op jit(solution)/shard_map/slices/pallas_call | solution.py:269
  666.6 1.3 add_reduce_fusion.1
  667.9 1.9 collective-permute-start.12
  669.7 1.8 collective-permute-done.12
  672.9 0.5 collective-permute-start.25
  673.4 0.5 collective-permute-start.17
  674.0 2.0 collective-permute-done.24.refs_13_
  676.0 11.4 %collective-permute-start.13 = (f32[1]{0:T(128)}, f32[1]{0:T(128)}, u32[]{:S(2)}, u32[]{:S(2)}) collective-permute-start(f32[1]{0:T(128)} %add.22), channel_id=1, source_target_pairs={{0,1},{1,0},{2,3},{3,2},{4,5},{5,4},{6,7},{7,6}} | collective-permute-start | bytes 20 | tf_op jit(solution)/shard_map/ppermute | solution.py:33
  687.9 0.6 compare_select_fusion.who_ref
  688.5 1.3 add_reduce_fusion
  691.5 1.9 collective-permute-start.26
  693.5 1.9 collective-permute-start.29
  695.4 96.1 %shard_map.214 = (bf16[2,896,4736]{2,1,0:T(8,128)(2,1)}, f32[2,896,4736]{2,1,0:T(8,128)}, f32[2,896,4736]{2,1,0:T(8,128)}, bf16[2,896,4736]{2,1,0:T(8,128)(2,1)}...) custom-call(s32[8,98]{1,0:T(8,128)} %constant.25.clone.table_ref, ...), custom_call_target="tpu_custom_call" | custom-call | flops 26148864000 | bytes 287637504 | tf_op jit(solution)/shard_map/pallas_call | solution.py:411
  791.9 35.5 %collective-permute-done.29.refs_10_ = bf16[896,1152]{1,0:T(8,128)(2,1)} collective-permute-done((bf16[896,1152]{1,0:T(8,128)(2,1)}, bf16[896,1152]{1,0:T(8,128)(2,1)}, u32[]{:S(2)}, u32[]{:S(2)}) %collective-permute-start.29) | collective-permute-done | bytes 2064416 | tf_op jit(solution)/shard_map/ppermute | solution.py:29
  827.4 46.5 %shard_map.215 = (bf16[2,896,4736]{2,1,0:T(8,128)(2,1)}, f32[2,896,4736]{2,1,0:T(8,128)}, f32[2,896,4736]{2,1,0:T(8,128)}, bf16[2,896,4736]{2,1,0:T(8,128)(2,1)}...) custom-call(s32[8,46]{1,0:T(8,128)} %constant.26.clone.table_ref, ...), custom_call_target="tpu_custom_call", output_to_operand_aliasing={{0}: (18, {}), {1}: (19, {}), {2}: (20, {}), {3}: (21, {}),... | custom-call | flops 12386304000 | bytes 136249344 | tf_op jit(solution)/shard_map/pallas_call | solution.py:411
  873.9 0.4 collective-permute-start.27
  874.4 39.4 %shard_map.216 = (bf16[2,896,4736]{2,1,0:T(8,128)(2,1)}, f32[2,896,4736]{2,1,0:T(8,128)}, f32[2,896,4736]{2,1,0:T(8,128)}, bf16[2,896,4736]{2,1,0:T(8,128)(2,1)}...) custom-call(s32[8,37]{1,0:T(8,128)} %constant.27.clone.table_ref, ...), custom_call_target="tpu_custom_call", output_to_operand_aliasing={{0}: (17, {}), {1}: (18, {}), {2}: (19, {}), {3}: (20, {}),... | custom-call | flops 10321920000 | bytes 113541120 | tf_op jit(solution)/shard_map/pallas_call | solution.py:411
  913.8 10.2 %shard_map.217 = (bf16[2,896,4736]{2,1,0:T(8,128)(2,1)}, f32[2,896,4736]{2,1,0:T(8,128)}, f32[2,896,4736]{2,1,0:T(8,128)}, bf16[2,896,4736]{2,1,0:T(8,128)(2,1)}...) custom-call(s32[8,9]{1,0:T(8,128)} %constant.28.clone.table_ref, ...), custom_call_target="tpu_custom_call", output_to_operand_aliasing={{0}: (13, {}), {1}: (14, {}), {2}: (15, {}), {3}: (16, {}),... | custom-call | flops 2064384000 | bytes 22708224 | tf_op jit(solution)/shard_map/pallas_call | solution.py:411
  (47 shorter events, 2.4 us)
Async XLA Ops:
  74.8 83.8 %collective-permute-start.2 = (bf16[2048,896]{1,0:T(8,128)(2,1)}, bf16[2048,896]{1,0:T(8,128)(2,1)}, u32[]{:S(2)}, u32[]{:S(2)}) collective-permute-start(bf16[2048,896]{1,0:T(8,128)(2,1)} %get-tuple-element.93.refs_1_.refs_0_), channel_id=1, source_target_pairs={{0,2},{2,0},{1,3},{3,1},{4,6},{6,4},{5,7},{7,5}} | collective-permute-start | bytes 11010056 | tf_op jit(solution)/shard_map/ppermute | solution.py:29
  78.1 158.4 %collective-permute-start.5 = (bf16[2048,896]{1,0:T(8,128)(2,1)}, bf16[2048,896]{1,0:T(8,128)(2,1)}, u32[]{:S(2)}, u32[]{:S(2)}) collective-permute-start(bf16[2048,896]{1,0:T(8,128)(2,1)} %bitcast.6), channel_id=1, source_target_pairs={{0,2},{2,0},{1,3},{3,1},{4,6},{6,4},{5,7},{7,5}} | collective-permute-start | bytes 11010056 | tf_op jit(solution)/shard_map/ppermute | solution.py:29
  78.2 277.1 %collective-permute-start.1 = (bf16[2048,896]{1,0:T(8,128)(2,1)}, bf16[2048,896]{1,0:T(8,128)(2,1)}, u32[]{:S(2)}, u32[]{:S(2)}) collective-permute-start(bf16[2048,896]{1,0:T(8,128)(2,1)} %get-tuple-element.93.refs_1_.refs_0_), channel_id=1, source_target_pairs={{0,1},{1,0},{2,3},{3,2},{4,5},{5,4},{6,7},{7,6}} | collective-permute-start | bytes 11010056 | tf_op jit(solution)/shard_map/ppermute | solution.py:33
  78.2 277.3 %collective-permute-start.4 = (bf16[2048,896]{1,0:T(8,128)(2,1)}, bf16[2048,896]{1,0:T(8,128)(2,1)}, u32[]{:S(2)}, u32[]{:S(2)}) collective-permute-start(bf16[2048,896]{1,0:T(8,128)(2,1)} %bitcast.7), channel_id=1, source_target_pairs={{0,1},{1,0},{2,3},{3,2},{4,5},{5,4},{6,7},{7,6}} | collective-permute-start | bytes 11010056 | tf_op jit(solution)/shard_map/ppermute | solution.py:33
  158.6 197.1 %collective-permute-start.3 = (bf16[2048,896]{1,0:T(8,128)(2,1)}, bf16[2048,896]{1,0:T(8,128)(2,1)}, u32[]{:S(2)}, u32[]{:S(2)}) collective-permute-start(bf16[2048,896]{1,0:T(8,128)(2,1)} %collective-permute-done.2.refs_3_), channel_id=1, source_target_pairs={{0,1},{1,0},{2,3},{3,2},{4,5},{5,4},{6,7},{7,6}} | collective-permute-start | bytes 11010056 | tf_op jit(solution)/shard_map/ppermute | solution.py:33
  236.5 119.2 %collective-permute-start.6 = (bf16[2048,896]{1,0:T(8,128)(2,1)}, bf16[2048,896]{1,0:T(8,128)(2,1)}, u32[]{:S(2)}, u32[]{:S(2)}) collective-permute-start(bf16[2048,896]{1,0:T(8,128)(2,1)} %collective-permute-done.5.refs_7_), channel_id=1, source_target_pairs={{0,1},{1,0},{2,3},{3,2},{4,5},{5,4},{6,7},{7,6}} | collective-permute-start | bytes 11010056 | tf_op jit(solution)/shard_map/ppermute | solution.py:33
  353.5 142.5 %collective-permute-start.8 = (bf16[2048,896]{1,0:T(8,128)(2,1)}, bf16[2048,896]{1,0:T(8,128)(2,1)}, u32[]{:S(2)}, u32[]{:S(2)}) collective-permute-start(bf16[2048,896]{1,0:T(8,128)(2,1)} %chain.1.refs_5_), channel_id=1, source_target_pairs={{0,2},{2,0},{1,3},{3,1},{4,6},{6,4},{5,7},{7,5}} | collective-permute-start | bytes 11010056 | tf_op jit(solution)/shard_map/ppermute | solution.py:29
  355.2 161.2 %collective-permute-start.10 = (bf16[2048,896]{1,0:T(8,128)(2,1)}, bf16[2048,896]{1,0:T(8,128)(2,1)}, u32[]{:S(2)}, u32[]{:S(2)}) collective-permute-start(bf16[2048,896]{1,0:T(8,128)(2,1)} %chain.1.refs_5_), channel_id=1, source_target_pairs={{0,1},{1,0},{2,3},{3,2},{4,5},{5,4},{6,7},{7,6}} | collective-permute-start | bytes 11010056 | tf_op jit(solution)/shard_map/ppermute | solution.py:33
  355.4 158.7 %collective-permute-start.7 = (bf16[2048,896]{1,0:T(8,128)(2,1)}, bf16[2048,896]{1,0:T(8,128)(2,1)}, u32[]{:S(2)}, u32[]{:S(2)}) collective-permute-start(bf16[2048,896]{1,0:T(8,128)(2,1)} %get-tuple-element.92.refs_1_), channel_id=1, source_target_pairs={{0,2},{2,0},{1,3},{3,1},{4,6},{6,4},{5,7},{7,5}} | collective-permute-start | bytes 11010056 | tf_op jit(solution)/shard_map/ppermute | solution.py:29
  355.8 160.7 %collective-permute-start = (bf16[2048,896]{1,0:T(8,128)(2,1)}, bf16[2048,896]{1,0:T(8,128)(2,1)}, u32[]{:S(2)}, u32[]{:S(2)}) collective-permute-start(bf16[2048,896]{1,0:T(8,128)(2,1)} %get-tuple-element.92.refs_1_), channel_id=1, source_target_pairs={{0,1},{1,0},{2,3},{3,2},{4,5},{5,4},{6,7},{7,6}} | collective-permute-start | bytes 11010056 | tf_op jit(solution)/shard_map/ppermute | solution.py:33
  514.2 6.8 collective-permute-start.11
  514.2 12.0 %collective-permute-start.9 = (bf16[2048,896]{1,0:T(8,128)(2,1)}, bf16[2048,896]{1,0:T(8,128)(2,1)}, u32[]{:S(2)}, u32[]{:S(2)}) collective-permute-start(bf16[2048,896]{1,0:T(8,128)(2,1)} %collective-permute-done.7.refs_3_), channel_id=1, source_target_pairs={{0,1},{1,0},{2,3},{3,2},{4,5},{5,4},{6,7},{7,6}} | collective-permute-start | bytes 11010056 | tf_op jit(solution)/shard_map/ppermute | solution.py:33
  514.7 158.1 %collective-permute-start.14 = (bf16[896,1152]{1,0:T(8,128)(2,1)}, bf16[896,1152]{1,0:T(8,128)(2,1)}, u32[]{:S(2)}, u32[]{:S(2)}) collective-permute-start(bf16[896,1152]{1,0:T(8,128)(2,1)} %get-tuple-element.117.refs_9_), channel_id=1, source_target_pairs={{0,2},{2,0},{1,3},{3,1},{4,6},{6,4},{5,7},{7,5}} | collective-permute-start | bytes 6193160 | tf_op jit(solution)/shard_map/ppermute | solution.py:29
  516.4 157.5 %collective-permute-start.23 = (bf16[896,1152]{1,0:T(8,128)(2,1)}, bf16[896,1152]{1,0:T(8,128)(2,1)}, u32[]{:S(2)}, u32[]{:S(2)}) collective-permute-start(bf16[896,1152]{1,0:T(8,128)(2,1)} %get-tuple-element.117.refs_9_), channel_id=1, source_target_pairs={{0,1},{1,0},{2,3},{3,2},{4,5},{5,4},{6,7},{7,6}} | collective-permute-start | bytes 6193160 | tf_op jit(solution)/shard_map/ppermute | solution.py:33
  516.5 156.9 %collective-permute-start.16 = (bf16[896,1152]{1,0:T(8,128)(2,1)}, bf16[896,1152]{1,0:T(8,128)(2,1)}, u32[]{:S(2)}, u32[]{:S(2)}) collective-permute-start(bf16[896,1152]{1,0:T(8,128)(2,1)} %get-tuple-element.118.refs_10_), channel_id=1, source_target_pairs={{0,2},{2,0},{1,3},{3,1},{4,6},{6,4},{5,7},{7,5}} | collective-permute-start | bytes 6193160 | tf_op jit(solution)/shard_map/ppermute | solution.py:29
  520.9 152.5 %collective-permute-start.18 = (bf16[1152,896]{1,0:T(8,128)(2,1)}, bf16[1152,896]{1,0:T(8,128)(2,1)}, u32[]{:S(2)}, u32[]{:S(2)}) collective-permute-start(bf16[1152,896]{1,0:T(8,128)(2,1)} %get-tuple-element.119.refs_11_), channel_id=1, source_target_pairs={{0,2},{2,0},{1,3},{3,1},{4,6},{6,4},{5,7},{7,5}} | collective-permute-start | bytes 6193160 | tf_op jit(solution)/shard_map/ppermute | solution.py:29
  667.9 3.7 collective-permute-start.12
  671.5 4.5 collective-permute-start.24
  672.9 18.2 %collective-permute-start.25 = (bf16[1152,896]{1,0:T(8,128)(2,1)}, bf16[1152,896]{1,0:T(8,128)(2,1)}, u32[]{:S(2)}, u32[]{:S(2)}) collective-permute-start(bf16[1152,896]{1,0:T(8,128)(2,1)} %get-tuple-element.119.refs_11_), channel_id=1, source_target_pairs={{0,1},{1,0},{2,3},{3,2},{4,5},{5,4},{6,7},{7,6}} | collective-permute-start | bytes 6193160 | tf_op jit(solution)/shard_map/ppermute | solution.py:33
  673.4 18.1 %collective-permute-start.15 = (bf16[896,1152]{1,0:T(8,128)(2,1)}, bf16[896,1152]{1,0:T(8,128)(2,1)}, u32[]{:S(2)}, u32[]{:S(2)}) collective-permute-start(bf16[896,1152]{1,0:T(8,128)(2,1)} %collective-permute-done.14.refs_15_), channel_id=1, source_target_pairs={{0,1},{1,0},{2,3},{3,2},{4,5},{5,4},{6,7},{7,6}} | collective-permute-start | bytes 6193160 | tf_op jit(solution)/shard_map/ppermute | solution.py:33
  673.4 19.9 %collective-permute-start.17 = (bf16[896,1152]{1,0:T(8,128)(2,1)}, bf16[896,1152]{1,0:T(8,128)(2,1)}, u32[]{:S(2)}, u32[]{:S(2)}) collective-permute-start(bf16[896,1152]{1,0:T(8,128)(2,1)} %collective-permute-done.16.refs_16_), channel_id=1, source_target_pairs={{0,1},{1,0},{2,3},{3,2},{4,5},{5,4},{6,7},{7,6}} | collective-permute-start | bytes 6193160 | tf_op jit(solution)/shard_map/ppermute | solution.py:33
  673.9 19.6 %collective-permute-start.19 = (bf16[1152,896]{1,0:T(8,128)(2,1)}, bf16[1152,896]{1,0:T(8,128)(2,1)}, u32[]{:S(2)}, u32[]{:S(2)}) collective-permute-start(bf16[1152,896]{1,0:T(8,128)(2,1)} %collective-permute-done.18.refs_17_), channel_id=1, source_target_pairs={{0,1},{1,0},{2,3},{3,2},{4,5},{5,4},{6,7},{7,6}} | collective-permute-start | bytes 6193160 | tf_op jit(solution)/shard_map/ppermute | solution.py:33
  676.0 11.8 %collective-permute-start.13 = (f32[1]{0:T(128)}, f32[1]{0:T(128)}, u32[]{:S(2)}, u32[]{:S(2)}) collective-permute-start(f32[1]{0:T(128)} %add.22), channel_id=1, source_target_pairs={{0,1},{1,0},{2,3},{3,2},{4,5},{5,4},{6,7},{7,6}} | collective-permute-start | bytes 20 | tf_op jit(solution)/shard_map/ppermute | solution.py:33
  687.8 5.7 collective-permute-start.20
  691.1 136.3 %collective-permute-start.22 = (bf16[1152,896]{1,0:T(8,128)(2,1)}, bf16[1152,896]{1,0:T(8,128)(2,1)}, u32[]{:S(2)}, u32[]{:S(2)}) collective-permute-start(bf16[1152,896]{1,0:T(8,128)(2,1)} %get-tuple-element.122.refs_20_), channel_id=1, source_target_pairs={{0,1},{1,0},{2,3},{3,2},{4,5},{5,4},{6,7},{7,6}} | collective-permute-start | bytes 6193160 | tf_op jit(solution)/shard_map/ppermute | solution.py:33
  691.5 182.4 %collective-permute-start.26 = (bf16[1152,896]{1,0:T(8,128)(2,1)}, bf16[1152,896]{1,0:T(8,128)(2,1)}, u32[]{:S(2)}, u32[]{:S(2)}) collective-permute-start(bf16[1152,896]{1,0:T(8,128)(2,1)} %get-tuple-element.122.refs_20_), channel_id=1, source_target_pairs={{0,2},{2,0},{1,3},{3,1},{4,6},{6,4},{5,7},{7,5}} | collective-permute-start | bytes 6193160 | tf_op jit(solution)/shard_map/ppermute | solution.py:29
  693.4 98.2 %collective-permute-start.28 = (bf16[896,1152]{1,0:T(8,128)(2,1)}, bf16[896,1152]{1,0:T(8,128)(2,1)}, u32[]{:S(2)}, u32[]{:S(2)}) collective-permute-start(bf16[896,1152]{1,0:T(8,128)(2,1)} %get-tuple-element.120.refs_18_), channel_id=1, source_target_pairs={{0,2},{2,0},{1,3},{3,1},{4,6},{6,4},{5,7},{7,5}} | collective-permute-start | bytes 6193160 | tf_op jit(solution)/shard_map/ppermute | solution.py:29
  693.5 133.9 %collective-permute-start.21 = (bf16[896,1152]{1,0:T(8,128)(2,1)}, bf16[896,1152]{1,0:T(8,128)(2,1)}, u32[]{:S(2)}, u32[]{:S(2)}) collective-permute-start(bf16[896,1152]{1,0:T(8,128)(2,1)} %get-tuple-element.121.refs_19_), channel_id=1, source_target_pairs={{0,1},{1,0},{2,3},{3,2},{4,5},{5,4},{6,7},{7,6}} | collective-permute-start | bytes 6193160 | tf_op jit(solution)/shard_map/ppermute | solution.py:33
  693.5 133.8 %collective-permute-start.29 = (bf16[896,1152]{1,0:T(8,128)(2,1)}, bf16[896,1152]{1,0:T(8,128)(2,1)}, u32[]{:S(2)}, u32[]{:S(2)}) collective-permute-start(bf16[896,1152]{1,0:T(8,128)(2,1)} %get-tuple-element.121.refs_19_), channel_id=1, source_target_pairs={{0,2},{2,0},{1,3},{3,1},{4,6},{6,4},{5,7},{7,5}} | collective-permute-start | bytes 6193160 | tf_op jit(solution)/shard_map/ppermute | solution.py:29
  791.5 82.8 %collective-permute-start.30 = (bf16[896,1152]{1,0:T(8,128)(2,1)}, bf16[896,1152]{1,0:T(8,128)(2,1)}, u32[]{:S(2)}, u32[]{:S(2)}) collective-permute-start(bf16[896,1152]{1,0:T(8,128)(2,1)} %collective-permute-done.28.refs_9_), channel_id=1, source_target_pairs={{0,1},{1,0},{2,3},{3,2},{4,5},{5,4},{6,7},{7,6}} | collective-permute-start | bytes 6193160 | tf_op jit(solution)/shard_map/ppermute | solution.py:33
  827.4 47.0 %collective-permute-start.31 = (bf16[896,1152]{1,0:T(8,128)(2,1)}, bf16[896,1152]{1,0:T(8,128)(2,1)}, u32[]{:S(2)}, u32[]{:S(2)}) collective-permute-start(bf16[896,1152]{1,0:T(8,128)(2,1)} %collective-permute-done.29.refs_10_), channel_id=1, source_target_pairs={{0,1},{1,0},{2,3},{3,2},{4,5},{5,4},{6,7},{7,6}} | collective-permute-start | bytes 6193160 | tf_op jit(solution)/shard_map/ppermute | solution.py:33
  873.9 39.9 %collective-permute-start.27 = (bf16[1152,896]{1,0:T(8,128)(2,1)}, bf16[1152,896]{1,0:T(8,128)(2,1)}, u32[]{:S(2)}, u32[]{:S(2)}) collective-permute-start(bf16[1152,896]{1,0:T(8,128)(2,1)} %collective-permute-done.26.refs_11_), channel_id=1, source_target_pairs={{0,1},{1,0},{2,3},{3,2},{4,5},{5,4},{6,7},{7,6}} | collective-permute-start | bytes 6193160 | tf_op jit(solution)/shard_map/ppermute | solution.py:33
  (2 other events, 326.7 us)

commit v5 on v4

--- a/solution.py
+++ b/solution.py
@@ -183,33 +183,82 @@
     )(a, dy, h, wg, wu, wd)
 
 
-def slices_kernel(own, me_ref, *refs):
-    a_refs, dy_refs = refs[:4], refs[4:8]
-    weights, outs, scratch = refs[8:14], refs[14:22], refs[22:]
-    wg_ref, wu_ref, wd_ref, accg_ref, accu_ref, accd_ref, a_buf, dy_buf, sems = scratch
+def slices_kernel(layer, own, count, *refs):
+    me = lax.axis_index("dp")
+    chip, core = me // 2, me % 2
+    partner = chip * 2 + 1 - core
+    others = (partner, (1 - chip) * 2 + core, (1 - chip) * 2 + 1 - core)
+    a_refs, dy_refs, (wg_hbm, wu_hbm, wd_hbm) = refs[:3], refs[3:6], refs[6:9]
+    final = count is not None
+    before = refs[9:11] if final else ()
+    refs = refs[11 if final else 9 :]
+    outs, scratch = refs[:8], refs[8:]
+    wg_ref, wu_ref, wd_ref, accg_ref, accu_ref, accd_ref, a_buf, dy_buf, a_far, dy_far, sums_ref, sems, w_sems, send_sems, recv_sems, *terms = scratch
     i, steps = pl.program_id(0), pl.num_programs(0)
-    tokens = a_refs[0].shape[0]
-    each = tokens // ROWS
-    me = me_ref[0]
+    each = a_refs[0].shape[0] // ROWS
+    width = wg_ref.shape[1]
 
     def fetch(step, do):
-        slot = lax.rem(step, 2)
-        owner, chunk = step // each, lax.rem(step, each)
-        away = (owner + me) % 2 + 2 * ((owner // 2 + me // 2) % 2)
-        rows = pl.ds(pl.multiple_of(chunk * ROWS, ROWS), ROWS)
-        for k in range(4):
-
-            @pl.when(away == k)
+        slot, who = lax.rem(step, 2), step // each
+        rows = pl.ds(pl.multiple_of(lax.rem(step, each) * ROWS, ROWS), ROWS)
+        for k, (a, dy) in enumerate(zip((*a_refs, a_far), (*dy_refs, dy_far), strict=True)):
+
+            @pl.when(who == k)
             def _():
-                do(pltpu.make_async_copy(a_refs[k].at[rows, :], a_buf.at[slot], sems.at[0, slot]))
-                do(pltpu.make_async_copy(dy_refs[k].at[rows, :], dy_buf.at[slot], sems.at[1, slot]))
+                do(pltpu.make_async_copy(a.at[rows, :], a_buf.at[slot], sems.at[0, slot]))
+                do(pltpu.make_async_copy(dy.at[rows, :], dy_buf.at[slot], sems.at[1, slot]))
+
+    def weights():
+        parts = ((pl.ds(pl.multiple_of(me * own, LANES), own), pl.ds(0, own)), (pl.ds(4 * own, width - own), pl.ds(own, width - own)))
+        return [
+            pltpu.make_async_copy(*((hbm.at[layer, there, :], ref.at[here, :]) if n == 2 else (hbm.at[layer, :, there], ref.at[:, here])), w_sems.at[n, m])
+            for n, (hbm, ref) in enumerate(((wg_hbm, wg_ref), (wu_hbm, wu_ref), (wd_hbm, wd_ref)))
+            for m, (there, here) in enumerate(parts)
+        ]
+
+    def onward(n):
+        return pltpu.make_async_remote_copy(
+            src_ref=(a_refs[2], dy_refs[2])[n],
+            dst_ref=(a_far, dy_far)[n],
+            send_sem=send_sems.at[n],
+            recv_sem=recv_sems.at[n],
+            device_id={"dp": partner},
+            device_id_type=pl.DeviceIdType.MESH,
+        )
+
+    def told(n):
+        return pltpu.make_async_remote_copy(
+            src_ref=sums_ref.at[0],
+            dst_ref=sums_ref.at[1 + n],
+            send_sem=send_sems.at[2 + n],
+            recv_sem=recv_sems.at[2 + n],
+            device_id={"dp": others[n]},
+            device_id_type=pl.DeviceIdType.MESH,
+        )
+
+    barrier = pltpu.get_barrier_semaphore()
+    spoken = others if final else others[:1]
 
     @pl.when(i == 0)
     def _():
+        for other in spoken:
+            pl.semaphore_signal(barrier, inc=1, device_id={"dp": other}, device_id_type=pl.DeviceIdType.MESH)
         fetch(i, lambda copy: copy.start())
-        wg_ref[:, :own], wg_ref[:, own:] = weights[0][0], weights[1][0]
-        wu_ref[:, :own], wu_ref[:, own:] = weights[2][0], weights[3][0]
-        wd_ref[:own, :], wd_ref[own:, :] = weights[4][0], weights[5][0]
+        for copy in weights():
+            copy.start()
+        for copy in weights():
+            copy.wait()
+
+    @pl.when(i == 1)
+    def _():
+        pl.semaphore_wait(barrier, len(spoken))
+        for n in range(2):
+            onward(n).start()
+
+    @pl.when(i == 3 * each - 1)
+    def _():
+        for n in range(2):
+            onward(n).wait()
 
     @pl.when(i + 1 < steps)
     def _():
@@ -220,7 +269,6 @@
     pltpu.make_async_copy(dy_refs[0].at[pl.ds(0, ROWS), :], dy_buf.at[slot], sems.at[1, slot]).wait()
     a, dy = a_buf[slot], dy_buf[slot]
     a_t, dy_t = a.T, dy.T
-    width = wg_ref.shape[1]
     blocks = [pl.ds(c, min(BLOCK, width - c)) for c in range(0, width, BLOCK)]
     held = {}
 
@@ -240,61 +288,77 @@
         back(c - 1)
     back(len(blocks) - 1)
 
+    rest = pl.ds(own, width - own)
+
+    @pl.when(lax.rem(i, each) == each - 1)
+    def _():
+        for acc, term in zip((accg_ref, accu_ref, accd_ref), terms, strict=True):
+            term[i // each] = acc[:, rest]
+            acc[:, rest] = jnp.zeros_like(acc[:, rest])
+
     @pl.when(i == steps - 1)
     def _():
         sums = [None, None]
-        for acc, out, out_s, turned in ((accg_ref, *outs[0:4:3], False), (accu_ref, *outs[1:5:3], False), (accd_ref, *outs[2:6:3], True)):
+        for acc, term, out, out_s, turned in (
+            (accg_ref, terms[0], *outs[0:4:3], False),
+            (accu_ref, terms[1], *outs[1:5:3], False),
+            (accd_ref, terms[2], *outs[2:6:3], True),
+        ):
+            at = [(core + s) % 2 + 2 * ((chip + s // 2) % 2) for s in range(4)]
+            whole = term[at[0]] + term[at[1]] + term[at[2]] + term[at[3]]
             for c in range(0, width, LANES):
-                part = acc[:, c : c + LANES].astype(BF16)
+                part = (acc[:, c : c + LANES] if c < own else whole[:, c - own : c - own + LANES]).astype(BF16)
+                ref, place = (out, pl.ds(c, LANES)) if c < own else (out_s, pl.ds(c - own, LANES))
                 if turned:
-                    ref, at = (out, pl.ds(c, LANES)) if c < own else (out_s, pl.ds(c - own, LANES))
-                    ref[at, :] = part.T
+                    ref[place, :] = part.T
                 else:
-                    ref, at = (out, pl.ds(c, LANES)) if c < own else (out_s, pl.ds(c - own, LANES))
-                    ref[:, at] = part
+                    ref[:, place] = part
                 square = part.astype(F32)
                 square = jnp.sum((square * square).reshape(-1, 8, LANES), 0)
                 sums[c >= own] = square if sums[c >= own] is None else sums[c >= own] + square
-        outs[6][...], outs[7][...] = sums
-
-
-def slices(layer, own, me, a_all, dy_all, wg, wu, wd):
+        if not final:
+            outs[6][...], outs[7][...] = sums
+        else:
+            sums_ref[0] = sums[0] + before[0][...]
+            shared = jnp.sum(sums[1] + before[1][...])
+            for n in range(3):
+                told(n).start()
+            for n in range(3):
+                told(n).wait()
+            total = sums_ref[at[0]] + sums_ref[at[1]] + sums_ref[at[2]] + sums_ref[at[3]]
+            total = jnp.full((8, LANES), jnp.sum(total) + shared, F32)
+            outs[6][...] = jnp.minimum(1.0, 0.5 * lax.rsqrt(total / count + 1e-30))
+            outs[7][...] = jnp.zeros((8, LANES), F32)
+
+
+def slices(layer, own, a_all, dy_all, wg, wu, wd, before=None, count=None):
     tokens, d = a_all[0].shape
     ff = wg.shape[2]
     rest = ff - 4 * own
     width = own + rest
     any_ = pl.BlockSpec(memory_space=pl.ANY)
-    at = lambda s: once(s, lambda i, me: (0, 0))
+    at = lambda s: once(s, lambda i: (0, 0))
     sizes = [(d, own), (d, own), (own, d), (d, rest), (d, rest), (rest, d)]
     return pl.pallas_call(
-        lambda *refs: slices_kernel(own, *refs),
-        grid_spec=pltpu.PrefetchScalarGridSpec(
-            num_scalar_prefetch=1,
-            grid=(4 * tokens // ROWS,),
-            in_specs=[any_] * 8
-            + [
-                once((1, d, own), lambda i, me: (layer, 0, me[0])),
-                once((1, d, rest), lambda i, me: (layer, 0, 4 * own // rest)),
-            ]
-            * 2
-            + [
-                once((1, own, d), lambda i, me: (layer, me[0], 0)),
-                once((1, rest, d), lambda i, me: (layer, 4 * own // rest, 0)),
-            ],
-            out_specs=[at(s) for s in sizes] + [at((8, LANES))] * 2,
-            scratch_shapes=[pltpu.VMEM((d, width), BF16)] * 2
-            + [pltpu.VMEM((width, d), BF16)]
-            + [pltpu.VMEM((d, width), F32)] * 3
-            + [pltpu.VMEM((2, ROWS, d), BF16)] * 2
-            + [pltpu.SemaphoreType.DMA((2, 2))],
-        ),
+        lambda *refs: slices_kernel(layer, own, count, *refs),
+        grid=(4 * tokens // ROWS,),
+        in_specs=[any_] * 9 + [at((8, LANES))] * len(before or ()),
+        out_specs=[at(s) for s in sizes] + [at((8, LANES))] * 2,
+        scratch_shapes=[pltpu.VMEM((d, width), BF16)] * 2
+        + [pltpu.VMEM((width, d), BF16)]
+        + [pltpu.VMEM((d, width), F32)] * 3
+        + [pltpu.VMEM((2, ROWS, d), BF16)] * 2
+        + [pltpu.VMEM((tokens, d), BF16)] * 2
+        + [pltpu.VMEM((4, 8, LANES), F32)]
+        + [pltpu.SemaphoreType.DMA(n) for n in ((2, 2), (3, 2), (5,), (5,))]
+        + [pltpu.VMEM((4, d, rest), F32)] * 3,
         out_shape=[jax.ShapeDtypeStruct(s, BF16) for s in sizes] + [jax.ShapeDtypeStruct((8, LANES), F32)] * 2,
         cost_estimate=pl.CostEstimate(
             flops=12 * 4 * tokens * d * width, bytes_accessed=16 * tokens * d, transcendentals=4 * tokens * width
         ),
-        compiler_params=params(),
+        compiler_params=pltpu.CompilerParams(vmem_limit_bytes=62 << 20, collective_id=layer, has_side_effects=True),
         name="slices",
-    )(me.reshape(1), *a_all, *dy_all, wg, wg, wu, wu, wd, wd)
+    )(*a_all, *dy_all, wg, wu, wd, *(before or ()))
 
 
 def adam_math(f, w, m, v, g):
@@ -440,21 +504,13 @@
         a0_x, a0_d = send(a0, px), send(a0, pd)
         dh1 = chain(a1, dy, h1, wg, wu, wd)
         dh1_x, dh1_d = send(dh1, px), send(dh1, pd)
-        a1_xd, dy_xd = send(a1_x, pd), send(dy_x, pd)
-        top = slices(1, own, me, [a1, a1_d, a1_x, a1_xd], [dy, dy_d, dy_x, dy_xd], wg, wu, wd)
-        top, a0_x, dh1_x = lax.optimization_barrier((top, a0_x, dh1_x))
-        a0_xd, dh1_xd = send(a0_x, pd), send(dh1_x, pd)
+        top = slices(1, own, [a1, a1_d, a1_x], [dy, dy_d, dy_x], wg, wu, wd)
         top_x = [send(top[n], px) for n in range(3)]
         top_d = [send(top[n], pd) for n in range(3)]
-        low = slices(0, own, me, [a0, a0_d, a0_x, a0_xd], [dh1, dh1_d, dh1_x, dh1_xd], wg, wu, wd)
-        total = jnp.sum(top[6] + low[6]).reshape(1)
-        total = total + px(total)
-        low, total = lax.optimization_barrier((low, total))
+        low = slices(0, own, [a0, a0_d, a0_x], [dh1, dh1_d, dh1_x], wg, wu, wd, top[6:8], wg.size + wu.size + wd.size)
+        factor = low[6][0, :1]
         low_x = [send(low[n], px) for n in range(3)]
         low_d = [send(low[n], pd) for n in range(3)]
-        total = total + pd(total) + jnp.sum(top[7] + low[7])
-        count = wg.size + wu.size + wd.size
-        factor = jnp.minimum(1.0, 0.5 * lax.rsqrt(total / count + 1e-30))
 
         top_xd = [send(top_x[n], pd) for n in range(3)]
         low_xd = [send(low_x[n], pd) for n in range(2)]

time: 932 us -> 795 us (0.85)
  waiting for transfers between devices: 223 us -> 92.7 us
  starting transfers between devices: 30.1 us -> 18.8 us
    ppermute x11 -> x10, waiting for transfers between devices: 213 us -> 88 us  [px(): return lax.ppermute(a, 'dp', PX)]
    ppermute x21 -> x16, starting transfers between devices: 15.1 us -> 4.15 us  [pd(): return lax.ppermute(a, 'dp', PD)]
  transfers between devices with their start and end apart: 32 -> 26, of which waited for: 9 -> 6; matrix products, arithmetic and copies ran while one was open for 0% -> 0% of each run, Pallas kernels for 63% -> 75%
where the time goes in v5:
time: 795 us; the launch traced here: 787 us
  Pallas kernels  673 us (85%)
  waiting for transfers between devices  92.7 us (12%)
  starting transfers between devices  18.8 us (2%)
    pallas_call x2, Pallas kernels, slices(): pl.pallas_call(lambda *refs: slices_kernel(layer, own, count, *refs), gri...  287 us
    pallas_call x4, Pallas kernels, adam(): pl.pallas_call(kernel, in_specs=[pl.BlockSpec(memory_space=pltpu.SMEM)] *...  195 us
    pallas_call x1, Pallas kernels, chain(): pl.pallas_call(lambda *refs: chain_kernel(ff - (steps - 1) * BLOCK, *refs...  117 us
    ppermute x10, waiting for transfers between devices, px(): return lax.ppermute(a, 'dp', PX)  88 us
    pallas_call x1, Pallas kernels, forward(): pl.pallas_call(lambda *refs: forward_kernel(ff - (steps - 1) * BLOCK, *re...  74.3 us
  transfers between devices with their start and end apart: 26, of which 6 were waited for; matrix products, arithmetic and copies ran while one was open for 0% of the time, Pallas kernels for 75%

profile of v5, /device:TPU:0, one launch (start us, length us, event | category | flops | bytes accessed | tf_op | source)
XLA Modules:
  0.0 787.0 jit_solution(4953301497392624713)
XLA Ops:
  0.6 74.3 %forward.1 = (bf16[2048,896]{1,0:T(8,128)(2,1)}, bf16[2048,896]{1,0:T(8,128)(2,1)}, bf16[2048,896]{1,0:T(8,128)(2,1)}) custom-call(bf16[2048,896]{1,0:T(8,128)(2,1)} %bitcast.3, bf16[2,896,4736]{2,1,0:T(8,128)(2,1)} %refs_0_.7, bf16[2,896,4736]{2,1,0:T(8,128)(2,1)} %refs_3_.11, bf16[2,4736,896]{2,1,0:T(8,128)(2,1)} %refs_6_.11), custom_call_target="tpu_custom_call" | custom-call | flops 52143587328 | bytes 25460736 | tf_op jit(solution)/shard_map/forward/pallas_call | solution.py:102
  74.9 0.8 collective-permute-start.4
  75.7 2.5 collective-permute-start.5
  78.2 0.2 collective-permute-start.6
  78.5 0.3 collective-permute-start.7
  78.7 116.9 %chain.1.refs_3_ = bf16[2048,896]{1,0:T(8,128)(2,1)} custom-call(bf16[2048,896]{1,0:T(8,128)(2,1)} %get-tuple-element.74.refs_0_, bf16[2048,896]{1,0:T(8,128)(2,1)} %bitcast.6, bf16[2048,896]{1,0:T(8,128)(2,1)} %get-tuple-element.75.refs_2_, bf16[2,896,4736]{2,1,0:T(8,128)(2,1)} %refs_0_.7, bf16[2,896,4736]{2,1,0:T(8,128)(2,1)} %refs_3_.11, ...), custom_call_target="tpu_custom_call" | custom-call | flops 86905978880 | bytes 25460736 | tf_op jit(solution)/shard_map/chain/pallas_call | solution.py:173
  195.7 1.8 collective-permute-start.3
  197.7 0.3 collective-permute-start.1
  198.0 39.4 %collective-permute-done.7.refs_5_ = bf16[2048,896]{1,0:T(8,128)(2,1)} collective-permute-done((bf16[2048,896]{1,0:T(8,128)(2,1)}, bf16[2048,896]{1,0:T(8,128)(2,1)}, u32[]{:S(2)}, u32[]{:S(2)}) %collective-permute-start.7) | collective-permute-done | bytes 3670048 | tf_op jit(solution)/shard_map/ppermute | solution.py:29
  237.4 141.9 %slices.2 = (bf16[896,1152]{1,0:T(8,128)(2,1)}, bf16[896,1152]{1,0:T(8,128)(2,1)}, bf16[1152,896]{1,0:T(8,128)(2,1)}, bf16[896,128]{1,0:T(8,128)(2,1)}, bf16[896...) custom-call(bf16[2048,896]{1,0:T(8,128)(2,1)} %get-tuple-element.74.refs_0_, ...), custom_call_target="tpu_custom_call" | custom-call | flops 112742891520 | bytes 29360128 | tf_op jit(solution)/shard_map/slices/pallas_call | solution.py:342
  379.3 2.0 collective-permute-start.8
  381.4 0.5 collective-permute-start.18
  381.9 12.8 %collective-permute-done.1.refs_2_ = bf16[2048,896]{1,0:T(8,128)(2,1)} collective-permute-done((bf16[2048,896]{1,0:T(8,128)(2,1)}, bf16[2048,896]{1,0:T(8,128)(2,1)}, u32[]{:S(2)}, u32[]{:S(2)}) %collective-permute-start.1) | collective-permute-done | bytes 3670048 | tf_op jit(solution)/shard_map/ppermute | solution.py:29
  394.7 2.0 collective-permute-start.12
  396.7 144.9 %slices.3 = (bf16[896,1152]{1,0:T(8,128)(2,1)}, bf16[896,1152]{1,0:T(8,128)(2,1)}, bf16[1152,896]{1,0:T(8,128)(2,1)}, bf16[896,128]{1,0:T(8,128)(2,1)}, bf16[896...) custom-call(bf16[2048,896]{1,0:T(8,128)(2,1)} %get-tuple-element.73.refs_0_, ...), custom_call_target="tpu_custom_call" | custom-call | flops 112742891520 | bytes 29360128 | tf_op jit(solution)/shard_map/slices/pallas_call | solution.py:342
  541.7 0.4 collective-permute-start.14
  542.2 0.4 collective-permute-start.16
  542.6 2.0 collective-permute-start.22
  544.7 0.5 compare_select_fusion.who_ref
  545.2 1.2 slice.3
  546.5 1.6 collective-permute-start.20
  548.1 0.9 collective-permute-done.14.refs_12_
  549.0 2.0 collective-permute-start.23
  551.0 0.9 collective-permute-done.15.refs_13_
  552.1 2.8 collective-permute-done.16.refs_14_
  555.1 35.7 %collective-permute-done.22.refs_9_ = bf16[896,1152]{1,0:T(8,128)(2,1)} collective-permute-done((bf16[896,1152]{1,0:T(8,128)(2,1)}, bf16[896,1152]{1,0:T(8,128)(2,1)}, u32[]{:S(2)}, u32[]{:S(2)}) %collective-permute-start.22) | collective-permute-done | bytes 2064416 | tf_op jit(solution)/shard_map/ppermute | solution.py:29
  590.8 96.8 %shard_map.214 = (bf16[2,896,4736]{2,1,0:T(8,128)(2,1)}, f32[2,896,4736]{2,1,0:T(8,128)}, f32[2,896,4736]{2,1,0:T(8,128)}, bf16[2,896,4736]{2,1,0:T(8,128)(2,1)}...) custom-call(s32[8,98]{1,0:T(8,128)} %constant.14.clone.table_ref, ...), custom_call_target="tpu_custom_call" | custom-call | flops 26148864000 | bytes 287637504 | tf_op jit(solution)/shard_map/pallas_call | solution.py:475
  687.6 0.6 collective-permute-start.24
  688.3 47.1 %shard_map.215 = (bf16[2,896,4736]{2,1,0:T(8,128)(2,1)}, f32[2,896,4736]{2,1,0:T(8,128)}, f32[2,896,4736]{2,1,0:T(8,128)}, bf16[2,896,4736]{2,1,0:T(8,128)(2,1)}...) custom-call(s32[8,46]{1,0:T(8,128)} %constant.15.clone.table_ref, ...), custom_call_target="tpu_custom_call", output_to_operand_aliasing={{0}: (18, {}), {1}: (19, {}), {2}: (20, {}), {3}: (21, {}),... | custom-call | flops 12386304000 | bytes 136249344 | tf_op jit(solution)/shard_map/pallas_call | solution.py:475
  735.4 0.5 collective-permute-start.21
  735.9 40.1 %shard_map.216 = (bf16[2,896,4736]{2,1,0:T(8,128)(2,1)}, f32[2,896,4736]{2,1,0:T(8,128)}, f32[2,896,4736]{2,1,0:T(8,128)}, bf16[2,896,4736]{2,1,0:T(8,128)(2,1)}...) custom-call(s32[8,37]{1,0:T(8,128)} %constant.16.clone.table_ref, ...), custom_call_target="tpu_custom_call", output_to_operand_aliasing={{0}: (17, {}), {1}: (18, {}), {2}: (19, {}), {3}: (20, {}),... | custom-call | flops 10321920000 | bytes 113541120 | tf_op jit(solution)/shard_map/pallas_call | solution.py:475
  776.0 10.8 %shard_map.217 = (bf16[2,896,4736]{2,1,0:T(8,128)(2,1)}, f32[2,896,4736]{2,1,0:T(8,128)}, f32[2,896,4736]{2,1,0:T(8,128)}, bf16[2,896,4736]{2,1,0:T(8,128)(2,1)}...) custom-call(s32[8,9]{1,0:T(8,128)} %constant.17.clone.table_ref, ...), custom_call_target="tpu_custom_call", output_to_operand_aliasing={{0}: (13, {}), {1}: (14, {}), {2}: (15, {}), {3}: (16, {}),... | custom-call | flops 2064384000 | bytes 22708224 | tf_op jit(solution)/shard_map/pallas_call | solution.py:475
  (30 shorter events, 0.9 us)
Async XLA Ops:
  74.9 120.8 %collective-permute-start.4 = (bf16[2048,896]{1,0:T(8,128)(2,1)}, bf16[2048,896]{1,0:T(8,128)(2,1)}, u32[]{:S(2)}, u32[]{:S(2)}) collective-permute-start(bf16[2048,896]{1,0:T(8,128)(2,1)} %get-tuple-element.74.refs_0_), channel_id=1, source_target_pairs={{0,1},{1,0},{2,3},{3,2},{4,5},{5,4},{6,7},{7,6}} | collective-permute-start | bytes 11010056 | tf_op jit(solution)/shard_map/ppermute | solution.py:33
  75.7 121.8 %collective-permute-start.5 = (bf16[2048,896]{1,0:T(8,128)(2,1)}, bf16[2048,896]{1,0:T(8,128)(2,1)}, u32[]{:S(2)}, u32[]{:S(2)}) collective-permute-start(bf16[2048,896]{1,0:T(8,128)(2,1)} %get-tuple-element.74.refs_0_), channel_id=1, source_target_pairs={{0,2},{2,0},{1,3},{3,1},{4,6},{6,4},{5,7},{7,5}} | collective-permute-start | bytes 11010056 | tf_op jit(solution)/shard_map/ppermute | solution.py:29
  78.2 119.4 %collective-permute-start.6 = (bf16[2048,896]{1,0:T(8,128)(2,1)}, bf16[2048,896]{1,0:T(8,128)(2,1)}, u32[]{:S(2)}, u32[]{:S(2)}) collective-permute-start(bf16[2048,896]{1,0:T(8,128)(2,1)} %bitcast.4), channel_id=1, source_target_pairs={{0,1},{1,0},{2,3},{3,2},{4,5},{5,4},{6,7},{7,6}} | collective-permute-start | bytes 11010056 | tf_op jit(solution)/shard_map/ppermute | solution.py:33
  78.5 158.9 %collective-permute-start.7 = (bf16[2048,896]{1,0:T(8,128)(2,1)}, bf16[2048,896]{1,0:T(8,128)(2,1)}, u32[]{:S(2)}, u32[]{:S(2)}) collective-permute-start(bf16[2048,896]{1,0:T(8,128)(2,1)} %bitcast.5), channel_id=1, source_target_pairs={{0,2},{2,0},{1,3},{3,1},{4,6},{6,4},{5,7},{7,5}} | collective-permute-start | bytes 11010056 | tf_op jit(solution)/shard_map/ppermute | solution.py:29
  195.7 185.7 %collective-permute-start.2 = (bf16[2048,896]{1,0:T(8,128)(2,1)}, bf16[2048,896]{1,0:T(8,128)(2,1)}, u32[]{:S(2)}, u32[]{:S(2)}) collective-permute-start(bf16[2048,896]{1,0:T(8,128)(2,1)} %chain.1.refs_3_), channel_id=1, source_target_pairs={{0,1},{1,0},{2,3},{3,2},{4,5},{5,4},{6,7},{7,6}} | collective-permute-start | bytes 11010056 | tf_op jit(solution)/shard_map/ppermute | solution.py:33
  195.7 185.6 %collective-permute-start.3 = (bf16[2048,896]{1,0:T(8,128)(2,1)}, bf16[2048,896]{1,0:T(8,128)(2,1)}, u32[]{:S(2)}, u32[]{:S(2)}) collective-permute-start(bf16[2048,896]{1,0:T(8,128)(2,1)} %chain.1.refs_3_), channel_id=1, source_target_pairs={{0,2},{2,0},{1,3},{3,1},{4,6},{6,4},{5,7},{7,5}} | collective-permute-start | bytes 11010056 | tf_op jit(solution)/shard_map/ppermute | solution.py:29
  197.5 183.9 %collective-permute-start = (bf16[2048,896]{1,0:T(8,128)(2,1)}, bf16[2048,896]{1,0:T(8,128)(2,1)}, u32[]{:S(2)}, u32[]{:S(2)}) collective-permute-start(bf16[2048,896]{1,0:T(8,128)(2,1)} %get-tuple-element.73.refs_0_), channel_id=1, source_target_pairs={{0,1},{1,0},{2,3},{3,2},{4,5},{5,4},{6,7},{7,6}} | collective-permute-start | bytes 11010056 | tf_op jit(solution)/shard_map/ppermute | solution.py:33
  197.7 197.0 %collective-permute-start.1 = (bf16[2048,896]{1,0:T(8,128)(2,1)}, bf16[2048,896]{1,0:T(8,128)(2,1)}, u32[]{:S(2)}, u32[]{:S(2)}) collective-permute-start(bf16[2048,896]{1,0:T(8,128)(2,1)} %get-tuple-element.73.refs_0_), channel_id=1, source_target_pairs={{0,2},{2,0},{1,3},{3,1},{4,6},{6,4},{5,7},{7,5}} | collective-permute-start | bytes 11010056 | tf_op jit(solution)/shard_map/ppermute | solution.py:29
  379.3 162.9 %collective-permute-start.8 = (bf16[896,1152]{1,0:T(8,128)(2,1)}, bf16[896,1152]{1,0:T(8,128)(2,1)}, u32[]{:S(2)}, u32[]{:S(2)}) collective-permute-start(bf16[896,1152]{1,0:T(8,128)(2,1)} %get-tuple-element.79.refs_9_), channel_id=1, source_target_pairs={{0,2},{2,0},{1,3},{3,1},{4,6},{6,4},{5,7},{7,5}} | collective-permute-start | bytes 6193160 | tf_op jit(solution)/shard_map/ppermute | solution.py:29
  381.3 160.9 %collective-permute-start.17 = (bf16[896,1152]{1,0:T(8,128)(2,1)}, bf16[896,1152]{1,0:T(8,128)(2,1)}, u32[]{:S(2)}, u32[]{:S(2)}) collective-permute-start(bf16[896,1152]{1,0:T(8,128)(2,1)} %get-tuple-element.79.refs_9_), channel_id=1, source_target_pairs={{0,1},{1,0},{2,3},{3,2},{4,5},{5,4},{6,7},{7,6}} | collective-permute-start | bytes 6193160 | tf_op jit(solution)/shard_map/ppermute | solution.py:33
  381.3 160.3 %collective-permute-start.10 = (bf16[896,1152]{1,0:T(8,128)(2,1)}, bf16[896,1152]{1,0:T(8,128)(2,1)}, u32[]{:S(2)}, u32[]{:S(2)}) collective-permute-start(bf16[896,1152]{1,0:T(8,128)(2,1)} %get-tuple-element.80.refs_10_), channel_id=1, source_target_pairs={{0,2},{2,0},{1,3},{3,1},{4,6},{6,4},{5,7},{7,5}} | collective-permute-start | bytes 6193160 | tf_op jit(solution)/shard_map/ppermute | solution.py:29
  381.4 161.2 %collective-permute-start.18 = (bf16[896,1152]{1,0:T(8,128)(2,1)}, bf16[896,1152]{1,0:T(8,128)(2,1)}, u32[]{:S(2)}, u32[]{:S(2)}) collective-permute-start(bf16[896,1152]{1,0:T(8,128)(2,1)} %get-tuple-element.80.refs_10_), channel_id=1, source_target_pairs={{0,1},{1,0},{2,3},{3,2},{4,5},{5,4},{6,7},{7,6}} | collective-permute-start | bytes 6193160 | tf_op jit(solution)/shard_map/ppermute | solution.py:33
  394.7 147.0 %collective-permute-start.12 = (bf16[1152,896]{1,0:T(8,128)(2,1)}, bf16[1152,896]{1,0:T(8,128)(2,1)}, u32[]{:S(2)}, u32[]{:S(2)}) collective-permute-start(bf16[1152,896]{1,0:T(8,128)(2,1)} %get-tuple-element.81.refs_11_), channel_id=1, source_target_pairs={{0,2},{2,0},{1,3},{3,1},{4,6},{6,4},{5,7},{7,5}} | collective-permute-start | bytes 6193160 | tf_op jit(solution)/shard_map/ppermute | solution.py:29
  541.6 4.9 collective-permute-start.19
  541.7 7.3 collective-permute-start.14
  542.1 9.8 %collective-permute-start.15 = (bf16[896,1152]{1,0:T(8,128)(2,1)}, bf16[896,1152]{1,0:T(8,128)(2,1)}, u32[]{:S(2)}, u32[]{:S(2)}) collective-permute-start(bf16[896,1152]{1,0:T(8,128)(2,1)} %get-tuple-element.83.refs_19_), channel_id=1, source_target_pairs={{0,1},{1,0},{2,3},{3,2},{4,5},{5,4},{6,7},{7,6}} | collective-permute-start | bytes 6193160 | tf_op jit(solution)/shard_map/ppermute | solution.py:33
  542.2 12.7 %collective-permute-start.16 = (bf16[1152,896]{1,0:T(8,128)(2,1)}, bf16[1152,896]{1,0:T(8,128)(2,1)}, u32[]{:S(2)}, u32[]{:S(2)}) collective-permute-start(bf16[1152,896]{1,0:T(8,128)(2,1)} %get-tuple-element.84.refs_20_), channel_id=1, source_target_pairs={{0,1},{1,0},{2,3},{3,2},{4,5},{5,4},{6,7},{7,6}} | collective-permute-start | bytes 6193160 | tf_op jit(solution)/shard_map/ppermute | solution.py:33
  542.6 48.1 %collective-permute-start.22 = (bf16[896,1152]{1,0:T(8,128)(2,1)}, bf16[896,1152]{1,0:T(8,128)(2,1)}, u32[]{:S(2)}, u32[]{:S(2)}) collective-permute-start(bf16[896,1152]{1,0:T(8,128)(2,1)} %get-tuple-element.82.refs_18_), channel_id=1, source_target_pairs={{0,2},{2,0},{1,3},{3,1},{4,6},{6,4},{5,7},{7,5}} | collective-permute-start | bytes 6193160 | tf_op jit(solution)/shard_map/ppermute | solution.py:29
  546.5 188.9 %collective-permute-start.20 = (bf16[1152,896]{1,0:T(8,128)(2,1)}, bf16[1152,896]{1,0:T(8,128)(2,1)}, u32[]{:S(2)}, u32[]{:S(2)}) collective-permute-start(bf16[1152,896]{1,0:T(8,128)(2,1)} %get-tuple-element.84.refs_20_), channel_id=1, source_target_pairs={{0,2},{2,0},{1,3},{3,1},{4,6},{6,4},{5,7},{7,5}} | collective-permute-start | bytes 6193160 | tf_op jit(solution)/shard_map/ppermute | solution.py:29
  549.0 138.6 %collective-permute-start.23 = (bf16[896,1152]{1,0:T(8,128)(2,1)}, bf16[896,1152]{1,0:T(8,128)(2,1)}, u32[]{:S(2)}, u32[]{:S(2)}) collective-permute-start(bf16[896,1152]{1,0:T(8,128)(2,1)} %get-tuple-element.83.refs_19_), channel_id=1, source_target_pairs={{0,2},{2,0},{1,3},{3,1},{4,6},{6,4},{5,7},{7,5}} | collective-permute-start | bytes 6193160 | tf_op jit(solution)/shard_map/ppermute | solution.py:29
  552.0 136.3 %collective-permute-start.11 = (bf16[896,1152]{1,0:T(8,128)(2,1)}, bf16[896,1152]{1,0:T(8,128)(2,1)}, u32[]{:S(2)}, u32[]{:S(2)}) collective-permute-start(bf16[896,1152]{1,0:T(8,128)(2,1)} %collective-permute-done.10.refs_16_), channel_id=1, source_target_pairs={{0,1},{1,0},{2,3},{3,2},{4,5},{5,4},{6,7},{7,6}} | collective-permute-start | bytes 6193160 | tf_op jit(solution)/shard_map/ppermute | solution.py:33
  554.9 133.4 %collective-permute-start.13 = (bf16[1152,896]{1,0:T(8,128)(2,1)}, bf16[1152,896]{1,0:T(8,128)(2,1)}, u32[]{:S(2)}, u32[]{:S(2)}) collective-permute-start(bf16[1152,896]{1,0:T(8,128)(2,1)} %collective-permute-done.12.refs_17_), channel_id=1, source_target_pairs={{0,1},{1,0},{2,3},{3,2},{4,5},{5,4},{6,7},{7,6}} | collective-permute-start | bytes 6193160 | tf_op jit(solution)/shard_map/ppermute | solution.py:33
  590.8 97.5 %collective-permute-start.9 = (bf16[896,1152]{1,0:T(8,128)(2,1)}, bf16[896,1152]{1,0:T(8,128)(2,1)}, u32[]{:S(2)}, u32[]{:S(2)}) collective-permute-start(bf16[896,1152]{1,0:T(8,128)(2,1)} %collective-permute-done.8.refs_15_), channel_id=1, source_target_pairs={{0,1},{1,0},{2,3},{3,2},{4,5},{5,4},{6,7},{7,6}} | collective-permute-start | bytes 6193160 | tf_op jit(solution)/shard_map/ppermute | solution.py:33
  687.6 48.3 %collective-permute-start.24 = (bf16[896,1152]{1,0:T(8,128)(2,1)}, bf16[896,1152]{1,0:T(8,128)(2,1)}, u32[]{:S(2)}, u32[]{:S(2)}) collective-permute-start(bf16[896,1152]{1,0:T(8,128)(2,1)} %collective-permute-done.22.refs_9_), channel_id=1, source_target_pairs={{0,1},{1,0},{2,3},{3,2},{4,5},{5,4},{6,7},{7,6}} | collective-permute-start | bytes 6193160 | tf_op jit(solution)/shard_map/ppermute | solution.py:33
  688.2 47.7 %collective-permute-start.25 = (bf16[896,1152]{1,0:T(8,128)(2,1)}, bf16[896,1152]{1,0:T(8,128)(2,1)}, u32[]{:S(2)}, u32[]{:S(2)}) collective-permute-start(bf16[896,1152]{1,0:T(8,128)(2,1)} %collective-permute-done.23.refs_10_), channel_id=1, source_target_pairs={{0,1},{1,0},{2,3},{3,2},{4,5},{5,4},{6,7},{7,6}} | collective-permute-start | bytes 6193160 | tf_op jit(solution)/shard_map/ppermute | solution.py:33
  735.4 40.6 %collective-permute-start.21 = (bf16[1152,896]{1,0:T(8,128)(2,1)}, bf16[1152,896]{1,0:T(8,128)(2,1)}, u32[]{:S(2)}, u32[]{:S(2)}) collective-permute-start(bf16[1152,896]{1,0:T(8,128)(2,1)} %collective-permute-done.20.refs_11_), channel_id=1, source_target_pairs={{0,1},{1,0},{2,3},{3,2},{4,5},{5,4},{6,7},{7,6}} | collective-permute-start | bytes 6193160 | tf_op jit(solution)/shard_map/ppermute | solution.py:33

commit v6 on v5

--- a/solution.py
+++ b/solution.py
@@ -10,7 +10,7 @@
 F32, BF16 = jnp.float32, jnp.bfloat16
 PX = ((0, 2), (2, 0), (1, 3), (3, 1))
 PD = ((0, 1), (1, 0), (2, 3), (3, 2))
-NN, NT = ((1,), (0,)), ((1,), (1,))
+NN = ((1,), (0,))
 
 LANES = 128
 BLOCK = 512
@@ -119,7 +119,7 @@
     return (dhid * u * (sig + act * (1 - sig))).astype(BF16), (dhid * act).astype(BF16), (act * u).astype(BF16)
 
 
-def chain_kernel(tail, a_ref, dy_ref, h_ref, wg_ref, wu_ref, wd_ref, dh_ref, acc_ref):
+def chain_kernel(tail, a_ref, dy_ref, h_ref, wg_ref, wu_ref, wd_ref, dh_ref, acc_ref, wgt_ref, wut_ref, wdt_ref):
     j, last = pl.program_id(0), pl.num_programs(0) - 1
     tokens = a_ref.shape[0]
     chunks = [pl.ds(r, ROWS) for r in range(0, tokens, ROWS)]
@@ -131,17 +131,20 @@
 
     def block(width):
         held = {}
+        wdt_ref[:, :width] = wd_ref[0, :width, :].T
+        wgt_ref[:width, :] = wg_ref[0, :, :width].T
+        wut_ref[:width, :] = wu_ref[0, :, :width].T
 
         def there(r):
             a, dy = a_ref[chunks[r], :], dy_ref[chunks[r], :]
             g = dot(a, wg_ref[0, :, :width], NN)
             u = dot(a, wu_ref[0, :, :width], NN)
-            dhid = dot(dy, wd_ref[0, :width, :], NT)
+            dhid = dot(dy, wdt_ref[:, :width], NN)
             held[r] = hidden_back(g, u, dhid)[:2]
 
         def back(r):
             dg, du = held.pop(r)
-            acc_ref[chunks[r], :] += dot(dg, wg_ref[0, :, :width], NT) + dot(du, wu_ref[0, :, :width], NT)
+            acc_ref[chunks[r], :] += dot(dg, wgt_ref[:width, :], NN) + dot(du, wut_ref[:width, :], NN)
 
         there(0)
         for r in range(1, len(chunks)):
@@ -176,7 +179,7 @@
         in_specs=[full, full, full, across, across, down],
         out_specs=full,
         out_shape=jax.ShapeDtypeStruct((tokens, d), BF16),
-        scratch_shapes=[pltpu.VMEM((tokens, d), F32)],
+        scratch_shapes=[pltpu.VMEM((tokens, d), F32)] + [pltpu.VMEM((BLOCK, d), BF16)] * 2 + [pltpu.VMEM((d, BLOCK), BF16)],
         cost_estimate=pl.CostEstimate(flops=10 * tokens * d * ff, bytes_accessed=6 * d * ff, transcendentals=tokens * ff),
         compiler_params=params(),
         name="chain",
@@ -193,7 +196,7 @@
     before = refs[9:11] if final else ()
     refs = refs[11 if final else 9 :]
     outs, scratch = refs[:8], refs[8:]
-    wg_ref, wu_ref, wd_ref, accg_ref, accu_ref, accd_ref, a_buf, dy_buf, a_far, dy_far, sums_ref, sems, w_sems, send_sems, recv_sems, *terms = scratch
+    wg_ref, wu_ref, wd_ref, accg_ref, accu_ref, accd_ref, a_buf, dy_buf, a_far, dy_far, sums_ref, sems, w_sems, send_sems, recv_sems, wdt_ref, *terms = scratch
     i, steps = pl.program_id(0), pl.num_programs(0)
     each = a_refs[0].shape[0] // ROWS
     width = wg_ref.shape[1]
@@ -248,6 +251,7 @@
             copy.start()
         for copy in weights():
             copy.wait()
+        wdt_ref[...] = wd_ref[...].T
 
     @pl.when(i == 1)
     def _():
@@ -274,7 +278,7 @@
 
     def there(c):
         s = blocks[c]
-        held[c] = hidden_back(dot(a, wg_ref[:, s], NN), dot(a, wu_ref[:, s], NN), dot(dy, wd_ref[s, :], NT))
+        held[c] = hidden_back(dot(a, wg_ref[:, s], NN), dot(a, wu_ref[:, s], NN), dot(dy, wdt_ref[:, s], NN))
 
     def back(c):
         s = blocks[c]
@@ -351,6 +355,7 @@
         + [pltpu.VMEM((tokens, d), BF16)] * 2
         + [pltpu.VMEM((4, 8, LANES), F32)]
         + [pltpu.SemaphoreType.DMA(n) for n in ((2, 2), (3, 2), (5,), (5,))]
+        + [pltpu.VMEM((d, width), BF16)]
         + [pltpu.VMEM((4, d, rest), F32)] * 3,
         out_shape=[jax.ShapeDtypeStruct(s, BF16) for s in sizes] + [jax.ShapeDtypeStruct((8, LANES), F32)] * 2,
         cost_estimate=pl.CostEstimate(

time: 795 us -> 796 us (level)
  no operation moved by 1% of the time
where the time goes in v6:
time: 796 us; the launch traced here: 788 us
  Pallas kernels  674 us (85%)
  waiting for transfers between devices  91.7 us (12%)
  starting transfers between devices  18.8 us (2%)
    pallas_call x2, Pallas kernels, slices(): pl.pallas_call(lambda *refs: slices_kernel(layer, own, count, *refs), gri...  288 us
    pallas_call x4, Pallas kernels, adam(): pl.pallas_call(kernel, in_specs=[pl.BlockSpec(memory_space=pltpu.SMEM)] *...  195 us
    pallas_call x1, Pallas kernels, chain(): pl.pallas_call(lambda *refs: chain_kernel(ff - (steps - 1) * BLOCK, *refs...  117 us
    ppermute x10, waiting for transfers between devices, px(): return lax.ppermute(a, 'dp', PX)  87 us
    pallas_call x1, Pallas kernels, forward(): pl.pallas_call(lambda *refs: forward_kernel(ff - (steps - 1) * BLOCK, *re...  74.2 us
  transfers between devices with their start and end apart: 26, of which 6 were waited for; matrix products, arithmetic and copies ran while one was open for 0% of the time, Pallas kernels for 75%

profile of v6, /device:TPU:0, one launch (start us, length us, event | category | flops | bytes accessed | tf_op | source)
XLA Modules:
  0.0 787.8 jit_solution(10305913257924545146)
XLA Ops:
  0.6 74.2 %forward.1 = (bf16[2048,896]{1,0:T(8,128)(2,1)}, bf16[2048,896]{1,0:T(8,128)(2,1)}, bf16[2048,896]{1,0:T(8,128)(2,1)}) custom-call(bf16[2048,896]{1,0:T(8,128)(2,1)} %bitcast.3, bf16[2,896,4736]{2,1,0:T(8,128)(2,1)} %refs_0_.7, bf16[2,896,4736]{2,1,0:T(8,128)(2,1)} %refs_3_.11, bf16[2,4736,896]{2,1,0:T(8,128)(2,1)} %refs_6_.11), custom_call_target="tpu_custom_call" | custom-call | flops 52143587328 | bytes 25460736 | tf_op jit(solution)/shard_map/forward/pallas_call | solution.py:102
  74.8 0.8 collective-permute-start.4
  75.7 2.5 collective-permute-start.5
  78.2 0.2 collective-permute-start.6
  78.4 0.3 collective-permute-start.7
  78.7 117.2 %chain.1.refs_3_ = bf16[2048,896]{1,0:T(8,128)(2,1)} custom-call(bf16[2048,896]{1,0:T(8,128)(2,1)} %get-tuple-element.74.refs_0_, bf16[2048,896]{1,0:T(8,128)(2,1)} %bitcast.6, bf16[2048,896]{1,0:T(8,128)(2,1)} %get-tuple-element.75.refs_2_, bf16[2,896,4736]{2,1,0:T(8,128)(2,1)} %refs_0_.7, bf16[2,896,4736]{2,1,0:T(8,128)(2,1)} %refs_3_.11, ...), custom_call_target="tpu_custom_call" | custom-call | flops 86905978880 | bytes 25460736 | tf_op jit(solution)/shard_map/chain/pallas_call | solution.py:176
  196.0 1.8 collective-permute-start.3
  197.9 0.3 collective-permute-start.1
  198.2 39.1 %collective-permute-done.7.refs_5_ = bf16[2048,896]{1,0:T(8,128)(2,1)} collective-permute-done((bf16[2048,896]{1,0:T(8,128)(2,1)}, bf16[2048,896]{1,0:T(8,128)(2,1)}, u32[]{:S(2)}, u32[]{:S(2)}) %collective-permute-start.7) | collective-permute-done | bytes 3670048 | tf_op jit(solution)/shard_map/ppermute | solution.py:29
  237.3 142.5 %slices.2 = (bf16[896,1152]{1,0:T(8,128)(2,1)}, bf16[896,1152]{1,0:T(8,128)(2,1)}, bf16[1152,896]{1,0:T(8,128)(2,1)}, bf16[896,128]{1,0:T(8,128)(2,1)}, bf16[896...) custom-call(bf16[2048,896]{1,0:T(8,128)(2,1)} %get-tuple-element.74.refs_0_, ...), custom_call_target="tpu_custom_call" | custom-call | flops 112742891520 | bytes 29360128 | tf_op jit(solution)/shard_map/slices/pallas_call | solution.py:346
  379.9 2.0 collective-permute-start.8
  382.0 0.5 collective-permute-start.18
  382.5 12.1 %collective-permute-done.1.refs_2_ = bf16[2048,896]{1,0:T(8,128)(2,1)} collective-permute-done((bf16[2048,896]{1,0:T(8,128)(2,1)}, bf16[2048,896]{1,0:T(8,128)(2,1)}, u32[]{:S(2)}, u32[]{:S(2)}) %collective-permute-start.1) | collective-permute-done | bytes 3670048 | tf_op jit(solution)/shard_map/ppermute | solution.py:29
  394.6 2.0 collective-permute-start.12
  396.6 145.5 %slices.3 = (bf16[896,1152]{1,0:T(8,128)(2,1)}, bf16[896,1152]{1,0:T(8,128)(2,1)}, bf16[1152,896]{1,0:T(8,128)(2,1)}, bf16[896,128]{1,0:T(8,128)(2,1)}, bf16[896...) custom-call(bf16[2048,896]{1,0:T(8,128)(2,1)} %get-tuple-element.73.refs_0_, ...), custom_call_target="tpu_custom_call" | custom-call | flops 112742891520 | bytes 29360128 | tf_op jit(solution)/shard_map/slices/pallas_call | solution.py:346
  542.3 0.4 collective-permute-start.14
  542.8 0.4 collective-permute-start.16
  543.2 2.0 collective-permute-start.22
  545.2 0.5 compare_select_fusion.who_ref
  545.8 1.2 slice.3
  547.0 1.6 collective-permute-start.20
  548.6 0.9 collective-permute-done.14.refs_12_
  549.6 2.0 collective-permute-start.23
  551.6 0.9 collective-permute-done.15.refs_13_
  552.7 2.8 collective-permute-done.16.refs_14_
  555.6 35.7 %collective-permute-done.22.refs_9_ = bf16[896,1152]{1,0:T(8,128)(2,1)} collective-permute-done((bf16[896,1152]{1,0:T(8,128)(2,1)}, bf16[896,1152]{1,0:T(8,128)(2,1)}, u32[]{:S(2)}, u32[]{:S(2)}) %collective-permute-start.22) | collective-permute-done | bytes 2064416 | tf_op jit(solution)/shard_map/ppermute | solution.py:29
  591.3 96.8 %shard_map.214 = (bf16[2,896,4736]{2,1,0:T(8,128)(2,1)}, f32[2,896,4736]{2,1,0:T(8,128)}, f32[2,896,4736]{2,1,0:T(8,128)}, bf16[2,896,4736]{2,1,0:T(8,128)(2,1)}...) custom-call(s32[8,98]{1,0:T(8,128)} %constant.14.clone.table_ref, ...), custom_call_target="tpu_custom_call" | custom-call | flops 26148864000 | bytes 287637504 | tf_op jit(solution)/shard_map/pallas_call | solution.py:480
  688.1 0.6 collective-permute-start.24
  688.8 47.1 %shard_map.215 = (bf16[2,896,4736]{2,1,0:T(8,128)(2,1)}, f32[2,896,4736]{2,1,0:T(8,128)}, f32[2,896,4736]{2,1,0:T(8,128)}, bf16[2,896,4736]{2,1,0:T(8,128)(2,1)}...) custom-call(s32[8,46]{1,0:T(8,128)} %constant.15.clone.table_ref, ...), custom_call_target="tpu_custom_call", output_to_operand_aliasing={{0}: (18, {}), {1}: (19, {}), {2}: (20, {}), {3}: (21, {}),... | custom-call | flops 12386304000 | bytes 136249344 | tf_op jit(solution)/shard_map/pallas_call | solution.py:480
  736.0 0.5 collective-permute-start.21
  736.5 40.1 %shard_map.216 = (bf16[2,896,4736]{2,1,0:T(8,128)(2,1)}, f32[2,896,4736]{2,1,0:T(8,128)}, f32[2,896,4736]{2,1,0:T(8,128)}, bf16[2,896,4736]{2,1,0:T(8,128)(2,1)}...) custom-call(s32[8,37]{1,0:T(8,128)} %constant.16.clone.table_ref, ...), custom_call_target="tpu_custom_call", output_to_operand_aliasing={{0}: (17, {}), {1}: (18, {}), {2}: (19, {}), {3}: (20, {}),... | custom-call | flops 10321920000 | bytes 113541120 | tf_op jit(solution)/shard_map/pallas_call | solution.py:480
  776.6 10.8 %shard_map.217 = (bf16[2,896,4736]{2,1,0:T(8,128)(2,1)}, f32[2,896,4736]{2,1,0:T(8,128)}, f32[2,896,4736]{2,1,0:T(8,128)}, bf16[2,896,4736]{2,1,0:T(8,128)(2,1)}...) custom-call(s32[8,9]{1,0:T(8,128)} %constant.17.clone.table_ref, ...), custom_call_target="tpu_custom_call", output_to_operand_aliasing={{0}: (13, {}), {1}: (14, {}), {2}: (15, {}), {3}: (16, {}),... | custom-call | flops 2064384000 | bytes 22708224 | tf_op jit(solution)/shard_map/pallas_call | solution.py:480
  (30 shorter events, 0.9 us)
Async XLA Ops:
  74.8 121.1 %collective-permute-start.4 = (bf16[2048,896]{1,0:T(8,128)(2,1)}, bf16[2048,896]{1,0:T(8,128)(2,1)}, u32[]{:S(2)}, u32[]{:S(2)}) collective-permute-start(bf16[2048,896]{1,0:T(8,128)(2,1)} %get-tuple-element.74.refs_0_), channel_id=1, source_target_pairs={{0,1},{1,0},{2,3},{3,2},{4,5},{5,4},{6,7},{7,6}} | collective-permute-start | bytes 11010056 | tf_op jit(solution)/shard_map/ppermute | solution.py:33
  75.7 122.0 %collective-permute-start.5 = (bf16[2048,896]{1,0:T(8,128)(2,1)}, bf16[2048,896]{1,0:T(8,128)(2,1)}, u32[]{:S(2)}, u32[]{:S(2)}) collective-permute-start(bf16[2048,896]{1,0:T(8,128)(2,1)} %get-tuple-element.74.refs_0_), channel_id=1, source_target_pairs={{0,2},{2,0},{1,3},{3,1},{4,6},{6,4},{5,7},{7,5}} | collective-permute-start | bytes 11010056 | tf_op jit(solution)/shard_map/ppermute | solution.py:29
  78.2 119.8 %collective-permute-start.6 = (bf16[2048,896]{1,0:T(8,128)(2,1)}, bf16[2048,896]{1,0:T(8,128)(2,1)}, u32[]{:S(2)}, u32[]{:S(2)}) collective-permute-start(bf16[2048,896]{1,0:T(8,128)(2,1)} %bitcast.4), channel_id=1, source_target_pairs={{0,1},{1,0},{2,3},{3,2},{4,5},{5,4},{6,7},{7,6}} | collective-permute-start | bytes 11010056 | tf_op jit(solution)/shard_map/ppermute | solution.py:33
  78.4 158.9 %collective-permute-start.7 = (bf16[2048,896]{1,0:T(8,128)(2,1)}, bf16[2048,896]{1,0:T(8,128)(2,1)}, u32[]{:S(2)}, u32[]{:S(2)}) collective-permute-start(bf16[2048,896]{1,0:T(8,128)(2,1)} %bitcast.5), channel_id=1, source_target_pairs={{0,2},{2,0},{1,3},{3,1},{4,6},{6,4},{5,7},{7,5}} | collective-permute-start | bytes 11010056 | tf_op jit(solution)/shard_map/ppermute | solution.py:29
  195.9 186.0 %collective-permute-start.2 = (bf16[2048,896]{1,0:T(8,128)(2,1)}, bf16[2048,896]{1,0:T(8,128)(2,1)}, u32[]{:S(2)}, u32[]{:S(2)}) collective-permute-start(bf16[2048,896]{1,0:T(8,128)(2,1)} %chain.1.refs_3_), channel_id=1, source_target_pairs={{0,1},{1,0},{2,3},{3,2},{4,5},{5,4},{6,7},{7,6}} | collective-permute-start | bytes 11010056 | tf_op jit(solution)/shard_map/ppermute | solution.py:33
  196.0 186.0 %collective-permute-start.3 = (bf16[2048,896]{1,0:T(8,128)(2,1)}, bf16[2048,896]{1,0:T(8,128)(2,1)}, u32[]{:S(2)}, u32[]{:S(2)}) collective-permute-start(bf16[2048,896]{1,0:T(8,128)(2,1)} %chain.1.refs_3_), channel_id=1, source_target_pairs={{0,2},{2,0},{1,3},{3,1},{4,6},{6,4},{5,7},{7,5}} | collective-permute-start | bytes 11010056 | tf_op jit(solution)/shard_map/ppermute | solution.py:29
  197.7 184.3 %collective-permute-start = (bf16[2048,896]{1,0:T(8,128)(2,1)}, bf16[2048,896]{1,0:T(8,128)(2,1)}, u32[]{:S(2)}, u32[]{:S(2)}) collective-permute-start(bf16[2048,896]{1,0:T(8,128)(2,1)} %get-tuple-element.73.refs_0_), channel_id=1, source_target_pairs={{0,1},{1,0},{2,3},{3,2},{4,5},{5,4},{6,7},{7,6}} | collective-permute-start | bytes 11010056 | tf_op jit(solution)/shard_map/ppermute | solution.py:33
  197.9 196.7 %collective-permute-start.1 = (bf16[2048,896]{1,0:T(8,128)(2,1)}, bf16[2048,896]{1,0:T(8,128)(2,1)}, u32[]{:S(2)}, u32[]{:S(2)}) collective-permute-start(bf16[2048,896]{1,0:T(8,128)(2,1)} %get-tuple-element.73.refs_0_), channel_id=1, source_target_pairs={{0,2},{2,0},{1,3},{3,1},{4,6},{6,4},{5,7},{7,5}} | collective-permute-start | bytes 11010056 | tf_op jit(solution)/shard_map/ppermute | solution.py:29
  379.9 162.8 %collective-permute-start.8 = (bf16[896,1152]{1,0:T(8,128)(2,1)}, bf16[896,1152]{1,0:T(8,128)(2,1)}, u32[]{:S(2)}, u32[]{:S(2)}) collective-permute-start(bf16[896,1152]{1,0:T(8,128)(2,1)} %get-tuple-element.79.refs_9_), channel_id=1, source_target_pairs={{0,2},{2,0},{1,3},{3,1},{4,6},{6,4},{5,7},{7,5}} | collective-permute-start | bytes 6193160 | tf_op jit(solution)/shard_map/ppermute | solution.py:29
  381.9 160.9 %collective-permute-start.17 = (bf16[896,1152]{1,0:T(8,128)(2,1)}, bf16[896,1152]{1,0:T(8,128)(2,1)}, u32[]{:S(2)}, u32[]{:S(2)}) collective-permute-start(bf16[896,1152]{1,0:T(8,128)(2,1)} %get-tuple-element.79.refs_9_), channel_id=1, source_target_pairs={{0,1},{1,0},{2,3},{3,2},{4,5},{5,4},{6,7},{7,6}} | collective-permute-start | bytes 6193160 | tf_op jit(solution)/shard_map/ppermute | solution.py:33
  381.9 160.2 %collective-permute-start.10 = (bf16[896,1152]{1,0:T(8,128)(2,1)}, bf16[896,1152]{1,0:T(8,128)(2,1)}, u32[]{:S(2)}, u32[]{:S(2)}) collective-permute-start(bf16[896,1152]{1,0:T(8,128)(2,1)} %get-tuple-element.80.refs_10_), channel_id=1, source_target_pairs={{0,2},{2,0},{1,3},{3,1},{4,6},{6,4},{5,7},{7,5}} | collective-permute-start | bytes 6193160 | tf_op jit(solution)/shard_map/ppermute | solution.py:29
  382.0 161.2 %collective-permute-start.18 = (bf16[896,1152]{1,0:T(8,128)(2,1)}, bf16[896,1152]{1,0:T(8,128)(2,1)}, u32[]{:S(2)}, u32[]{:S(2)}) collective-permute-start(bf16[896,1152]{1,0:T(8,128)(2,1)} %get-tuple-element.80.refs_10_), channel_id=1, source_target_pairs={{0,1},{1,0},{2,3},{3,2},{4,5},{5,4},{6,7},{7,6}} | collective-permute-start | bytes 6193160 | tf_op jit(solution)/shard_map/ppermute | solution.py:33
  394.6 147.7 %collective-permute-start.12 = (bf16[1152,896]{1,0:T(8,128)(2,1)}, bf16[1152,896]{1,0:T(8,128)(2,1)}, u32[]{:S(2)}, u32[]{:S(2)}) collective-permute-start(bf16[1152,896]{1,0:T(8,128)(2,1)} %get-tuple-element.81.refs_11_), channel_id=1, source_target_pairs={{0,2},{2,0},{1,3},{3,1},{4,6},{6,4},{5,7},{7,5}} | collective-permute-start | bytes 6193160 | tf_op jit(solution)/shard_map/ppermute | solution.py:29
  542.1 4.9 collective-permute-start.19
  542.3 7.3 collective-permute-start.14
  542.7 9.8 %collective-permute-start.15 = (bf16[896,1152]{1,0:T(8,128)(2,1)}, bf16[896,1152]{1,0:T(8,128)(2,1)}, u32[]{:S(2)}, u32[]{:S(2)}) collective-permute-start(bf16[896,1152]{1,0:T(8,128)(2,1)} %get-tuple-element.83.refs_19_), channel_id=1, source_target_pairs={{0,1},{1,0},{2,3},{3,2},{4,5},{5,4},{6,7},{7,6}} | collective-permute-start | bytes 6193160 | tf_op jit(solution)/shard_map/ppermute | solution.py:33
  542.8 12.7 %collective-permute-start.16 = (bf16[1152,896]{1,0:T(8,128)(2,1)}, bf16[1152,896]{1,0:T(8,128)(2,1)}, u32[]{:S(2)}, u32[]{:S(2)}) collective-permute-start(bf16[1152,896]{1,0:T(8,128)(2,1)} %get-tuple-element.84.refs_20_), channel_id=1, source_target_pairs={{0,1},{1,0},{2,3},{3,2},{4,5},{5,4},{6,7},{7,6}} | collective-permute-start | bytes 6193160 | tf_op jit(solution)/shard_map/ppermute | solution.py:33
  543.2 48.1 %collective-permute-start.22 = (bf16[896,1152]{1,0:T(8,128)(2,1)}, bf16[896,1152]{1,0:T(8,128)(2,1)}, u32[]{:S(2)}, u32[]{:S(2)}) collective-permute-start(bf16[896,1152]{1,0:T(8,128)(2,1)} %get-tuple-element.82.refs_18_), channel_id=1, source_target_pairs={{0,2},{2,0},{1,3},{3,1},{4,6},{6,4},{5,7},{7,5}} | collective-permute-start | bytes 6193160 | tf_op jit(solution)/shard_map/ppermute | solution.py:29
  547.0 188.9 %collective-permute-start.20 = (bf16[1152,896]{1,0:T(8,128)(2,1)}, bf16[1152,896]{1,0:T(8,128)(2,1)}, u32[]{:S(2)}, u32[]{:S(2)}) collective-permute-start(bf16[1152,896]{1,0:T(8,128)(2,1)} %get-tuple-element.84.refs_20_), channel_id=1, source_target_pairs={{0,2},{2,0},{1,3},{3,1},{4,6},{6,4},{5,7},{7,5}} | collective-permute-start | bytes 6193160 | tf_op jit(solution)/shard_map/ppermute | solution.py:29
  549.6 138.6 %collective-permute-start.23 = (bf16[896,1152]{1,0:T(8,128)(2,1)}, bf16[896,1152]{1,0:T(8,128)(2,1)}, u32[]{:S(2)}, u32[]{:S(2)}) collective-permute-start(bf16[896,1152]{1,0:T(8,128)(2,1)} %get-tuple-element.83.refs_19_), channel_id=1, source_target_pairs={{0,2},{2,0},{1,3},{3,1},{4,6},{6,4},{5,7},{7,5}} | collective-permute-start | bytes 6193160 | tf_op jit(solution)/shard_map/ppermute | solution.py:29
  552.5 136.3 %collective-permute-start.11 = (bf16[896,1152]{1,0:T(8,128)(2,1)}, bf16[896,1152]{1,0:T(8,128)(2,1)}, u32[]{:S(2)}, u32[]{:S(2)}) collective-permute-start(bf16[896,1152]{1,0:T(8,128)(2,1)} %collective-permute-done.10.refs_16_), channel_id=1, source_target_pairs={{0,1},{1,0},{2,3},{3,2},{4,5},{5,4},{6,7},{7,6}} | collective-permute-start | bytes 6193160 | tf_op jit(solution)/shard_map/ppermute | solution.py:33
  555.5 133.4 %collective-permute-start.13 = (bf16[1152,896]{1,0:T(8,128)(2,1)}, bf16[1152,896]{1,0:T(8,128)(2,1)}, u32[]{:S(2)}, u32[]{:S(2)}) collective-permute-start(bf16[1152,896]{1,0:T(8,128)(2,1)} %collective-permute-done.12.refs_17_), channel_id=1, source_target_pairs={{0,1},{1,0},{2,3},{3,2},{4,5},{5,4},{6,7},{7,6}} | collective-permute-start | bytes 6193160 | tf_op jit(solution)/shard_map/ppermute | solution.py:33
  591.3 97.5 %collective-permute-start.9 = (bf16[896,1152]{1,0:T(8,128)(2,1)}, bf16[896,1152]{1,0:T(8,128)(2,1)}, u32[]{:S(2)}, u32[]{:S(2)}) collective-permute-start(bf16[896,1152]{1,0:T(8,128)(2,1)} %collective-permute-done.8.refs_15_), channel_id=1, source_target_pairs={{0,1},{1,0},{2,3},{3,2},{4,5},{5,4},{6,7},{7,6}} | collective-permute-start | bytes 6193160 | tf_op jit(solution)/shard_map/ppermute | solution.py:33
  688.1 48.3 %collective-permute-start.24 = (bf16[896,1152]{1,0:T(8,128)(2,1)}, bf16[896,1152]{1,0:T(8,128)(2,1)}, u32[]{:S(2)}, u32[]{:S(2)}) collective-permute-start(bf16[896,1152]{1,0:T(8,128)(2,1)} %collective-permute-done.22.refs_9_), channel_id=1, source_target_pairs={{0,1},{1,0},{2,3},{3,2},{4,5},{5,4},{6,7},{7,6}} | collective-permute-start | bytes 6193160 | tf_op jit(solution)/shard_map/ppermute | solution.py:33
  688.8 47.7 %collective-permute-start.25 = (bf16[896,1152]{1,0:T(8,128)(2,1)}, bf16[896,1152]{1,0:T(8,128)(2,1)}, u32[]{:S(2)}, u32[]{:S(2)}) collective-permute-start(bf16[896,1152]{1,0:T(8,128)(2,1)} %collective-permute-done.23.refs_10_), channel_id=1, source_target_pairs={{0,1},{1,0},{2,3},{3,2},{4,5},{5,4},{6,7},{7,6}} | collective-permute-start | bytes 6193160 | tf_op jit(solution)/shard_map/ppermute | solution.py:33
  736.0 40.6 %collective-permute-start.21 = (bf16[1152,896]{1,0:T(8,128)(2,1)}, bf16[1152,896]{1,0:T(8,128)(2,1)}, u32[]{:S(2)}, u32[]{:S(2)}) collective-permute-start(bf16[1152,896]{1,0:T(8,128)(2,1)} %collective-permute-done.20.refs_11_), channel_id=1, source_target_pairs={{0,1},{1,0},{2,3},{3,2},{4,5},{5,4},{6,7},{7,6}} | collective-permute-start | bytes 6193160 | tf_op jit(solution)/shard_map/ppermute | solution.py:33

commit v7 on v6

--- a/solution.py
+++ b/solution.py
@@ -10,7 +10,7 @@
 F32, BF16 = jnp.float32, jnp.bfloat16
 PX = ((0, 2), (2, 0), (1, 3), (3, 1))
 PD = ((0, 1), (1, 0), (2, 3), (3, 2))
-NN = ((1,), (0,))
+NN, NT = ((1,), (0,)), ((1,), (1,))
 
 LANES = 128
 BLOCK = 512
@@ -191,12 +191,14 @@
     chip, core = me // 2, me % 2
     partner = chip * 2 + 1 - core
     others = (partner, (1 - chip) * 2 + core, (1 - chip) * 2 + 1 - core)
-    a_refs, dy_refs, (wg_hbm, wu_hbm, wd_hbm) = refs[:3], refs[3:6], refs[6:9]
+    (a_own, a_across), (dy_own, dy_across), (wg_hbm, wu_hbm, wd_hbm) = refs[:2], refs[2:4], refs[4:7]
     final = count is not None
-    before = refs[9:11] if final else ()
-    refs = refs[11 if final else 9 :]
-    outs, scratch = refs[:8], refs[8:]
-    wg_ref, wu_ref, wd_ref, accg_ref, accu_ref, accd_ref, a_buf, dy_buf, a_far, dy_far, sums_ref, sems, w_sems, send_sems, recv_sems, wdt_ref, *terms = scratch
+    before = refs[7:9] if final else ()
+    refs = refs[9 if final else 7 :]
+    outs, landed, scratch = refs[:8], refs[8:10], refs[10:]
+    a_refs = (a_own, landed[0].at[0], a_across, landed[0].at[1])
+    dy_refs = (dy_own, landed[1].at[0], dy_across, landed[1].at[1])
+    wg_ref, wu_ref, wd_ref, accg_ref, accu_ref, accd_ref, a_buf, dy_buf, sums_ref, sems, w_sems, send_sems, recv_sems, *terms = scratch
     i, steps = pl.program_id(0), pl.num_programs(0)
     each = a_refs[0].shape[0] // ROWS
     width = wg_ref.shape[1]
@@ -204,7 +206,7 @@
     def fetch(step, do):
         slot, who = lax.rem(step, 2), step // each
         rows = pl.ds(pl.multiple_of(lax.rem(step, each) * ROWS, ROWS), ROWS)
-        for k, (a, dy) in enumerate(zip((*a_refs, a_far), (*dy_refs, dy_far), strict=True)):
+        for k, (a, dy) in enumerate(zip(a_refs, dy_refs, strict=True)):
 
             @pl.when(who == k)
             def _():
@@ -219,12 +221,12 @@
             for m, (there, here) in enumerate(parts)
         ]
 
-    def onward(n):
+    def onward(which, n):
         return pltpu.make_async_remote_copy(
-            src_ref=(a_refs[2], dy_refs[2])[n],
-            dst_ref=(a_far, dy_far)[n],
-            send_sem=send_sems.at[n],
-            recv_sem=recv_sems.at[n],
+            src_ref=(a_refs, dy_refs)[n][2 * which],
+            dst_ref=landed[n].at[which],
+            send_sem=send_sems.at[2 * which + n],
+            recv_sem=recv_sems.at[2 * which + n],
             device_id={"dp": partner},
             device_id_type=pl.DeviceIdType.MESH,
         )
@@ -233,8 +235,8 @@
         return pltpu.make_async_remote_copy(
             src_ref=sums_ref.at[0],
             dst_ref=sums_ref.at[1 + n],
-            send_sem=send_sems.at[2 + n],
-            recv_sem=recv_sems.at[2 + n],
+            send_sem=send_sems.at[4 + n],
+            recv_sem=recv_sems.at[4 + n],
             device_id={"dp": others[n]},
             device_id_type=pl.DeviceIdType.MESH,
         )
@@ -251,18 +253,20 @@
             copy.start()
         for copy in weights():
             copy.wait()
-        wdt_ref[...] = wd_ref[...].T
 
     @pl.when(i == 1)
     def _():
         pl.semaphore_wait(barrier, len(spoken))
-        for n in range(2):
-            onward(n).start()
-
-    @pl.when(i == 3 * each - 1)
-    def _():
-        for n in range(2):
-            onward(n).wait()
+        for which in range(2):
+            for n in range(2):
+                onward(which, n).start()
+
+    for which in range(2):
+
+        @pl.when(i == (2 * which + 1) * each - 1)
+        def _():
+            for n in range(2):
+                onward(which, n).wait()
 
     @pl.when(i + 1 < steps)
     def _():
@@ -278,7 +282,7 @@
 
     def there(c):
         s = blocks[c]
-        held[c] = hidden_back(dot(a, wg_ref[:, s], NN), dot(a, wu_ref[:, s], NN), dot(dy, wdt_ref[:, s], NN))
+        held[c] = hidden_back(dot(a, wg_ref[:, s], NN), dot(a, wu_ref[:, s], NN), dot(dy, wd_ref[s, :], NT))
 
     def back(c):
         s = blocks[c]
@@ -346,18 +350,17 @@
     return pl.pallas_call(
         lambda *refs: slices_kernel(layer, own, count, *refs),
         grid=(4 * tokens // ROWS,),
-        in_specs=[any_] * 9 + [at((8, LANES))] * len(before or ()),
-        out_specs=[at(s) for s in sizes] + [at((8, LANES))] * 2,
+        in_specs=[any_] * 7 + [at((8, LANES))] * len(before or ()),
+        out_specs=[at(s) for s in sizes] + [at((8, LANES))] * 2 + [any_] * 2,
         scratch_shapes=[pltpu.VMEM((d, width), BF16)] * 2
         + [pltpu.VMEM((width, d), BF16)]
         + [pltpu.VMEM((d, width), F32)] * 3
         + [pltpu.VMEM((2, ROWS, d), BF16)] * 2
-        + [pltpu.VMEM((tokens, d), BF16)] * 2
         + [pltpu.VMEM((4, 8, LANES), F32)]
-        + [pltpu.SemaphoreType.DMA(n) for n in ((2, 2), (3, 2), (5,), (5,))]
-        + [pltpu.VMEM((d, width), BF16)]
+        + [pltpu.SemaphoreType.DMA(n) for n in ((2, 2), (3, 2), (7,), (7,))]
         + [pltpu.VMEM((4, d, rest), F32)] * 3,
-        out_shape=[jax.ShapeDtypeStruct(s, BF16) for s in sizes] + [jax.ShapeDtypeStruct((8, LANES), F32)] * 2,
+        out_shape=[jax.ShapeDtypeStruct(s, BF16) for s in sizes] + [jax.ShapeDtypeStruct((8, LANES), F32)] * 2
+        + [jax.ShapeDtypeStruct((2, tokens, d), BF16)] * 2,
         cost_estimate=pl.CostEstimate(
             flops=12 * 4 * tokens * d * width, bytes_accessed=16 * tokens * d, transcendentals=4 * tokens * width
         ),
@@ -373,10 +376,10 @@
     return (0.998 * w.astype(F32) - 0.02 * (m * lax.rsqrt(v + 1e-8))).astype(BF16), m, v
 
 
-SLOTS, AHEAD = 6, 3
-
-
-def adam(own, factor, who, arrays, pieces, outs):
+SLOTS, AHEAD = 8, 4
+
+
+def adam(own, factor, arrays, pieces, outs):
     d, _ = arrays[0][0].shape[1:]
     shapes = ((LANES, own), (LANES, d), (d, LANES))
     rows = []
@@ -389,17 +392,19 @@
     kinds = sorted({row[0] for row in rows})
     n_in = 9 + len(pieces)
 
-    def kernel(table_ref, who_ref, f_ref, *refs):
+    def kernel(table_ref, f_ref, *refs):
         weights, grads = refs[:9], refs[9:n_in]
         refs = refs[n_in + (9 if outs is not None else 0) :]
         results, scratch = refs[:9], refs[9:]
         buffers = {kind: scratch[4 * n : 4 * n + 4] for n, kind in enumerate(kinds)}
         sem_in, sem_out = scratch[-2:]
-        f = f_ref[0]
+        f = f_ref[:1, :1]
+        me = lax.axis_index("dp")
 
         def place(step):
             kind, which, layer = (table_ref[n, step] for n in range(3))
-            unit = who_ref[table_ref[4, step]]
+            slot = table_ref[4, step]
+            unit = jnp.where(slot < 4, (me + slot) % 2 + 2 * ((me // 2 + slot // 2) % 2), slot)
             row, col = table_ref[5, step] + table_ref[6, step] * unit, table_ref[7, step] * unit
             return kind, which, lambda shape: (layer, pl.ds(pl.multiple_of(row, 16), shape[0]), pl.ds(pl.multiple_of(col, LANES), shape[1]))
 
@@ -479,23 +484,20 @@
     elements = sum(piece[3].size for piece in pieces)
     new = pl.pallas_call(
         kernel,
-        in_specs=[pl.BlockSpec(memory_space=pltpu.SMEM)] * 3 + [any_] * (n_in + len(before)),
+        in_specs=[pl.BlockSpec(memory_space=pltpu.SMEM), pl.BlockSpec(memory_space=pltpu.VMEM)] + [any_] * (n_in + len(before)),
         out_specs=[any_] * 9,
         out_shape=[jax.ShapeDtypeStruct(a.shape, a.dtype) for a in given],
         scratch_shapes=[pltpu.VMEM((SLOTS, *shapes[q]), t) for q in kinds for t in (BF16, F32, F32, BF16)]
         + [pltpu.SemaphoreType.DMA((4, SLOTS)), pltpu.SemaphoreType.DMA((3, SLOTS))],
-        input_output_aliases={3 + n_in + n: n for n in range(len(before))},
+        input_output_aliases={2 + n_in + n: n for n in range(len(before))},
         cost_estimate=pl.CostEstimate(flops=2000 * elements, bytes_accessed=22 * elements, transcendentals=elements),
         compiler_params=params(),
-    )(table, who, factor, *given, *(piece[3] for piece in pieces), *before)
+    )(table, factor, *given, *(piece[3] for piece in pieces), *before)
     return tuple(tuple(new[3 * n : 3 * n + 3]) for n in range(3))
 
 
 def solution(mesh):
     def step(x, dy, wg, wu, wd, mg, mu, md, vg, vu, vd):
-        me = lax.axis_index("dp")
-        places = jnp.arange(5, dtype=jnp.int32)
-        who = jnp.where(places < 4, me ^ places, places)
         x, dy = x[0], dy[0]
         ff = wg.shape[2]
         own = ff // LANES // 4 * LANES
@@ -503,17 +505,16 @@
         def send(a, perm):
             return perm(a)
 
-        dy_x, dy_d = send(dy, px), send(dy, pd)
+        dy_x = send(dy, px)
         h1, a1, a0 = forward(x, wg, wu, wd)
-        a1_x, a1_d = send(a1, px), send(a1, pd)
-        a0_x, a0_d = send(a0, px), send(a0, pd)
+        a1_x = send(a1, px)
+        a0_x = send(a0, px)
         dh1 = chain(a1, dy, h1, wg, wu, wd)
-        dh1_x, dh1_d = send(dh1, px), send(dh1, pd)
-        top = slices(1, own, [a1, a1_d, a1_x], [dy, dy_d, dy_x], wg, wu, wd)
+        dh1_x = send(dh1, px)
+        top = slices(1, own, [a1, a1_x], [dy, dy_x], wg, wu, wd)
         top_x = [send(top[n], px) for n in range(3)]
         top_d = [send(top[n], pd) for n in range(3)]
-        low = slices(0, own, [a0, a0_d, a0_x], [dh1, dh1_d, dh1_x], wg, wu, wd, top[6:8], wg.size + wu.size + wd.size)
-        factor = low[6][0, :1]
+        low = slices(0, own, [a0, a0_x], [dh1, dh1_x], wg, wu, wd, top[6:8], wg.size + wu.size + wd.size)
         low_x = [send(low[n], px) for n in range(3)]
         low_d = [send(low[n], pd) for n in range(3)]
 
@@ -526,12 +527,12 @@
 
         first = pieces(1, 0, top) + pieces(1, 1, top_d) + pieces(1, 2, top_x) + pieces(0, 0, low)
         shared = pieces(1, 4, top[3:6]) + pieces(0, 4, low[3:6])
-        outs = adam(own, factor, who, arrays, first + shared, None)
-        outs = adam(own, factor, who, arrays, pieces(1, 3, top_xd) + pieces(0, 1, low_d), outs)
+        outs = adam(own, low[6], arrays, first + shared, None)
+        outs = adam(own, low[6], arrays, pieces(1, 3, top_xd) + pieces(0, 1, low_d), outs)
         outs, low_x[2] = lax.optimization_barrier((outs, low_x[2]))
         low_xd.append(send(low_x[2], pd))
-        outs = adam(own, factor, who, arrays, pieces(0, 2, low_x) + pieces(0, 3, low_xd, (0, 1)), outs)
-        outs = adam(own, factor, who, arrays, pieces(0, 3, low_xd, (2,)), outs)
+        outs = adam(own, low[6], arrays, pieces(0, 2, low_x) + pieces(0, 3, low_xd, (0, 1)), outs)
+        outs = adam(own, low[6], arrays, pieces(0, 3, low_xd, (2,)), outs)
         return tuple(outs[name][which] for which in range(3) for name in range(3))
 
     return jax.shard_map(

time: 796 us -> 789 us (level)
  Pallas kernels: 674 us -> 666 us
  transfers between devices with their start and end apart: 26 -> 22, of which waited for: 6 -> 7; matrix products, arithmetic and copies ran while one was open for 0% -> 0% of each run, Pallas kernels for 75% -> 74%
where the time goes in v7:
time: 789 us; the launch traced here: 781 us
  Pallas kernels  666 us (84%)
  waiting for transfers between devices  96.1 us (12%)
  starting transfers between devices  18.4 us (2%)
    pallas_call x2, Pallas kernels, slices(): pl.pallas_call(lambda *refs: slices_kernel(layer, own, count, *refs), gri...  283 us
    pallas_call x4, Pallas kernels, adam(): pl.pallas_call(kernel, in_specs=[pl.BlockSpec(memory_space=pltpu.SMEM), p...  191 us
    pallas_call x1, Pallas kernels, chain(): pl.pallas_call(lambda *refs: chain_kernel(ff - (steps - 1) * BLOCK, *refs...  117 us
    ppermute x10, waiting for transfers between devices, px(): return lax.ppermute(a, 'dp', PX)  90 us
    pallas_call x1, Pallas kernels, forward(): pl.pallas_call(lambda *refs: forward_kernel(ff - (steps - 1) * BLOCK, *re...  74.3 us
  transfers between devices with their start and end apart: 22, of which 7 were waited for; matrix products, arithmetic and copies ran while one was open for 0% of the time, Pallas kernels for 74%

profile of v7, /device:TPU:0, one launch (start us, length us, event | category | flops | bytes accessed | tf_op | source)
XLA Modules:
  0.0 781.2 jit_solution(5093947772914300151)
XLA Ops:
  0.6 74.3 %forward.1 = (bf16[2048,896]{1,0:T(8,128)(2,1)}, bf16[2048,896]{1,0:T(8,128)(2,1)}, bf16[2048,896]{1,0:T(8,128)(2,1)}) custom-call(bf16[2048,896]{1,0:T(8,128)(2,1)} %bitcast.2, bf16[2,896,4736]{2,1,0:T(8,128)(2,1)} %refs_0_.7, bf16[2,896,4736]{2,1,0:T(8,128)(2,1)} %refs_3_.11, bf16[2,4736,896]{2,1,0:T(8,128)(2,1)} %refs_6_.11), custom_call_target="tpu_custom_call" | custom-call | flops 52143587328 | bytes 25460736 | tf_op jit(solution)/shard_map/forward/pallas_call | solution.py:102
  74.9 3.3 collective-permute-start.2
  78.3 117.3 %chain.1.refs_2_ = bf16[2048,896]{1,0:T(8,128)(2,1)} custom-call(bf16[2048,896]{1,0:T(8,128)(2,1)} %get-tuple-element.74.refs_0_, bf16[2048,896]{1,0:T(8,128)(2,1)} %bitcast.4, bf16[2048,896]{1,0:T(8,128)(2,1)} %get-tuple-element.75.refs_2_, bf16[2,896,4736]{2,1,0:T(8,128)(2,1)} %refs_0_.7, bf16[2,896,4736]{2,1,0:T(8,128)(2,1)} %refs_3_.11, ...), custom_call_target="tpu_custom_call" | custom-call | flops 86905978880 | bytes 25460736 | tf_op jit(solution)/shard_map/chain/pallas_call | solution.py:176
  195.6 2.0 collective-permute-start.1
  197.6 39.8 %collective-permute-done.3.refs_3_ = bf16[2048,896]{1,0:T(8,128)(2,1)} collective-permute-done((bf16[2048,896]{1,0:T(8,128)(2,1)}, bf16[2048,896]{1,0:T(8,128)(2,1)}, u32[]{:S(2)}, u32[]{:S(2)}) %collective-permute-start.3) | collective-permute-done | bytes 3670048 | tf_op jit(solution)/shard_map/ppermute | solution.py:29
  237.4 140.1 %slices.2 = (bf16[896,1152]{1,0:T(8,128)(2,1)}, bf16[896,1152]{1,0:T(8,128)(2,1)}, bf16[1152,896]{1,0:T(8,128)(2,1)}, bf16[896,128]{1,0:T(8,128)(2,1)}, bf16[896...) custom-call(bf16[2048,896]{1,0:T(8,128)(2,1)} %get-tuple-element.74., ...), custom_call_target="tpu_custom_call" | custom-call | flops 112742891520 | bytes 29360128 | tf_op jit(solution)/shard_map/slices/pallas_call | solution.py:350
  377.5 2.1 collective-permute-start.4
  379.6 0.1 collective-permute-start.6
  379.7 0.4 collective-permute-start.14
  380.1 14.6 %collective-permute-done.refs_1_ = bf16[2048,896]{1,0:T(8,128)(2,1)} collective-permute-done((bf16[2048,896]{1,0:T(8,128)(2,1)}, bf16[2048,896]{1,0:T(8,128)(2,1)}, u32[]{:S(2)}, u32[]{:S(2)}) %collective-permute-start) | collective-permute-done | bytes 3670048 | tf_op jit(solution)/shard_map/ppermute | solution.py:29
  394.7 2.0 collective-permute-start.8
  396.7 143.1 %slices.3 = (bf16[896,1152]{1,0:T(8,128)(2,1)}, bf16[896,1152]{1,0:T(8,128)(2,1)}, bf16[1152,896]{1,0:T(8,128)(2,1)}, bf16[896,128]{1,0:T(8,128)(2,1)}, bf16[896...) custom-call(bf16[2048,896]{1,0:T(8,128)(2,1)} %get-tuple-element.73., ...), custom_call_target="tpu_custom_call" | custom-call | flops 112742891520 | bytes 29360128 | tf_op jit(solution)/shard_map/slices/pallas_call | solution.py:350
  539.9 0.1 collective-permute-start.15
  540.0 0.4 collective-permute-start.10
  540.4 0.1 collective-permute-start.11
  540.5 0.4 collective-permute-start.12
  540.9 2.0 collective-permute-start.18
  542.9 1.4 collective-permute-done.15.refs_14_
  544.3 2.0 collective-permute-start.16
  546.4 0.9 collective-permute-done.10.refs_12_
  547.3 2.0 collective-permute-start.19
  549.3 0.9 collective-permute-done.11.refs_13_
  550.2 0.1 collective-permute-start.5
  550.4 2.8 collective-permute-done.12.refs_14_
  553.2 0.1 collective-permute-start.7
  553.3 35.7 %collective-permute-done.18.refs_9_ = bf16[896,1152]{1,0:T(8,128)(2,1)} collective-permute-done((bf16[896,1152]{1,0:T(8,128)(2,1)}, bf16[896,1152]{1,0:T(8,128)(2,1)}, u32[]{:S(2)}, u32[]{:S(2)}) %collective-permute-start.18) | collective-permute-done | bytes 2064416 | tf_op jit(solution)/shard_map/ppermute | solution.py:29
  589.0 95.1 %shard_map.214 = (bf16[2,896,4736]{2,1,0:T(8,128)(2,1)}, f32[2,896,4736]{2,1,0:T(8,128)}, f32[2,896,4736]{2,1,0:T(8,128)}, bf16[2,896,4736]{2,1,0:T(8,128)(2,1)}...) custom-call(s32[8,98]{1,0:T(8,128)} %constant.8.clone.table_ref, ...), custom_call_target="tpu_custom_call" | custom-call | flops 26148864000 | bytes 287637504 | tf_op jit(solution)/shard_map/pallas_call | solution.py:485
  684.2 0.5 collective-permute-start.20
  684.8 46.6 %shard_map.215 = (bf16[2,896,4736]{2,1,0:T(8,128)(2,1)}, f32[2,896,4736]{2,1,0:T(8,128)}, f32[2,896,4736]{2,1,0:T(8,128)}, bf16[2,896,4736]{2,1,0:T(8,128)(2,1)}...) custom-call(s32[8,46]{1,0:T(8,128)} %constant.9.clone.table_ref, ...), custom_call_target="tpu_custom_call", output_to_operand_aliasing={{0}: (17, {}), {1}: (18, {}), {2}: (19, {}), {3}: (20, {}),... | custom-call | flops 12386304000 | bytes 136249344 | tf_op jit(solution)/shard_map/pallas_call | solution.py:485
  731.4 0.4 collective-permute-start.17
  731.8 39.3 %shard_map.216 = (bf16[2,896,4736]{2,1,0:T(8,128)(2,1)}, f32[2,896,4736]{2,1,0:T(8,128)}, f32[2,896,4736]{2,1,0:T(8,128)}, bf16[2,896,4736]{2,1,0:T(8,128)(2,1)}...) custom-call(s32[8,37]{1,0:T(8,128)} %constant.10.clone.table_ref, ...), custom_call_target="tpu_custom_call", output_to_operand_aliasing={{0}: (16, {}), {1}: (17, {}), {2}: (18, {}), {3}: (19, {}),... | custom-call | flops 10321920000 | bytes 113541120 | tf_op jit(solution)/shard_map/pallas_call | solution.py:485
  771.2 9.7 %shard_map.217 = (bf16[2,896,4736]{2,1,0:T(8,128)(2,1)}, f32[2,896,4736]{2,1,0:T(8,128)}, f32[2,896,4736]{2,1,0:T(8,128)}, bf16[2,896,4736]{2,1,0:T(8,128)(2,1)}...) custom-call(s32[8,9]{1,0:T(8,128)} %constant.11.clone.table_ref, ...), custom_call_target="tpu_custom_call", output_to_operand_aliasing={{0}: (12, {}), {1}: (13, {}), {2}: (14, {}), {3}: (15, {}),... | custom-call | flops 2064384000 | bytes 22708224 | tf_op jit(solution)/shard_map/pallas_call | solution.py:485
  (20 shorter events, 0.1 us)
Async XLA Ops:
  74.9 122.7 %collective-permute-start.2 = (bf16[2048,896]{1,0:T(8,128)(2,1)}, bf16[2048,896]{1,0:T(8,128)(2,1)}, u32[]{:S(2)}, u32[]{:S(2)}) collective-permute-start(bf16[2048,896]{1,0:T(8,128)(2,1)} %get-tuple-element.74.refs_0_), channel_id=1, source_target_pairs={{0,2},{2,0},{1,3},{3,1},{4,6},{6,4},{5,7},{7,5}} | collective-permute-start | bytes 11010056 | tf_op jit(solution)/shard_map/ppermute | solution.py:29
  78.2 159.1 %collective-permute-start.3 = (bf16[2048,896]{1,0:T(8,128)(2,1)}, bf16[2048,896]{1,0:T(8,128)(2,1)}, u32[]{:S(2)}, u32[]{:S(2)}) collective-permute-start(bf16[2048,896]{1,0:T(8,128)(2,1)} %bitcast.3), channel_id=1, source_target_pairs={{0,2},{2,0},{1,3},{3,1},{4,6},{6,4},{5,7},{7,5}} | collective-permute-start | bytes 11010056 | tf_op jit(solution)/shard_map/ppermute | solution.py:29
  195.6 184.1 %collective-permute-start.1 = (bf16[2048,896]{1,0:T(8,128)(2,1)}, bf16[2048,896]{1,0:T(8,128)(2,1)}, u32[]{:S(2)}, u32[]{:S(2)}) collective-permute-start(bf16[2048,896]{1,0:T(8,128)(2,1)} %chain.1.refs_2_), channel_id=1, source_target_pairs={{0,2},{2,0},{1,3},{3,1},{4,6},{6,4},{5,7},{7,5}} | collective-permute-start | bytes 11010056 | tf_op jit(solution)/shard_map/ppermute | solution.py:29
  197.6 197.1 %collective-permute-start = (bf16[2048,896]{1,0:T(8,128)(2,1)}, bf16[2048,896]{1,0:T(8,128)(2,1)}, u32[]{:S(2)}, u32[]{:S(2)}) collective-permute-start(bf16[2048,896]{1,0:T(8,128)(2,1)} %get-tuple-element.73.refs_0_), channel_id=1, source_target_pairs={{0,2},{2,0},{1,3},{3,1},{4,6},{6,4},{5,7},{7,5}} | collective-permute-start | bytes 11010056 | tf_op jit(solution)/shard_map/ppermute | solution.py:29
  377.5 162.3 %collective-permute-start.4 = (bf16[896,1152]{1,0:T(8,128)(2,1)}, bf16[896,1152]{1,0:T(8,128)(2,1)}, u32[]{:S(2)}, u32[]{:S(2)}) collective-permute-start(bf16[896,1152]{1,0:T(8,128)(2,1)} %get-tuple-element.79.refs_9_), channel_id=1, source_target_pairs={{0,2},{2,0},{1,3},{3,1},{4,6},{6,4},{5,7},{7,5}} | collective-permute-start | bytes 6193160 | tf_op jit(solution)/shard_map/ppermute | solution.py:29
  379.6 160.9 %collective-permute-start.13 = (bf16[896,1152]{1,0:T(8,128)(2,1)}, bf16[896,1152]{1,0:T(8,128)(2,1)}, u32[]{:S(2)}, u32[]{:S(2)}) collective-permute-start(bf16[896,1152]{1,0:T(8,128)(2,1)} %get-tuple-element.79.refs_9_), channel_id=1, source_target_pairs={{0,1},{1,0},{2,3},{3,2},{4,5},{5,4},{6,7},{7,6}} | collective-permute-start | bytes 6193160 | tf_op jit(solution)/shard_map/ppermute | solution.py:33
  379.6 160.4 %collective-permute-start.6 = (bf16[896,1152]{1,0:T(8,128)(2,1)}, bf16[896,1152]{1,0:T(8,128)(2,1)}, u32[]{:S(2)}, u32[]{:S(2)}) collective-permute-start(bf16[896,1152]{1,0:T(8,128)(2,1)} %get-tuple-element.80.refs_10_), channel_id=1, source_target_pairs={{0,2},{2,0},{1,3},{3,1},{4,6},{6,4},{5,7},{7,5}} | collective-permute-start | bytes 6193160 | tf_op jit(solution)/shard_map/ppermute | solution.py:29
  379.7 161.2 %collective-permute-start.14 = (bf16[896,1152]{1,0:T(8,128)(2,1)}, bf16[896,1152]{1,0:T(8,128)(2,1)}, u32[]{:S(2)}, u32[]{:S(2)}) collective-permute-start(bf16[896,1152]{1,0:T(8,128)(2,1)} %get-tuple-element.80.refs_10_), channel_id=1, source_target_pairs={{0,1},{1,0},{2,3},{3,2},{4,5},{5,4},{6,7},{7,6}} | collective-permute-start | bytes 6193160 | tf_op jit(solution)/shard_map/ppermute | solution.py:33
  394.7 145.7 %collective-permute-start.8 = (bf16[1152,896]{1,0:T(8,128)(2,1)}, bf16[1152,896]{1,0:T(8,128)(2,1)}, u32[]{:S(2)}, u32[]{:S(2)}) collective-permute-start(bf16[1152,896]{1,0:T(8,128)(2,1)} %get-tuple-element.81.refs_11_), channel_id=1, source_target_pairs={{0,2},{2,0},{1,3},{3,1},{4,6},{6,4},{5,7},{7,5}} | collective-permute-start | bytes 6193160 | tf_op jit(solution)/shard_map/ppermute | solution.py:29
  539.9 4.5 collective-permute-start.15
  540.0 7.3 collective-permute-start.10
  540.4 9.8 %collective-permute-start.11 = (bf16[896,1152]{1,0:T(8,128)(2,1)}, bf16[896,1152]{1,0:T(8,128)(2,1)}, u32[]{:S(2)}, u32[]{:S(2)}) collective-permute-start(bf16[896,1152]{1,0:T(8,128)(2,1)} %get-tuple-element.83.refs_19_), channel_id=1, source_target_pairs={{0,1},{1,0},{2,3},{3,2},{4,5},{5,4},{6,7},{7,6}} | collective-permute-start | bytes 6193160 | tf_op jit(solution)/shard_map/ppermute | solution.py:33
  540.5 12.7 %collective-permute-start.12 = (bf16[1152,896]{1,0:T(8,128)(2,1)}, bf16[1152,896]{1,0:T(8,128)(2,1)}, u32[]{:S(2)}, u32[]{:S(2)}) collective-permute-start(bf16[1152,896]{1,0:T(8,128)(2,1)} %get-tuple-element.84.refs_20_), channel_id=1, source_target_pairs={{0,1},{1,0},{2,3},{3,2},{4,5},{5,4},{6,7},{7,6}} | collective-permute-start | bytes 6193160 | tf_op jit(solution)/shard_map/ppermute | solution.py:33
  540.9 48.1 %collective-permute-start.18 = (bf16[896,1152]{1,0:T(8,128)(2,1)}, bf16[896,1152]{1,0:T(8,128)(2,1)}, u32[]{:S(2)}, u32[]{:S(2)}) collective-permute-start(bf16[896,1152]{1,0:T(8,128)(2,1)} %get-tuple-element.82.refs_18_), channel_id=1, source_target_pairs={{0,2},{2,0},{1,3},{3,1},{4,6},{6,4},{5,7},{7,5}} | collective-permute-start | bytes 6193160 | tf_op jit(solution)/shard_map/ppermute | solution.py:29
  544.3 187.0 %collective-permute-start.16 = (bf16[1152,896]{1,0:T(8,128)(2,1)}, bf16[1152,896]{1,0:T(8,128)(2,1)}, u32[]{:S(2)}, u32[]{:S(2)}) collective-permute-start(bf16[1152,896]{1,0:T(8,128)(2,1)} %get-tuple-element.84.refs_20_), channel_id=1, source_target_pairs={{0,2},{2,0},{1,3},{3,1},{4,6},{6,4},{5,7},{7,5}} | collective-permute-start | bytes 6193160 | tf_op jit(solution)/shard_map/ppermute | solution.py:29
  547.3 136.9 %collective-permute-start.19 = (bf16[896,1152]{1,0:T(8,128)(2,1)}, bf16[896,1152]{1,0:T(8,128)(2,1)}, u32[]{:S(2)}, u32[]{:S(2)}) collective-permute-start(bf16[896,1152]{1,0:T(8,128)(2,1)} %get-tuple-element.83.refs_19_), channel_id=1, source_target_pairs={{0,2},{2,0},{1,3},{3,1},{4,6},{6,4},{5,7},{7,5}} | collective-permute-start | bytes 6193160 | tf_op jit(solution)/shard_map/ppermute | solution.py:29
  550.2 134.5 %collective-permute-start.5 = (bf16[896,1152]{1,0:T(8,128)(2,1)}, bf16[896,1152]{1,0:T(8,128)(2,1)}, u32[]{:S(2)}, u32[]{:S(2)}) collective-permute-start(bf16[896,1152]{1,0:T(8,128)(2,1)} %collective-permute-done.4.refs_15_), channel_id=1, source_target_pairs={{0,1},{1,0},{2,3},{3,2},{4,5},{5,4},{6,7},{7,6}} | collective-permute-start | bytes 6193160 | tf_op jit(solution)/shard_map/ppermute | solution.py:33
  553.2 131.6 %collective-permute-start.7 = (bf16[896,1152]{1,0:T(8,128)(2,1)}, bf16[896,1152]{1,0:T(8,128)(2,1)}, u32[]{:S(2)}, u32[]{:S(2)}) collective-permute-start(bf16[896,1152]{1,0:T(8,128)(2,1)} %collective-permute-done.6.refs_16_), channel_id=1, source_target_pairs={{0,1},{1,0},{2,3},{3,2},{4,5},{5,4},{6,7},{7,6}} | collective-permute-start | bytes 6193160 | tf_op jit(solution)/shard_map/ppermute | solution.py:33
  589.0 95.7 %collective-permute-start.9 = (bf16[1152,896]{1,0:T(8,128)(2,1)}, bf16[1152,896]{1,0:T(8,128)(2,1)}, u32[]{:S(2)}, u32[]{:S(2)}) collective-permute-start(bf16[1152,896]{1,0:T(8,128)(2,1)} %collective-permute-done.8.refs_17_), channel_id=1, source_target_pairs={{0,1},{1,0},{2,3},{3,2},{4,5},{5,4},{6,7},{7,6}} | collective-permute-start | bytes 6193160 | tf_op jit(solution)/shard_map/ppermute | solution.py:33
  684.2 47.7 %collective-permute-start.20 = (bf16[896,1152]{1,0:T(8,128)(2,1)}, bf16[896,1152]{1,0:T(8,128)(2,1)}, u32[]{:S(2)}, u32[]{:S(2)}) collective-permute-start(bf16[896,1152]{1,0:T(8,128)(2,1)} %collective-permute-done.18.refs_9_), channel_id=1, source_target_pairs={{0,1},{1,0},{2,3},{3,2},{4,5},{5,4},{6,7},{7,6}} | collective-permute-start | bytes 6193160 | tf_op jit(solution)/shard_map/ppermute | solution.py:33
  684.7 47.1 %collective-permute-start.21 = (bf16[896,1152]{1,0:T(8,128)(2,1)}, bf16[896,1152]{1,0:T(8,128)(2,1)}, u32[]{:S(2)}, u32[]{:S(2)}) collective-permute-start(bf16[896,1152]{1,0:T(8,128)(2,1)} %collective-permute-done.19.refs_10_), channel_id=1, source_target_pairs={{0,1},{1,0},{2,3},{3,2},{4,5},{5,4},{6,7},{7,6}} | collective-permute-start | bytes 6193160 | tf_op jit(solution)/shard_map/ppermute | solution.py:33
  731.4 39.8 %collective-permute-start.17 = (bf16[1152,896]{1,0:T(8,128)(2,1)}, bf16[1152,896]{1,0:T(8,128)(2,1)}, u32[]{:S(2)}, u32[]{:S(2)}) collective-permute-start(bf16[1152,896]{1,0:T(8,128)(2,1)} %collective-permute-done.16.refs_11_), channel_id=1, source_target_pairs={{0,1},{1,0},{2,3},{3,2},{4,5},{5,4},{6,7},{7,6}} | collective-permute-start | bytes 6193160 | tf_op jit(solution)/shard_map/ppermute | solution.py:33

commit v8 on v7

--- a/solution.py
+++ b/solution.py
@@ -1,3 +1,5 @@
+import functools
+
 import jax
 import jax.numpy as jnp
 import numpy as np
@@ -14,7 +16,7 @@
 
 LANES = 128
 BLOCK = 512
-ROWS = 512
+ROWS, FEW, TOGETHER = 512, 64, 4
 
 
 def dot(a, b, dims):
@@ -50,46 +52,55 @@
     return (wide * norm_scale(wide)).astype(BF16)
 
 
+def looped(count, rows, body, together=1):
+    def one(n, carry):
+        for part in range(together):
+            body(pl.ds(pl.multiple_of((n * together + part) * rows, rows), rows))
+        return carry
+
+    lax.fori_loop(0, count // together, one, 0)
+
+
 def forward_kernel(tail, x_ref, wg_ref, wu_ref, wd_ref, h_ref, a_ref, a0_ref, acc_ref):
     j, last = pl.program_id(0), pl.num_programs(0) - 1
     tokens = x_ref.shape[0]
-    chunks = [pl.ds(r, ROWS) for r in range(0, tokens, ROWS)]
 
     @pl.when(j == 0)
     def _():
-        for r in chunks:
+        def start(r):
             a0_ref[r, :] = normed(x_ref[r, :])
-            acc_ref[r, :] = jnp.zeros((ROWS, acc_ref.shape[1]), F32)
-
-    def block(width):
-        hid = {}
-
-        def up(r):
-            a = a0_ref[chunks[r], :]
-            g = dot(a, wg_ref[0, :, :width], NN)
-            u = dot(a, wu_ref[0, :, :width], NN)
-            hid[r] = (g * sigmoid(g) * u).astype(BF16)
-
-        def down(r):
-            acc_ref[chunks[r], :] += dot(hid.pop(r), wd_ref[0, :width, :], NN)
-
-        up(0)
-        for r in range(1, len(chunks)):
-            up(r)
-            down(r - 1)
-        down(len(chunks) - 1)
+            acc_ref[r, :] = jnp.zeros((FEW, acc_ref.shape[1]), F32)
+
+        looped(tokens // FEW, FEW, start, TOGETHER)
+
+    def up(r, width):
+        a = a0_ref[r, :]
+        g = dot(a, wg_ref[0, :, :width], NN)
+        u = dot(a, wu_ref[0, :, :width], NN)
+        return (g * sigmoid(g) * u).astype(BF16)
+
+    def down(r, hid):
+        acc_ref[r, :] += dot(hid, wd_ref[0, : hid.shape[1], :], NN)
 
     @pl.when(j < last)
     def _():
-        block(wg_ref.shape[2])
+        chunks = [pl.ds(r, ROWS) for r in range(0, tokens, ROWS)]
+        hid = up(chunks[0], wg_ref.shape[2])
+        for r, following in zip(chunks, chunks[1:] + [None], strict=True):
+            ahead = None if following is None else up(following, wg_ref.shape[2])
+            down(r, hid)
+            hid = ahead
 
     @pl.when(j == last)
     def _():
-        block(tail)
-        for r in chunks:
+        looped(tokens // ROWS, ROWS, lambda r: down(r, up(r, tail)))
+
+        def end(r):
             h = (x_ref[r, :].astype(F32) + acc_ref[r, :].astype(BF16).astype(F32)).astype(BF16)
             h_ref[r, :] = h
             a_ref[r, :] = normed(h)
+
+        looped(tokens // FEW, FEW, end, TOGETHER)
 
 
 def forward(x, wg, wu, wd):
@@ -119,51 +130,51 @@
     return (dhid * u * (sig + act * (1 - sig))).astype(BF16), (dhid * act).astype(BF16), (act * u).astype(BF16)
 
 
-def chain_kernel(tail, a_ref, dy_ref, h_ref, wg_ref, wu_ref, wd_ref, dh_ref, acc_ref, wgt_ref, wut_ref, wdt_ref):
+def chain_kernel(tail, a_ref, dy_ref, h_ref, wg_ref, wu_ref, wd_ref, dh_ref, acc_ref):
     j, last = pl.program_id(0), pl.num_programs(0) - 1
     tokens = a_ref.shape[0]
-    chunks = [pl.ds(r, ROWS) for r in range(0, tokens, ROWS)]
 
     @pl.when(j == 0)
     def _():
-        for r in chunks:
-            acc_ref[r, :] = jnp.zeros((ROWS, acc_ref.shape[1]), F32)
-
-    def block(width):
-        held = {}
-        wdt_ref[:, :width] = wd_ref[0, :width, :].T
-        wgt_ref[:width, :] = wg_ref[0, :, :width].T
-        wut_ref[:width, :] = wu_ref[0, :, :width].T
-
-        def there(r):
-            a, dy = a_ref[chunks[r], :], dy_ref[chunks[r], :]
-            g = dot(a, wg_ref[0, :, :width], NN)
-            u = dot(a, wu_ref[0, :, :width], NN)
-            dhid = dot(dy, wdt_ref[:, :width], NN)
-            held[r] = hidden_back(g, u, dhid)[:2]
-
-        def back(r):
-            dg, du = held.pop(r)
-            acc_ref[chunks[r], :] += dot(dg, wgt_ref[:width, :], NN) + dot(du, wut_ref[:width, :], NN)
-
-        there(0)
-        for r in range(1, len(chunks)):
-            there(r)
-            back(r - 1)
-        back(len(chunks) - 1)
+        def start(r):
+            acc_ref[r, :] = jnp.zeros((FEW, acc_ref.shape[1]), F32)
+
+        looped(tokens // FEW, FEW, start, TOGETHER)
+
+    def there(r, width):
+        a, dy = a_ref[r, :], dy_ref[r, :]
+        g = dot(a, wg_ref[0, :, :width], NN)
+        u = dot(a, wu_ref[0, :, :width], NN)
+        dhid = dot(dy, wd_ref[0, :width, :], NT)
+        return hidden_back(g, u, dhid)[:2]
+
+    def back(r, held):
+        dg, du = held
+        width = dg.shape[1]
+        acc_ref[r, :] += dot(dg, wg_ref[0, :, :width], NT) + dot(du, wu_ref[0, :, :width], NT)
+
+    def two(width, r):
+        low, high = (pl.ds(pl.multiple_of(r.start + n * ROWS, ROWS), ROWS) for n in range(2))
+        held = there(low, width)
+        ahead = there(high, width)
+        back(low, held)
+        back(high, ahead)
 
     @pl.when(j < last)
     def _():
-        block(wg_ref.shape[2])
+        looped(tokens // (2 * ROWS), 2 * ROWS, functools.partial(two, wg_ref.shape[2]))
 
     @pl.when(j == last)
     def _():
-        block(tail)
-        for r in chunks:
+        looped(tokens // (2 * ROWS), 2 * ROWS, functools.partial(two, tail))
+
+        def end(r):
             wide, da = h_ref[r, :].astype(F32), acc_ref[r, :].astype(BF16).astype(F32)
             scale = norm_scale(wide)
-            back = scale * da - wide * (scale * scale * scale * jnp.mean(wide * da, -1, keepdims=True))
-            dh_ref[r, :] = (dy_ref[r, :].astype(F32) + back.astype(BF16).astype(F32)).astype(BF16)
+            through = scale * da - wide * (scale * scale * scale * jnp.mean(wide * da, -1, keepdims=True))
+            dh_ref[r, :] = (dy_ref[r, :].astype(F32) + through.astype(BF16).astype(F32)).astype(BF16)
+
+        looped(tokens // FEW, FEW, end, TOGETHER)
 
 
 def chain(a, dy, h, wg, wu, wd):
@@ -179,7 +190,7 @@
         in_specs=[full, full, full, across, across, down],
         out_specs=full,
         out_shape=jax.ShapeDtypeStruct((tokens, d), BF16),
-        scratch_shapes=[pltpu.VMEM((tokens, d), F32)] + [pltpu.VMEM((BLOCK, d), BF16)] * 2 + [pltpu.VMEM((d, BLOCK), BF16)],
+        scratch_shapes=[pltpu.VMEM((tokens, d), F32)],
         cost_estimate=pl.CostEstimate(flops=10 * tokens * d * ff, bytes_accessed=6 * d * ff, transcendentals=tokens * ff),
         compiler_params=params(),
         name="chain",
@@ -306,24 +317,34 @@
 
     @pl.when(i == steps - 1)
     def _():
-        sums = [None, None]
-        for acc, term, out, out_s, turned in (
-            (accg_ref, terms[0], *outs[0:4:3], False),
-            (accu_ref, terms[1], *outs[1:5:3], False),
-            (accd_ref, terms[2], *outs[2:6:3], True),
-        ):
-            at = [(core + s) % 2 + 2 * ((chip + s // 2) % 2) for s in range(4)]
-            whole = term[at[0]] + term[at[1]] + term[at[2]] + term[at[3]]
-            for c in range(0, width, LANES):
-                part = (acc[:, c : c + LANES] if c < own else whole[:, c - own : c - own + LANES]).astype(BF16)
-                ref, place = (out, pl.ds(c, LANES)) if c < own else (out_s, pl.ds(c - own, LANES))
-                if turned:
-                    ref[place, :] = part.T
-                else:
-                    ref[:, place] = part
-                square = part.astype(F32)
-                square = jnp.sum((square * square).reshape(-1, 8, LANES), 0)
-                sums[c >= own] = square if sums[c >= own] is None else sums[c >= own] + square
+        def rounded(part, total):
+            part = part.astype(BF16)
+            wide = part.astype(F32)
+            return part, total + jnp.sum((wide * wide).reshape(-1, 8, LANES), 0)
+
+        accs = (accg_ref, accu_ref, accd_ref)
+
+        def rows(r, total):
+            at = pl.ds(pl.multiple_of(r * LANES, LANES), LANES)
+            for n, acc in enumerate(accs):
+                for c in range(0, own, LANES):
+                    part, total = rounded(acc[at, c : c + LANES], total)
+                    if n < 2:
+                        outs[n][at, c : c + LANES] = part
+            return total
+
+        def turn(c, carry):
+            at = pl.ds(pl.multiple_of(c * LANES, LANES), LANES)
+            for r in range(0, a.shape[1], LANES):
+                outs[2][at, r : r + LANES] = accd_ref[r : r + LANES, at].astype(BF16).T
+            return carry
+
+        at = [(core + s) % 2 + 2 * ((chip + s // 2) % 2) for s in range(4)]
+        sums = [lax.fori_loop(0, a.shape[1] // LANES, rows, jnp.zeros((8, LANES), F32)), jnp.zeros((8, LANES), F32)]
+        lax.fori_loop(0, own // LANES, turn, 0)
+        for n, term in enumerate(terms):
+            part, sums[1] = rounded(term[at[0]] + term[at[1]] + term[at[2]] + term[at[3]], sums[1])
+            outs[3 + n][...] = part if n < 2 else part.T
         if not final:
             outs[6][...], outs[7][...] = sums
         else:

time: 789 us -> 784 us (level)
  transfers between devices with their start and end apart: 22 -> 22, of which waited for: 7 -> 7; matrix products, arithmetic and copies ran while one was open for 0% -> 0% of each run, Pallas kernels for 74% -> 75%
where the time goes in v8:
time: 784 us; the launch traced here: 783 us
  Pallas kernels  670 us (85%)
  waiting for transfers between devices  94.1 us (12%)
  starting transfers between devices  18.3 us (2%)
    pallas_call x2, Pallas kernels, slices(): pl.pallas_call(lambda *refs: slices_kernel(layer, own, count, *refs), gri...  284 us
    pallas_call x4, Pallas kernels, adam(): pl.pallas_call(kernel, in_specs=[pl.BlockSpec(memory_space=pltpu.SMEM), p...  191 us
    pallas_call x1, Pallas kernels, chain(): pl.pallas_call(lambda *refs: chain_kernel(ff - (steps - 1) * BLOCK, *refs...  119 us
    ppermute x10, waiting for transfers between devices, px(): return lax.ppermute(a, 'dp', PX)  88 us
    pallas_call x1, Pallas kernels, forward(): pl.pallas_call(lambda *refs: forward_kernel(ff - (steps - 1) * BLOCK, *re...  76.2 us
  transfers between devices with their start and end apart: 22, of which 7 were waited for; matrix products, arithmetic and copies ran while one was open for 0% of the time, Pallas kernels for 75%

profile of v8, /device:TPU:0, one launch (start us, length us, event | category | flops | bytes accessed | tf_op | source)
XLA Modules:
  0.0 783.5 jit_solution(11827758799041290436)
XLA Ops:
  0.6 76.2 %forward.1 = (bf16[2048,896]{1,0:T(8,128)(2,1)}, bf16[2048,896]{1,0:T(8,128)(2,1)}, bf16[2048,896]{1,0:T(8,128)(2,1)}) custom-call(bf16[2048,896]{1,0:T(8,128)(2,1)} %bitcast.2, bf16[2,896,4736]{2,1,0:T(8,128)(2,1)} %refs_0_.7, bf16[2,896,4736]{2,1,0:T(8,128)(2,1)} %refs_3_.11, bf16[2,4736,896]{2,1,0:T(8,128)(2,1)} %refs_6_.11), custom_call_target="tpu_custom_call" | custom-call | flops 52143587328 | bytes 25460736 | tf_op jit(solution)/shard_map/forward/pallas_call | solution.py:113
  76.9 3.3 collective-permute-start.2
  80.2 118.9 %chain.1.refs_2_ = bf16[2048,896]{1,0:T(8,128)(2,1)} custom-call(bf16[2048,896]{1,0:T(8,128)(2,1)} %get-tuple-element.74.refs_0_, bf16[2048,896]{1,0:T(8,128)(2,1)} %bitcast.4, bf16[2048,896]{1,0:T(8,128)(2,1)} %get-tuple-element.75.refs_2_, bf16[2,896,4736]{2,1,0:T(8,128)(2,1)} %refs_0_.7, bf16[2,896,4736]{2,1,0:T(8,128)(2,1)} %refs_3_.11, ...), custom_call_target="tpu_custom_call" | custom-call | flops 86905978880 | bytes 25460736 | tf_op jit(solution)/shard_map/chain/pallas_call | solution.py:187
  199.1 2.0 collective-permute-start.1
  201.2 38.1 %collective-permute-done.3.refs_3_ = bf16[2048,896]{1,0:T(8,128)(2,1)} collective-permute-done((bf16[2048,896]{1,0:T(8,128)(2,1)}, bf16[2048,896]{1,0:T(8,128)(2,1)}, u32[]{:S(2)}, u32[]{:S(2)}) %collective-permute-start.3) | collective-permute-done | bytes 3670048 | tf_op jit(solution)/shard_map/ppermute | solution.py:31
  239.3 140.6 %slices.2 = (bf16[896,1152]{1,0:T(8,128)(2,1)}, bf16[896,1152]{1,0:T(8,128)(2,1)}, bf16[1152,896]{1,0:T(8,128)(2,1)}, bf16[896,128]{1,0:T(8,128)(2,1)}, bf16[896...) custom-call(bf16[2048,896]{1,0:T(8,128)(2,1)} %get-tuple-element.74., ...), custom_call_target="tpu_custom_call" | custom-call | flops 112742891520 | bytes 29360128 | tf_op jit(solution)/shard_map/slices/pallas_call | solution.py:371
  379.9 2.1 collective-permute-start.4
  382.0 0.1 collective-permute-start.6
  382.1 0.4 collective-permute-start.14
  382.5 14.1 %collective-permute-done.refs_1_ = bf16[2048,896]{1,0:T(8,128)(2,1)} collective-permute-done((bf16[2048,896]{1,0:T(8,128)(2,1)}, bf16[2048,896]{1,0:T(8,128)(2,1)}, u32[]{:S(2)}, u32[]{:S(2)}) %collective-permute-start) | collective-permute-done | bytes 3670048 | tf_op jit(solution)/shard_map/ppermute | solution.py:31
  396.6 2.0 collective-permute-start.8
  398.6 143.5 %slices.3 = (bf16[896,1152]{1,0:T(8,128)(2,1)}, bf16[896,1152]{1,0:T(8,128)(2,1)}, bf16[1152,896]{1,0:T(8,128)(2,1)}, bf16[896,128]{1,0:T(8,128)(2,1)}, bf16[896...) custom-call(bf16[2048,896]{1,0:T(8,128)(2,1)} %get-tuple-element.73., ...), custom_call_target="tpu_custom_call" | custom-call | flops 112742891520 | bytes 29360128 | tf_op jit(solution)/shard_map/slices/pallas_call | solution.py:371
  542.2 0.1 collective-permute-start.15
  542.3 0.4 collective-permute-start.10
  542.7 0.1 collective-permute-start.11
  542.8 0.4 collective-permute-start.12
  543.2 2.0 collective-permute-start.18
  545.3 1.4 collective-permute-done.15.refs_14_
  546.7 2.0 collective-permute-start.16
  548.7 0.9 collective-permute-done.10.refs_12_
  549.6 2.0 collective-permute-start.19
  551.6 0.9 collective-permute-done.11.refs_13_
  552.6 0.1 collective-permute-start.5
  552.7 2.8 collective-permute-done.12.refs_14_
  555.5 0.1 collective-permute-start.7
  555.7 35.7 %collective-permute-done.18.refs_9_ = bf16[896,1152]{1,0:T(8,128)(2,1)} collective-permute-done((bf16[896,1152]{1,0:T(8,128)(2,1)}, bf16[896,1152]{1,0:T(8,128)(2,1)}, u32[]{:S(2)}, u32[]{:S(2)}) %collective-permute-start.18) | collective-permute-done | bytes 2064416 | tf_op jit(solution)/shard_map/ppermute | solution.py:31
  591.4 95.1 %shard_map.214 = (bf16[2,896,4736]{2,1,0:T(8,128)(2,1)}, f32[2,896,4736]{2,1,0:T(8,128)}, f32[2,896,4736]{2,1,0:T(8,128)}, bf16[2,896,4736]{2,1,0:T(8,128)(2,1)}...) custom-call(s32[8,98]{1,0:T(8,128)} %constant.8.clone.table_ref, ...), custom_call_target="tpu_custom_call" | custom-call | flops 26148864000 | bytes 287637504 | tf_op jit(solution)/shard_map/pallas_call | solution.py:506
  686.5 0.5 collective-permute-start.20
  687.1 46.6 %shard_map.215 = (bf16[2,896,4736]{2,1,0:T(8,128)(2,1)}, f32[2,896,4736]{2,1,0:T(8,128)}, f32[2,896,4736]{2,1,0:T(8,128)}, bf16[2,896,4736]{2,1,0:T(8,128)(2,1)}...) custom-call(s32[8,46]{1,0:T(8,128)} %constant.9.clone.table_ref, ...), custom_call_target="tpu_custom_call", output_to_operand_aliasing={{0}: (17, {}), {1}: (18, {}), {2}: (19, {}), {3}: (20, {}),... | custom-call | flops 12386304000 | bytes 136249344 | tf_op jit(solution)/shard_map/pallas_call | solution.py:506
  733.7 0.4 collective-permute-start.17
  734.2 39.3 %shard_map.216 = (bf16[2,896,4736]{2,1,0:T(8,128)(2,1)}, f32[2,896,4736]{2,1,0:T(8,128)}, f32[2,896,4736]{2,1,0:T(8,128)}, bf16[2,896,4736]{2,1,0:T(8,128)(2,1)}...) custom-call(s32[8,37]{1,0:T(8,128)} %constant.10.clone.table_ref, ...), custom_call_target="tpu_custom_call", output_to_operand_aliasing={{0}: (16, {}), {1}: (17, {}), {2}: (18, {}), {3}: (19, {}),... | custom-call | flops 10321920000 | bytes 113541120 | tf_op jit(solution)/shard_map/pallas_call | solution.py:506
  773.5 9.7 %shard_map.217 = (bf16[2,896,4736]{2,1,0:T(8,128)(2,1)}, f32[2,896,4736]{2,1,0:T(8,128)}, f32[2,896,4736]{2,1,0:T(8,128)}, bf16[2,896,4736]{2,1,0:T(8,128)(2,1)}...) custom-call(s32[8,9]{1,0:T(8,128)} %constant.11.clone.table_ref, ...), custom_call_target="tpu_custom_call", output_to_operand_aliasing={{0}: (12, {}), {1}: (13, {}), {2}: (14, {}), {3}: (15, {}),... | custom-call | flops 2064384000 | bytes 22708224 | tf_op jit(solution)/shard_map/pallas_call | solution.py:506
  (20 shorter events, 0.2 us)
Async XLA Ops:
  76.9 124.3 %collective-permute-start.2 = (bf16[2048,896]{1,0:T(8,128)(2,1)}, bf16[2048,896]{1,0:T(8,128)(2,1)}, u32[]{:S(2)}, u32[]{:S(2)}) collective-permute-start(bf16[2048,896]{1,0:T(8,128)(2,1)} %get-tuple-element.74.refs_0_), channel_id=1, source_target_pairs={{0,2},{2,0},{1,3},{3,1},{4,6},{6,4},{5,7},{7,5}} | collective-permute-start | bytes 11010056 | tf_op jit(solution)/shard_map/ppermute | solution.py:31
  80.2 159.1 %collective-permute-start.3 = (bf16[2048,896]{1,0:T(8,128)(2,1)}, bf16[2048,896]{1,0:T(8,128)(2,1)}, u32[]{:S(2)}, u32[]{:S(2)}) collective-permute-start(bf16[2048,896]{1,0:T(8,128)(2,1)} %bitcast.3), channel_id=1, source_target_pairs={{0,2},{2,0},{1,3},{3,1},{4,6},{6,4},{5,7},{7,5}} | collective-permute-start | bytes 11010056 | tf_op jit(solution)/shard_map/ppermute | solution.py:31
  199.1 182.9 %collective-permute-start.1 = (bf16[2048,896]{1,0:T(8,128)(2,1)}, bf16[2048,896]{1,0:T(8,128)(2,1)}, u32[]{:S(2)}, u32[]{:S(2)}) collective-permute-start(bf16[2048,896]{1,0:T(8,128)(2,1)} %chain.1.refs_2_), channel_id=1, source_target_pairs={{0,2},{2,0},{1,3},{3,1},{4,6},{6,4},{5,7},{7,5}} | collective-permute-start | bytes 11010056 | tf_op jit(solution)/shard_map/ppermute | solution.py:31
  201.1 195.5 %collective-permute-start = (bf16[2048,896]{1,0:T(8,128)(2,1)}, bf16[2048,896]{1,0:T(8,128)(2,1)}, u32[]{:S(2)}, u32[]{:S(2)}) collective-permute-start(bf16[2048,896]{1,0:T(8,128)(2,1)} %get-tuple-element.73.refs_0_), channel_id=1, source_target_pairs={{0,2},{2,0},{1,3},{3,1},{4,6},{6,4},{5,7},{7,5}} | collective-permute-start | bytes 11010056 | tf_op jit(solution)/shard_map/ppermute | solution.py:31
  379.9 162.2 %collective-permute-start.4 = (bf16[896,1152]{1,0:T(8,128)(2,1)}, bf16[896,1152]{1,0:T(8,128)(2,1)}, u32[]{:S(2)}, u32[]{:S(2)}) collective-permute-start(bf16[896,1152]{1,0:T(8,128)(2,1)} %get-tuple-element.79.refs_9_), channel_id=1, source_target_pairs={{0,2},{2,0},{1,3},{3,1},{4,6},{6,4},{5,7},{7,5}} | collective-permute-start | bytes 6193160 | tf_op jit(solution)/shard_map/ppermute | solution.py:31
  382.0 160.8 %collective-permute-start.13 = (bf16[896,1152]{1,0:T(8,128)(2,1)}, bf16[896,1152]{1,0:T(8,128)(2,1)}, u32[]{:S(2)}, u32[]{:S(2)}) collective-permute-start(bf16[896,1152]{1,0:T(8,128)(2,1)} %get-tuple-element.79.refs_9_), channel_id=1, source_target_pairs={{0,1},{1,0},{2,3},{3,2},{4,5},{5,4},{6,7},{7,6}} | collective-permute-start | bytes 6193160 | tf_op jit(solution)/shard_map/ppermute | solution.py:35
  382.0 160.3 %collective-permute-start.6 = (bf16[896,1152]{1,0:T(8,128)(2,1)}, bf16[896,1152]{1,0:T(8,128)(2,1)}, u32[]{:S(2)}, u32[]{:S(2)}) collective-permute-start(bf16[896,1152]{1,0:T(8,128)(2,1)} %get-tuple-element.80.refs_10_), channel_id=1, source_target_pairs={{0,2},{2,0},{1,3},{3,1},{4,6},{6,4},{5,7},{7,5}} | collective-permute-start | bytes 6193160 | tf_op jit(solution)/shard_map/ppermute | solution.py:31
  382.1 161.2 %collective-permute-start.14 = (bf16[896,1152]{1,0:T(8,128)(2,1)}, bf16[896,1152]{1,0:T(8,128)(2,1)}, u32[]{:S(2)}, u32[]{:S(2)}) collective-permute-start(bf16[896,1152]{1,0:T(8,128)(2,1)} %get-tuple-element.80.refs_10_), channel_id=1, source_target_pairs={{0,1},{1,0},{2,3},{3,2},{4,5},{5,4},{6,7},{7,6}} | collective-permute-start | bytes 6193160 | tf_op jit(solution)/shard_map/ppermute | solution.py:35
  396.6 146.1 %collective-permute-start.8 = (bf16[1152,896]{1,0:T(8,128)(2,1)}, bf16[1152,896]{1,0:T(8,128)(2,1)}, u32[]{:S(2)}, u32[]{:S(2)}) collective-permute-start(bf16[1152,896]{1,0:T(8,128)(2,1)} %get-tuple-element.81.refs_11_), channel_id=1, source_target_pairs={{0,2},{2,0},{1,3},{3,1},{4,6},{6,4},{5,7},{7,5}} | collective-permute-start | bytes 6193160 | tf_op jit(solution)/shard_map/ppermute | solution.py:31
  542.2 4.5 collective-permute-start.15
  542.3 7.3 collective-permute-start.10
  542.7 9.8 %collective-permute-start.11 = (bf16[896,1152]{1,0:T(8,128)(2,1)}, bf16[896,1152]{1,0:T(8,128)(2,1)}, u32[]{:S(2)}, u32[]{:S(2)}) collective-permute-start(bf16[896,1152]{1,0:T(8,128)(2,1)} %get-tuple-element.83.refs_19_), channel_id=1, source_target_pairs={{0,1},{1,0},{2,3},{3,2},{4,5},{5,4},{6,7},{7,6}} | collective-permute-start | bytes 6193160 | tf_op jit(solution)/shard_map/ppermute | solution.py:35
  542.8 12.7 %collective-permute-start.12 = (bf16[1152,896]{1,0:T(8,128)(2,1)}, bf16[1152,896]{1,0:T(8,128)(2,1)}, u32[]{:S(2)}, u32[]{:S(2)}) collective-permute-start(bf16[1152,896]{1,0:T(8,128)(2,1)} %get-tuple-element.84.refs_20_), channel_id=1, source_target_pairs={{0,1},{1,0},{2,3},{3,2},{4,5},{5,4},{6,7},{7,6}} | collective-permute-start | bytes 6193160 | tf_op jit(solution)/shard_map/ppermute | solution.py:35
  543.2 48.1 %collective-permute-start.18 = (bf16[896,1152]{1,0:T(8,128)(2,1)}, bf16[896,1152]{1,0:T(8,128)(2,1)}, u32[]{:S(2)}, u32[]{:S(2)}) collective-permute-start(bf16[896,1152]{1,0:T(8,128)(2,1)} %get-tuple-element.82.refs_18_), channel_id=1, source_target_pairs={{0,2},{2,0},{1,3},{3,1},{4,6},{6,4},{5,7},{7,5}} | collective-permute-start | bytes 6193160 | tf_op jit(solution)/shard_map/ppermute | solution.py:31
  546.7 187.0 %collective-permute-start.16 = (bf16[1152,896]{1,0:T(8,128)(2,1)}, bf16[1152,896]{1,0:T(8,128)(2,1)}, u32[]{:S(2)}, u32[]{:S(2)}) collective-permute-start(bf16[1152,896]{1,0:T(8,128)(2,1)} %get-tuple-element.84.refs_20_), channel_id=1, source_target_pairs={{0,2},{2,0},{1,3},{3,1},{4,6},{6,4},{5,7},{7,5}} | collective-permute-start | bytes 6193160 | tf_op jit(solution)/shard_map/ppermute | solution.py:31
  549.6 136.9 %collective-permute-start.19 = (bf16[896,1152]{1,0:T(8,128)(2,1)}, bf16[896,1152]{1,0:T(8,128)(2,1)}, u32[]{:S(2)}, u32[]{:S(2)}) collective-permute-start(bf16[896,1152]{1,0:T(8,128)(2,1)} %get-tuple-element.83.refs_19_), channel_id=1, source_target_pairs={{0,2},{2,0},{1,3},{3,1},{4,6},{6,4},{5,7},{7,5}} | collective-permute-start | bytes 6193160 | tf_op jit(solution)/shard_map/ppermute | solution.py:31
  552.6 134.5 %collective-permute-start.5 = (bf16[896,1152]{1,0:T(8,128)(2,1)}, bf16[896,1152]{1,0:T(8,128)(2,1)}, u32[]{:S(2)}, u32[]{:S(2)}) collective-permute-start(bf16[896,1152]{1,0:T(8,128)(2,1)} %collective-permute-done.4.refs_15_), channel_id=1, source_target_pairs={{0,1},{1,0},{2,3},{3,2},{4,5},{5,4},{6,7},{7,6}} | collective-permute-start | bytes 6193160 | tf_op jit(solution)/shard_map/ppermute | solution.py:35
  555.5 131.6 %collective-permute-start.7 = (bf16[896,1152]{1,0:T(8,128)(2,1)}, bf16[896,1152]{1,0:T(8,128)(2,1)}, u32[]{:S(2)}, u32[]{:S(2)}) collective-permute-start(bf16[896,1152]{1,0:T(8,128)(2,1)} %collective-permute-done.6.refs_16_), channel_id=1, source_target_pairs={{0,1},{1,0},{2,3},{3,2},{4,5},{5,4},{6,7},{7,6}} | collective-permute-start | bytes 6193160 | tf_op jit(solution)/shard_map/ppermute | solution.py:35
  591.4 95.7 %collective-permute-start.9 = (bf16[1152,896]{1,0:T(8,128)(2,1)}, bf16[1152,896]{1,0:T(8,128)(2,1)}, u32[]{:S(2)}, u32[]{:S(2)}) collective-permute-start(bf16[1152,896]{1,0:T(8,128)(2,1)} %collective-permute-done.8.refs_17_), channel_id=1, source_target_pairs={{0,1},{1,0},{2,3},{3,2},{4,5},{5,4},{6,7},{7,6}} | collective-permute-start | bytes 6193160 | tf_op jit(solution)/shard_map/ppermute | solution.py:35
  686.5 47.7 %collective-permute-start.20 = (bf16[896,1152]{1,0:T(8,128)(2,1)}, bf16[896,1152]{1,0:T(8,128)(2,1)}, u32[]{:S(2)}, u32[]{:S(2)}) collective-permute-start(bf16[896,1152]{1,0:T(8,128)(2,1)} %collective-permute-done.18.refs_9_), channel_id=1, source_target_pairs={{0,1},{1,0},{2,3},{3,2},{4,5},{5,4},{6,7},{7,6}} | collective-permute-start | bytes 6193160 | tf_op jit(solution)/shard_map/ppermute | solution.py:35
  687.0 47.1 %collective-permute-start.21 = (bf16[896,1152]{1,0:T(8,128)(2,1)}, bf16[896,1152]{1,0:T(8,128)(2,1)}, u32[]{:S(2)}, u32[]{:S(2)}) collective-permute-start(bf16[896,1152]{1,0:T(8,128)(2,1)} %collective-permute-done.19.refs_10_), channel_id=1, source_target_pairs={{0,1},{1,0},{2,3},{3,2},{4,5},{5,4},{6,7},{7,6}} | collective-permute-start | bytes 6193160 | tf_op jit(solution)/shard_map/ppermute | solution.py:35
  733.7 39.8 %collective-permute-start.17 = (bf16[1152,896]{1,0:T(8,128)(2,1)}, bf16[1152,896]{1,0:T(8,128)(2,1)}, u32[]{:S(2)}, u32[]{:S(2)}) collective-permute-start(bf16[1152,896]{1,0:T(8,128)(2,1)} %collective-permute-done.16.refs_11_), channel_id=1, source_target_pairs={{0,1},{1,0},{2,3},{3,2},{4,5},{5,4},{6,7},{7,6}} | collective-permute-start | bytes 6193160 | tf_op jit(solution)/shard_map/ppermute | solution.py:35

commit v9 on v8

--- a/solution.py
+++ b/solution.py
@@ -82,14 +82,16 @@
     def down(r, hid):
         acc_ref[r, :] += dot(hid, wd_ref[0, : hid.shape[1], :], NN)
 
+    def two(width, r):
+        low, high = (pl.ds(pl.multiple_of(r.start + n * ROWS, ROWS), ROWS) for n in range(2))
+        hid = up(low, width)
+        ahead = up(high, width)
+        down(low, hid)
+        down(high, ahead)
+
     @pl.when(j < last)
     def _():
-        chunks = [pl.ds(r, ROWS) for r in range(0, tokens, ROWS)]
-        hid = up(chunks[0], wg_ref.shape[2])
-        for r, following in zip(chunks, chunks[1:] + [None], strict=True):
-            ahead = None if following is None else up(following, wg_ref.shape[2])
-            down(r, hid)
-            hid = ahead
+        looped(tokens // (2 * ROWS), 2 * ROWS, functools.partial(two, wg_ref.shape[2]))
 
     @pl.when(j == last)
     def _():
@@ -130,9 +132,13 @@
     return (dhid * u * (sig + act * (1 - sig))).astype(BF16), (dhid * act).astype(BF16), (act * u).astype(BF16)
 
 
-def chain_kernel(tail, a_ref, dy_ref, h_ref, wg_ref, wu_ref, wd_ref, dh_ref, acc_ref):
+def chain_kernel(tail, own, a_ref, dy_ref, h_ref, wg_ref, wu_ref, wd_ref, dh_ref, mine_ref, theirs_ref, acc_ref, stage_ref, sems):
     j, last = pl.program_id(0), pl.num_programs(0) - 1
     tokens = a_ref.shape[0]
+    me = lax.axis_index("dp")
+    holders = (me, me // 2 * 2 + 1 - me % 2)
+    blocks = own // BLOCK
+    extra = own - blocks * BLOCK
 
     @pl.when(j == 0)
     def _():
@@ -141,32 +147,62 @@
 
         looped(tokens // FEW, FEW, start, TOGETHER)
 
-    def there(r, width):
+    def written(step, half, do):
+        rows = pl.ds(pl.multiple_of(half * 2 * ROWS, 2 * ROWS), 2 * ROWS)
+        for n, (out, holder) in enumerate(zip((mine_ref, theirs_ref), holders, strict=True)):
+
+            def copy(here, there):
+                do(pltpu.make_async_copy(stage_ref.at[half, :, :, here], out.at[:, rows, there], sems.at[n, half]))
+
+            @pl.when((step < 4 * blocks) & (step // blocks == holder))
+            def _():
+                copy(pl.ds(0, BLOCK), pl.ds(pl.multiple_of(lax.rem(step, blocks) * BLOCK, BLOCK), BLOCK))
+
+            @pl.when(step == 4 * blocks)
+            def _():
+                copy(pl.ds(pl.multiple_of(holder * extra, LANES), extra), pl.ds(blocks * BLOCK, extra))
+
+            @pl.when(step == last)
+            def _():
+                copy(pl.ds(0, tail), pl.ds(own, tail))
+
+    def there(half, n, r, width):
         a, dy = a_ref[r, :], dy_ref[r, :]
         g = dot(a, wg_ref[0, :, :width], NN)
         u = dot(a, wu_ref[0, :, :width], NN)
-        dhid = dot(dy, wd_ref[0, :width, :], NT)
-        return hidden_back(g, u, dhid)[:2]
+        held = hidden_back(g, u, dot(dy, wd_ref[0, :width, :], NT))
+        for k in range(3):
+            stage_ref[half, k, n * ROWS : (n + 1) * ROWS, :width] = held[k]
+        return held[:2]
 
     def back(r, held):
         dg, du = held
         width = dg.shape[1]
         acc_ref[r, :] += dot(dg, wg_ref[0, :, :width], NT) + dot(du, wu_ref[0, :, :width], NT)
 
-    def two(width, r):
-        low, high = (pl.ds(pl.multiple_of(r.start + n * ROWS, ROWS), ROWS) for n in range(2))
-        held = there(low, width)
-        ahead = there(high, width)
-        back(low, held)
-        back(high, ahead)
+    def block(width):
+        def two(half, carry):
+            @pl.when(j > 0)
+            def _():
+                written(j - 1, half, lambda copy: copy.wait())
+
+            low, high = (pl.ds(pl.multiple_of((2 * half + n) * ROWS, ROWS), ROWS) for n in range(2))
+            held = there(half, 0, low, width)
+            ahead = there(half, 1, high, width)
+            back(low, held)
+            back(high, ahead)
+            written(j, half, lambda copy: copy.start())
+            return carry
+
+        lax.fori_loop(0, tokens // (2 * ROWS), two, 0)
 
     @pl.when(j < last)
     def _():
-        looped(tokens // (2 * ROWS), 2 * ROWS, functools.partial(two, wg_ref.shape[2]))
+        block(wg_ref.shape[2])
 
     @pl.when(j == last)
     def _():
-        looped(tokens // (2 * ROWS), 2 * ROWS, functools.partial(two, tail))
+        block(tail)
 
         def end(r):
             wide, da = h_ref[r, :].astype(F32), acc_ref[r, :].astype(BF16).astype(F32)
@@ -175,79 +211,110 @@
             dh_ref[r, :] = (dy_ref[r, :].astype(F32) + through.astype(BF16).astype(F32)).astype(BF16)
 
         looped(tokens // FEW, FEW, end, TOGETHER)
-
-
-def chain(a, dy, h, wg, wu, wd):
+        for half in range(tokens // (2 * ROWS)):
+            written(j, half, lambda copy: copy.wait())
+
+
+def chain(own, a, dy, h, wg, wu, wd):
     tokens, d = a.shape
     ff = wg.shape[2]
     steps = pl.cdiv(ff, BLOCK)
+    tail = ff - (steps - 1) * BLOCK
     full = once((tokens, d), lambda j: (0, 0))
     across = pl.BlockSpec((1, d, BLOCK), lambda j: (1, 0, j))
     down = pl.BlockSpec((1, BLOCK, d), lambda j: (1, j, 0))
+    kept = jax.ShapeDtypeStruct((3, tokens, own + tail), BF16)
     return pl.pallas_call(
-        lambda *refs: chain_kernel(ff - (steps - 1) * BLOCK, *refs),
+        lambda *refs: chain_kernel(tail, own, *refs),
         grid=(steps,),
         in_specs=[full, full, full, across, across, down],
-        out_specs=full,
-        out_shape=jax.ShapeDtypeStruct((tokens, d), BF16),
-        scratch_shapes=[pltpu.VMEM((tokens, d), F32)],
+        out_specs=[full] + [pl.BlockSpec(memory_space=pl.ANY)] * 2,
+        out_shape=[jax.ShapeDtypeStruct((tokens, d), BF16), kept, kept],
+        scratch_shapes=[
+            pltpu.VMEM((tokens, d), F32),
+            pltpu.VMEM((tokens // (2 * ROWS), 3, 2 * ROWS, BLOCK), BF16),
+            pltpu.SemaphoreType.DMA((2, tokens // (2 * ROWS))),
+        ],
         cost_estimate=pl.CostEstimate(flops=10 * tokens * d * ff, bytes_accessed=6 * d * ff, transcendentals=tokens * ff),
         compiler_params=params(),
         name="chain",
     )(a, dy, h, wg, wu, wd)
 
 
-def slices_kernel(layer, own, count, *refs):
+def slices_kernel(layer, own, kept, count, *refs):
     me = lax.axis_index("dp")
     chip, core = me // 2, me % 2
     partner = chip * 2 + 1 - core
     others = (partner, (1 - chip) * 2 + core, (1 - chip) * 2 + 1 - core)
-    (a_own, a_across), (dy_own, dy_across), (wg_hbm, wu_hbm, wd_hbm) = refs[:2], refs[2:4], refs[4:7]
     final = count is not None
-    before = refs[7:9] if final else ()
-    refs = refs[9 if final else 7 :]
-    outs, landed, scratch = refs[:8], refs[8:10], refs[10:]
-    a_refs = (a_own, landed[0].at[0], a_across, landed[0].at[1])
-    dy_refs = (dy_own, landed[1].at[0], dy_across, landed[1].at[1])
-    wg_ref, wu_ref, wd_ref, accg_ref, accu_ref, accd_ref, a_buf, dy_buf, sums_ref, sems, w_sems, send_sems, recv_sems, *terms = scratch
+
+    def take(n):
+        nonlocal refs
+        taken, refs = refs[:n], refs[n:]
+        return taken
+
+    a_own, a_across, dy_own, dy_across, wg_hbm, wu_hbm, wd_hbm = take(7)
+    mine, theirs = take(2) if kept else (None, None)
+    before = take(2) if final else ()
+    outs, (a_land, dy_land), held_land = take(8), take(2), take(1) if kept else ()
+    wg_ref, wu_ref, wd_ref, accg_ref, accu_ref, accd_ref, a_buf, dy_buf, sums_ref = take(9)
+    sems, w_sems, send_sems, recv_sems = take(4)
+    terms, held_buf = take(3), take(1)[0] if kept else None
+    a_refs = (a_own, a_across, a_land.at[0], a_land.at[1])
+    dy_refs = (dy_own, dy_across, dy_land.at[0], dy_land.at[1])
+    held_refs = (mine, None, held_land[0], None) if kept else (None,) * 4
     i, steps = pl.program_id(0), pl.num_programs(0)
-    each = a_refs[0].shape[0] // ROWS
+    each = a_own.shape[0] // ROWS
     width = wg_ref.shape[1]
+    main = own // BLOCK * BLOCK
 
     def fetch(step, do):
         slot, who = lax.rem(step, 2), step // each
         rows = pl.ds(pl.multiple_of(lax.rem(step, each) * ROWS, ROWS), ROWS)
-        for k, (a, dy) in enumerate(zip(a_refs, dy_refs, strict=True)):
+        for k, (a, dy, held) in enumerate(zip(a_refs, dy_refs, held_refs, strict=True)):
 
             @pl.when(who == k)
             def _():
                 do(pltpu.make_async_copy(a.at[rows, :], a_buf.at[slot], sems.at[0, slot]))
                 do(pltpu.make_async_copy(dy.at[rows, :], dy_buf.at[slot], sems.at[1, slot]))
+                if held is not None:
+                    do(pltpu.make_async_copy(held.at[:, rows, :], held_buf.at[slot], sems.at[2, slot]))
 
     def weights():
-        parts = ((pl.ds(pl.multiple_of(me * own, LANES), own), pl.ds(0, own)), (pl.ds(4 * own, width - own), pl.ds(own, width - own)))
+        extra = own - main
+        parts = (
+            (pl.ds(pl.multiple_of(me * main, LANES), main), pl.ds(0, main)),
+            (pl.ds(pl.multiple_of(4 * main + me * extra, LANES), extra), pl.ds(main, extra)),
+            (pl.ds(4 * own, width - own), pl.ds(own, width - own)),
+        )
         return [
             pltpu.make_async_copy(*((hbm.at[layer, there, :], ref.at[here, :]) if n == 2 else (hbm.at[layer, :, there], ref.at[:, here])), w_sems.at[n, m])
             for n, (hbm, ref) in enumerate(((wg_hbm, wg_ref), (wu_hbm, wu_ref), (wd_hbm, wd_ref)))
             for m, (there, here) in enumerate(parts)
         ]
 
-    def onward(which, n):
-        return pltpu.make_async_remote_copy(
-            src_ref=(a_refs, dy_refs)[n][2 * which],
-            dst_ref=landed[n].at[which],
-            send_sem=send_sems.at[2 * which + n],
-            recv_sem=recv_sems.at[2 * which + n],
-            device_id={"dp": partner},
-            device_id_type=pl.DeviceIdType.MESH,
-        )
+    def onward(which):
+        pairs = [(a_refs[which], a_land.at[which]), (dy_refs[which], dy_land.at[which])]
+        if kept and which == 0:
+            pairs.append((theirs, held_land[0]))
+        return [
+            pltpu.make_async_remote_copy(
+                src_ref=src,
+                dst_ref=dst,
+                send_sem=send_sems.at[3 * which + n],
+                recv_sem=recv_sems.at[3 * which + n],
+                device_id={"dp": partner},
+                device_id_type=pl.DeviceIdType.MESH,
+            )
+            for n, (src, dst) in enumerate(pairs)
+        ]
 
     def told(n):
         return pltpu.make_async_remote_copy(
             src_ref=sums_ref.at[0],
             dst_ref=sums_ref.at[1 + n],
-            send_sem=send_sems.at[4 + n],
-            recv_sem=recv_sems.at[4 + n],
+            send_sem=send_sems.at[6 + n],
+            recv_sem=recv_sems.at[6 + n],
             device_id={"dp": others[n]},
             device_id_type=pl.DeviceIdType.MESH,
         )
@@ -269,43 +336,57 @@
     def _():
         pl.semaphore_wait(barrier, len(spoken))
         for which in range(2):
-            for n in range(2):
-                onward(which, n).start()
+            for copy in onward(which):
+                copy.start()
 
     for which in range(2):
 
-        @pl.when(i == (2 * which + 1) * each - 1)
+        @pl.when(i == (2 + which) * each - 1)
         def _():
-            for n in range(2):
-                onward(which, n).wait()
+            for copy in onward(which):
+                copy.wait()
 
     @pl.when(i + 1 < steps)
     def _():
         fetch(i + 1, lambda copy: copy.start())
 
     slot = lax.rem(i, 2)
-    pltpu.make_async_copy(a_refs[0].at[pl.ds(0, ROWS), :], a_buf.at[slot], sems.at[0, slot]).wait()
-    pltpu.make_async_copy(dy_refs[0].at[pl.ds(0, ROWS), :], dy_buf.at[slot], sems.at[1, slot]).wait()
-    a, dy = a_buf[slot], dy_buf[slot]
-    a_t, dy_t = a.T, dy.T
+    pltpu.make_async_copy(a_own.at[pl.ds(0, ROWS), :], a_buf.at[slot], sems.at[0, slot]).wait()
+    pltpu.make_async_copy(dy_own.at[pl.ds(0, ROWS), :], dy_buf.at[slot], sems.at[1, slot]).wait()
     blocks = [pl.ds(c, min(BLOCK, width - c)) for c in range(0, width, BLOCK)]
-    held = {}
-
-    def there(c):
-        s = blocks[c]
-        held[c] = hidden_back(dot(a, wg_ref[:, s], NN), dot(a, wu_ref[:, s], NN), dot(dy, wd_ref[s, :], NT))
-
-    def back(c):
-        s = blocks[c]
-        dg, du, hid = held.pop(c)
-        for acc, left, right in ((accg_ref, a_t, dg), (accu_ref, a_t, du), (accd_ref, dy_t, hid)):
-            acc[:, s] = jnp.where(i == 0, 0.0, acc[:, s]) + dot(left, right, NN)
-
-    there(0)
-    for c in range(1, len(blocks)):
-        there(c)
-        back(c - 1)
-    back(len(blocks) - 1)
+
+    def through(there, first):
+        a_t, dy_t = a_buf[slot].T, dy_buf[slot].T
+
+        def back(s, held):
+            dg, du, hid = held
+            for acc, left, right in ((accg_ref, a_t, dg), (accu_ref, a_t, du), (accd_ref, dy_t, hid)):
+                acc[:, s] = (jnp.where(i == 0, 0.0, acc[:, s]) if first else acc[:, s]) + dot(left, right, NN)
+
+        held = there(blocks[0])
+        for s, following in zip(blocks, blocks[1:] + [None], strict=True):
+            ahead = None if following is None else there(following)
+            back(s, held)
+            held = ahead
+
+    def anew(s):
+        a, dy = a_buf[slot], dy_buf[slot]
+        return hidden_back(dot(a, wg_ref[:, s], NN), dot(a, wu_ref[:, s], NN), dot(dy, wd_ref[s, :], NT))
+
+    if kept:
+        known = lax.rem(i // each, 2) == 0
+
+        @pl.when(known)
+        def _():
+            pltpu.make_async_copy(mine.at[:, pl.ds(0, ROWS), :], held_buf.at[slot], sems.at[2, slot]).wait()
+            through(lambda s: [held_buf[slot, n, :, s] for n in range(3)], True)
+
+        @pl.when(jnp.logical_not(known))
+        def _():
+            through(anew, False)
+
+    else:
+        through(anew, True)
 
     rest = pl.ds(own, width - own)
 
@@ -335,12 +416,13 @@
 
         def turn(c, carry):
             at = pl.ds(pl.multiple_of(c * LANES, LANES), LANES)
-            for r in range(0, a.shape[1], LANES):
+            for r in range(0, a_buf.shape[2], LANES):
                 outs[2][at, r : r + LANES] = accd_ref[r : r + LANES, at].astype(BF16).T
             return carry
 
-        at = [(core + s) % 2 + 2 * ((chip + s // 2) % 2) for s in range(4)]
-        sums = [lax.fori_loop(0, a.shape[1] // LANES, rows, jnp.zeros((8, LANES), F32)), jnp.zeros((8, LANES), F32)]
+        at = [(chip + s // 2) % 2 + 2 * ((core + s) % 2) for s in range(4)]
+        place = [(core + s) % 2 + 2 * ((chip + s // 2) % 2) for s in range(4)]
+        sums = [lax.fori_loop(0, a_buf.shape[2] // LANES, rows, jnp.zeros((8, LANES), F32)), jnp.zeros((8, LANES), F32)]
         lax.fori_loop(0, own // LANES, turn, 0)
         for n, term in enumerate(terms):
             part, sums[1] = rounded(term[at[0]] + term[at[1]] + term[at[2]] + term[at[3]], sums[1])
@@ -354,13 +436,13 @@
                 told(n).start()
             for n in range(3):
                 told(n).wait()
-            total = sums_ref[at[0]] + sums_ref[at[1]] + sums_ref[at[2]] + sums_ref[at[3]]
+            total = sums_ref[place[0]] + sums_ref[place[1]] + sums_ref[place[2]] + sums_ref[place[3]]
             total = jnp.full((8, LANES), jnp.sum(total) + shared, F32)
             outs[6][...] = jnp.minimum(1.0, 0.5 * lax.rsqrt(total / count + 1e-30))
             outs[7][...] = jnp.zeros((8, LANES), F32)
 
 
-def slices(layer, own, a_all, dy_all, wg, wu, wd, before=None, count=None):
+def slices(layer, own, a_all, dy_all, wg, wu, wd, kept=(), before=(), count=None):
     tokens, d = a_all[0].shape
     ff = wg.shape[2]
     rest = ff - 4 * own
@@ -368,26 +450,29 @@
     any_ = pl.BlockSpec(memory_space=pl.ANY)
     at = lambda s: once(s, lambda i: (0, 0))
     sizes = [(d, own), (d, own), (own, d), (d, rest), (d, rest), (rest, d)]
+    landed = [(2, tokens, d)] * 2 + ([(3, tokens, width)] if kept else [])
     return pl.pallas_call(
-        lambda *refs: slices_kernel(layer, own, count, *refs),
+        lambda *refs: slices_kernel(layer, own, bool(kept), count, *refs),
         grid=(4 * tokens // ROWS,),
-        in_specs=[any_] * 7 + [at((8, LANES))] * len(before or ()),
-        out_specs=[at(s) for s in sizes] + [at((8, LANES))] * 2 + [any_] * 2,
+        in_specs=[any_] * (7 + len(kept)) + [at((8, LANES))] * len(before),
+        out_specs=[at(s) for s in sizes] + [at((8, LANES))] * 2 + [any_] * len(landed),
         scratch_shapes=[pltpu.VMEM((d, width), BF16)] * 2
         + [pltpu.VMEM((width, d), BF16)]
         + [pltpu.VMEM((d, width), F32)] * 3
         + [pltpu.VMEM((2, ROWS, d), BF16)] * 2
         + [pltpu.VMEM((4, 8, LANES), F32)]
-        + [pltpu.SemaphoreType.DMA(n) for n in ((2, 2), (3, 2), (7,), (7,))]
-        + [pltpu.VMEM((4, d, rest), F32)] * 3,
-        out_shape=[jax.ShapeDtypeStruct(s, BF16) for s in sizes] + [jax.ShapeDtypeStruct((8, LANES), F32)] * 2
-        + [jax.ShapeDtypeStruct((2, tokens, d), BF16)] * 2,
+        + [pltpu.SemaphoreType.DMA(n) for n in ((3, 2), (3, 3), (9,), (9,))]
+        + [pltpu.VMEM((4, d, rest), F32)] * 3
+        + ([pltpu.VMEM((2, 3, ROWS, width), BF16)] if kept else []),
+        out_shape=[jax.ShapeDtypeStruct(s, BF16) for s in sizes]
+        + [jax.ShapeDtypeStruct((8, LANES), F32)] * 2
+        + [jax.ShapeDtypeStruct(s, BF16) for s in landed],
         cost_estimate=pl.CostEstimate(
             flops=12 * 4 * tokens * d * width, bytes_accessed=16 * tokens * d, transcendentals=4 * tokens * width
         ),
         compiler_params=pltpu.CompilerParams(vmem_limit_bytes=62 << 20, collective_id=layer, has_side_effects=True),
         name="slices",
-    )(*a_all, *dy_all, wg, wu, wd, *(before or ()))
+    )(*a_all, *dy_all, wg, wu, wd, *kept, *before)
 
 
 def adam_math(f, w, m, v, g):
@@ -402,12 +487,19 @@
 
 def adam(own, factor, arrays, pieces, outs):
     d, _ = arrays[0][0].shape[1:]
+    main, extra = own // BLOCK * BLOCK, own % BLOCK
     shapes = ((LANES, own), (LANES, d), (d, LANES))
     rows = []
     for n, (which, layer, slot, g) in enumerate(pieces):
         kind = 1 if which == 2 else 2 if slot == 4 else 0
         for r in range(0, g.shape[0], shapes[kind][0]):
-            rows.append((kind, which, layer, n, slot, r, *((own, 0) if which == 2 else (0, own))))
+            if kind != 1:
+                first = (r, 0)
+            elif slot == 4:
+                first = (4 * own + r, 0)
+            else:
+                first = (r, main) if r < main else (4 * main + r - main, extra)
+            rows.append((kind, which, layer, n, slot, r, *first))
     table = np.array(rows, np.int32).T
     total = len(rows)
     kinds = sorted({row[0] for row in rows})
@@ -422,25 +514,33 @@
         f = f_ref[:1, :1]
         me = lax.axis_index("dp")
 
-        def place(step):
+        def moved(step, do):
             kind, which, layer = (table_ref[n, step] for n in range(3))
             slot = table_ref[4, step]
-            unit = jnp.where(slot < 4, (me + slot) % 2 + 2 * ((me // 2 + slot // 2) % 2), slot)
-            row, col = table_ref[5, step] + table_ref[6, step] * unit, table_ref[7, step] * unit
-            return kind, which, lambda shape: (layer, pl.ds(pl.multiple_of(row, 16), shape[0]), pl.ds(pl.multiple_of(col, LANES), shape[1]))
+            unit = (me + slot) % 2 + 2 * ((me // 2 + slot // 2) % 2)
+            row = table_ref[6, step] + table_ref[7, step] * unit
+            for k in range(3):
+                for q in [q for q in kinds if (q == 1) == (k == 2)]:
+                    if q == 0:
+                        columns = ((unit * main, 0, main), (4 * main + unit * extra, main, extra))
+                    else:
+                        columns = ((0 if q == 1 else 4 * own, 0, shapes[q][1]),)
+
+                    @pl.when((which == k) & (kind == q))
+                    def _():
+                        for first, here, size in columns:
+                            first = first if isinstance(first, int) else pl.multiple_of(first, LANES)
+                            there = (layer, pl.ds(pl.multiple_of(row, LANES), shapes[q][0]), pl.ds(first, size))
+                            do(3 * k, there, buffers[q], (lax.rem(step, SLOTS), slice(None), pl.ds(here, size)))
 
         def fetch(step):
             slot = lax.rem(step, SLOTS)
-            kind, which, at = place(step)
-            for k in range(3):
-                its = [q for q in kinds if (q == 1) == (k == 2)]
-                for q in its:
-
-                    @pl.when((which == k) & (kind == q))
-                    def _():
-                        for n in range(3):
-                            pltpu.make_async_copy(weights[3 * k + n].at[at(shapes[q])], buffers[q][n].at[slot], sem_in.at[n, slot]).start()
-
+
+            def get(k, there, buffer, here):
+                for n in range(3):
+                    pltpu.make_async_copy(weights[k + n].at[there], buffer[n].at[here], sem_in.at[n, slot]).start()
+
+            moved(step, get)
             piece, row = table_ref[3, step], table_ref[5, step]
             for n, (which_, _, slot_, _) in enumerate(pieces):
                 q = 1 if which_ == 2 else 2 if slot_ == 4 else 0
@@ -452,17 +552,18 @@
 
         def stored(step, do):
             slot = lax.rem(step, SLOTS)
-            kind, which, at = place(step)
-            for k in range(3):
-                for q in [q for q in kinds if (q == 1) == (k == 2)]:
-
-                    @pl.when((which == k) & (kind == q))
-                    def _():
-                        for n in range(3):
-                            do(pltpu.make_async_copy(buffers[q][n].at[slot], results[3 * k + n].at[at(shapes[q])], sem_out.at[n, slot]))
-
-        for step in range(min(AHEAD, total)):
-            fetch(jnp.int32(step))
+
+            def put(k, there, buffer, here):
+                for n in range(3):
+                    do(pltpu.make_async_copy(buffer[n].at[here], results[k + n].at[there], sem_out.at[n, slot]))
+
+            moved(step, put)
+
+        def early(step, carry):
+            fetch(step)
+            return carry
+
+        lax.fori_loop(0, min(AHEAD, total), early, 0)
 
         def body(step, carry):
             @pl.when(step + AHEAD < total)
@@ -479,9 +580,8 @@
                 @pl.when(table_ref[0, step] == q)
                 def _():
                     w, m, v, g = buffers[q]
-                    for n in range(3):
-                        pltpu.make_async_copy(weights[n].at[0, pl.ds(0, shapes[q][0]), pl.ds(0, shapes[q][1])], buffers[q][n].at[slot], sem_in.at[n, slot]).wait()
-                    pltpu.make_async_copy(buffers[q][3].at[slot], buffers[q][3].at[slot], sem_in.at[3, slot]).wait()
+                    for n in range(4):
+                        pltpu.make_async_copy(buffers[q][n].at[slot], buffers[q][n].at[slot], sem_in.at[n, slot]).wait()
                     some = 32 if shapes[q][1] > LANES else 224
 
                     def part(r, carry):
@@ -496,8 +596,12 @@
             return carry
 
         lax.fori_loop(0, total, body, 0)
-        for step in range(max(0, total - SLOTS), total):
-            stored(jnp.int32(step), lambda copy: copy.wait())
+
+        def late(step, carry):
+            stored(step, lambda copy: copy.wait())
+            return carry
+
+        lax.fori_loop(max(0, total - SLOTS), total, late, 0)
 
     any_ = pl.BlockSpec(memory_space=pl.ANY)
     given = [a for three in arrays for a in three]
@@ -530,12 +634,12 @@
         h1, a1, a0 = forward(x, wg, wu, wd)
         a1_x = send(a1, px)
         a0_x = send(a0, px)
-        dh1 = chain(a1, dy, h1, wg, wu, wd)
+        dh1, *kept = chain(own, a1, dy, h1, wg, wu, wd)
         dh1_x = send(dh1, px)
-        top = slices(1, own, [a1, a1_x], [dy, dy_x], wg, wu, wd)
+        top = slices(1, own, [a1, a1_x], [dy, dy_x], wg, wu, wd, kept)
         top_x = [send(top[n], px) for n in range(3)]
         top_d = [send(top[n], pd) for n in range(3)]
-        low = slices(0, own, [a0, a0_x], [dh1, dh1_x], wg, wu, wd, top[6:8], wg.size + wu.size + wd.size)
+        low = slices(0, own, [a0, a0_x], [dh1, dh1_x], wg, wu, wd, (), top[6:8], wg.size + wu.size + wd.size)
         low_x = [send(low[n], px) for n in range(3)]
         low_d = [send(low[n], pd) for n in range(3)]
 

time: 784 us -> 786 us (level)
  waiting for transfers between devices: 94.1 us -> 122 us
  Pallas kernels: 670 us -> 644 us
    ppermute x10, waiting for transfers between devices: 88 us -> 116 us  [px(): return lax.ppermute(a, 'dp', PX)]
    pallas_call x3, Pallas kernels: 403 us -> 375 us  [the longest x2 252 us: slices(): pl.pallas_call(lambda *refs: slices_kernel(layer, own, bool(kept), count,...]
  transfers between devices with their start and end apart: 22 -> 22, of which waited for: 7 -> 7; matrix products, arithmetic and copies ran while one was open for 0% -> 0% of each run, Pallas kernels for 75% -> 71%
where the time goes in v9:
time: 786 us
  Pallas kernels  644 us (82%)
  waiting for transfers between devices  122 us (16%)
  starting transfers between devices  18.5 us (2%)
    pallas_call x2, Pallas kernels, slices(): pl.pallas_call(lambda *refs: slices_kernel(layer, own, bool(kept), count,...  252 us
    pallas_call x4, Pallas kernels, adam(): pl.pallas_call(kernel, in_specs=[pl.BlockSpec(memory_space=pltpu.SMEM), p...  191 us
    pallas_call x1, Pallas kernels, chain(): pl.pallas_call(lambda *refs: chain_kernel(tail, own, *refs), grid=(steps,...  123 us
    ppermute x10, waiting for transfers between devices, px(): return lax.ppermute(a, 'dp', PX)  116 us
    pallas_call x1, Pallas kernels, forward(): pl.pallas_call(lambda *refs: forward_kernel(ff - (steps - 1) * BLOCK, *re...  78 us
    ppermute x10, starting transfers between devices, px(): return lax.ppermute(a, 'dp', PX)  15.8 us
  transfers between devices with their start and end apart: 22, of which 7 were waited for; matrix products, arithmetic and copies ran while one was open for 0% of the time, Pallas kernels for 71%

profile of v9, /device:TPU:0, one launch (start us, length us, event | category | flops | bytes accessed | tf_op | source)
XLA Modules:
  0.0 785.8 jit_solution(7573741324240135368)
XLA Ops:
  0.6 78.0 %forward.1 = (bf16[2048,896]{1,0:T(8,128)(2,1)}, bf16[2048,896]{1,0:T(8,128)(2,1)}, bf16[2048,896]{1,0:T(8,128)(2,1)}) custom-call(bf16[2048,896]{1,0:T(8,128)(2,1)} %bitcast.2, bf16[2,896,4736]{2,1,0:T(8,128)(2,1)} %refs_0_.7, bf16[2,896,4736]{2,1,0:T(8,128)(2,1)} %refs_3_.11, bf16[2,4736,896]{2,1,0:T(8,128)(2,1)} %refs_6_.11), custom_call_target="tpu_custom_call" | custom-call | flops 52143587328 | bytes 25460736 | tf_op jit(solution)/shard_map/forward/pallas_call | solution.py:115
  78.7 3.3 collective-permute-start.2
  82.0 123.2 %chain.1 = (bf16[2048,896]{1,0:T(8,128)(2,1)}, bf16[3,2048,1280]{2,1,0:T(8,128)(2,1)}, bf16[3,2048,1280]{2,1,0:T(8,128)(2,1)}) custom-call(bf16[2048,896]{1,0:T(8,128)(2,1)} %get-tuple-element.77.refs_0_, bf16[2048,896]{1,0:T(8,128)(2,1)} %bitcast.4, bf16[2048,896]{1,0:T(8,128)(2,1)} %get-tuple-element.78.refs_2_, bf16[2,896,4736]{2,1,0:T(8,128)(2,1)} %refs_0_.7, ...), custom_call_target="tpu_custom_call" | custom-call | flops 86905978880 | bytes 25460736 | tf_op jit(solution)/shard_map/chain/pallas_call | solution.py:227
  205.2 2.0 collective-permute-start.1
  207.2 33.9 %collective-permute-done.3.refs_3_ = bf16[2048,896]{1,0:T(8,128)(2,1)} collective-permute-done((bf16[2048,896]{1,0:T(8,128)(2,1)}, bf16[2048,896]{1,0:T(8,128)(2,1)}, u32[]{:S(2)}, u32[]{:S(2)}) %collective-permute-start.3) | collective-permute-done | bytes 3670048 | tf_op jit(solution)/shard_map/ppermute | solution.py:31
  241.1 108.4 %slices.2 = (bf16[896,1152]{1,0:T(8,128)(2,1)}, bf16[896,1152]{1,0:T(8,128)(2,1)}, bf16[1152,896]{1,0:T(8,128)(2,1)}, bf16[896,128]{1,0:T(8,128)(2,1)}, bf16[896...) custom-call(bf16[2048,896]{1,0:T(8,128)(2,1)} %get-tuple-element.77., ...), custom_call_target="tpu_custom_call" | custom-call | flops 112742891520 | bytes 29360128 | tf_op jit(solution)/shard_map/slices/pallas_call | solution.py:454
  349.6 2.0 collective-permute-start.4
  351.6 0.1 collective-permute-start.6
  351.7 0.4 collective-permute-start.14
  352.1 46.3 %collective-permute-done.refs_1_ = bf16[2048,896]{1,0:T(8,128)(2,1)} collective-permute-done((bf16[2048,896]{1,0:T(8,128)(2,1)}, bf16[2048,896]{1,0:T(8,128)(2,1)}, u32[]{:S(2)}, u32[]{:S(2)}) %collective-permute-start) | collective-permute-done | bytes 3670048 | tf_op jit(solution)/shard_map/ppermute | solution.py:31
  398.4 2.0 collective-permute-start.8
  400.4 143.7 %slices.3 = (bf16[896,1152]{1,0:T(8,128)(2,1)}, bf16[896,1152]{1,0:T(8,128)(2,1)}, bf16[1152,896]{1,0:T(8,128)(2,1)}, bf16[896,128]{1,0:T(8,128)(2,1)}, bf16[896...) custom-call(bf16[2048,896]{1,0:T(8,128)(2,1)} %get-tuple-element.76., ...), custom_call_target="tpu_custom_call" | custom-call | flops 112742891520 | bytes 29360128 | tf_op jit(solution)/shard_map/slices/pallas_call | solution.py:454
  544.2 0.1 collective-permute-start.15
  544.3 0.4 collective-permute-start.10
  544.7 0.1 collective-permute-start.11
  544.8 0.4 collective-permute-start.12
  545.2 2.1 collective-permute-start.18
  547.3 1.3 collective-permute-done.15.refs_14_
  548.7 2.1 collective-permute-start.16
  550.7 0.9 collective-permute-done.10.refs_12_
  551.6 2.1 collective-permute-start.19
  553.7 0.9 collective-permute-done.11.refs_13_
  554.6 0.1 collective-permute-start.5
  554.7 2.8 collective-permute-done.12.refs_14_
  557.5 0.1 collective-permute-start.7
  557.7 35.8 %collective-permute-done.18.refs_9_ = bf16[896,1152]{1,0:T(8,128)(2,1)} collective-permute-done((bf16[896,1152]{1,0:T(8,128)(2,1)}, bf16[896,1152]{1,0:T(8,128)(2,1)}, u32[]{:S(2)}, u32[]{:S(2)}) %collective-permute-start.18) | collective-permute-done | bytes 2064416 | tf_op jit(solution)/shard_map/ppermute | solution.py:31
  593.4 95.1 %shard_map.214 = (bf16[2,896,4736]{2,1,0:T(8,128)(2,1)}, f32[2,896,4736]{2,1,0:T(8,128)}, f32[2,896,4736]{2,1,0:T(8,128)}, bf16[2,896,4736]{2,1,0:T(8,128)(2,1)}...) custom-call(s32[8,98]{1,0:T(8,128)} %constant.8.clone.table_ref, ...), custom_call_target="tpu_custom_call" | custom-call | flops 26148864000 | bytes 287637504 | tf_op jit(solution)/shard_map/pallas_call | solution.py:610
  688.6 0.5 collective-permute-start.20
  689.1 46.8 %shard_map.215 = (bf16[2,896,4736]{2,1,0:T(8,128)(2,1)}, f32[2,896,4736]{2,1,0:T(8,128)}, f32[2,896,4736]{2,1,0:T(8,128)}, bf16[2,896,4736]{2,1,0:T(8,128)(2,1)}...) custom-call(s32[8,46]{1,0:T(8,128)} %constant.9.clone.table_ref, ...), custom_call_target="tpu_custom_call", output_to_operand_aliasing={{0}: (17, {}), {1}: (18, {}), {2}: (19, {}), {3}: (20, {}),... | custom-call | flops 12386304000 | bytes 136249344 | tf_op jit(solution)/shard_map/pallas_call | solution.py:610
  735.9 0.4 collective-permute-start.17
  736.4 39.5 %shard_map.216 = (bf16[2,896,4736]{2,1,0:T(8,128)(2,1)}, f32[2,896,4736]{2,1,0:T(8,128)}, f32[2,896,4736]{2,1,0:T(8,128)}, bf16[2,896,4736]{2,1,0:T(8,128)(2,1)}...) custom-call(s32[8,37]{1,0:T(8,128)} %constant.10.clone.table_ref, ...), custom_call_target="tpu_custom_call", output_to_operand_aliasing={{0}: (16, {}), {1}: (17, {}), {2}: (18, {}), {3}: (19, {}),... | custom-call | flops 10321920000 | bytes 113541120 | tf_op jit(solution)/shard_map/pallas_call | solution.py:610
  775.9 9.8 %shard_map.217 = (bf16[2,896,4736]{2,1,0:T(8,128)(2,1)}, f32[2,896,4736]{2,1,0:T(8,128)}, f32[2,896,4736]{2,1,0:T(8,128)}, bf16[2,896,4736]{2,1,0:T(8,128)(2,1)}...) custom-call(s32[8,9]{1,0:T(8,128)} %constant.11.clone.table_ref, ...), custom_call_target="tpu_custom_call", output_to_operand_aliasing={{0}: (12, {}), {1}: (13, {}), {2}: (14, {}), {3}: (15, {}),... | custom-call | flops 2064384000 | bytes 22708224 | tf_op jit(solution)/shard_map/pallas_call | solution.py:610
  (20 shorter events, 0.1 us)
Async XLA Ops:
  78.7 128.6 %collective-permute-start.2 = (bf16[2048,896]{1,0:T(8,128)(2,1)}, bf16[2048,896]{1,0:T(8,128)(2,1)}, u32[]{:S(2)}, u32[]{:S(2)}) collective-permute-start(bf16[2048,896]{1,0:T(8,128)(2,1)} %get-tuple-element.77.refs_0_), channel_id=1, source_target_pairs={{0,2},{2,0},{1,3},{3,1},{4,6},{6,4},{5,7},{7,5}} | collective-permute-start | bytes 11010056 | tf_op jit(solution)/shard_map/ppermute | solution.py:31
  82.0 159.1 %collective-permute-start.3 = (bf16[2048,896]{1,0:T(8,128)(2,1)}, bf16[2048,896]{1,0:T(8,128)(2,1)}, u32[]{:S(2)}, u32[]{:S(2)}) collective-permute-start(bf16[2048,896]{1,0:T(8,128)(2,1)} %bitcast.3), channel_id=1, source_target_pairs={{0,2},{2,0},{1,3},{3,1},{4,6},{6,4},{5,7},{7,5}} | collective-permute-start | bytes 11010056 | tf_op jit(solution)/shard_map/ppermute | solution.py:31
  205.2 146.5 %collective-permute-start.1 = (bf16[2048,896]{1,0:T(8,128)(2,1)}, bf16[2048,896]{1,0:T(8,128)(2,1)}, u32[]{:S(2)}, u32[]{:S(2)}) collective-permute-start(bf16[2048,896]{1,0:T(8,128)(2,1)} %get-tuple-element.79.refs_2_), channel_id=1, source_target_pairs={{0,2},{2,0},{1,3},{3,1},{4,6},{6,4},{5,7},{7,5}} | collective-permute-start | bytes 11010056 | tf_op jit(solution)/shard_map/ppermute | solution.py:31
  207.2 191.2 %collective-permute-start = (bf16[2048,896]{1,0:T(8,128)(2,1)}, bf16[2048,896]{1,0:T(8,128)(2,1)}, u32[]{:S(2)}, u32[]{:S(2)}) collective-permute-start(bf16[2048,896]{1,0:T(8,128)(2,1)} %get-tuple-element.76.refs_0_), channel_id=1, source_target_pairs={{0,2},{2,0},{1,3},{3,1},{4,6},{6,4},{5,7},{7,5}} | collective-permute-start | bytes 11010056 | tf_op jit(solution)/shard_map/ppermute | solution.py:31
  349.6 194.6 %collective-permute-start.4 = (bf16[896,1152]{1,0:T(8,128)(2,1)}, bf16[896,1152]{1,0:T(8,128)(2,1)}, u32[]{:S(2)}, u32[]{:S(2)}) collective-permute-start(bf16[896,1152]{1,0:T(8,128)(2,1)} %get-tuple-element.85.refs_9_), channel_id=1, source_target_pairs={{0,2},{2,0},{1,3},{3,1},{4,6},{6,4},{5,7},{7,5}} | collective-permute-start | bytes 6193160 | tf_op jit(solution)/shard_map/ppermute | solution.py:31
  351.6 193.2 %collective-permute-start.13 = (bf16[896,1152]{1,0:T(8,128)(2,1)}, bf16[896,1152]{1,0:T(8,128)(2,1)}, u32[]{:S(2)}, u32[]{:S(2)}) collective-permute-start(bf16[896,1152]{1,0:T(8,128)(2,1)} %get-tuple-element.85.refs_9_), channel_id=1, source_target_pairs={{0,1},{1,0},{2,3},{3,2},{4,5},{5,4},{6,7},{7,6}} | collective-permute-start | bytes 6193160 | tf_op jit(solution)/shard_map/ppermute | solution.py:35
  351.6 192.7 %collective-permute-start.6 = (bf16[896,1152]{1,0:T(8,128)(2,1)}, bf16[896,1152]{1,0:T(8,128)(2,1)}, u32[]{:S(2)}, u32[]{:S(2)}) collective-permute-start(bf16[896,1152]{1,0:T(8,128)(2,1)} %get-tuple-element.86.refs_10_), channel_id=1, source_target_pairs={{0,2},{2,0},{1,3},{3,1},{4,6},{6,4},{5,7},{7,5}} | collective-permute-start | bytes 6193160 | tf_op jit(solution)/shard_map/ppermute | solution.py:31
  351.7 193.6 %collective-permute-start.14 = (bf16[896,1152]{1,0:T(8,128)(2,1)}, bf16[896,1152]{1,0:T(8,128)(2,1)}, u32[]{:S(2)}, u32[]{:S(2)}) collective-permute-start(bf16[896,1152]{1,0:T(8,128)(2,1)} %get-tuple-element.86.refs_10_), channel_id=1, source_target_pairs={{0,1},{1,0},{2,3},{3,2},{4,5},{5,4},{6,7},{7,6}} | collective-permute-start | bytes 6193160 | tf_op jit(solution)/shard_map/ppermute | solution.py:35
  398.4 146.3 %collective-permute-start.8 = (bf16[1152,896]{1,0:T(8,128)(2,1)}, bf16[1152,896]{1,0:T(8,128)(2,1)}, u32[]{:S(2)}, u32[]{:S(2)}) collective-permute-start(bf16[1152,896]{1,0:T(8,128)(2,1)} %get-tuple-element.87.refs_11_), channel_id=1, source_target_pairs={{0,2},{2,0},{1,3},{3,1},{4,6},{6,4},{5,7},{7,5}} | collective-permute-start | bytes 6193160 | tf_op jit(solution)/shard_map/ppermute | solution.py:31
  544.2 4.5 collective-permute-start.15
  544.3 7.3 collective-permute-start.10
  544.7 9.8 %collective-permute-start.11 = (bf16[896,1152]{1,0:T(8,128)(2,1)}, bf16[896,1152]{1,0:T(8,128)(2,1)}, u32[]{:S(2)}, u32[]{:S(2)}) collective-permute-start(bf16[896,1152]{1,0:T(8,128)(2,1)} %get-tuple-element.89.refs_19_), channel_id=1, source_target_pairs={{0,1},{1,0},{2,3},{3,2},{4,5},{5,4},{6,7},{7,6}} | collective-permute-start | bytes 6193160 | tf_op jit(solution)/shard_map/ppermute | solution.py:35
  544.8 12.7 %collective-permute-start.12 = (bf16[1152,896]{1,0:T(8,128)(2,1)}, bf16[1152,896]{1,0:T(8,128)(2,1)}, u32[]{:S(2)}, u32[]{:S(2)}) collective-permute-start(bf16[1152,896]{1,0:T(8,128)(2,1)} %get-tuple-element.90.refs_20_), channel_id=1, source_target_pairs={{0,1},{1,0},{2,3},{3,2},{4,5},{5,4},{6,7},{7,6}} | collective-permute-start | bytes 6193160 | tf_op jit(solution)/shard_map/ppermute | solution.py:35
  545.2 48.2 %collective-permute-start.18 = (bf16[896,1152]{1,0:T(8,128)(2,1)}, bf16[896,1152]{1,0:T(8,128)(2,1)}, u32[]{:S(2)}, u32[]{:S(2)}) collective-permute-start(bf16[896,1152]{1,0:T(8,128)(2,1)} %get-tuple-element.88.refs_18_), channel_id=1, source_target_pairs={{0,2},{2,0},{1,3},{3,1},{4,6},{6,4},{5,7},{7,5}} | collective-permute-start | bytes 6193160 | tf_op jit(solution)/shard_map/ppermute | solution.py:31
  548.7 187.3 %collective-permute-start.16 = (bf16[1152,896]{1,0:T(8,128)(2,1)}, bf16[1152,896]{1,0:T(8,128)(2,1)}, u32[]{:S(2)}, u32[]{:S(2)}) collective-permute-start(bf16[1152,896]{1,0:T(8,128)(2,1)} %get-tuple-element.90.refs_20_), channel_id=1, source_target_pairs={{0,2},{2,0},{1,3},{3,1},{4,6},{6,4},{5,7},{7,5}} | collective-permute-start | bytes 6193160 | tf_op jit(solution)/shard_map/ppermute | solution.py:31
  551.6 136.9 %collective-permute-start.19 = (bf16[896,1152]{1,0:T(8,128)(2,1)}, bf16[896,1152]{1,0:T(8,128)(2,1)}, u32[]{:S(2)}, u32[]{:S(2)}) collective-permute-start(bf16[896,1152]{1,0:T(8,128)(2,1)} %get-tuple-element.89.refs_19_), channel_id=1, source_target_pairs={{0,2},{2,0},{1,3},{3,1},{4,6},{6,4},{5,7},{7,5}} | collective-permute-start | bytes 6193160 | tf_op jit(solution)/shard_map/ppermute | solution.py:31
  554.6 134.5 %collective-permute-start.5 = (bf16[896,1152]{1,0:T(8,128)(2,1)}, bf16[896,1152]{1,0:T(8,128)(2,1)}, u32[]{:S(2)}, u32[]{:S(2)}) collective-permute-start(bf16[896,1152]{1,0:T(8,128)(2,1)} %collective-permute-done.4.refs_15_), channel_id=1, source_target_pairs={{0,1},{1,0},{2,3},{3,2},{4,5},{5,4},{6,7},{7,6}} | collective-permute-start | bytes 6193160 | tf_op jit(solution)/shard_map/ppermute | solution.py:35
  557.5 131.6 %collective-permute-start.7 = (bf16[896,1152]{1,0:T(8,128)(2,1)}, bf16[896,1152]{1,0:T(8,128)(2,1)}, u32[]{:S(2)}, u32[]{:S(2)}) collective-permute-start(bf16[896,1152]{1,0:T(8,128)(2,1)} %collective-permute-done.6.refs_16_), channel_id=1, source_target_pairs={{0,1},{1,0},{2,3},{3,2},{4,5},{5,4},{6,7},{7,6}} | collective-permute-start | bytes 6193160 | tf_op jit(solution)/shard_map/ppermute | solution.py:35
  593.4 95.7 %collective-permute-start.9 = (bf16[1152,896]{1,0:T(8,128)(2,1)}, bf16[1152,896]{1,0:T(8,128)(2,1)}, u32[]{:S(2)}, u32[]{:S(2)}) collective-permute-start(bf16[1152,896]{1,0:T(8,128)(2,1)} %collective-permute-done.8.refs_17_), channel_id=1, source_target_pairs={{0,1},{1,0},{2,3},{3,2},{4,5},{5,4},{6,7},{7,6}} | collective-permute-start | bytes 6193160 | tf_op jit(solution)/shard_map/ppermute | solution.py:35
  688.6 47.8 %collective-permute-start.20 = (bf16[896,1152]{1,0:T(8,128)(2,1)}, bf16[896,1152]{1,0:T(8,128)(2,1)}, u32[]{:S(2)}, u32[]{:S(2)}) collective-permute-start(bf16[896,1152]{1,0:T(8,128)(2,1)} %collective-permute-done.18.refs_9_), channel_id=1, source_target_pairs={{0,1},{1,0},{2,3},{3,2},{4,5},{5,4},{6,7},{7,6}} | collective-permute-start | bytes 6193160 | tf_op jit(solution)/shard_map/ppermute | solution.py:35
  689.1 47.3 %collective-permute-start.21 = (bf16[896,1152]{1,0:T(8,128)(2,1)}, bf16[896,1152]{1,0:T(8,128)(2,1)}, u32[]{:S(2)}, u32[]{:S(2)}) collective-permute-start(bf16[896,1152]{1,0:T(8,128)(2,1)} %collective-permute-done.19.refs_10_), channel_id=1, source_target_pairs={{0,1},{1,0},{2,3},{3,2},{4,5},{5,4},{6,7},{7,6}} | collective-permute-start | bytes 6193160 | tf_op jit(solution)/shard_map/ppermute | solution.py:35
  735.9 39.9 %collective-permute-start.17 = (bf16[1152,896]{1,0:T(8,128)(2,1)}, bf16[1152,896]{1,0:T(8,128)(2,1)}, u32[]{:S(2)}, u32[]{:S(2)}) collective-permute-start(bf16[1152,896]{1,0:T(8,128)(2,1)} %collective-permute-done.16.refs_11_), channel_id=1, source_target_pairs={{0,1},{1,0},{2,3},{3,2},{4,5},{5,4},{6,7},{7,6}} | collective-permute-start | bytes 6193160 | tf_op jit(solution)/shard_map/ppermute | solution.py:35

commit v10 on v9

--- a/solution.py
+++ b/solution.py
@@ -1,5 +1,3 @@
-import functools
-
 import jax
 import jax.numpy as jnp
 import numpy as np
@@ -61,9 +59,54 @@
     lax.fori_loop(0, count // together, one, 0)
 
 
-def forward_kernel(tail, x_ref, wg_ref, wu_ref, wd_ref, h_ref, a_ref, a0_ref, acc_ref):
+def written(step, last, half, own, tail, stage_ref, outs, sems, do):
+    me = lax.axis_index("dp")
+    blocks = own // BLOCK
+    extra = own - blocks * BLOCK
+    rows = pl.ds(pl.multiple_of(half * 2 * ROWS, 2 * ROWS), 2 * ROWS)
+    for n, (out, holder) in enumerate(zip(outs, (me, me // 2 * 2 + 1 - me % 2), strict=True)):
+
+        def copy(here, there):
+            do(pltpu.make_async_copy(stage_ref.at[half, :, :, here], out.at[:, rows, there], sems.at[n, half]))
+
+        @pl.when((step < 4 * blocks) & (step // blocks == holder))
+        def _():
+            copy(pl.ds(0, BLOCK), pl.ds(pl.multiple_of(lax.rem(step, blocks) * BLOCK, BLOCK), BLOCK))
+
+        @pl.when(step == 4 * blocks)
+        def _():
+            copy(pl.ds(pl.multiple_of(holder * extra, LANES), extra), pl.ds(blocks * BLOCK, extra))
+
+        @pl.when(step == last)
+        def _():
+            copy(pl.ds(0, tail), pl.ds(own, tail))
+
+
+def halves(tokens, width, moved, there, back):
+    j = pl.program_id(0)
+
+    def two(half, carry):
+        @pl.when(j > 0)
+        def _():
+            moved(j - 1, half, lambda copy: copy.wait())
+
+        low, high = (pl.ds(pl.multiple_of((2 * half + n) * ROWS, ROWS), ROWS) for n in range(2))
+        held = there(half, 0, low, width)
+        ahead = there(half, 1, high, width)
+        back(half, 0, low, width, held)
+        back(half, 1, high, width, ahead)
+        moved(j, half, lambda copy: copy.start())
+        return carry
+
+    lax.fori_loop(0, tokens // (2 * ROWS), two, 0)
+
+
+def forward_kernel(tail, own, x_ref, wg_ref, wu_ref, wd_ref, h_ref, a_ref, a0_ref, mine_ref, theirs_ref, acc_ref, stage_ref, sems):
     j, last = pl.program_id(0), pl.num_programs(0) - 1
     tokens = x_ref.shape[0]
+
+    def moved(step, half, do):
+        written(step, last, half, own, tail, stage_ref, (mine_ref, theirs_ref), sems, do)
 
     @pl.when(j == 0)
     def _():
@@ -73,29 +116,24 @@
 
         looped(tokens // FEW, FEW, start, TOGETHER)
 
-    def up(r, width):
+    def up(half, n, r, width):
         a = a0_ref[r, :]
         g = dot(a, wg_ref[0, :, :width], NN)
         u = dot(a, wu_ref[0, :, :width], NN)
+        for k, value in enumerate((g, u)):
+            stage_ref[half, k, n * ROWS : (n + 1) * ROWS, :width] = value
         return (g * sigmoid(g) * u).astype(BF16)
 
-    def down(r, hid):
-        acc_ref[r, :] += dot(hid, wd_ref[0, : hid.shape[1], :], NN)
-
-    def two(width, r):
-        low, high = (pl.ds(pl.multiple_of(r.start + n * ROWS, ROWS), ROWS) for n in range(2))
-        hid = up(low, width)
-        ahead = up(high, width)
-        down(low, hid)
-        down(high, ahead)
+    def down(half, n, r, width, hid):
+        acc_ref[r, :] += dot(hid, wd_ref[0, :width, :], NN)
 
     @pl.when(j < last)
     def _():
-        looped(tokens // (2 * ROWS), 2 * ROWS, functools.partial(two, wg_ref.shape[2]))
+        halves(tokens, wg_ref.shape[2], moved, up, down)
 
     @pl.when(j == last)
     def _():
-        looped(tokens // ROWS, ROWS, lambda r: down(r, up(r, tail)))
+        halves(tokens, tail, moved, up, down)
 
         def end(r):
             h = (x_ref[r, :].astype(F32) + acc_ref[r, :].astype(BF16).astype(F32)).astype(BF16)
@@ -103,22 +141,32 @@
             a_ref[r, :] = normed(h)
 
         looped(tokens // FEW, FEW, end, TOGETHER)
-
-
-def forward(x, wg, wu, wd):
+        for half in range(tokens // (2 * ROWS)):
+            moved(j, half, lambda copy: copy.wait())
+
+
+def keeping(tokens, count, columns, dtype):
+    kept = [jax.ShapeDtypeStruct((count, tokens, columns), dtype)] * 2
+    parts = tokens // (2 * ROWS)
+    return kept, [pltpu.VMEM((parts, count, 2 * ROWS, BLOCK), dtype), pltpu.SemaphoreType.DMA((2, parts))]
+
+
+def forward(own, x, wg, wu, wd):
     tokens, d = x.shape
     ff = wg.shape[2]
     steps = pl.cdiv(ff, BLOCK)
+    tail = ff - (steps - 1) * BLOCK
     full = once((tokens, d), lambda j: (0, 0))
     across = pl.BlockSpec((1, d, BLOCK), lambda j: (0, 0, j))
     down = pl.BlockSpec((1, BLOCK, d), lambda j: (0, j, 0))
+    kept, stage = keeping(tokens, 2, own + tail, F32)
     return pl.pallas_call(
-        lambda *refs: forward_kernel(ff - (steps - 1) * BLOCK, *refs),
+        lambda *refs: forward_kernel(tail, own, *refs),
         grid=(steps,),
         in_specs=[full, across, across, down],
-        out_specs=[full] * 3,
-        out_shape=[jax.ShapeDtypeStruct((tokens, d), BF16)] * 3,
-        scratch_shapes=[pltpu.VMEM((tokens, d), F32)],
+        out_specs=[full] * 3 + [pl.BlockSpec(memory_space=pl.ANY)] * 2,
+        out_shape=[jax.ShapeDtypeStruct((tokens, d), BF16)] * 3 + kept,
+        scratch_shapes=[pltpu.VMEM((tokens, d), F32)] + stage,
         cost_estimate=pl.CostEstimate(flops=6 * tokens * d * ff, bytes_accessed=6 * d * ff, transcendentals=tokens * ff),
         compiler_params=params(),
         name="forward",
@@ -135,10 +183,9 @@
 def chain_kernel(tail, own, a_ref, dy_ref, h_ref, wg_ref, wu_ref, wd_ref, dh_ref, mine_ref, theirs_ref, acc_ref, stage_ref, sems):
     j, last = pl.program_id(0), pl.num_programs(0) - 1
     tokens = a_ref.shape[0]
-    me = lax.axis_index("dp")
-    holders = (me, me // 2 * 2 + 1 - me % 2)
-    blocks = own // BLOCK
-    extra = own - blocks * BLOCK
+
+    def moved(step, half, do):
+        written(step, last, half, own, tail, stage_ref, (mine_ref, theirs_ref), sems, do)
 
     @pl.when(j == 0)
     def _():
@@ -146,63 +193,25 @@
             acc_ref[r, :] = jnp.zeros((FEW, acc_ref.shape[1]), F32)
 
         looped(tokens // FEW, FEW, start, TOGETHER)
-
-    def written(step, half, do):
-        rows = pl.ds(pl.multiple_of(half * 2 * ROWS, 2 * ROWS), 2 * ROWS)
-        for n, (out, holder) in enumerate(zip((mine_ref, theirs_ref), holders, strict=True)):
-
-            def copy(here, there):
-                do(pltpu.make_async_copy(stage_ref.at[half, :, :, here], out.at[:, rows, there], sems.at[n, half]))
-
-            @pl.when((step < 4 * blocks) & (step // blocks == holder))
-            def _():
-                copy(pl.ds(0, BLOCK), pl.ds(pl.multiple_of(lax.rem(step, blocks) * BLOCK, BLOCK), BLOCK))
-
-            @pl.when(step == 4 * blocks)
-            def _():
-                copy(pl.ds(pl.multiple_of(holder * extra, LANES), extra), pl.ds(blocks * BLOCK, extra))
-
-            @pl.when(step == last)
-            def _():
-                copy(pl.ds(0, tail), pl.ds(own, tail))
 
     def there(half, n, r, width):
         a, dy = a_ref[r, :], dy_ref[r, :]
         g = dot(a, wg_ref[0, :, :width], NN)
         u = dot(a, wu_ref[0, :, :width], NN)
-        held = hidden_back(g, u, dot(dy, wd_ref[0, :width, :], NT))
-        for k in range(3):
-            stage_ref[half, k, n * ROWS : (n + 1) * ROWS, :width] = held[k]
-        return held[:2]
-
-    def back(r, held):
-        dg, du = held
-        width = dg.shape[1]
+        for k, value in enumerate(hidden_back(g, u, dot(dy, wd_ref[0, :width, :], NT))):
+            stage_ref[half, k, n * ROWS : (n + 1) * ROWS, :width] = value
+
+    def back(half, n, r, width, held):
+        dg, du = (stage_ref[half, k, n * ROWS : (n + 1) * ROWS, :width] for k in range(2))
         acc_ref[r, :] += dot(dg, wg_ref[0, :, :width], NT) + dot(du, wu_ref[0, :, :width], NT)
 
-    def block(width):
-        def two(half, carry):
-            @pl.when(j > 0)
-            def _():
-                written(j - 1, half, lambda copy: copy.wait())
-
-            low, high = (pl.ds(pl.multiple_of((2 * half + n) * ROWS, ROWS), ROWS) for n in range(2))
-            held = there(half, 0, low, width)
-            ahead = there(half, 1, high, width)
-            back(low, held)
-            back(high, ahead)
-            written(j, half, lambda copy: copy.start())
-            return carry
-
-        lax.fori_loop(0, tokens // (2 * ROWS), two, 0)
-
     @pl.when(j < last)
     def _():
-        block(wg_ref.shape[2])
+        halves(tokens, wg_ref.shape[2], moved, there, back)
 
     @pl.when(j == last)
     def _():
-        block(tail)
+        halves(tokens, tail, moved, there, back)
 
         def end(r):
             wide, da = h_ref[r, :].astype(F32), acc_ref[r, :].astype(BF16).astype(F32)
@@ -212,7 +221,7 @@
 
         looped(tokens // FEW, FEW, end, TOGETHER)
         for half in range(tokens // (2 * ROWS)):
-            written(j, half, lambda copy: copy.wait())
+            moved(j, half, lambda copy: copy.wait())
 
 
 def chain(own, a, dy, h, wg, wu, wd):
@@ -223,18 +232,14 @@
     full = once((tokens, d), lambda j: (0, 0))
     across = pl.BlockSpec((1, d, BLOCK), lambda j: (1, 0, j))
     down = pl.BlockSpec((1, BLOCK, d), lambda j: (1, j, 0))
-    kept = jax.ShapeDtypeStruct((3, tokens, own + tail), BF16)
+    kept, stage = keeping(tokens, 3, own + tail, BF16)
     return pl.pallas_call(
         lambda *refs: chain_kernel(tail, own, *refs),
         grid=(steps,),
         in_specs=[full, full, full, across, across, down],
         out_specs=[full] + [pl.BlockSpec(memory_space=pl.ANY)] * 2,
-        out_shape=[jax.ShapeDtypeStruct((tokens, d), BF16), kept, kept],
-        scratch_shapes=[
-            pltpu.VMEM((tokens, d), F32),
-            pltpu.VMEM((tokens // (2 * ROWS), 3, 2 * ROWS, BLOCK), BF16),
-            pltpu.SemaphoreType.DMA((2, tokens // (2 * ROWS))),
-        ],
+        out_shape=[jax.ShapeDtypeStruct((tokens, d), BF16)] + kept,
+        scratch_shapes=[pltpu.VMEM((tokens, d), F32)] + stage,
         cost_estimate=pl.CostEstimate(flops=10 * tokens * d * ff, bytes_accessed=6 * d * ff, transcendentals=tokens * ff),
         compiler_params=params(),
         name="chain",
@@ -254,15 +259,15 @@
         return taken
 
     a_own, a_across, dy_own, dy_across, wg_hbm, wu_hbm, wd_hbm = take(7)
-    mine, theirs = take(2) if kept else (None, None)
+    mine, theirs = take(2)
     before = take(2) if final else ()
-    outs, (a_land, dy_land), held_land = take(8), take(2), take(1) if kept else ()
+    outs, (a_land, dy_land, held_land) = take(8), take(3)
     wg_ref, wu_ref, wd_ref, accg_ref, accu_ref, accd_ref, a_buf, dy_buf, sums_ref = take(9)
     sems, w_sems, send_sems, recv_sems = take(4)
-    terms, held_buf = take(3), take(1)[0] if kept else None
+    terms, (held_buf,) = take(3), take(1)
     a_refs = (a_own, a_across, a_land.at[0], a_land.at[1])
     dy_refs = (dy_own, dy_across, dy_land.at[0], dy_land.at[1])
-    held_refs = (mine, None, held_land[0], None) if kept else (None,) * 4
+    held_refs = (mine, None, held_land, None)
     i, steps = pl.program_id(0), pl.num_programs(0)
     each = a_own.shape[0] // ROWS
     width = wg_ref.shape[1]
@@ -295,8 +300,8 @@
 
     def onward(which):
         pairs = [(a_refs[which], a_land.at[which]), (dy_refs[which], dy_land.at[which])]
-        if kept and which == 0:
-            pairs.append((theirs, held_land[0]))
+        if which == 0:
+            pairs.append((theirs, held_land))
         return [
             pltpu.make_async_remote_copy(
                 src_ref=src,
@@ -369,24 +374,31 @@
             back(s, held)
             held = ahead
 
-    def anew(s):
-        a, dy = a_buf[slot], dy_buf[slot]
-        return hidden_back(dot(a, wg_ref[:, s], NN), dot(a, wu_ref[:, s], NN), dot(dy, wd_ref[s, :], NT))
-
-    if kept:
-        known = lax.rem(i // each, 2) == 0
+    known = lax.rem(i // each, 2) == 0
+
+    @pl.when(known)
+    def _():
+        pltpu.make_async_copy(mine.at[:, pl.ds(0, ROWS), :], held_buf.at[slot], sems.at[2, slot]).wait()
+
+    if kept == 2:
+
+        @pl.when(jnp.logical_not(known))
+        def _():
+            for s in blocks:
+                held_buf[slot, 0, :, s] = dot(a_buf[slot], wg_ref[:, s], NN)
+                held_buf[slot, 1, :, s] = dot(a_buf[slot], wu_ref[:, s], NN)
+
+        through(lambda s: hidden_back(held_buf[slot, 0, :, s], held_buf[slot, 1, :, s], dot(dy_buf[slot], wd_ref[s, :], NT)), True)
+    else:
 
         @pl.when(known)
         def _():
-            pltpu.make_async_copy(mine.at[:, pl.ds(0, ROWS), :], held_buf.at[slot], sems.at[2, slot]).wait()
             through(lambda s: [held_buf[slot, n, :, s] for n in range(3)], True)
 
         @pl.when(jnp.logical_not(known))
         def _():
-            through(anew, False)
-
-    else:
-        through(anew, True)
+            a, dy = a_buf[slot], dy_buf[slot]
+            through(lambda s: hidden_back(dot(a, wg_ref[:, s], NN), dot(a, wu_ref[:, s], NN), dot(dy, wd_ref[s, :], NT)), False)
 
     rest = pl.ds(own, width - own)
 
@@ -442,7 +454,7 @@
             outs[7][...] = jnp.zeros((8, LANES), F32)
 
 
-def slices(layer, own, a_all, dy_all, wg, wu, wd, kept=(), before=(), count=None):
+def slices(layer, own, a_all, dy_all, wg, wu, wd, kept, before=(), count=None):
     tokens, d = a_all[0].shape
     ff = wg.shape[2]
     rest = ff - 4 * own
@@ -450,9 +462,9 @@
     any_ = pl.BlockSpec(memory_space=pl.ANY)
     at = lambda s: once(s, lambda i: (0, 0))
     sizes = [(d, own), (d, own), (own, d), (d, rest), (d, rest), (rest, d)]
-    landed = [(2, tokens, d)] * 2 + ([(3, tokens, width)] if kept else [])
+    landed = [jax.ShapeDtypeStruct((2, tokens, d), BF16)] * 2 + [kept[0]]
     return pl.pallas_call(
-        lambda *refs: slices_kernel(layer, own, bool(kept), count, *refs),
+        lambda *refs: slices_kernel(layer, own, kept[0].shape[0], count, *refs),
         grid=(4 * tokens // ROWS,),
         in_specs=[any_] * (7 + len(kept)) + [at((8, LANES))] * len(before),
         out_specs=[at(s) for s in sizes] + [at((8, LANES))] * 2 + [any_] * len(landed),
@@ -463,10 +475,10 @@
         + [pltpu.VMEM((4, 8, LANES), F32)]
         + [pltpu.SemaphoreType.DMA(n) for n in ((3, 2), (3, 3), (9,), (9,))]
         + [pltpu.VMEM((4, d, rest), F32)] * 3
-        + ([pltpu.VMEM((2, 3, ROWS, width), BF16)] if kept else []),
+        + [pltpu.VMEM((2, kept[0].shape[0], ROWS, width), kept[0].dtype)],
         out_shape=[jax.ShapeDtypeStruct(s, BF16) for s in sizes]
         + [jax.ShapeDtypeStruct((8, LANES), F32)] * 2
-        + [jax.ShapeDtypeStruct(s, BF16) for s in landed],
+        + [jax.ShapeDtypeStruct(s.shape, s.dtype) for s in landed],
         cost_estimate=pl.CostEstimate(
             flops=12 * 4 * tokens * d * width, bytes_accessed=16 * tokens * d, transcendentals=4 * tokens * width
         ),
@@ -631,7 +643,7 @@
             return perm(a)
 
         dy_x = send(dy, px)
-        h1, a1, a0 = forward(x, wg, wu, wd)
+        h1, a1, a0, *made = forward(own, x, wg, wu, wd)
         a1_x = send(a1, px)
         a0_x = send(a0, px)
         dh1, *kept = chain(own, a1, dy, h1, wg, wu, wd)
@@ -639,7 +651,7 @@
         top = slices(1, own, [a1, a1_x], [dy, dy_x], wg, wu, wd, kept)
         top_x = [send(top[n], px) for n in range(3)]
         top_d = [send(top[n], pd) for n in range(3)]
-        low = slices(0, own, [a0, a0_x], [dh1, dh1_x], wg, wu, wd, (), top[6:8], wg.size + wu.size + wd.size)
+        low = slices(0, own, [a0, a0_x], [dh1, dh1_x], wg, wu, wd, made, top[6:8], wg.size + wu.size + wd.size)
         low_x = [send(low[n], px) for n in range(3)]
         low_d = [send(low[n], pd) for n in range(3)]
 

time: 786 us -> 777 us (0.989)
  Pallas kernels: 644 us -> 636 us
    pallas_call x3, Pallas kernels: 330 us -> 321 us  [the longest x2 242 us: slices(): pl.pallas_call(lambda *refs: slices_kernel(layer, own, kept[0].shape[0],...]
where the time goes in v10:
time: 777 us; the launch traced here: 776 us
  Pallas kernels  636 us (82%)
  waiting for transfers between devices  121 us (16%)
  starting transfers between devices  17.4 us (2%)
    pallas_call x2, Pallas kernels, slices(): pl.pallas_call(lambda *refs: slices_kernel(layer, own, kept[0].shape[0],...  242 us
    pallas_call x4, Pallas kernels, adam(): pl.pallas_call(kernel, in_specs=[pl.BlockSpec(memory_space=pltpu.SMEM), p...  191 us
    pallas_call x1, Pallas kernels, chain(): pl.pallas_call(lambda *refs: chain_kernel(tail, own, *refs), grid=(steps,...  125 us
    ppermute x10, waiting for transfers between devices, px(): return lax.ppermute(a, 'dp', PX)  114 us
    pallas_call x1, Pallas kernels, forward(): pl.pallas_call(lambda *refs: forward_kernel(tail, own, *refs), grid=(step...  79 us
  transfers between devices with their start and end apart: 22, of which 7 were waited for; matrix products, arithmetic and copies ran while one was open for 0% of the time, Pallas kernels for 71%

profile of v10, /device:TPU:0, one launch (start us, length us, event | category | flops | bytes accessed | tf_op | source)
XLA Modules:
  0.0 776.2 jit_solution(6052293337333799201)
XLA Ops:
  0.6 79.0 %forward.1 = (bf16[2048,896]{1,0:T(8,128)(2,1)}, bf16[2048,896]{1,0:T(8,128)(2,1)}, bf16[2048,896]{1,0:T(8,128)(2,1)}, f32[2,2048,1280]{2,1,0:T(8,128)}, f32[2,2048,1280]{2,1,0:T(8,128)}) custom-call(bf16[2048,896]{1,0:T(8,128)(2,1)} %bitcast.2, bf16[2,896,4736]{2,1,0:T(8,128)(2,1)} %refs_0_.7, bf16[2,896,4736]{2,1,0:T(8,128)(2,1)} %refs_3_.11, ...), custom_call_target="tpu_custom_call" | custom-call | flops 52143587328 | bytes 25460736 | tf_op jit(solution)/shard_map/forward/pallas_call | solution.py:163
  79.7 3.3 collective-permute-start.2
  83.0 124.6 %chain.1 = (bf16[2048,896]{1,0:T(8,128)(2,1)}, bf16[3,2048,1280]{2,1,0:T(8,128)(2,1)}, bf16[3,2048,1280]{2,1,0:T(8,128)(2,1)}) custom-call(bf16[2048,896]{1,0:T(8,128)(2,1)} %get-tuple-element.79.refs_0_, bf16[2048,896]{1,0:T(8,128)(2,1)} %bitcast.4, bf16[2048,896]{1,0:T(8,128)(2,1)} %get-tuple-element.80.refs_2_, bf16[2,896,4736]{2,1,0:T(8,128)(2,1)} %refs_0_.7, ...), custom_call_target="tpu_custom_call" | custom-call | flops 86905978880 | bytes 25460736 | tf_op jit(solution)/shard_map/chain/pallas_call | solution.py:236
  207.7 2.0 collective-permute-start.1
  209.7 32.4 %collective-permute-done.3.refs_3_ = bf16[2048,896]{1,0:T(8,128)(2,1)} collective-permute-done((bf16[2048,896]{1,0:T(8,128)(2,1)}, bf16[2048,896]{1,0:T(8,128)(2,1)}, u32[]{:S(2)}, u32[]{:S(2)}) %collective-permute-start.3) | collective-permute-done | bytes 3670048 | tf_op jit(solution)/shard_map/ppermute | solution.py:29
  242.2 108.6 %slices.2 = (bf16[896,1152]{1,0:T(8,128)(2,1)}, bf16[896,1152]{1,0:T(8,128)(2,1)}, bf16[1152,896]{1,0:T(8,128)(2,1)}, bf16[896,128]{1,0:T(8,128)(2,1)}, bf16[896...) custom-call(bf16[2048,896]{1,0:T(8,128)(2,1)} %get-tuple-element.79., ...), custom_call_target="tpu_custom_call" | custom-call | flops 112742891520 | bytes 29360128 | tf_op jit(solution)/shard_map/slices/pallas_call | solution.py:466
  350.7 1.9 collective-permute-start.4
  352.7 0.1 collective-permute-start.6
  352.8 0.4 collective-permute-start.14
  353.2 46.3 %collective-permute-done.refs_1_ = bf16[2048,896]{1,0:T(8,128)(2,1)} collective-permute-done((bf16[2048,896]{1,0:T(8,128)(2,1)}, bf16[2048,896]{1,0:T(8,128)(2,1)}, u32[]{:S(2)}, u32[]{:S(2)}) %collective-permute-start) | collective-permute-done | bytes 3670048 | tf_op jit(solution)/shard_map/ppermute | solution.py:29
  399.5 2.0 collective-permute-start.8
  401.5 133.1 %slices.3 = (bf16[896,1152]{1,0:T(8,128)(2,1)}, bf16[896,1152]{1,0:T(8,128)(2,1)}, bf16[1152,896]{1,0:T(8,128)(2,1)}, bf16[896,128]{1,0:T(8,128)(2,1)}, bf16[896...) custom-call(bf16[2048,896]{1,0:T(8,128)(2,1)} %get-tuple-element.78., ...), custom_call_target="tpu_custom_call" | custom-call | flops 112742891520 | bytes 29360128 | tf_op jit(solution)/shard_map/slices/pallas_call | solution.py:466
  534.6 0.1 collective-permute-start.15
  534.8 0.4 collective-permute-start.10
  535.2 0.1 collective-permute-start.11
  535.3 0.4 collective-permute-start.12
  535.7 1.7 collective-permute-start.18
  537.4 1.7 collective-permute-done.15.refs_14_
  539.1 1.7 collective-permute-start.16
  540.8 1.2 collective-permute-done.10.refs_12_
  542.1 1.7 collective-permute-start.19
  543.8 1.2 collective-permute-done.11.refs_13_
  545.0 0.1 collective-permute-start.5
  545.2 2.8 collective-permute-done.12.refs_14_
  548.0 0.1 collective-permute-start.7
  548.1 35.7 %collective-permute-done.18.refs_9_ = bf16[896,1152]{1,0:T(8,128)(2,1)} collective-permute-done((bf16[896,1152]{1,0:T(8,128)(2,1)}, bf16[896,1152]{1,0:T(8,128)(2,1)}, u32[]{:S(2)}, u32[]{:S(2)}) %collective-permute-start.18) | collective-permute-done | bytes 2064416 | tf_op jit(solution)/shard_map/ppermute | solution.py:29
  583.8 95.1 %shard_map.214 = (bf16[2,896,4736]{2,1,0:T(8,128)(2,1)}, f32[2,896,4736]{2,1,0:T(8,128)}, f32[2,896,4736]{2,1,0:T(8,128)}, bf16[2,896,4736]{2,1,0:T(8,128)(2,1)}...) custom-call(s32[8,98]{1,0:T(8,128)} %constant.8.clone.table_ref, ...), custom_call_target="tpu_custom_call" | custom-call | flops 26148864000 | bytes 287637504 | tf_op jit(solution)/shard_map/pallas_call | solution.py:622
  679.0 0.5 collective-permute-start.20
  679.5 46.8 %shard_map.215 = (bf16[2,896,4736]{2,1,0:T(8,128)(2,1)}, f32[2,896,4736]{2,1,0:T(8,128)}, f32[2,896,4736]{2,1,0:T(8,128)}, bf16[2,896,4736]{2,1,0:T(8,128)(2,1)}...) custom-call(s32[8,46]{1,0:T(8,128)} %constant.9.clone.table_ref, ...), custom_call_target="tpu_custom_call", output_to_operand_aliasing={{0}: (17, {}), {1}: (18, {}), {2}: (19, {}), {3}: (20, {}),... | custom-call | flops 12386304000 | bytes 136249344 | tf_op jit(solution)/shard_map/pallas_call | solution.py:622
  726.3 0.4 collective-permute-start.17
  726.8 39.5 %shard_map.216 = (bf16[2,896,4736]{2,1,0:T(8,128)(2,1)}, f32[2,896,4736]{2,1,0:T(8,128)}, f32[2,896,4736]{2,1,0:T(8,128)}, bf16[2,896,4736]{2,1,0:T(8,128)(2,1)}...) custom-call(s32[8,37]{1,0:T(8,128)} %constant.10.clone.table_ref, ...), custom_call_target="tpu_custom_call", output_to_operand_aliasing={{0}: (16, {}), {1}: (17, {}), {2}: (18, {}), {3}: (19, {}),... | custom-call | flops 10321920000 | bytes 113541120 | tf_op jit(solution)/shard_map/pallas_call | solution.py:622
  766.2 9.8 %shard_map.217 = (bf16[2,896,4736]{2,1,0:T(8,128)(2,1)}, f32[2,896,4736]{2,1,0:T(8,128)}, f32[2,896,4736]{2,1,0:T(8,128)}, bf16[2,896,4736]{2,1,0:T(8,128)(2,1)}...) custom-call(s32[8,9]{1,0:T(8,128)} %constant.11.clone.table_ref, ...), custom_call_target="tpu_custom_call", output_to_operand_aliasing={{0}: (12, {}), {1}: (13, {}), {2}: (14, {}), {3}: (15, {}),... | custom-call | flops 2064384000 | bytes 22708224 | tf_op jit(solution)/shard_map/pallas_call | solution.py:622
  (20 shorter events, 0.2 us)
Async XLA Ops:
  79.7 130.0 %collective-permute-start.2 = (bf16[2048,896]{1,0:T(8,128)(2,1)}, bf16[2048,896]{1,0:T(8,128)(2,1)}, u32[]{:S(2)}, u32[]{:S(2)}) collective-permute-start(bf16[2048,896]{1,0:T(8,128)(2,1)} %get-tuple-element.79.refs_0_), channel_id=1, source_target_pairs={{0,2},{2,0},{1,3},{3,1},{4,6},{6,4},{5,7},{7,5}} | collective-permute-start | bytes 11010056 | tf_op jit(solution)/shard_map/ppermute | solution.py:29
  83.0 159.2 %collective-permute-start.3 = (bf16[2048,896]{1,0:T(8,128)(2,1)}, bf16[2048,896]{1,0:T(8,128)(2,1)}, u32[]{:S(2)}, u32[]{:S(2)}) collective-permute-start(bf16[2048,896]{1,0:T(8,128)(2,1)} %bitcast.3), channel_id=1, source_target_pairs={{0,2},{2,0},{1,3},{3,1},{4,6},{6,4},{5,7},{7,5}} | collective-permute-start | bytes 11010056 | tf_op jit(solution)/shard_map/ppermute | solution.py:29
  207.7 145.1 %collective-permute-start.1 = (bf16[2048,896]{1,0:T(8,128)(2,1)}, bf16[2048,896]{1,0:T(8,128)(2,1)}, u32[]{:S(2)}, u32[]{:S(2)}) collective-permute-start(bf16[2048,896]{1,0:T(8,128)(2,1)} %get-tuple-element.81.refs_2_), channel_id=1, source_target_pairs={{0,2},{2,0},{1,3},{3,1},{4,6},{6,4},{5,7},{7,5}} | collective-permute-start | bytes 11010056 | tf_op jit(solution)/shard_map/ppermute | solution.py:29
  209.7 189.8 %collective-permute-start = (bf16[2048,896]{1,0:T(8,128)(2,1)}, bf16[2048,896]{1,0:T(8,128)(2,1)}, u32[]{:S(2)}, u32[]{:S(2)}) collective-permute-start(bf16[2048,896]{1,0:T(8,128)(2,1)} %get-tuple-element.78.refs_0_), channel_id=1, source_target_pairs={{0,2},{2,0},{1,3},{3,1},{4,6},{6,4},{5,7},{7,5}} | collective-permute-start | bytes 11010056 | tf_op jit(solution)/shard_map/ppermute | solution.py:29
  350.7 183.9 %collective-permute-start.4 = (bf16[896,1152]{1,0:T(8,128)(2,1)}, bf16[896,1152]{1,0:T(8,128)(2,1)}, u32[]{:S(2)}, u32[]{:S(2)}) collective-permute-start(bf16[896,1152]{1,0:T(8,128)(2,1)} %get-tuple-element.89.refs_9_), channel_id=1, source_target_pairs={{0,2},{2,0},{1,3},{3,1},{4,6},{6,4},{5,7},{7,5}} | collective-permute-start | bytes 6193160 | tf_op jit(solution)/shard_map/ppermute | solution.py:29
  352.6 182.6 %collective-permute-start.13 = (bf16[896,1152]{1,0:T(8,128)(2,1)}, bf16[896,1152]{1,0:T(8,128)(2,1)}, u32[]{:S(2)}, u32[]{:S(2)}) collective-permute-start(bf16[896,1152]{1,0:T(8,128)(2,1)} %get-tuple-element.89.refs_9_), channel_id=1, source_target_pairs={{0,1},{1,0},{2,3},{3,2},{4,5},{5,4},{6,7},{7,6}} | collective-permute-start | bytes 6193160 | tf_op jit(solution)/shard_map/ppermute | solution.py:33
  352.7 182.1 %collective-permute-start.6 = (bf16[896,1152]{1,0:T(8,128)(2,1)}, bf16[896,1152]{1,0:T(8,128)(2,1)}, u32[]{:S(2)}, u32[]{:S(2)}) collective-permute-start(bf16[896,1152]{1,0:T(8,128)(2,1)} %get-tuple-element.90.refs_10_), channel_id=1, source_target_pairs={{0,2},{2,0},{1,3},{3,1},{4,6},{6,4},{5,7},{7,5}} | collective-permute-start | bytes 6193160 | tf_op jit(solution)/shard_map/ppermute | solution.py:29
  352.8 182.9 %collective-permute-start.14 = (bf16[896,1152]{1,0:T(8,128)(2,1)}, bf16[896,1152]{1,0:T(8,128)(2,1)}, u32[]{:S(2)}, u32[]{:S(2)}) collective-permute-start(bf16[896,1152]{1,0:T(8,128)(2,1)} %get-tuple-element.90.refs_10_), channel_id=1, source_target_pairs={{0,1},{1,0},{2,3},{3,2},{4,5},{5,4},{6,7},{7,6}} | collective-permute-start | bytes 6193160 | tf_op jit(solution)/shard_map/ppermute | solution.py:33
  399.5 135.7 %collective-permute-start.8 = (bf16[1152,896]{1,0:T(8,128)(2,1)}, bf16[1152,896]{1,0:T(8,128)(2,1)}, u32[]{:S(2)}, u32[]{:S(2)}) collective-permute-start(bf16[1152,896]{1,0:T(8,128)(2,1)} %get-tuple-element.91.refs_11_), channel_id=1, source_target_pairs={{0,2},{2,0},{1,3},{3,1},{4,6},{6,4},{5,7},{7,5}} | collective-permute-start | bytes 6193160 | tf_op jit(solution)/shard_map/ppermute | solution.py:29
  534.6 4.5 collective-permute-start.15
  534.8 7.3 collective-permute-start.10
  535.2 9.8 %collective-permute-start.11 = (bf16[896,1152]{1,0:T(8,128)(2,1)}, bf16[896,1152]{1,0:T(8,128)(2,1)}, u32[]{:S(2)}, u32[]{:S(2)}) collective-permute-start(bf16[896,1152]{1,0:T(8,128)(2,1)} %get-tuple-element.93.refs_19_), channel_id=1, source_target_pairs={{0,1},{1,0},{2,3},{3,2},{4,5},{5,4},{6,7},{7,6}} | collective-permute-start | bytes 6193160 | tf_op jit(solution)/shard_map/ppermute | solution.py:33
  535.3 12.7 %collective-permute-start.12 = (bf16[1152,896]{1,0:T(8,128)(2,1)}, bf16[1152,896]{1,0:T(8,128)(2,1)}, u32[]{:S(2)}, u32[]{:S(2)}) collective-permute-start(bf16[1152,896]{1,0:T(8,128)(2,1)} %get-tuple-element.94.refs_20_), channel_id=1, source_target_pairs={{0,1},{1,0},{2,3},{3,2},{4,5},{5,4},{6,7},{7,6}} | collective-permute-start | bytes 6193160 | tf_op jit(solution)/shard_map/ppermute | solution.py:33
  535.7 48.1 %collective-permute-start.18 = (bf16[896,1152]{1,0:T(8,128)(2,1)}, bf16[896,1152]{1,0:T(8,128)(2,1)}, u32[]{:S(2)}, u32[]{:S(2)}) collective-permute-start(bf16[896,1152]{1,0:T(8,128)(2,1)} %get-tuple-element.92.refs_18_), channel_id=1, source_target_pairs={{0,2},{2,0},{1,3},{3,1},{4,6},{6,4},{5,7},{7,5}} | collective-permute-start | bytes 6193160 | tf_op jit(solution)/shard_map/ppermute | solution.py:29
  539.1 187.2 %collective-permute-start.16 = (bf16[1152,896]{1,0:T(8,128)(2,1)}, bf16[1152,896]{1,0:T(8,128)(2,1)}, u32[]{:S(2)}, u32[]{:S(2)}) collective-permute-start(bf16[1152,896]{1,0:T(8,128)(2,1)} %get-tuple-element.94.refs_20_), channel_id=1, source_target_pairs={{0,2},{2,0},{1,3},{3,1},{4,6},{6,4},{5,7},{7,5}} | collective-permute-start | bytes 6193160 | tf_op jit(solution)/shard_map/ppermute | solution.py:29
  542.1 136.9 %collective-permute-start.19 = (bf16[896,1152]{1,0:T(8,128)(2,1)}, bf16[896,1152]{1,0:T(8,128)(2,1)}, u32[]{:S(2)}, u32[]{:S(2)}) collective-permute-start(bf16[896,1152]{1,0:T(8,128)(2,1)} %get-tuple-element.93.refs_19_), channel_id=1, source_target_pairs={{0,2},{2,0},{1,3},{3,1},{4,6},{6,4},{5,7},{7,5}} | collective-permute-start | bytes 6193160 | tf_op jit(solution)/shard_map/ppermute | solution.py:29
  545.0 134.5 %collective-permute-start.5 = (bf16[896,1152]{1,0:T(8,128)(2,1)}, bf16[896,1152]{1,0:T(8,128)(2,1)}, u32[]{:S(2)}, u32[]{:S(2)}) collective-permute-start(bf16[896,1152]{1,0:T(8,128)(2,1)} %collective-permute-done.4.refs_15_), channel_id=1, source_target_pairs={{0,1},{1,0},{2,3},{3,2},{4,5},{5,4},{6,7},{7,6}} | collective-permute-start | bytes 6193160 | tf_op jit(solution)/shard_map/ppermute | solution.py:33
  548.0 131.6 %collective-permute-start.7 = (bf16[896,1152]{1,0:T(8,128)(2,1)}, bf16[896,1152]{1,0:T(8,128)(2,1)}, u32[]{:S(2)}, u32[]{:S(2)}) collective-permute-start(bf16[896,1152]{1,0:T(8,128)(2,1)} %collective-permute-done.6.refs_16_), channel_id=1, source_target_pairs={{0,1},{1,0},{2,3},{3,2},{4,5},{5,4},{6,7},{7,6}} | collective-permute-start | bytes 6193160 | tf_op jit(solution)/shard_map/ppermute | solution.py:33
  583.8 95.7 %collective-permute-start.9 = (bf16[1152,896]{1,0:T(8,128)(2,1)}, bf16[1152,896]{1,0:T(8,128)(2,1)}, u32[]{:S(2)}, u32[]{:S(2)}) collective-permute-start(bf16[1152,896]{1,0:T(8,128)(2,1)} %collective-permute-done.8.refs_17_), channel_id=1, source_target_pairs={{0,1},{1,0},{2,3},{3,2},{4,5},{5,4},{6,7},{7,6}} | collective-permute-start | bytes 6193160 | tf_op jit(solution)/shard_map/ppermute | solution.py:33
  679.0 47.8 %collective-permute-start.20 = (bf16[896,1152]{1,0:T(8,128)(2,1)}, bf16[896,1152]{1,0:T(8,128)(2,1)}, u32[]{:S(2)}, u32[]{:S(2)}) collective-permute-start(bf16[896,1152]{1,0:T(8,128)(2,1)} %collective-permute-done.18.refs_9_), channel_id=1, source_target_pairs={{0,1},{1,0},{2,3},{3,2},{4,5},{5,4},{6,7},{7,6}} | collective-permute-start | bytes 6193160 | tf_op jit(solution)/shard_map/ppermute | solution.py:33
  679.5 47.3 %collective-permute-start.21 = (bf16[896,1152]{1,0:T(8,128)(2,1)}, bf16[896,1152]{1,0:T(8,128)(2,1)}, u32[]{:S(2)}, u32[]{:S(2)}) collective-permute-start(bf16[896,1152]{1,0:T(8,128)(2,1)} %collective-permute-done.19.refs_10_), channel_id=1, source_target_pairs={{0,1},{1,0},{2,3},{3,2},{4,5},{5,4},{6,7},{7,6}} | collective-permute-start | bytes 6193160 | tf_op jit(solution)/shard_map/ppermute | solution.py:33
  726.3 39.9 %collective-permute-start.17 = (bf16[1152,896]{1,0:T(8,128)(2,1)}, bf16[1152,896]{1,0:T(8,128)(2,1)}, u32[]{:S(2)}, u32[]{:S(2)}) collective-permute-start(bf16[1152,896]{1,0:T(8,128)(2,1)} %collective-permute-done.16.refs_11_), channel_id=1, source_target_pairs={{0,1},{1,0},{2,3},{3,2},{4,5},{5,4},{6,7},{7,6}} | collective-permute-start | bytes 6193160 | tf_op jit(solution)/shard_map/ppermute | solution.py:33

commit v11 on v10

--- a/solution.py
+++ b/solution.py
@@ -50,10 +50,12 @@
     return (wide * norm_scale(wide)).astype(BF16)
 
 
-def looped(count, rows, body, together=1):
+def looped(count, rows, body, together=1, after=None):
     def one(n, carry):
         for part in range(together):
             body(pl.ds(pl.multiple_of((n * together + part) * rows, rows), rows))
+        if after is not None:
+            after(pl.ds(pl.multiple_of(n * together * rows, together * rows), together * rows))
         return carry
 
     lax.fori_loop(0, count // together, one, 0)
@@ -101,7 +103,8 @@
     lax.fori_loop(0, tokens // (2 * ROWS), two, 0)
 
 
-def forward_kernel(tail, own, x_ref, wg_ref, wu_ref, wd_ref, h_ref, a_ref, a0_ref, mine_ref, theirs_ref, acc_ref, stage_ref, sems):
+def forward_kernel(tail, own, x_ref, wg_ref, wu_ref, wd_ref, *refs):
+    h_out, a_out, a0_out, mine_ref, theirs_ref, acc_ref, stage_ref, sems, h_ref, a_ref, a0_ref, out_sems = refs
     j, last = pl.program_id(0), pl.num_programs(0) - 1
     tokens = x_ref.shape[0]
 
@@ -115,6 +118,12 @@
             acc_ref[r, :] = jnp.zeros((FEW, acc_ref.shape[1]), F32)
 
         looped(tokens // FEW, FEW, start, TOGETHER)
+
+    early = pltpu.make_async_copy(a0_ref, a0_out, out_sems.at[2])
+
+    @pl.when(j == 1)
+    def _():
+        early.start()
 
     def up(half, n, r, width):
         a = a0_ref[r, :]
@@ -140,7 +149,13 @@
             h_ref[r, :] = h
             a_ref[r, :] = normed(h)
 
-        looped(tokens // FEW, FEW, end, TOGETHER)
+        def leave(n, r):
+            return pltpu.make_async_copy((a_ref, h_ref)[n].at[r, :], (a_out, h_out)[n].at[r, :], out_sems.at[n])
+
+        looped(tokens // FEW, FEW, end, TOGETHER, lambda r: [leave(n, r).start() for n in range(2)])
+        for n in range(2):
+            leave(n, pl.ds(0, tokens)).wait()
+        early.wait()
         for half in range(tokens // (2 * ROWS)):
             moved(j, half, lambda copy: copy.wait())
 
@@ -164,9 +179,9 @@
         lambda *refs: forward_kernel(tail, own, *refs),
         grid=(steps,),
         in_specs=[full, across, across, down],
-        out_specs=[full] * 3 + [pl.BlockSpec(memory_space=pl.ANY)] * 2,
+        out_specs=[pl.BlockSpec(memory_space=pl.ANY)] * 5,
         out_shape=[jax.ShapeDtypeStruct((tokens, d), BF16)] * 3 + kept,
-        scratch_shapes=[pltpu.VMEM((tokens, d), F32)] + stage,
+        scratch_shapes=[pltpu.VMEM((tokens, d), F32)] + stage + [pltpu.VMEM((tokens, d), BF16)] * 3 + [pltpu.SemaphoreType.DMA((3,))],
         cost_estimate=pl.CostEstimate(flops=6 * tokens * d * ff, bytes_accessed=6 * d * ff, transcendentals=tokens * ff),
         compiler_params=params(),
         name="forward",
@@ -180,19 +195,23 @@
     return (dhid * u * (sig + act * (1 - sig))).astype(BF16), (dhid * act).astype(BF16), (act * u).astype(BF16)
 
 
-def chain_kernel(tail, own, a_ref, dy_ref, h_ref, wg_ref, wu_ref, wd_ref, dh_ref, mine_ref, theirs_ref, acc_ref, stage_ref, sems):
+def chain_kernel(tail, own, a_ref, dy_ref, h_in, wg_ref, wu_ref, wd_ref, dh_out, mine_ref, theirs_ref, *scratch):
+    acc_ref, stage_ref, sems, h_ref, dh_ref, out_sems = scratch
     j, last = pl.program_id(0), pl.num_programs(0) - 1
     tokens = a_ref.shape[0]
 
     def moved(step, half, do):
         written(step, last, half, own, tail, stage_ref, (mine_ref, theirs_ref), sems, do)
 
+    late = pltpu.make_async_copy(h_in, h_ref, out_sems.at[0])
+
     @pl.when(j == 0)
     def _():
         def start(r):
             acc_ref[r, :] = jnp.zeros((FEW, acc_ref.shape[1]), F32)
 
         looped(tokens // FEW, FEW, start, TOGETHER)
+        late.start()
 
     def there(half, n, r, width):
         a, dy = a_ref[r, :], dy_ref[r, :]
@@ -212,6 +231,7 @@
     @pl.when(j == last)
     def _():
         halves(tokens, tail, moved, there, back)
+        late.wait()
 
         def end(r):
             wide, da = h_ref[r, :].astype(F32), acc_ref[r, :].astype(BF16).astype(F32)
@@ -219,7 +239,11 @@
             through = scale * da - wide * (scale * scale * scale * jnp.mean(wide * da, -1, keepdims=True))
             dh_ref[r, :] = (dy_ref[r, :].astype(F32) + through.astype(BF16).astype(F32)).astype(BF16)
 
-        looped(tokens // FEW, FEW, end, TOGETHER)
+        def leave(r):
+            return pltpu.make_async_copy(dh_ref.at[r, :], dh_out.at[r, :], out_sems.at[1])
+
+        looped(tokens // FEW, FEW, end, TOGETHER, lambda r: leave(r).start())
+        leave(pl.ds(0, tokens)).wait()
         for half in range(tokens // (2 * ROWS)):
             moved(j, half, lambda copy: copy.wait())
 
@@ -236,10 +260,10 @@
     return pl.pallas_call(
         lambda *refs: chain_kernel(tail, own, *refs),
         grid=(steps,),
-        in_specs=[full, full, full, across, across, down],
-        out_specs=[full] + [pl.BlockSpec(memory_space=pl.ANY)] * 2,
+        in_specs=[full, full, pl.BlockSpec(memory_space=pl.ANY), across, across, down],
+        out_specs=[pl.BlockSpec(memory_space=pl.ANY)] * 3,
         out_shape=[jax.ShapeDtypeStruct((tokens, d), BF16)] + kept,
-        scratch_shapes=[pltpu.VMEM((tokens, d), F32)] + stage,
+        scratch_shapes=[pltpu.VMEM((tokens, d), F32)] + stage + [pltpu.VMEM((tokens, d), BF16)] * 2 + [pltpu.SemaphoreType.DMA((2,))],
         cost_estimate=pl.CostEstimate(flops=10 * tokens * d * ff, bytes_accessed=6 * d * ff, transcendentals=tokens * ff),
         compiler_params=params(),
         name="chain",
@@ -264,10 +288,10 @@
     outs, (a_land, dy_land, held_land) = take(8), take(3)
     wg_ref, wu_ref, wd_ref, accg_ref, accu_ref, accd_ref, a_buf, dy_buf, sums_ref = take(9)
     sems, w_sems, send_sems, recv_sems = take(4)
-    terms, (held_buf,) = take(3), take(1)
-    a_refs = (a_own, a_across, a_land.at[0], a_land.at[1])
-    dy_refs = (dy_own, dy_across, dy_land.at[0], dy_land.at[1])
-    held_refs = (mine, None, held_land, None)
+    terms, (held_buf,), results = take(3), take(1), take(3)
+    a_refs = (a_own, a_across, a_land.at[1], a_land.at[0])
+    dy_refs = (dy_own, dy_across, dy_land.at[1], dy_land.at[0])
+    held_refs = (mine, None, None, held_land)
     i, steps = pl.program_id(0), pl.num_programs(0)
     each = a_own.shape[0] // ROWS
     width = wg_ref.shape[1]
@@ -340,13 +364,13 @@
     @pl.when(i == 1)
     def _():
         pl.semaphore_wait(barrier, len(spoken))
-        for which in range(2):
+        for which in (1, 0):
             for copy in onward(which):
                 copy.start()
 
     for which in range(2):
 
-        @pl.when(i == (2 + which) * each - 1)
+        @pl.when(i == (3 - which) * each - 1)
         def _():
             for copy in onward(which):
                 copy.wait()
@@ -374,7 +398,7 @@
             back(s, held)
             held = ahead
 
-    known = lax.rem(i // each, 2) == 0
+    known = (i // each == 0) | (i // each == 3)
 
     @pl.when(known)
     def _():
@@ -416,6 +440,9 @@
             return part, total + jnp.sum((wide * wide).reshape(-1, 8, LANES), 0)
 
         accs = (accg_ref, accu_ref, accd_ref)
+
+        def leave(n, at):
+            return pltpu.make_async_copy(results[n].at[at, :], outs[n].at[at, :], w_sems.at[n, 0])
 
         def rows(r, total):
             at = pl.ds(pl.multiple_of(r * LANES, LANES), LANES)
@@ -423,22 +450,27 @@
                 for c in range(0, own, LANES):
                     part, total = rounded(acc[at, c : c + LANES], total)
                     if n < 2:
-                        outs[n][at, c : c + LANES] = part
+                        results[n][at, c : c + LANES] = part
+            for n in range(2):
+                leave(n, at).start()
             return total
 
         def turn(c, carry):
             at = pl.ds(pl.multiple_of(c * LANES, LANES), LANES)
             for r in range(0, a_buf.shape[2], LANES):
-                outs[2][at, r : r + LANES] = accd_ref[r : r + LANES, at].astype(BF16).T
+                results[2][at, r : r + LANES] = accd_ref[r : r + LANES, at].astype(BF16).T
+            leave(2, at).start()
             return carry
 
-        at = [(chip + s // 2) % 2 + 2 * ((core + s) % 2) for s in range(4)]
+        at = [3 * ((core + s) % 2) + (chip + s // 2) % 2 * (1 - 2 * ((core + s) % 2)) for s in range(4)]
         place = [(core + s) % 2 + 2 * ((chip + s // 2) % 2) for s in range(4)]
         sums = [lax.fori_loop(0, a_buf.shape[2] // LANES, rows, jnp.zeros((8, LANES), F32)), jnp.zeros((8, LANES), F32)]
         lax.fori_loop(0, own // LANES, turn, 0)
         for n, term in enumerate(terms):
             part, sums[1] = rounded(term[at[0]] + term[at[1]] + term[at[2]] + term[at[3]], sums[1])
             outs[3 + n][...] = part if n < 2 else part.T
+        for n, result in enumerate(results):
+            leave(n, pl.ds(0, result.shape[0])).wait()
         if not final:
             outs[6][...], outs[7][...] = sums
         else:
@@ -467,7 +499,7 @@
         lambda *refs: slices_kernel(layer, own, kept[0].shape[0], count, *refs),
         grid=(4 * tokens // ROWS,),
         in_specs=[any_] * (7 + len(kept)) + [at((8, LANES))] * len(before),
-        out_specs=[at(s) for s in sizes] + [at((8, LANES))] * 2 + [any_] * len(landed),
+        out_specs=[any_] * 3 + [at(s) for s in sizes[3:]] + [at((8, LANES))] * 2 + [any_] * len(landed),
         scratch_shapes=[pltpu.VMEM((d, width), BF16)] * 2
         + [pltpu.VMEM((width, d), BF16)]
         + [pltpu.VMEM((d, width), F32)] * 3
@@ -475,7 +507,8 @@
         + [pltpu.VMEM((4, 8, LANES), F32)]
         + [pltpu.SemaphoreType.DMA(n) for n in ((3, 2), (3, 3), (9,), (9,))]
         + [pltpu.VMEM((4, d, rest), F32)] * 3
-        + [pltpu.VMEM((2, kept[0].shape[0], ROWS, width), kept[0].dtype)],
+        + [pltpu.VMEM((2, kept[0].shape[0], ROWS, width), kept[0].dtype)]
+        + [pltpu.VMEM(s, BF16) for s in sizes[:3]],
         out_shape=[jax.ShapeDtypeStruct(s, BF16) for s in sizes]
         + [jax.ShapeDtypeStruct((8, LANES), F32)] * 2
         + [jax.ShapeDtypeStruct(s.shape, s.dtype) for s in landed],

time: 777 us -> 772 us (level)
  Pallas kernels: 636 us -> 627 us
  transfers between devices with their start and end apart: 22 -> 22, of which waited for: 7 -> 7; matrix products, arithmetic and copies ran while one was open for 0% -> 0% of each run, Pallas kernels for 71% -> 70%
where the time goes in v11:
time: 772 us; the launch traced here: 771 us
  Pallas kernels  627 us (81%)
  waiting for transfers between devices  126 us (16%)
  starting transfers between devices  17.4 us (2%)
    pallas_call x2, Pallas kernels, slices(): pl.pallas_call(lambda *refs: slices_kernel(layer, own, kept[0].shape[0],...  238 us
    pallas_call x4, Pallas kernels, adam(): pl.pallas_call(kernel, in_specs=[pl.BlockSpec(memory_space=pltpu.SMEM), p...  191 us
    pallas_call x1, Pallas kernels, chain(): pl.pallas_call(lambda *refs: chain_kernel(tail, own, *refs), grid=(steps,...  122 us
    ppermute x10, waiting for transfers between devices, px(): return lax.ppermute(a, 'dp', PX)  119 us
    pallas_call x1, Pallas kernels, forward(): pl.pallas_call(lambda *refs: forward_kernel(tail, own, *refs), grid=(step...  76.2 us
  transfers between devices with their start and end apart: 22, of which 7 were waited for; matrix products, arithmetic and copies ran while one was open for 0% of the time, Pallas kernels for 70%

profile of v11, /device:TPU:0, one launch (start us, length us, event | category | flops | bytes accessed | tf_op | source)
XLA Modules:
  0.0 771.4 jit_solution(11828674748246297281)
XLA Ops:
  0.6 76.2 %forward.1 = (bf16[2048,896]{1,0:T(8,128)(2,1)}, bf16[2048,896]{1,0:T(8,128)(2,1)}, bf16[2048,896]{1,0:T(8,128)(2,1)}, f32[2,2048,1280]{2,1,0:T(8,128)}, f32[2,2048,1280]{2,1,0:T(8,128)}) custom-call(bf16[2048,896]{1,0:T(8,128)(2,1)} %bitcast.2, bf16[2,896,4736]{2,1,0:T(8,128)(2,1)} %refs_0_.7, bf16[2,896,4736]{2,1,0:T(8,128)(2,1)} %refs_3_.11, ...), custom_call_target="tpu_custom_call" | custom-call | flops 52143587328 | bytes 25460736 | tf_op jit(solution)/shard_map/forward/pallas_call | solution.py:178
  76.8 3.3 collective-permute-start.2
  80.2 122.4 %chain.1 = (bf16[2048,896]{1,0:T(8,128)(2,1)}, bf16[3,2048,1280]{2,1,0:T(8,128)(2,1)}, bf16[3,2048,1280]{2,1,0:T(8,128)(2,1)}) custom-call(bf16[2048,896]{1,0:T(8,128)(2,1)} %get-tuple-element.79.refs_0_, bf16[2048,896]{1,0:T(8,128)(2,1)} %bitcast.4, bf16[2048,896]{1,0:T(8,128)(2,1)} %get-tuple-element.80.refs_2_, bf16[2,896,4736]{2,1,0:T(8,128)(2,1)} %refs_0_.7, ...), custom_call_target="tpu_custom_call" | custom-call | flops 86905978880 | bytes 25460736 | tf_op jit(solution)/shard_map/chain/pallas_call | solution.py:260
  202.6 2.0 collective-permute-start.1
  204.7 34.6 %collective-permute-done.3.refs_3_ = bf16[2048,896]{1,0:T(8,128)(2,1)} collective-permute-done((bf16[2048,896]{1,0:T(8,128)(2,1)}, bf16[2048,896]{1,0:T(8,128)(2,1)}, u32[]{:S(2)}, u32[]{:S(2)}) %collective-permute-start.3) | collective-permute-done | bytes 3670048 | tf_op jit(solution)/shard_map/ppermute | solution.py:29
  239.3 106.6 %slices.2 = (bf16[896,1152]{1,0:T(8,128)(2,1)}, bf16[896,1152]{1,0:T(8,128)(2,1)}, bf16[1152,896]{1,0:T(8,128)(2,1)}, bf16[896,128]{1,0:T(8,128)(2,1)}, bf16[896...) custom-call(bf16[2048,896]{1,0:T(8,128)(2,1)} %get-tuple-element.79., ...), custom_call_target="tpu_custom_call" | custom-call | flops 112742891520 | bytes 29360128 | tf_op jit(solution)/shard_map/slices/pallas_call | solution.py:498
  345.9 1.9 collective-permute-start.4
  347.9 0.1 collective-permute-start.6
  348.0 0.4 collective-permute-start.14
  348.4 48.2 %collective-permute-done.refs_1_ = bf16[2048,896]{1,0:T(8,128)(2,1)} collective-permute-done((bf16[2048,896]{1,0:T(8,128)(2,1)}, bf16[2048,896]{1,0:T(8,128)(2,1)}, u32[]{:S(2)}, u32[]{:S(2)}) %collective-permute-start) | collective-permute-done | bytes 3670048 | tf_op jit(solution)/shard_map/ppermute | solution.py:29
  396.6 2.0 collective-permute-start.8
  398.6 131.2 %slices.3 = (bf16[896,1152]{1,0:T(8,128)(2,1)}, bf16[896,1152]{1,0:T(8,128)(2,1)}, bf16[1152,896]{1,0:T(8,128)(2,1)}, bf16[896,128]{1,0:T(8,128)(2,1)}, bf16[896...) custom-call(bf16[2048,896]{1,0:T(8,128)(2,1)} %get-tuple-element.78., ...), custom_call_target="tpu_custom_call" | custom-call | flops 112742891520 | bytes 29360128 | tf_op jit(solution)/shard_map/slices/pallas_call | solution.py:498
  529.8 0.1 collective-permute-start.15
  530.0 0.4 collective-permute-start.10
  530.4 0.1 collective-permute-start.11
  530.5 0.4 collective-permute-start.12
  530.9 1.7 collective-permute-start.18
  532.6 1.7 collective-permute-done.15.refs_14_
  534.3 1.7 collective-permute-start.16
  536.1 1.2 collective-permute-done.10.refs_12_
  537.3 1.7 collective-permute-start.19
  539.0 1.2 collective-permute-done.11.refs_13_
  540.2 0.1 collective-permute-start.5
  540.4 2.8 collective-permute-done.12.refs_14_
  543.2 0.1 collective-permute-start.7
  543.3 35.7 %collective-permute-done.18.refs_9_ = bf16[896,1152]{1,0:T(8,128)(2,1)} collective-permute-done((bf16[896,1152]{1,0:T(8,128)(2,1)}, bf16[896,1152]{1,0:T(8,128)(2,1)}, u32[]{:S(2)}, u32[]{:S(2)}) %collective-permute-start.18) | collective-permute-done | bytes 2064416 | tf_op jit(solution)/shard_map/ppermute | solution.py:29
  579.0 95.1 %shard_map.214 = (bf16[2,896,4736]{2,1,0:T(8,128)(2,1)}, f32[2,896,4736]{2,1,0:T(8,128)}, f32[2,896,4736]{2,1,0:T(8,128)}, bf16[2,896,4736]{2,1,0:T(8,128)(2,1)}...) custom-call(s32[8,98]{1,0:T(8,128)} %constant.8.clone.table_ref, ...), custom_call_target="tpu_custom_call" | custom-call | flops 26148864000 | bytes 287637504 | tf_op jit(solution)/shard_map/pallas_call | solution.py:655
  674.2 0.5 collective-permute-start.20
  674.7 46.8 %shard_map.215 = (bf16[2,896,4736]{2,1,0:T(8,128)(2,1)}, f32[2,896,4736]{2,1,0:T(8,128)}, f32[2,896,4736]{2,1,0:T(8,128)}, bf16[2,896,4736]{2,1,0:T(8,128)(2,1)}...) custom-call(s32[8,46]{1,0:T(8,128)} %constant.9.clone.table_ref, ...), custom_call_target="tpu_custom_call", output_to_operand_aliasing={{0}: (17, {}), {1}: (18, {}), {2}: (19, {}), {3}: (20, {}),... | custom-call | flops 12386304000 | bytes 136249344 | tf_op jit(solution)/shard_map/pallas_call | solution.py:655
  721.5 0.4 collective-permute-start.17
  722.0 39.5 %shard_map.216 = (bf16[2,896,4736]{2,1,0:T(8,128)(2,1)}, f32[2,896,4736]{2,1,0:T(8,128)}, f32[2,896,4736]{2,1,0:T(8,128)}, bf16[2,896,4736]{2,1,0:T(8,128)(2,1)}...) custom-call(s32[8,37]{1,0:T(8,128)} %constant.10.clone.table_ref, ...), custom_call_target="tpu_custom_call", output_to_operand_aliasing={{0}: (16, {}), {1}: (17, {}), {2}: (18, {}), {3}: (19, {}),... | custom-call | flops 10321920000 | bytes 113541120 | tf_op jit(solution)/shard_map/pallas_call | solution.py:655
  761.5 9.8 %shard_map.217 = (bf16[2,896,4736]{2,1,0:T(8,128)(2,1)}, f32[2,896,4736]{2,1,0:T(8,128)}, f32[2,896,4736]{2,1,0:T(8,128)}, bf16[2,896,4736]{2,1,0:T(8,128)(2,1)}...) custom-call(s32[8,9]{1,0:T(8,128)} %constant.11.clone.table_ref, ...), custom_call_target="tpu_custom_call", output_to_operand_aliasing={{0}: (12, {}), {1}: (13, {}), {2}: (14, {}), {3}: (15, {}),... | custom-call | flops 2064384000 | bytes 22708224 | tf_op jit(solution)/shard_map/pallas_call | solution.py:655
  (20 shorter events, 0.2 us)
Async XLA Ops:
  76.8 127.9 %collective-permute-start.2 = (bf16[2048,896]{1,0:T(8,128)(2,1)}, bf16[2048,896]{1,0:T(8,128)(2,1)}, u32[]{:S(2)}, u32[]{:S(2)}) collective-permute-start(bf16[2048,896]{1,0:T(8,128)(2,1)} %get-tuple-element.79.refs_0_), channel_id=1, source_target_pairs={{0,2},{2,0},{1,3},{3,1},{4,6},{6,4},{5,7},{7,5}} | collective-permute-start | bytes 11010056 | tf_op jit(solution)/shard_map/ppermute | solution.py:29
  80.2 159.2 %collective-permute-start.3 = (bf16[2048,896]{1,0:T(8,128)(2,1)}, bf16[2048,896]{1,0:T(8,128)(2,1)}, u32[]{:S(2)}, u32[]{:S(2)}) collective-permute-start(bf16[2048,896]{1,0:T(8,128)(2,1)} %bitcast.3), channel_id=1, source_target_pairs={{0,2},{2,0},{1,3},{3,1},{4,6},{6,4},{5,7},{7,5}} | collective-permute-start | bytes 11010056 | tf_op jit(solution)/shard_map/ppermute | solution.py:29
  202.6 145.3 %collective-permute-start.1 = (bf16[2048,896]{1,0:T(8,128)(2,1)}, bf16[2048,896]{1,0:T(8,128)(2,1)}, u32[]{:S(2)}, u32[]{:S(2)}) collective-permute-start(bf16[2048,896]{1,0:T(8,128)(2,1)} %get-tuple-element.81.refs_2_), channel_id=1, source_target_pairs={{0,2},{2,0},{1,3},{3,1},{4,6},{6,4},{5,7},{7,5}} | collective-permute-start | bytes 11010056 | tf_op jit(solution)/shard_map/ppermute | solution.py:29
  204.6 192.0 %collective-permute-start = (bf16[2048,896]{1,0:T(8,128)(2,1)}, bf16[2048,896]{1,0:T(8,128)(2,1)}, u32[]{:S(2)}, u32[]{:S(2)}) collective-permute-start(bf16[2048,896]{1,0:T(8,128)(2,1)} %get-tuple-element.78.refs_0_), channel_id=1, source_target_pairs={{0,2},{2,0},{1,3},{3,1},{4,6},{6,4},{5,7},{7,5}} | collective-permute-start | bytes 11010056 | tf_op jit(solution)/shard_map/ppermute | solution.py:29
  345.9 183.9 %collective-permute-start.4 = (bf16[896,1152]{1,0:T(8,128)(2,1)}, bf16[896,1152]{1,0:T(8,128)(2,1)}, u32[]{:S(2)}, u32[]{:S(2)}) collective-permute-start(bf16[896,1152]{1,0:T(8,128)(2,1)} %get-tuple-element.89.refs_9_), channel_id=1, source_target_pairs={{0,2},{2,0},{1,3},{3,1},{4,6},{6,4},{5,7},{7,5}} | collective-permute-start | bytes 6193160 | tf_op jit(solution)/shard_map/ppermute | solution.py:29
  347.8 182.6 %collective-permute-start.13 = (bf16[896,1152]{1,0:T(8,128)(2,1)}, bf16[896,1152]{1,0:T(8,128)(2,1)}, u32[]{:S(2)}, u32[]{:S(2)}) collective-permute-start(bf16[896,1152]{1,0:T(8,128)(2,1)} %get-tuple-element.89.refs_9_), channel_id=1, source_target_pairs={{0,1},{1,0},{2,3},{3,2},{4,5},{5,4},{6,7},{7,6}} | collective-permute-start | bytes 6193160 | tf_op jit(solution)/shard_map/ppermute | solution.py:33
  347.9 182.1 %collective-permute-start.6 = (bf16[896,1152]{1,0:T(8,128)(2,1)}, bf16[896,1152]{1,0:T(8,128)(2,1)}, u32[]{:S(2)}, u32[]{:S(2)}) collective-permute-start(bf16[896,1152]{1,0:T(8,128)(2,1)} %get-tuple-element.90.refs_10_), channel_id=1, source_target_pairs={{0,2},{2,0},{1,3},{3,1},{4,6},{6,4},{5,7},{7,5}} | collective-permute-start | bytes 6193160 | tf_op jit(solution)/shard_map/ppermute | solution.py:29
  348.0 182.9 %collective-permute-start.14 = (bf16[896,1152]{1,0:T(8,128)(2,1)}, bf16[896,1152]{1,0:T(8,128)(2,1)}, u32[]{:S(2)}, u32[]{:S(2)}) collective-permute-start(bf16[896,1152]{1,0:T(8,128)(2,1)} %get-tuple-element.90.refs_10_), channel_id=1, source_target_pairs={{0,1},{1,0},{2,3},{3,2},{4,5},{5,4},{6,7},{7,6}} | collective-permute-start | bytes 6193160 | tf_op jit(solution)/shard_map/ppermute | solution.py:33
  396.6 133.8 %collective-permute-start.8 = (bf16[1152,896]{1,0:T(8,128)(2,1)}, bf16[1152,896]{1,0:T(8,128)(2,1)}, u32[]{:S(2)}, u32[]{:S(2)}) collective-permute-start(bf16[1152,896]{1,0:T(8,128)(2,1)} %get-tuple-element.91.refs_11_), channel_id=1, source_target_pairs={{0,2},{2,0},{1,3},{3,1},{4,6},{6,4},{5,7},{7,5}} | collective-permute-start | bytes 6193160 | tf_op jit(solution)/shard_map/ppermute | solution.py:29
  529.8 4.5 collective-permute-start.15
  530.0 7.3 collective-permute-start.10
  530.4 9.8 %collective-permute-start.11 = (bf16[896,1152]{1,0:T(8,128)(2,1)}, bf16[896,1152]{1,0:T(8,128)(2,1)}, u32[]{:S(2)}, u32[]{:S(2)}) collective-permute-start(bf16[896,1152]{1,0:T(8,128)(2,1)} %get-tuple-element.93.refs_19_), channel_id=1, source_target_pairs={{0,1},{1,0},{2,3},{3,2},{4,5},{5,4},{6,7},{7,6}} | collective-permute-start | bytes 6193160 | tf_op jit(solution)/shard_map/ppermute | solution.py:33
  530.5 12.7 %collective-permute-start.12 = (bf16[1152,896]{1,0:T(8,128)(2,1)}, bf16[1152,896]{1,0:T(8,128)(2,1)}, u32[]{:S(2)}, u32[]{:S(2)}) collective-permute-start(bf16[1152,896]{1,0:T(8,128)(2,1)} %get-tuple-element.94.refs_20_), channel_id=1, source_target_pairs={{0,1},{1,0},{2,3},{3,2},{4,5},{5,4},{6,7},{7,6}} | collective-permute-start | bytes 6193160 | tf_op jit(solution)/shard_map/ppermute | solution.py:33
  530.9 48.1 %collective-permute-start.18 = (bf16[896,1152]{1,0:T(8,128)(2,1)}, bf16[896,1152]{1,0:T(8,128)(2,1)}, u32[]{:S(2)}, u32[]{:S(2)}) collective-permute-start(bf16[896,1152]{1,0:T(8,128)(2,1)} %get-tuple-element.92.refs_18_), channel_id=1, source_target_pairs={{0,2},{2,0},{1,3},{3,1},{4,6},{6,4},{5,7},{7,5}} | collective-permute-start | bytes 6193160 | tf_op jit(solution)/shard_map/ppermute | solution.py:29
  534.3 187.2 %collective-permute-start.16 = (bf16[1152,896]{1,0:T(8,128)(2,1)}, bf16[1152,896]{1,0:T(8,128)(2,1)}, u32[]{:S(2)}, u32[]{:S(2)}) collective-permute-start(bf16[1152,896]{1,0:T(8,128)(2,1)} %get-tuple-element.94.refs_20_), channel_id=1, source_target_pairs={{0,2},{2,0},{1,3},{3,1},{4,6},{6,4},{5,7},{7,5}} | collective-permute-start | bytes 6193160 | tf_op jit(solution)/shard_map/ppermute | solution.py:29
  537.3 136.9 %collective-permute-start.19 = (bf16[896,1152]{1,0:T(8,128)(2,1)}, bf16[896,1152]{1,0:T(8,128)(2,1)}, u32[]{:S(2)}, u32[]{:S(2)}) collective-permute-start(bf16[896,1152]{1,0:T(8,128)(2,1)} %get-tuple-element.93.refs_19_), channel_id=1, source_target_pairs={{0,2},{2,0},{1,3},{3,1},{4,6},{6,4},{5,7},{7,5}} | collective-permute-start | bytes 6193160 | tf_op jit(solution)/shard_map/ppermute | solution.py:29
  540.2 134.5 %collective-permute-start.5 = (bf16[896,1152]{1,0:T(8,128)(2,1)}, bf16[896,1152]{1,0:T(8,128)(2,1)}, u32[]{:S(2)}, u32[]{:S(2)}) collective-permute-start(bf16[896,1152]{1,0:T(8,128)(2,1)} %collective-permute-done.4.refs_15_), channel_id=1, source_target_pairs={{0,1},{1,0},{2,3},{3,2},{4,5},{5,4},{6,7},{7,6}} | collective-permute-start | bytes 6193160 | tf_op jit(solution)/shard_map/ppermute | solution.py:33
  543.2 131.6 %collective-permute-start.7 = (bf16[896,1152]{1,0:T(8,128)(2,1)}, bf16[896,1152]{1,0:T(8,128)(2,1)}, u32[]{:S(2)}, u32[]{:S(2)}) collective-permute-start(bf16[896,1152]{1,0:T(8,128)(2,1)} %collective-permute-done.6.refs_16_), channel_id=1, source_target_pairs={{0,1},{1,0},{2,3},{3,2},{4,5},{5,4},{6,7},{7,6}} | collective-permute-start | bytes 6193160 | tf_op jit(solution)/shard_map/ppermute | solution.py:33
  579.0 95.7 %collective-permute-start.9 = (bf16[1152,896]{1,0:T(8,128)(2,1)}, bf16[1152,896]{1,0:T(8,128)(2,1)}, u32[]{:S(2)}, u32[]{:S(2)}) collective-permute-start(bf16[1152,896]{1,0:T(8,128)(2,1)} %collective-permute-done.8.refs_17_), channel_id=1, source_target_pairs={{0,1},{1,0},{2,3},{3,2},{4,5},{5,4},{6,7},{7,6}} | collective-permute-start | bytes 6193160 | tf_op jit(solution)/shard_map/ppermute | solution.py:33
  674.2 47.8 %collective-permute-start.20 = (bf16[896,1152]{1,0:T(8,128)(2,1)}, bf16[896,1152]{1,0:T(8,128)(2,1)}, u32[]{:S(2)}, u32[]{:S(2)}) collective-permute-start(bf16[896,1152]{1,0:T(8,128)(2,1)} %collective-permute-done.18.refs_9_), channel_id=1, source_target_pairs={{0,1},{1,0},{2,3},{3,2},{4,5},{5,4},{6,7},{7,6}} | collective-permute-start | bytes 6193160 | tf_op jit(solution)/shard_map/ppermute | solution.py:33
  674.7 47.3 %collective-permute-start.21 = (bf16[896,1152]{1,0:T(8,128)(2,1)}, bf16[896,1152]{1,0:T(8,128)(2,1)}, u32[]{:S(2)}, u32[]{:S(2)}) collective-permute-start(bf16[896,1152]{1,0:T(8,128)(2,1)} %collective-permute-done.19.refs_10_), channel_id=1, source_target_pairs={{0,1},{1,0},{2,3},{3,2},{4,5},{5,4},{6,7},{7,6}} | collective-permute-start | bytes 6193160 | tf_op jit(solution)/shard_map/ppermute | solution.py:33
  721.5 39.9 %collective-permute-start.17 = (bf16[1152,896]{1,0:T(8,128)(2,1)}, bf16[1152,896]{1,0:T(8,128)(2,1)}, u32[]{:S(2)}, u32[]{:S(2)}) collective-permute-start(bf16[1152,896]{1,0:T(8,128)(2,1)} %collective-permute-done.16.refs_11_), channel_id=1, source_target_pairs={{0,1},{1,0},{2,3},{3,2},{4,5},{5,4},{6,7},{7,6}} | collective-permute-start | bytes 6193160 | tf_op jit(solution)/shard_map/ppermute | solution.py:33

commit v12 on v11

--- a/solution.py
+++ b/solution.py
@@ -8,13 +8,13 @@
 
 
 F32, BF16 = jnp.float32, jnp.bfloat16
-PX = ((0, 2), (2, 0), (1, 3), (3, 1))
-PD = ((0, 1), (1, 0), (2, 3), (3, 2))
+PX, PD = (tuple((device, device ^ bit) for device in range(4)) for bit in (2, 1))
 NN, NT = ((1,), (0,)), ((1,), (1,))
 
 LANES = 128
 BLOCK = 512
 ROWS, FEW, TOGETHER = 512, 64, 4
+HALF = 2 * ROWS
 
 
 def dot(a, b, dims):
@@ -65,7 +65,7 @@
     me = lax.axis_index("dp")
     blocks = own // BLOCK
     extra = own - blocks * BLOCK
-    rows = pl.ds(pl.multiple_of(half * 2 * ROWS, 2 * ROWS), 2 * ROWS)
+    rows = pl.ds(pl.multiple_of(half * HALF, HALF), HALF)
     for n, (out, holder) in enumerate(zip(outs, (me, me // 2 * 2 + 1 - me % 2), strict=True)):
 
         def copy(here, there):
@@ -92,15 +92,24 @@
         def _():
             moved(j - 1, half, lambda copy: copy.wait())
 
-        low, high = (pl.ds(pl.multiple_of((2 * half + n) * ROWS, ROWS), ROWS) for n in range(2))
-        held = there(half, 0, low, width)
-        ahead = there(half, 1, high, width)
-        back(half, 0, low, width, held)
-        back(half, 1, high, width, ahead)
+        def run(n):
+            return half, n, pl.ds(pl.multiple_of(half * HALF + n * ROWS, ROWS), ROWS), width
+
+        def one(n, carry):
+            back(*run(n), there(*run(n)))
+            return carry
+
+        if width < BLOCK:
+            lax.fori_loop(0, HALF // ROWS, one, 0)
+        else:
+            held = there(*run(0))
+            ahead = there(*run(1))
+            back(*run(0), held)
+            back(*run(1), ahead)
         moved(j, half, lambda copy: copy.start())
         return carry
 
-    lax.fori_loop(0, tokens // (2 * ROWS), two, 0)
+    lax.fori_loop(0, tokens // HALF, two, 0)
 
 
 def forward_kernel(tail, own, x_ref, wg_ref, wu_ref, wd_ref, *refs):
@@ -130,7 +139,7 @@
         g = dot(a, wg_ref[0, :, :width], NN)
         u = dot(a, wu_ref[0, :, :width], NN)
         for k, value in enumerate((g, u)):
-            stage_ref[half, k, n * ROWS : (n + 1) * ROWS, :width] = value
+            stage_ref[half, k, pl.ds(pl.multiple_of(n * ROWS, ROWS), ROWS), :width] = value
         return (g * sigmoid(g) * u).astype(BF16)
 
     def down(half, n, r, width, hid):
@@ -156,14 +165,14 @@
         for n in range(2):
             leave(n, pl.ds(0, tokens)).wait()
         early.wait()
-        for half in range(tokens // (2 * ROWS)):
+        for half in range(tokens // (HALF)):
             moved(j, half, lambda copy: copy.wait())
 
 
 def keeping(tokens, count, columns, dtype):
     kept = [jax.ShapeDtypeStruct((count, tokens, columns), dtype)] * 2
-    parts = tokens // (2 * ROWS)
-    return kept, [pltpu.VMEM((parts, count, 2 * ROWS, BLOCK), dtype), pltpu.SemaphoreType.DMA((2, parts))]
+    parts = tokens // (HALF)
+    return kept, [pltpu.VMEM((parts, count, HALF, BLOCK), dtype), pltpu.SemaphoreType.DMA((2, parts))]
 
 
 def forward(own, x, wg, wu, wd):
@@ -218,10 +227,10 @@
         g = dot(a, wg_ref[0, :, :width], NN)
         u = dot(a, wu_ref[0, :, :width], NN)
         for k, value in enumerate(hidden_back(g, u, dot(dy, wd_ref[0, :width, :], NT))):
-            stage_ref[half, k, n * ROWS : (n + 1) * ROWS, :width] = value
+            stage_ref[half, k, pl.ds(pl.multiple_of(n * ROWS, ROWS), ROWS), :width] = value
 
     def back(half, n, r, width, held):
-        dg, du = (stage_ref[half, k, n * ROWS : (n + 1) * ROWS, :width] for k in range(2))
+        dg, du = (stage_ref[half, k, pl.ds(pl.multiple_of(n * ROWS, ROWS), ROWS), :width] for k in range(2))
         acc_ref[r, :] += dot(dg, wg_ref[0, :, :width], NT) + dot(du, wu_ref[0, :, :width], NT)
 
     @pl.when(j < last)
@@ -244,7 +253,7 @@
 
         looped(tokens // FEW, FEW, end, TOGETHER, lambda r: leave(r).start())
         leave(pl.ds(0, tokens)).wait()
-        for half in range(tokens // (2 * ROWS)):
+        for half in range(tokens // (HALF)):
             moved(j, half, lambda copy: copy.wait())
 
 
@@ -533,7 +542,7 @@
 def adam(own, factor, arrays, pieces, outs):
     d, _ = arrays[0][0].shape[1:]
     main, extra = own // BLOCK * BLOCK, own % BLOCK
-    shapes = ((LANES, own), (LANES, d), (d, LANES))
+    shapes = ((LANES, own), (LANES, d), (d // 2, LANES))
     rows = []
     for n, (which, layer, slot, g) in enumerate(pieces):
         kind = 1 if which == 2 else 2 if slot == 4 else 0
@@ -650,6 +659,9 @@
 
     any_ = pl.BlockSpec(memory_space=pl.ANY)
     given = [a for three in arrays for a in three]
+    given = [pltpu.with_memory_space_constraint(a, pltpu.HBM) for a in given]
+    if outs is None:
+        pieces = [(*piece[:3], pltpu.with_memory_space_constraint(piece[3], pltpu.HBM)) for piece in pieces]
     before = [a for three in outs for a in three] if outs is not None else []
     elements = sum(piece[3].size for piece in pieces)
     new = pl.pallas_call(
@@ -661,7 +673,7 @@
         + [pltpu.SemaphoreType.DMA((4, SLOTS)), pltpu.SemaphoreType.DMA((3, SLOTS))],
         input_output_aliases={2 + n_in + n: n for n in range(len(before))},
         cost_estimate=pl.CostEstimate(flops=2000 * elements, bytes_accessed=22 * elements, transcendentals=elements),
-        compiler_params=params(),
+        compiler_params=params(30),
     )(table, factor, *given, *(piece[3] for piece in pieces), *before)
     return tuple(tuple(new[3 * n : 3 * n + 3]) for n in range(3))
 

time: 772 us -> 766 us (level)
  no operation moved by 1% of the time
where the time goes in v12:
time: 766 us
  Pallas kernels  624 us (81%)
  waiting for transfers between devices  122 us (16%)
  starting transfers between devices  17.5 us (2%)
    pallas_call x2, Pallas kernels, slices(): pl.pallas_call(lambda *refs: slices_kernel(layer, own, kept[0].shape[0],...  238 us
    pallas_call x4, Pallas kernels, adam(): pl.pallas_call(kernel, in_specs=[pl.BlockSpec(memory_space=pltpu.SMEM), p...  184 us
    pallas_call x1, Pallas kernels, chain(): pl.pallas_call(lambda *refs: chain_kernel(tail, own, *refs), grid=(steps,...  126 us
    ppermute x10, waiting for transfers between devices, px(): return lax.ppermute(a, 'dp', PX)  115 us
    pallas_call x1, Pallas kernels, forward(): pl.pallas_call(lambda *refs: forward_kernel(tail, own, *refs), grid=(step...  77 us
  transfers between devices with their start and end apart: 22, of which 7 were waited for; matrix products, arithmetic and copies ran while one was open for 0% of the time, Pallas kernels for 70%

profile of v12, /device:TPU:0, one launch (start us, length us, event | category | flops | bytes accessed | tf_op | source)
XLA Modules:
  0.0 765.8 jit_solution(11518035725010488309)
XLA Ops:
  0.6 77.0 %forward.1 = (bf16[2048,896]{1,0:T(8,128)(2,1)}, bf16[2048,896]{1,0:T(8,128)(2,1)}, bf16[2048,896]{1,0:T(8,128)(2,1)}, f32[2,2048,1280]{2,1,0:T(8,128)}, f32[2,2048,1280]{2,1,0:T(8,128)}) custom-call(bf16[2048,896]{1,0:T(8,128)(2,1)} %bitcast.2, bf16[2,896,4736]{2,1,0:T(8,128)(2,1)} %refs_0_.7, bf16[2,896,4736]{2,1,0:T(8,128)(2,1)} %refs_3_.11, ...), custom_call_target="tpu_custom_call" | custom-call | flops 52143587328 | bytes 25460736 | tf_op jit(solution)/shard_map/forward/pallas_call | solution.py:187
  77.7 3.3 collective-permute-start.2
  81.0 125.7 %chain.1 = (bf16[2048,896]{1,0:T(8,128)(2,1)}, bf16[3,2048,1280]{2,1,0:T(8,128)(2,1)}, bf16[3,2048,1280]{2,1,0:T(8,128)(2,1)}) custom-call(bf16[2048,896]{1,0:T(8,128)(2,1)} %get-tuple-element.79.refs_0_, bf16[2048,896]{1,0:T(8,128)(2,1)} %bitcast.4, bf16[2048,896]{1,0:T(8,128)(2,1)} %get-tuple-element.80.refs_2_, bf16[2,896,4736]{2,1,0:T(8,128)(2,1)} %refs_0_.7, ...), custom_call_target="tpu_custom_call" | custom-call | flops 86905978880 | bytes 25460736 | tf_op jit(solution)/shard_map/chain/pallas_call | solution.py:269
  206.7 2.0 collective-permute-start.1
  208.8 31.4 %collective-permute-done.3.refs_3_ = bf16[2048,896]{1,0:T(8,128)(2,1)} collective-permute-done((bf16[2048,896]{1,0:T(8,128)(2,1)}, bf16[2048,896]{1,0:T(8,128)(2,1)}, u32[]{:S(2)}, u32[]{:S(2)}) %collective-permute-start.3) | collective-permute-done | bytes 3670048 | tf_op jit(solution)/shard_map/ppermute | solution.py:29
  240.1 106.6 %slices.2 = (bf16[896,1152]{1,0:T(8,128)(2,1)}, bf16[896,1152]{1,0:T(8,128)(2,1)}, bf16[1152,896]{1,0:T(8,128)(2,1)}, bf16[896,128]{1,0:T(8,128)(2,1)}, bf16[896...) custom-call(bf16[2048,896]{1,0:T(8,128)(2,1)} %get-tuple-element.79., ...), custom_call_target="tpu_custom_call" | custom-call | flops 112742891520 | bytes 29360128 | tf_op jit(solution)/shard_map/slices/pallas_call | solution.py:507
  346.7 1.9 collective-permute-start.4
  348.7 0.1 collective-permute-start.6
  348.8 0.4 collective-permute-start.14
  349.2 48.3 %collective-permute-done.refs_1_ = bf16[2048,896]{1,0:T(8,128)(2,1)} collective-permute-done((bf16[2048,896]{1,0:T(8,128)(2,1)}, bf16[2048,896]{1,0:T(8,128)(2,1)}, u32[]{:S(2)}, u32[]{:S(2)}) %collective-permute-start) | collective-permute-done | bytes 3670048 | tf_op jit(solution)/shard_map/ppermute | solution.py:29
  397.4 2.0 collective-permute-start.8
  399.5 131.2 %slices.3 = (bf16[896,1152]{1,0:T(8,128)(2,1)}, bf16[896,1152]{1,0:T(8,128)(2,1)}, bf16[1152,896]{1,0:T(8,128)(2,1)}, bf16[896,128]{1,0:T(8,128)(2,1)}, bf16[896...) custom-call(bf16[2048,896]{1,0:T(8,128)(2,1)} %get-tuple-element.78., ...), custom_call_target="tpu_custom_call" | custom-call | flops 112742891520 | bytes 29360128 | tf_op jit(solution)/shard_map/slices/pallas_call | solution.py:507
  530.7 0.1 collective-permute-start.15
  530.8 0.4 collective-permute-start.10
  531.3 0.4 collective-permute-start.12
  531.7 1.7 collective-permute-start.18
  533.5 1.5 collective-permute-done.15.refs_14_
  535.0 1.7 collective-permute-start.16
  536.8 1.2 collective-permute-done.10.refs_12_
  538.0 1.7 collective-permute-start.19
  539.7 1.2 collective-permute-done.11.refs_13_
  540.9 0.1 collective-permute-start.5
  541.1 2.8 collective-permute-done.12.refs_14_
  543.9 0.1 collective-permute-start.7
  544.0 35.7 %collective-permute-done.18.refs_9_ = bf16[896,1152]{1,0:T(8,128)(2,1)S(1)} collective-permute-done((bf16[896,1152]{1,0:T(8,128)(2,1)}, bf16[896,1152]{1,0:T(8,128)(2,1)S(1)}, u32[]{:S(2)}, u32[]{:S(2)}) %collective-permute-start.18) | collective-permute-done | bytes 2064416 | tf_op jit(solution)/shard_map/ppermute | solution.py:29
  579.8 0.7 copy-done
  580.4 95.4 %shard_map.214 = (bf16[2,896,4736]{2,1,0:T(8,128)(2,1)}, f32[2,896,4736]{2,1,0:T(8,128)}, f32[2,896,4736]{2,1,0:T(8,128)}, bf16[2,896,4736]{2,1,0:T(8,128)(2,1)}...) custom-call(s32[8,102]{1,0:T(8,128)S(1)} %copy-done.3, ...), custom_call_target="tpu_custom_call" | custom-call | flops 26148864000 | bytes 287637504 | tf_op jit(solution)/shard_map/pallas_call | solution.py:667
  675.9 0.5 collective-permute-start.20
  676.5 43.3 %shard_map.215 = (bf16[2,896,4736]{2,1,0:T(8,128)(2,1)}, f32[2,896,4736]{2,1,0:T(8,128)}, f32[2,896,4736]{2,1,0:T(8,128)}, bf16[2,896,4736]{2,1,0:T(8,128)(2,1)}...) custom-call(s32[8,46]{1,0:T(8,128)S(1)} %copy-done.2, ...), custom_call_target="tpu_custom_call", output_to_operand_aliasing={{0}: (17, {}), {1}: (18, {}), {2}: (19, {}), {3}: (20, {}),... | custom-call | flops 12386304000 | bytes 136249344 | tf_op jit(solution)/shard_map/pallas_call | solution.py:667
  719.8 0.5 collective-permute-start.17
  720.3 36.3 %shard_map.216 = (bf16[2,896,4736]{2,1,0:T(8,128)(2,1)}, f32[2,896,4736]{2,1,0:T(8,128)}, f32[2,896,4736]{2,1,0:T(8,128)}, bf16[2,896,4736]{2,1,0:T(8,128)(2,1)}...) custom-call(s32[8,37]{1,0:T(8,128)S(1)} %copy-done.1, ...), custom_call_target="tpu_custom_call", output_to_operand_aliasing={{0}: (16, {}), {1}: (17, {}), {2}: (18, {}), {3}: (19, {}),... | custom-call | flops 10321920000 | bytes 113541120 | tf_op jit(solution)/shard_map/pallas_call | solution.py:667
  756.6 9.0 %shard_map.217 = (bf16[2,896,4736]{2,1,0:T(8,128)(2,1)}, f32[2,896,4736]{2,1,0:T(8,128)}, f32[2,896,4736]{2,1,0:T(8,128)}, bf16[2,896,4736]{2,1,0:T(8,128)(2,1)}...) custom-call(s32[8,9]{1,0:T(8,128)S(1)} %copy-done.4, ...), custom_call_target="tpu_custom_call", output_to_operand_aliasing={{0}: (12, {}), {1}: (13, {}), {2}: (14, {}), {3}: (15, {}),... | custom-call | flops 2064384000 | bytes 22708224 | tf_op jit(solution)/shard_map/pallas_call | solution.py:667
  (32 shorter events, 0.3 us)
Async XLA Ops:
  77.7 131.1 %collective-permute-start.2 = (bf16[2048,896]{1,0:T(8,128)(2,1)}, bf16[2048,896]{1,0:T(8,128)(2,1)}, u32[]{:S(2)}, u32[]{:S(2)}) collective-permute-start(bf16[2048,896]{1,0:T(8,128)(2,1)} %get-tuple-element.79.refs_0_), channel_id=1, source_target_pairs={{0,2},{1,3},{2,0},{3,1},{4,6},{5,7},{6,4},{7,5}} | collective-permute-start | bytes 11010056 | tf_op jit(solution)/shard_map/ppermute | solution.py:29
  81.0 159.2 %collective-permute-start.3 = (bf16[2048,896]{1,0:T(8,128)(2,1)}, bf16[2048,896]{1,0:T(8,128)(2,1)}, u32[]{:S(2)}, u32[]{:S(2)}) collective-permute-start(bf16[2048,896]{1,0:T(8,128)(2,1)} %bitcast.3), channel_id=1, source_target_pairs={{0,2},{1,3},{2,0},{3,1},{4,6},{5,7},{6,4},{7,5}} | collective-permute-start | bytes 11010056 | tf_op jit(solution)/shard_map/ppermute | solution.py:29
  206.7 142.1 %collective-permute-start.1 = (bf16[2048,896]{1,0:T(8,128)(2,1)}, bf16[2048,896]{1,0:T(8,128)(2,1)}, u32[]{:S(2)}, u32[]{:S(2)}) collective-permute-start(bf16[2048,896]{1,0:T(8,128)(2,1)} %get-tuple-element.81.refs_2_), channel_id=1, source_target_pairs={{0,2},{1,3},{2,0},{3,1},{4,6},{5,7},{6,4},{7,5}} | collective-permute-start | bytes 11010056 | tf_op jit(solution)/shard_map/ppermute | solution.py:29
  208.7 188.7 %collective-permute-start = (bf16[2048,896]{1,0:T(8,128)(2,1)}, bf16[2048,896]{1,0:T(8,128)(2,1)}, u32[]{:S(2)}, u32[]{:S(2)}) collective-permute-start(bf16[2048,896]{1,0:T(8,128)(2,1)} %get-tuple-element.78.refs_0_), channel_id=1, source_target_pairs={{0,2},{1,3},{2,0},{3,1},{4,6},{5,7},{6,4},{7,5}} | collective-permute-start | bytes 11010056 | tf_op jit(solution)/shard_map/ppermute | solution.py:29
  346.7 183.9 %collective-permute-start.4 = (bf16[896,1152]{1,0:T(8,128)(2,1)}, bf16[896,1152]{1,0:T(8,128)(2,1)}, u32[]{:S(2)}, u32[]{:S(2)}) collective-permute-start(bf16[896,1152]{1,0:T(8,128)(2,1)} %get-tuple-element.89.refs_9_), channel_id=1, source_target_pairs={{0,2},{1,3},{2,0},{3,1},{4,6},{5,7},{6,4},{7,5}} | collective-permute-start | bytes 6193160 | tf_op jit(solution)/shard_map/ppermute | solution.py:29
  348.7 182.7 %collective-permute-start.13 = (bf16[896,1152]{1,0:T(8,128)(2,1)}, bf16[896,1152]{1,0:T(8,128)(2,1)}, u32[]{:S(2)}, u32[]{:S(2)}) collective-permute-start(bf16[896,1152]{1,0:T(8,128)(2,1)} %get-tuple-element.89.refs_9_), channel_id=1, source_target_pairs={{0,1},{1,0},{2,3},{3,2},{4,5},{5,4},{6,7},{7,6}} | collective-permute-start | bytes 6193160 | tf_op jit(solution)/shard_map/ppermute | solution.py:33
  348.7 182.2 %collective-permute-start.6 = (bf16[896,1152]{1,0:T(8,128)(2,1)}, bf16[896,1152]{1,0:T(8,128)(2,1)}, u32[]{:S(2)}, u32[]{:S(2)}) collective-permute-start(bf16[896,1152]{1,0:T(8,128)(2,1)} %get-tuple-element.90.refs_10_), channel_id=1, source_target_pairs={{0,2},{1,3},{2,0},{3,1},{4,6},{5,7},{6,4},{7,5}} | collective-permute-start | bytes 6193160 | tf_op jit(solution)/shard_map/ppermute | solution.py:29
  348.8 183.0 %collective-permute-start.14 = (bf16[896,1152]{1,0:T(8,128)(2,1)}, bf16[896,1152]{1,0:T(8,128)(2,1)}, u32[]{:S(2)}, u32[]{:S(2)}) collective-permute-start(bf16[896,1152]{1,0:T(8,128)(2,1)} %get-tuple-element.90.refs_10_), channel_id=1, source_target_pairs={{0,1},{1,0},{2,3},{3,2},{4,5},{5,4},{6,7},{7,6}} | collective-permute-start | bytes 6193160 | tf_op jit(solution)/shard_map/ppermute | solution.py:33
  397.4 133.8 %collective-permute-start.8 = (bf16[1152,896]{1,0:T(8,128)(2,1)}, bf16[1152,896]{1,0:T(8,128)(2,1)}, u32[]{:S(2)}, u32[]{:S(2)}) collective-permute-start(bf16[1152,896]{1,0:T(8,128)(2,1)} %get-tuple-element.91.refs_11_), channel_id=1, source_target_pairs={{0,2},{1,3},{2,0},{3,1},{4,6},{5,7},{6,4},{7,5}} | collective-permute-start | bytes 6193160 | tf_op jit(solution)/shard_map/ppermute | solution.py:29
  399.5 180.3 %copy-start.3 = (s32[8,102]{1,0:T(8,128)S(1)}, s32[8,102]{1,0:T(8,128)}, u32[]{:S(2)}) copy-start(s32[8,102]{1,0:T(8,128)} %constant.8.clone.table_ref) | copy-start | bytes 9796
  530.7 4.3 collective-permute-start.15
  530.8 7.2 collective-permute-start.10
  531.2 9.7 %collective-permute-start.11 = (bf16[896,1152]{1,0:T(8,128)(2,1)}, bf16[896,1152]{1,0:T(8,128)(2,1)S(1)}, u32[]{:S(2)}, u32[]{:S(2)}) collective-permute-start(bf16[896,1152]{1,0:T(8,128)(2,1)} %get-tuple-element.93.refs_19_), channel_id=1, source_target_pairs={{0,1},{1,0},{2,3},{3,2},{4,5},{5,4},{6,7},{7,6}} | collective-permute-start | bytes 6193160 | tf_op jit(solution)/shard_map/ppermute | solution.py:33
  531.3 12.5 %collective-permute-start.12 = (bf16[1152,896]{1,0:T(8,128)(2,1)}, bf16[1152,896]{1,0:T(8,128)(2,1)S(1)}, u32[]{:S(2)}, u32[]{:S(2)}) collective-permute-start(bf16[1152,896]{1,0:T(8,128)(2,1)} %get-tuple-element.94.refs_20_), channel_id=1, source_target_pairs={{0,1},{1,0},{2,3},{3,2},{4,5},{5,4},{6,7},{7,6}} | collective-permute-start | bytes 6193160 | tf_op jit(solution)/shard_map/ppermute | solution.py:33
  531.7 48.0 %collective-permute-start.18 = (bf16[896,1152]{1,0:T(8,128)(2,1)}, bf16[896,1152]{1,0:T(8,128)(2,1)S(1)}, u32[]{:S(2)}, u32[]{:S(2)}) collective-permute-start(bf16[896,1152]{1,0:T(8,128)(2,1)} %get-tuple-element.92.refs_18_), channel_id=1, source_target_pairs={{0,2},{1,3},{2,0},{3,1},{4,6},{5,7},{6,4},{7,5}} | collective-permute-start | bytes 6193160 | tf_op jit(solution)/shard_map/ppermute | solution.py:29
  535.0 44.7 %copy-start.5 = (bf16[1152,896]{1,0:T(8,128)(2,1)}, bf16[1152,896]{1,0:T(8,128)(2,1)S(1)}, u32[]{:S(2)}) copy-start(bf16[1152,896]{1,0:T(8,128)(2,1)S(1)} %collective-permute-done.15.refs_14_) | copy-start | bytes 6193156
  535.0 184.8 %collective-permute-start.16 = (bf16[1152,896]{1,0:T(8,128)(2,1)}, bf16[1152,896]{1,0:T(8,128)(2,1)}, u32[]{:S(2)}, u32[]{:S(2)}) collective-permute-start(bf16[1152,896]{1,0:T(8,128)(2,1)} %get-tuple-element.94.refs_20_), channel_id=1, source_target_pairs={{0,2},{1,3},{2,0},{3,1},{4,6},{5,7},{6,4},{7,5}} | collective-permute-start | bytes 6193160 | tf_op jit(solution)/shard_map/ppermute | solution.py:29
  538.0 137.9 %collective-permute-start.19 = (bf16[896,1152]{1,0:T(8,128)(2,1)}, bf16[896,1152]{1,0:T(8,128)(2,1)S(1)}, u32[]{:S(2)}, u32[]{:S(2)}) collective-permute-start(bf16[896,1152]{1,0:T(8,128)(2,1)} %get-tuple-element.93.refs_19_), channel_id=1, source_target_pairs={{0,2},{1,3},{2,0},{3,1},{4,6},{5,7},{6,4},{7,5}} | collective-permute-start | bytes 6193160 | tf_op jit(solution)/shard_map/ppermute | solution.py:29
  540.9 135.5 %collective-permute-start.5 = (bf16[896,1152]{1,0:T(8,128)(2,1)}, bf16[896,1152]{1,0:T(8,128)(2,1)S(1)}, u32[]{:S(2)}, u32[]{:S(2)}) collective-permute-start(bf16[896,1152]{1,0:T(8,128)(2,1)} %collective-permute-done.4.refs_15_), channel_id=1, source_target_pairs={{0,1},{1,0},{2,3},{3,2},{4,5},{5,4},{6,7},{7,6}} | collective-permute-start | bytes 6193160 | tf_op jit(solution)/shard_map/ppermute | solution.py:33
  543.9 132.6 %collective-permute-start.7 = (bf16[896,1152]{1,0:T(8,128)(2,1)}, bf16[896,1152]{1,0:T(8,128)(2,1)S(1)}, u32[]{:S(2)}, u32[]{:S(2)}) collective-permute-start(bf16[896,1152]{1,0:T(8,128)(2,1)} %collective-permute-done.6.refs_16_), channel_id=1, source_target_pairs={{0,1},{1,0},{2,3},{3,2},{4,5},{5,4},{6,7},{7,6}} | collective-permute-start | bytes 6193160 | tf_op jit(solution)/shard_map/ppermute | solution.py:33
  579.8 96.7 %collective-permute-start.9 = (bf16[1152,896]{1,0:T(8,128)(2,1)}, bf16[1152,896]{1,0:T(8,128)(2,1)S(1)}, u32[]{:S(2)}, u32[]{:S(2)}) collective-permute-start(bf16[1152,896]{1,0:T(8,128)(2,1)} %collective-permute-done.8.refs_17_), channel_id=1, source_target_pairs={{0,1},{1,0},{2,3},{3,2},{4,5},{5,4},{6,7},{7,6}} | collective-permute-start | bytes 6193160 | tf_op jit(solution)/shard_map/ppermute | solution.py:33
  579.8 0.7 copy-start
  580.4 96.0 %copy-start.2 = (s32[8,46]{1,0:T(8,128)S(1)}, s32[8,46]{1,0:T(8,128)}, u32[]{:S(2)}) copy-start(s32[8,46]{1,0:T(8,128)} %constant.9.clone.table_ref) | copy-start | bytes 4420
  675.9 44.4 %collective-permute-start.20 = (bf16[896,1152]{1,0:T(8,128)(2,1)S(1)}, bf16[896,1152]{1,0:T(8,128)(2,1)S(1)}, u32[]{:S(2)}, u32[]{:S(2)}) collective-permute-start(bf16[896,1152]{1,0:T(8,128)(2,1)S(1)} %collective-permute-done.18.refs_9_), channel_id=1, source_target_pairs={{0,1},{1,0},{2,3},{3,2},{4,5},{5,4},{6,7},{7,6}} | collective-permute-start | bytes 6193160 | tf_op jit(solution)/shard_map/ppermute | solution.py:33
  676.4 43.9 %collective-permute-start.21 = (bf16[896,1152]{1,0:T(8,128)(2,1)S(1)}, bf16[896,1152]{1,0:T(8,128)(2,1)S(1)}, u32[]{:S(2)}, u32[]{:S(2)}) collective-permute-start(bf16[896,1152]{1,0:T(8,128)(2,1)S(1)} %collective-permute-done.19.refs_10_), channel_id=1, source_target_pairs={{0,1},{1,0},{2,3},{3,2},{4,5},{5,4},{6,7},{7,6}} | collective-permute-start | bytes 6193160 | tf_op jit(solution)/shard_map/ppermute | solution.py:33
  676.4 43.9 %copy-start.1 = (s32[8,37]{1,0:T(8,128)S(1)}, s32[8,37]{1,0:T(8,128)}, u32[]{:S(2)}) copy-start(s32[8,37]{1,0:T(8,128)} %constant.10.clone.table_ref) | copy-start | bytes 3556
  719.8 36.8 %copy-start.4 = (s32[8,9]{1,0:T(8,128)S(1)}, s32[8,9]{1,0:T(8,128)}, u32[]{:S(2)}) copy-start(s32[8,9]{1,0:T(8,128)} %constant.11.clone.table_ref) | copy-start | bytes 868
  719.8 36.8 %collective-permute-start.17 = (bf16[1152,896]{1,0:T(8,128)(2,1)}, bf16[1152,896]{1,0:T(8,128)(2,1)S(1)}, u32[]{:S(2)}, u32[]{:S(2)}) collective-permute-start(bf16[1152,896]{1,0:T(8,128)(2,1)} %collective-permute-done.16.refs_11_), channel_id=1, source_target_pairs={{0,1},{1,0},{2,3},{3,2},{4,5},{5,4},{6,7},{7,6}} | collective-permute-start | bytes 6193160 | tf_op jit(solution)/shard_map/ppermute | solution.py:33

commit v13 on v12

--- a/solution.py
+++ b/solution.py
@@ -279,6 +279,9 @@
     )(a, dy, h, wg, wu, wd)
 
 
+GATE_UP, DOWN = (0, 1), (2,)
+
+
 def slices_kernel(layer, own, kept, count, *refs):
     me = lax.axis_index("dp")
     chip, core = me // 2, me % 2
@@ -318,7 +321,7 @@
                 if held is not None:
                     do(pltpu.make_async_copy(held.at[:, rows, :], held_buf.at[slot], sems.at[2, slot]))
 
-    def weights():
+    def weights(which):
         extra = own - main
         parts = (
             (pl.ds(pl.multiple_of(me * main, LANES), main), pl.ds(0, main)),
@@ -328,6 +331,7 @@
         return [
             pltpu.make_async_copy(*((hbm.at[layer, there, :], ref.at[here, :]) if n == 2 else (hbm.at[layer, :, there], ref.at[:, here])), w_sems.at[n, m])
             for n, (hbm, ref) in enumerate(((wg_hbm, wg_ref), (wu_hbm, wu_ref), (wd_hbm, wd_ref)))
+            if n in which
             for m, (there, here) in enumerate(parts)
         ]
 
@@ -364,14 +368,18 @@
     def _():
         for other in spoken:
             pl.semaphore_signal(barrier, inc=1, device_id={"dp": other}, device_id_type=pl.DeviceIdType.MESH)
+        for copy in weights(DOWN) if kept == 2 else ():
+            copy.start()
         fetch(i, lambda copy: copy.start())
-        for copy in weights():
+        for copy in weights(GATE_UP if kept == 2 else GATE_UP + DOWN):
             copy.start()
-        for copy in weights():
+        for copy in weights(DOWN) if kept == 2 else ():
             copy.wait()
 
     @pl.when(i == 1)
     def _():
+        for copy in weights(GATE_UP if kept == 2 else GATE_UP + DOWN):
+            copy.wait()
         pl.semaphore_wait(barrier, len(spoken))
         for which in (1, 0):
             for copy in onward(which):
@@ -474,7 +482,10 @@
         at = [3 * ((core + s) % 2) + (chip + s // 2) % 2 * (1 - 2 * ((core + s) % 2)) for s in range(4)]
         place = [(core + s) % 2 + 2 * ((chip + s // 2) % 2) for s in range(4)]
         sums = [lax.fori_loop(0, a_buf.shape[2] // LANES, rows, jnp.zeros((8, LANES), F32)), jnp.zeros((8, LANES), F32)]
+        sums_ref[0] = sums[0] + before[0][...] if final else sums[0]
         lax.fori_loop(0, own // LANES, turn, 0)
+        for n in range(len(others)) if final else ():
+            told(n).start()
         for n, term in enumerate(terms):
             part, sums[1] = rounded(term[at[0]] + term[at[1]] + term[at[2]] + term[at[3]], sums[1])
             outs[3 + n][...] = part if n < 2 else part.T
@@ -483,11 +494,8 @@
         if not final:
             outs[6][...], outs[7][...] = sums
         else:
-            sums_ref[0] = sums[0] + before[0][...]
             shared = jnp.sum(sums[1] + before[1][...])
-            for n in range(3):
-                told(n).start()
-            for n in range(3):
+            for n in range(len(others)):
                 told(n).wait()
             total = sums_ref[place[0]] + sums_ref[place[1]] + sums_ref[place[2]] + sums_ref[place[3]]
             total = jnp.full((8, LANES), jnp.sum(total) + shared, F32)

time: 766 us -> 766 us (level)
  no operation moved by 1% of the time
where the time goes in v13:
time: 766 us
  Pallas kernels  623 us (81%)
  waiting for transfers between devices  124 us (16%)
  starting transfers between devices  17.6 us (2%)
    pallas_call x2, Pallas kernels, slices(): pl.pallas_call(lambda *refs: slices_kernel(layer, own, kept[0].shape[0],...  236 us
    pallas_call x4, Pallas kernels, adam(): pl.pallas_call(kernel, in_specs=[pl.BlockSpec(memory_space=pltpu.SMEM), p...  184 us
    pallas_call x1, Pallas kernels, chain(): pl.pallas_call(lambda *refs: chain_kernel(tail, own, *refs), grid=(steps,...  126 us
    ppermute x10, waiting for transfers between devices, px(): return lax.ppermute(a, 'dp', PX)  117 us
    pallas_call x1, Pallas kernels, forward(): pl.pallas_call(lambda *refs: forward_kernel(tail, own, *refs), grid=(step...  77 us
  transfers between devices with their start and end apart: 22, of which 7 were waited for; matrix products, arithmetic and copies ran while one was open for 0% of the time, Pallas kernels for 70%

profile of v13, /device:TPU:0, one launch (start us, length us, event | category | flops | bytes accessed | tf_op | source)
XLA Modules:
  0.0 765.8 jit_solution(11483668772857908920)
XLA Ops:
  0.6 77.0 %forward.1 = (bf16[2048,896]{1,0:T(8,128)(2,1)}, bf16[2048,896]{1,0:T(8,128)(2,1)}, bf16[2048,896]{1,0:T(8,128)(2,1)}, f32[2,2048,1280]{2,1,0:T(8,128)}, f32[2,2048,1280]{2,1,0:T(8,128)}) custom-call(bf16[2048,896]{1,0:T(8,128)(2,1)} %bitcast.2, bf16[2,896,4736]{2,1,0:T(8,128)(2,1)} %refs_0_.7, bf16[2,896,4736]{2,1,0:T(8,128)(2,1)} %refs_3_.11, ...), custom_call_target="tpu_custom_call" | custom-call | flops 52143587328 | bytes 25460736 | tf_op jit(solution)/shard_map/forward/pallas_call | solution.py:187
  77.7 3.3 collective-permute-start.2
  81.0 125.7 %chain.1 = (bf16[2048,896]{1,0:T(8,128)(2,1)}, bf16[3,2048,1280]{2,1,0:T(8,128)(2,1)}, bf16[3,2048,1280]{2,1,0:T(8,128)(2,1)}) custom-call(bf16[2048,896]{1,0:T(8,128)(2,1)} %get-tuple-element.79.refs_0_, bf16[2048,896]{1,0:T(8,128)(2,1)} %bitcast.4, bf16[2048,896]{1,0:T(8,128)(2,1)} %get-tuple-element.80.refs_2_, bf16[2,896,4736]{2,1,0:T(8,128)(2,1)} %refs_0_.7, ...), custom_call_target="tpu_custom_call" | custom-call | flops 86905978880 | bytes 25460736 | tf_op jit(solution)/shard_map/chain/pallas_call | solution.py:269
  206.7 2.0 collective-permute-start.1
  208.8 31.4 %collective-permute-done.3.refs_3_ = bf16[2048,896]{1,0:T(8,128)(2,1)} collective-permute-done((bf16[2048,896]{1,0:T(8,128)(2,1)}, bf16[2048,896]{1,0:T(8,128)(2,1)}, u32[]{:S(2)}, u32[]{:S(2)}) %collective-permute-start.3) | collective-permute-done | bytes 3670048 | tf_op jit(solution)/shard_map/ppermute | solution.py:29
  240.1 105.1 %slices.2 = (bf16[896,1152]{1,0:T(8,128)(2,1)}, bf16[896,1152]{1,0:T(8,128)(2,1)}, bf16[1152,896]{1,0:T(8,128)(2,1)}, bf16[896,128]{1,0:T(8,128)(2,1)}, bf16[896...) custom-call(bf16[2048,896]{1,0:T(8,128)(2,1)} %get-tuple-element.79., ...), custom_call_target="tpu_custom_call" | custom-call | flops 112742891520 | bytes 29360128 | tf_op jit(solution)/shard_map/slices/pallas_call | solution.py:515
  345.3 2.0 collective-permute-start.4
  347.4 0.4 collective-permute-start.14
  347.8 49.6 %collective-permute-done.refs_1_ = bf16[2048,896]{1,0:T(8,128)(2,1)} collective-permute-done((bf16[2048,896]{1,0:T(8,128)(2,1)}, bf16[2048,896]{1,0:T(8,128)(2,1)}, u32[]{:S(2)}, u32[]{:S(2)}) %collective-permute-start) | collective-permute-done | bytes 3670048 | tf_op jit(solution)/shard_map/ppermute | solution.py:29
  397.4 2.0 collective-permute-start.8
  399.5 131.2 %slices.3 = (bf16[896,1152]{1,0:T(8,128)(2,1)}, bf16[896,1152]{1,0:T(8,128)(2,1)}, bf16[1152,896]{1,0:T(8,128)(2,1)}, bf16[896,128]{1,0:T(8,128)(2,1)}, bf16[896...) custom-call(bf16[2048,896]{1,0:T(8,128)(2,1)} %get-tuple-element.78., ...), custom_call_target="tpu_custom_call" | custom-call | flops 112742891520 | bytes 29360128 | tf_op jit(solution)/shard_map/slices/pallas_call | solution.py:515
  530.7 0.1 collective-permute-start.15
  530.8 0.4 collective-permute-start.10
  531.2 0.1 collective-permute-start.11
  531.3 0.4 collective-permute-start.12
  531.7 1.7 collective-permute-start.18
  533.5 1.5 collective-permute-done.15.refs_14_
  535.0 1.7 collective-permute-start.16
  536.8 1.2 collective-permute-done.10.refs_12_
  538.0 1.7 collective-permute-start.19
  539.7 1.2 collective-permute-done.11.refs_13_
  540.9 0.1 collective-permute-start.5
  541.1 2.8 collective-permute-done.12.refs_14_
  543.9 0.1 collective-permute-start.7
  544.0 35.7 %collective-permute-done.18.refs_9_ = bf16[896,1152]{1,0:T(8,128)(2,1)S(1)} collective-permute-done((bf16[896,1152]{1,0:T(8,128)(2,1)}, bf16[896,1152]{1,0:T(8,128)(2,1)S(1)}, u32[]{:S(2)}, u32[]{:S(2)}) %collective-permute-start.18) | collective-permute-done | bytes 2064416 | tf_op jit(solution)/shard_map/ppermute | solution.py:29
  579.8 0.7 copy-done
  580.4 95.4 %shard_map.214 = (bf16[2,896,4736]{2,1,0:T(8,128)(2,1)}, f32[2,896,4736]{2,1,0:T(8,128)}, f32[2,896,4736]{2,1,0:T(8,128)}, bf16[2,896,4736]{2,1,0:T(8,128)(2,1)}...) custom-call(s32[8,102]{1,0:T(8,128)S(1)} %copy-done.3, ...), custom_call_target="tpu_custom_call" | custom-call | flops 26148864000 | bytes 287637504 | tf_op jit(solution)/shard_map/pallas_call | solution.py:675
  675.9 0.5 collective-permute-start.20
  676.5 43.3 %shard_map.215 = (bf16[2,896,4736]{2,1,0:T(8,128)(2,1)}, f32[2,896,4736]{2,1,0:T(8,128)}, f32[2,896,4736]{2,1,0:T(8,128)}, bf16[2,896,4736]{2,1,0:T(8,128)(2,1)}...) custom-call(s32[8,46]{1,0:T(8,128)S(1)} %copy-done.2, ...), custom_call_target="tpu_custom_call", output_to_operand_aliasing={{0}: (17, {}), {1}: (18, {}), {2}: (19, {}), {3}: (20, {}),... | custom-call | flops 12386304000 | bytes 136249344 | tf_op jit(solution)/shard_map/pallas_call | solution.py:675
  719.8 0.5 collective-permute-start.17
  720.3 36.3 %shard_map.216 = (bf16[2,896,4736]{2,1,0:T(8,128)(2,1)}, f32[2,896,4736]{2,1,0:T(8,128)}, f32[2,896,4736]{2,1,0:T(8,128)}, bf16[2,896,4736]{2,1,0:T(8,128)(2,1)}...) custom-call(s32[8,37]{1,0:T(8,128)S(1)} %copy-done.1, ...), custom_call_target="tpu_custom_call", output_to_operand_aliasing={{0}: (16, {}), {1}: (17, {}), {2}: (18, {}), {3}: (19, {}),... | custom-call | flops 10321920000 | bytes 113541120 | tf_op jit(solution)/shard_map/pallas_call | solution.py:675
  756.6 9.0 %shard_map.217 = (bf16[2,896,4736]{2,1,0:T(8,128)(2,1)}, f32[2,896,4736]{2,1,0:T(8,128)}, f32[2,896,4736]{2,1,0:T(8,128)}, bf16[2,896,4736]{2,1,0:T(8,128)(2,1)}...) custom-call(s32[8,9]{1,0:T(8,128)S(1)} %copy-done.4, ...), custom_call_target="tpu_custom_call", output_to_operand_aliasing={{0}: (12, {}), {1}: (13, {}), {2}: (14, {}), {3}: (15, {}),... | custom-call | flops 2064384000 | bytes 22708224 | tf_op jit(solution)/shard_map/pallas_call | solution.py:675
  (32 shorter events, 0.3 us)
Async XLA Ops:
  77.7 131.1 %collective-permute-start.2 = (bf16[2048,896]{1,0:T(8,128)(2,1)}, bf16[2048,896]{1,0:T(8,128)(2,1)}, u32[]{:S(2)}, u32[]{:S(2)}) collective-permute-start(bf16[2048,896]{1,0:T(8,128)(2,1)} %get-tuple-element.79.refs_0_), channel_id=1, source_target_pairs={{0,2},{1,3},{2,0},{3,1},{4,6},{5,7},{6,4},{7,5}} | collective-permute-start | bytes 11010056 | tf_op jit(solution)/shard_map/ppermute | solution.py:29
  81.0 159.2 %collective-permute-start.3 = (bf16[2048,896]{1,0:T(8,128)(2,1)}, bf16[2048,896]{1,0:T(8,128)(2,1)}, u32[]{:S(2)}, u32[]{:S(2)}) collective-permute-start(bf16[2048,896]{1,0:T(8,128)(2,1)} %bitcast.3), channel_id=1, source_target_pairs={{0,2},{1,3},{2,0},{3,1},{4,6},{5,7},{6,4},{7,5}} | collective-permute-start | bytes 11010056 | tf_op jit(solution)/shard_map/ppermute | solution.py:29
  206.7 140.7 %collective-permute-start.1 = (bf16[2048,896]{1,0:T(8,128)(2,1)}, bf16[2048,896]{1,0:T(8,128)(2,1)}, u32[]{:S(2)}, u32[]{:S(2)}) collective-permute-start(bf16[2048,896]{1,0:T(8,128)(2,1)} %get-tuple-element.81.refs_2_), channel_id=1, source_target_pairs={{0,2},{1,3},{2,0},{3,1},{4,6},{5,7},{6,4},{7,5}} | collective-permute-start | bytes 11010056 | tf_op jit(solution)/shard_map/ppermute | solution.py:29
  208.7 188.7 %collective-permute-start = (bf16[2048,896]{1,0:T(8,128)(2,1)}, bf16[2048,896]{1,0:T(8,128)(2,1)}, u32[]{:S(2)}, u32[]{:S(2)}) collective-permute-start(bf16[2048,896]{1,0:T(8,128)(2,1)} %get-tuple-element.78.refs_0_), channel_id=1, source_target_pairs={{0,2},{1,3},{2,0},{3,1},{4,6},{5,7},{6,4},{7,5}} | collective-permute-start | bytes 11010056 | tf_op jit(solution)/shard_map/ppermute | solution.py:29
  345.3 185.4 %collective-permute-start.4 = (bf16[896,1152]{1,0:T(8,128)(2,1)}, bf16[896,1152]{1,0:T(8,128)(2,1)}, u32[]{:S(2)}, u32[]{:S(2)}) collective-permute-start(bf16[896,1152]{1,0:T(8,128)(2,1)} %get-tuple-element.89.refs_9_), channel_id=1, source_target_pairs={{0,2},{1,3},{2,0},{3,1},{4,6},{5,7},{6,4},{7,5}} | collective-permute-start | bytes 6193160 | tf_op jit(solution)/shard_map/ppermute | solution.py:29
  347.3 184.0 %collective-permute-start.13 = (bf16[896,1152]{1,0:T(8,128)(2,1)}, bf16[896,1152]{1,0:T(8,128)(2,1)}, u32[]{:S(2)}, u32[]{:S(2)}) collective-permute-start(bf16[896,1152]{1,0:T(8,128)(2,1)} %get-tuple-element.89.refs_9_), channel_id=1, source_target_pairs={{0,1},{1,0},{2,3},{3,2},{4,5},{5,4},{6,7},{7,6}} | collective-permute-start | bytes 6193160 | tf_op jit(solution)/shard_map/ppermute | solution.py:33
  347.3 183.5 %collective-permute-start.6 = (bf16[896,1152]{1,0:T(8,128)(2,1)}, bf16[896,1152]{1,0:T(8,128)(2,1)}, u32[]{:S(2)}, u32[]{:S(2)}) collective-permute-start(bf16[896,1152]{1,0:T(8,128)(2,1)} %get-tuple-element.90.refs_10_), channel_id=1, source_target_pairs={{0,2},{1,3},{2,0},{3,1},{4,6},{5,7},{6,4},{7,5}} | collective-permute-start | bytes 6193160 | tf_op jit(solution)/shard_map/ppermute | solution.py:29
  347.4 184.4 %collective-permute-start.14 = (bf16[896,1152]{1,0:T(8,128)(2,1)}, bf16[896,1152]{1,0:T(8,128)(2,1)}, u32[]{:S(2)}, u32[]{:S(2)}) collective-permute-start(bf16[896,1152]{1,0:T(8,128)(2,1)} %get-tuple-element.90.refs_10_), channel_id=1, source_target_pairs={{0,1},{1,0},{2,3},{3,2},{4,5},{5,4},{6,7},{7,6}} | collective-permute-start | bytes 6193160 | tf_op jit(solution)/shard_map/ppermute | solution.py:33
  397.4 133.8 %collective-permute-start.8 = (bf16[1152,896]{1,0:T(8,128)(2,1)}, bf16[1152,896]{1,0:T(8,128)(2,1)}, u32[]{:S(2)}, u32[]{:S(2)}) collective-permute-start(bf16[1152,896]{1,0:T(8,128)(2,1)} %get-tuple-element.91.refs_11_), channel_id=1, source_target_pairs={{0,2},{1,3},{2,0},{3,1},{4,6},{5,7},{6,4},{7,5}} | collective-permute-start | bytes 6193160 | tf_op jit(solution)/shard_map/ppermute | solution.py:29
  399.5 180.3 %copy-start.3 = (s32[8,102]{1,0:T(8,128)S(1)}, s32[8,102]{1,0:T(8,128)}, u32[]{:S(2)}) copy-start(s32[8,102]{1,0:T(8,128)} %constant.8.clone.table_ref) | copy-start | bytes 9796
  530.7 4.3 collective-permute-start.15
  530.8 7.2 collective-permute-start.10
  531.2 9.7 %collective-permute-start.11 = (bf16[896,1152]{1,0:T(8,128)(2,1)}, bf16[896,1152]{1,0:T(8,128)(2,1)S(1)}, u32[]{:S(2)}, u32[]{:S(2)}) collective-permute-start(bf16[896,1152]{1,0:T(8,128)(2,1)} %get-tuple-element.93.refs_19_), channel_id=1, source_target_pairs={{0,1},{1,0},{2,3},{3,2},{4,5},{5,4},{6,7},{7,6}} | collective-permute-start | bytes 6193160 | tf_op jit(solution)/shard_map/ppermute | solution.py:33
  531.3 12.5 %collective-permute-start.12 = (bf16[1152,896]{1,0:T(8,128)(2,1)}, bf16[1152,896]{1,0:T(8,128)(2,1)S(1)}, u32[]{:S(2)}, u32[]{:S(2)}) collective-permute-start(bf16[1152,896]{1,0:T(8,128)(2,1)} %get-tuple-element.94.refs_20_), channel_id=1, source_target_pairs={{0,1},{1,0},{2,3},{3,2},{4,5},{5,4},{6,7},{7,6}} | collective-permute-start | bytes 6193160 | tf_op jit(solution)/shard_map/ppermute | solution.py:33
  531.7 48.0 %collective-permute-start.18 = (bf16[896,1152]{1,0:T(8,128)(2,1)}, bf16[896,1152]{1,0:T(8,128)(2,1)S(1)}, u32[]{:S(2)}, u32[]{:S(2)}) collective-permute-start(bf16[896,1152]{1,0:T(8,128)(2,1)} %get-tuple-element.92.refs_18_), channel_id=1, source_target_pairs={{0,2},{1,3},{2,0},{3,1},{4,6},{5,7},{6,4},{7,5}} | collective-permute-start | bytes 6193160 | tf_op jit(solution)/shard_map/ppermute | solution.py:29
  535.0 44.7 %copy-start.5 = (bf16[1152,896]{1,0:T(8,128)(2,1)}, bf16[1152,896]{1,0:T(8,128)(2,1)S(1)}, u32[]{:S(2)}) copy-start(bf16[1152,896]{1,0:T(8,128)(2,1)S(1)} %collective-permute-done.15.refs_14_) | copy-start | bytes 6193156
  535.0 184.8 %collective-permute-start.16 = (bf16[1152,896]{1,0:T(8,128)(2,1)}, bf16[1152,896]{1,0:T(8,128)(2,1)}, u32[]{:S(2)}, u32[]{:S(2)}) collective-permute-start(bf16[1152,896]{1,0:T(8,128)(2,1)} %get-tuple-element.94.refs_20_), channel_id=1, source_target_pairs={{0,2},{1,3},{2,0},{3,1},{4,6},{5,7},{6,4},{7,5}} | collective-permute-start | bytes 6193160 | tf_op jit(solution)/shard_map/ppermute | solution.py:29
  538.0 137.9 %collective-permute-start.19 = (bf16[896,1152]{1,0:T(8,128)(2,1)}, bf16[896,1152]{1,0:T(8,128)(2,1)S(1)}, u32[]{:S(2)}, u32[]{:S(2)}) collective-permute-start(bf16[896,1152]{1,0:T(8,128)(2,1)} %get-tuple-element.93.refs_19_), channel_id=1, source_target_pairs={{0,2},{1,3},{2,0},{3,1},{4,6},{5,7},{6,4},{7,5}} | collective-permute-start | bytes 6193160 | tf_op jit(solution)/shard_map/ppermute | solution.py:29
  540.9 135.5 %collective-permute-start.5 = (bf16[896,1152]{1,0:T(8,128)(2,1)}, bf16[896,1152]{1,0:T(8,128)(2,1)S(1)}, u32[]{:S(2)}, u32[]{:S(2)}) collective-permute-start(bf16[896,1152]{1,0:T(8,128)(2,1)} %collective-permute-done.4.refs_15_), channel_id=1, source_target_pairs={{0,1},{1,0},{2,3},{3,2},{4,5},{5,4},{6,7},{7,6}} | collective-permute-start | bytes 6193160 | tf_op jit(solution)/shard_map/ppermute | solution.py:33
  543.9 132.6 %collective-permute-start.7 = (bf16[896,1152]{1,0:T(8,128)(2,1)}, bf16[896,1152]{1,0:T(8,128)(2,1)S(1)}, u32[]{:S(2)}, u32[]{:S(2)}) collective-permute-start(bf16[896,1152]{1,0:T(8,128)(2,1)} %collective-permute-done.6.refs_16_), channel_id=1, source_target_pairs={{0,1},{1,0},{2,3},{3,2},{4,5},{5,4},{6,7},{7,6}} | collective-permute-start | bytes 6193160 | tf_op jit(solution)/shard_map/ppermute | solution.py:33
  579.8 96.7 %collective-permute-start.9 = (bf16[1152,896]{1,0:T(8,128)(2,1)}, bf16[1152,896]{1,0:T(8,128)(2,1)S(1)}, u32[]{:S(2)}, u32[]{:S(2)}) collective-permute-start(bf16[1152,896]{1,0:T(8,128)(2,1)} %collective-permute-done.8.refs_17_), channel_id=1, source_target_pairs={{0,1},{1,0},{2,3},{3,2},{4,5},{5,4},{6,7},{7,6}} | collective-permute-start | bytes 6193160 | tf_op jit(solution)/shard_map/ppermute | solution.py:33
  579.8 0.7 copy-start
  580.4 96.0 %copy-start.2 = (s32[8,46]{1,0:T(8,128)S(1)}, s32[8,46]{1,0:T(8,128)}, u32[]{:S(2)}) copy-start(s32[8,46]{1,0:T(8,128)} %constant.9.clone.table_ref) | copy-start | bytes 4420
  675.9 44.4 %collective-permute-start.20 = (bf16[896,1152]{1,0:T(8,128)(2,1)S(1)}, bf16[896,1152]{1,0:T(8,128)(2,1)S(1)}, u32[]{:S(2)}, u32[]{:S(2)}) collective-permute-start(bf16[896,1152]{1,0:T(8,128)(2,1)S(1)} %collective-permute-done.18.refs_9_), channel_id=1, source_target_pairs={{0,1},{1,0},{2,3},{3,2},{4,5},{5,4},{6,7},{7,6}} | collective-permute-start | bytes 6193160 | tf_op jit(solution)/shard_map/ppermute | solution.py:33
  676.4 43.9 %collective-permute-start.21 = (bf16[896,1152]{1,0:T(8,128)(2,1)S(1)}, bf16[896,1152]{1,0:T(8,128)(2,1)S(1)}, u32[]{:S(2)}, u32[]{:S(2)}) collective-permute-start(bf16[896,1152]{1,0:T(8,128)(2,1)S(1)} %collective-permute-done.19.refs_10_), channel_id=1, source_target_pairs={{0,1},{1,0},{2,3},{3,2},{4,5},{5,4},{6,7},{7,6}} | collective-permute-start | bytes 6193160 | tf_op jit(solution)/shard_map/ppermute | solution.py:33
  676.4 43.9 %copy-start.1 = (s32[8,37]{1,0:T(8,128)S(1)}, s32[8,37]{1,0:T(8,128)}, u32[]{:S(2)}) copy-start(s32[8,37]{1,0:T(8,128)} %constant.10.clone.table_ref) | copy-start | bytes 3556
  719.8 36.8 %copy-start.4 = (s32[8,9]{1,0:T(8,128)S(1)}, s32[8,9]{1,0:T(8,128)}, u32[]{:S(2)}) copy-start(s32[8,9]{1,0:T(8,128)} %constant.11.clone.table_ref) | copy-start | bytes 868
  719.8 36.8 %collective-permute-start.17 = (bf16[1152,896]{1,0:T(8,128)(2,1)}, bf16[1152,896]{1,0:T(8,128)(2,1)S(1)}, u32[]{:S(2)}, u32[]{:S(2)}) collective-permute-start(bf16[1152,896]{1,0:T(8,128)(2,1)} %collective-permute-done.16.refs_11_), channel_id=1, source_target_pairs={{0,1},{1,0},{2,3},{3,2},{4,5},{5,4},{6,7},{7,6}} | collective-permute-start | bytes 6193160 | tf_op jit(solution)/shard_map/ppermute | solution.py:33

commit v14 on v13

--- a/solution.py
+++ b/solution.py
@@ -297,7 +297,8 @@
     a_own, a_across, dy_own, dy_across, wg_hbm, wu_hbm, wd_hbm = take(7)
     mine, theirs = take(2)
     before = take(2) if final else ()
-    outs, (a_land, dy_land, held_land) = take(8), take(3)
+    outs, (a_land, dy_land) = take(8), take(2)
+    held_land = take(1)[0] if kept == 3 else theirs
     wg_ref, wu_ref, wd_ref, accg_ref, accu_ref, accd_ref, a_buf, dy_buf, sums_ref = take(9)
     sems, w_sems, send_sems, recv_sems = take(4)
     terms, (held_buf,), results = take(3), take(1), take(3)
@@ -337,7 +338,7 @@
 
     def onward(which):
         pairs = [(a_refs[which], a_land.at[which]), (dy_refs[which], dy_land.at[which])]
-        if which == 0:
+        if which == 0 and kept == 3:
             pairs.append((theirs, held_land))
         return [
             pltpu.make_async_remote_copy(
@@ -511,7 +512,7 @@
     any_ = pl.BlockSpec(memory_space=pl.ANY)
     at = lambda s: once(s, lambda i: (0, 0))
     sizes = [(d, own), (d, own), (own, d), (d, rest), (d, rest), (rest, d)]
-    landed = [jax.ShapeDtypeStruct((2, tokens, d), BF16)] * 2 + [kept[0]]
+    landed = [jax.ShapeDtypeStruct((2, tokens, d), BF16)] * 2 + [kept[0]] * (kept[0].shape[0] == 3)
     return pl.pallas_call(
         lambda *refs: slices_kernel(layer, own, kept[0].shape[0], count, *refs),
         grid=(4 * tokens // ROWS,),
@@ -699,6 +700,7 @@
         h1, a1, a0, *made = forward(own, x, wg, wu, wd)
         a1_x = send(a1, px)
         a0_x = send(a0, px)
+        made[1] = send(made[1], pd)
         dh1, *kept = chain(own, a1, dy, h1, wg, wu, wd)
         dh1_x = send(dh1, px)
         top = slices(1, own, [a1, a1_x], [dy, dy_x], wg, wu, wd, kept)

time: 766 us -> 793 us (1.035)
  waiting for transfers between devices: 124 us -> 165 us
  Pallas kernels: 623 us -> 612 us
    ppermute x10, waiting for transfers between devices: 117 us -> 155 us  [px(): return lax.ppermute(a, 'dp', PX)]
    pallas_call x2, Pallas kernels: 236 us -> 225 us  [slices(): pl.pallas_call(lambda *refs: slices_kernel(layer, own, kept[0].shape[0],...]
  transfers between devices with their start and end apart: 22 -> 23, of which waited for: 7 -> 8; matrix products, arithmetic and copies ran while one was open for 0% -> 0% of each run, Pallas kernels for 70% -> 66%
where the time goes in v14:
time: 793 us
  Pallas kernels  612 us (77%)
  waiting for transfers between devices  165 us (21%)
  starting transfers between devices  14.3 us (2%)
    pallas_call x2, Pallas kernels, slices(): pl.pallas_call(lambda *refs: slices_kernel(layer, own, kept[0].shape[0],...  225 us
    pallas_call x4, Pallas kernels, adam(): pl.pallas_call(kernel, in_specs=[pl.BlockSpec(memory_space=pltpu.SMEM), p...  184 us
    ppermute x10, waiting for transfers between devices, px(): return lax.ppermute(a, 'dp', PX)  155 us
    pallas_call x1, Pallas kernels, chain(): pl.pallas_call(lambda *refs: chain_kernel(tail, own, *refs), grid=(steps,...  126 us
    pallas_call x1, Pallas kernels, forward(): pl.pallas_call(lambda *refs: forward_kernel(tail, own, *refs), grid=(step...  77 us
  transfers between devices with their start and end apart: 23, of which 8 were waited for; matrix products, arithmetic and copies ran while one was open for 0% of the time, Pallas kernels for 66%

profile of v14, /device:TPU:0, one launch (start us, length us, event | category | flops | bytes accessed | tf_op | source)
XLA Modules:
  0.0 793.2 jit_solution(2960740385379753799)
XLA Ops:
  0.6 77.0 %forward.1 = (bf16[2048,896]{1,0:T(8,128)(2,1)}, bf16[2048,896]{1,0:T(8,128)(2,1)}, bf16[2048,896]{1,0:T(8,128)(2,1)}, f32[2,2048,1280]{2,1,0:T(8,128)}, f32[2,2048,1280]{2,1,0:T(8,128)}) custom-call(bf16[2048,896]{1,0:T(8,128)(2,1)} %bitcast.2, bf16[2,896,4736]{2,1,0:T(8,128)(2,1)} %refs_0_.7, bf16[2,896,4736]{2,1,0:T(8,128)(2,1)} %refs_3_.11, ...), custom_call_target="tpu_custom_call" | custom-call | flops 52143587328 | bytes 25460736 | tf_op jit(solution)/shard_map/forward/pallas_call | solution.py:187
  77.7 0.9 collective-permute-start.2
  78.5 2.5 collective-permute-start.3
  81.1 125.7 %chain.1 = (bf16[2048,896]{1,0:T(8,128)(2,1)}, bf16[3,2048,1280]{2,1,0:T(8,128)(2,1)}, bf16[3,2048,1280]{2,1,0:T(8,128)(2,1)}) custom-call(bf16[2048,896]{1,0:T(8,128)(2,1)} %get-tuple-element.79.refs_0_, bf16[2048,896]{1,0:T(8,128)(2,1)} %bitcast.4, bf16[2048,896]{1,0:T(8,128)(2,1)} %get-tuple-element.80.refs_2_, bf16[2,896,4736]{2,1,0:T(8,128)(2,1)} %refs_0_.7, ...), custom_call_target="tpu_custom_call" | custom-call | flops 86905978880 | bytes 25460736 | tf_op jit(solution)/shard_map/chain/pallas_call | solution.py:269
  206.8 2.0 collective-permute-start.1
  208.8 31.4 %collective-permute-done.4.refs_3_ = bf16[2048,896]{1,0:T(8,128)(2,1)} collective-permute-done((bf16[2048,896]{1,0:T(8,128)(2,1)}, bf16[2048,896]{1,0:T(8,128)(2,1)}, u32[]{:S(2)}, u32[]{:S(2)}) %collective-permute-start.4) | collective-permute-done | bytes 3670048 | tf_op jit(solution)/shard_map/ppermute | solution.py:29
  240.2 105.1 %slices.2 = (bf16[896,1152]{1,0:T(8,128)(2,1)}, bf16[896,1152]{1,0:T(8,128)(2,1)}, bf16[1152,896]{1,0:T(8,128)(2,1)}, bf16[896,128]{1,0:T(8,128)(2,1)}, bf16[896...) custom-call(bf16[2048,896]{1,0:T(8,128)(2,1)} %get-tuple-element.79., ...), custom_call_target="tpu_custom_call" | custom-call | flops 112742891520 | bytes 29360128 | tf_op jit(solution)/shard_map/slices/pallas_call | solution.py:516
  345.3 2.0 collective-permute-start.5
  347.4 50.0 %collective-permute-done.refs_1_ = bf16[2048,896]{1,0:T(8,128)(2,1)} collective-permute-done((bf16[2048,896]{1,0:T(8,128)(2,1)}, bf16[2048,896]{1,0:T(8,128)(2,1)}, u32[]{:S(2)}, u32[]{:S(2)}) %collective-permute-start) | collective-permute-done | bytes 3670048 | tf_op jit(solution)/shard_map/ppermute | solution.py:29
  397.5 44.1 %collective-permute-done.5.refs_15_ = bf16[896,1152]{1,0:T(8,128)(2,1)S(1)} collective-permute-done((bf16[896,1152]{1,0:T(8,128)(2,1)}, bf16[896,1152]{1,0:T(8,128)(2,1)S(1)}, u32[]{:S(2)}, u32[]{:S(2)}) %collective-permute-start.5) | collective-permute-done | bytes 2064416 | tf_op jit(solution)/shard_map/ppermute | solution.py:29
  441.6 2.0 collective-permute-start.9
  443.7 120.1 %slices.3 = (bf16[896,1152]{1,0:T(8,128)(2,1)}, bf16[896,1152]{1,0:T(8,128)(2,1)}, bf16[1152,896]{1,0:T(8,128)(2,1)}, bf16[896,128]{1,0:T(8,128)(2,1)}, bf16[896...) custom-call(bf16[2048,896]{1,0:T(8,128)(2,1)} %get-tuple-element.78., ...), custom_call_target="tpu_custom_call" | custom-call | flops 112742891520 | bytes 29360128 | tf_op jit(solution)/shard_map/slices/pallas_call | solution.py:516
  563.8 0.1 collective-permute-start.10
  563.9 0.4 collective-permute-start.6
  564.3 0.1 collective-permute-start.8
  564.4 0.4 collective-permute-start.11
  564.8 0.1 collective-permute-start.13
  564.9 3.2 collective-permute-done.10.refs_11_
  568.1 1.0 collective-permute-start.17
  569.1 2.0 collective-permute-done.6.refs_9_
  571.1 1.0 collective-permute-start.19
  572.0 2.0 collective-permute-done.8.refs_10_
  574.0 0.1 collective-permute-start.12
  574.2 2.8 collective-permute-done.11.refs_12_
  577.0 1.0 collective-permute-start.20
  577.9 0.7 copy-done
  578.6 95.4 %shard_map.214 = (bf16[2,896,4736]{2,1,0:T(8,128)(2,1)}, f32[2,896,4736]{2,1,0:T(8,128)}, f32[2,896,4736]{2,1,0:T(8,128)}, bf16[2,896,4736]{2,1,0:T(8,128)(2,1)}...) custom-call(s32[8,102]{1,0:T(8,128)S(1)} %copy-done.3, ...), custom_call_target="tpu_custom_call" | custom-call | flops 26148864000 | bytes 287637504 | tf_op jit(solution)/shard_map/pallas_call | solution.py:676
  674.1 29.7 %collective-permute-done.20.refs_10_ = bf16[896,1152]{1,0:T(8,128)(2,1)S(1)} collective-permute-done((bf16[896,1152]{1,0:T(8,128)(2,1)}, bf16[896,1152]{1,0:T(8,128)(2,1)S(1)}, u32[]{:S(2)}, u32[]{:S(2)}) %collective-permute-start.20) | collective-permute-done | bytes 2064416 | tf_op jit(solution)/shard_map/ppermute | solution.py:29
  703.8 43.3 %shard_map.215 = (bf16[2,896,4736]{2,1,0:T(8,128)(2,1)}, f32[2,896,4736]{2,1,0:T(8,128)}, f32[2,896,4736]{2,1,0:T(8,128)}, bf16[2,896,4736]{2,1,0:T(8,128)(2,1)}...) custom-call(s32[8,46]{1,0:T(8,128)S(1)} %copy-done.2, ...), custom_call_target="tpu_custom_call", output_to_operand_aliasing={{0}: (17, {}), {1}: (18, {}), {2}: (19, {}), {3}: (20, {}),... | custom-call | flops 12386304000 | bytes 136249344 | tf_op jit(solution)/shard_map/pallas_call | solution.py:676
  747.2 0.5 collective-permute-start.18
  747.7 36.3 %shard_map.216 = (bf16[2,896,4736]{2,1,0:T(8,128)(2,1)}, f32[2,896,4736]{2,1,0:T(8,128)}, f32[2,896,4736]{2,1,0:T(8,128)}, bf16[2,896,4736]{2,1,0:T(8,128)(2,1)}...) custom-call(s32[8,37]{1,0:T(8,128)S(1)} %copy-done.1, ...), custom_call_target="tpu_custom_call", output_to_operand_aliasing={{0}: (16, {}), {1}: (17, {}), {2}: (18, {}), {3}: (19, {}),... | custom-call | flops 10321920000 | bytes 113541120 | tf_op jit(solution)/shard_map/pallas_call | solution.py:676
  784.0 9.0 %shard_map.217 = (bf16[2,896,4736]{2,1,0:T(8,128)(2,1)}, f32[2,896,4736]{2,1,0:T(8,128)}, f32[2,896,4736]{2,1,0:T(8,128)}, bf16[2,896,4736]{2,1,0:T(8,128)(2,1)}...) custom-call(s32[8,9]{1,0:T(8,128)S(1)} %copy-done.4, ...), custom_call_target="tpu_custom_call", output_to_operand_aliasing={{0}: (12, {}), {1}: (13, {}), {2}: (14, {}), {3}: (15, {}),... | custom-call | flops 2064384000 | bytes 22708224 | tf_op jit(solution)/shard_map/pallas_call | solution.py:676
  (34 shorter events, 0.3 us)
Async XLA Ops:
  77.7 366.0 %collective-permute-start.2 = (f32[2,2048,1280]{2,1,0:T(8,128)}, f32[2,2048,1280]{2,1,0:T(8,128)}, u32[]{:S(2)}, u32[]{:S(2)}) collective-permute-start(f32[2,2048,1280]{2,1,0:T(8,128)} %get-tuple-element.83), channel_id=1, source_target_pairs={{0,1},{1,0},{2,3},{3,2},{4,5},{5,4},{6,7},{7,6}} | collective-permute-start | bytes 62914568 | tf_op jit(solution)/shard_map/ppermute | solution.py:33
  78.5 130.3 %collective-permute-start.3 = (bf16[2048,896]{1,0:T(8,128)(2,1)}, bf16[2048,896]{1,0:T(8,128)(2,1)}, u32[]{:S(2)}, u32[]{:S(2)}) collective-permute-start(bf16[2048,896]{1,0:T(8,128)(2,1)} %get-tuple-element.79.refs_0_), channel_id=1, source_target_pairs={{0,2},{1,3},{2,0},{3,1},{4,6},{5,7},{6,4},{7,5}} | collective-permute-start | bytes 11010056 | tf_op jit(solution)/shard_map/ppermute | solution.py:29
  81.0 159.2 %collective-permute-start.4 = (bf16[2048,896]{1,0:T(8,128)(2,1)}, bf16[2048,896]{1,0:T(8,128)(2,1)}, u32[]{:S(2)}, u32[]{:S(2)}) collective-permute-start(bf16[2048,896]{1,0:T(8,128)(2,1)} %bitcast.3), channel_id=1, source_target_pairs={{0,2},{1,3},{2,0},{3,1},{4,6},{5,7},{6,4},{7,5}} | collective-permute-start | bytes 11010056 | tf_op jit(solution)/shard_map/ppermute | solution.py:29
  206.8 140.6 %collective-permute-start.1 = (bf16[2048,896]{1,0:T(8,128)(2,1)}, bf16[2048,896]{1,0:T(8,128)(2,1)}, u32[]{:S(2)}, u32[]{:S(2)}) collective-permute-start(bf16[2048,896]{1,0:T(8,128)(2,1)} %get-tuple-element.81.refs_2_), channel_id=1, source_target_pairs={{0,2},{1,3},{2,0},{3,1},{4,6},{5,7},{6,4},{7,5}} | collective-permute-start | bytes 11010056 | tf_op jit(solution)/shard_map/ppermute | solution.py:29
  208.8 188.7 %collective-permute-start = (bf16[2048,896]{1,0:T(8,128)(2,1)}, bf16[2048,896]{1,0:T(8,128)(2,1)}, u32[]{:S(2)}, u32[]{:S(2)}) collective-permute-start(bf16[2048,896]{1,0:T(8,128)(2,1)} %get-tuple-element.78.refs_0_), channel_id=1, source_target_pairs={{0,2},{1,3},{2,0},{3,1},{4,6},{5,7},{6,4},{7,5}} | collective-permute-start | bytes 11010056 | tf_op jit(solution)/shard_map/ppermute | solution.py:29
  345.3 96.3 %collective-permute-start.5 = (bf16[896,1152]{1,0:T(8,128)(2,1)}, bf16[896,1152]{1,0:T(8,128)(2,1)S(1)}, u32[]{:S(2)}, u32[]{:S(2)}) collective-permute-start(bf16[896,1152]{1,0:T(8,128)(2,1)} %get-tuple-element.89.refs_9_), channel_id=1, source_target_pairs={{0,2},{1,3},{2,0},{3,1},{4,6},{5,7},{6,4},{7,5}} | collective-permute-start | bytes 6193160 | tf_op jit(solution)/shard_map/ppermute | solution.py:29
  347.4 216.9 %collective-permute-start.14 = (bf16[896,1152]{1,0:T(8,128)(2,1)}, bf16[896,1152]{1,0:T(8,128)(2,1)}, u32[]{:S(2)}, u32[]{:S(2)}) collective-permute-start(bf16[896,1152]{1,0:T(8,128)(2,1)} %get-tuple-element.89.refs_9_), channel_id=1, source_target_pairs={{0,1},{1,0},{2,3},{3,2},{4,5},{5,4},{6,7},{7,6}} | collective-permute-start | bytes 6193160 | tf_op jit(solution)/shard_map/ppermute | solution.py:33
  347.4 216.5 %collective-permute-start.7 = (bf16[896,1152]{1,0:T(8,128)(2,1)}, bf16[896,1152]{1,0:T(8,128)(2,1)}, u32[]{:S(2)}, u32[]{:S(2)}) collective-permute-start(bf16[896,1152]{1,0:T(8,128)(2,1)} %get-tuple-element.90.refs_10_), channel_id=1, source_target_pairs={{0,2},{1,3},{2,0},{3,1},{4,6},{5,7},{6,4},{7,5}} | collective-permute-start | bytes 6193160 | tf_op jit(solution)/shard_map/ppermute | solution.py:29
  397.5 166.9 %collective-permute-start.15 = (bf16[896,1152]{1,0:T(8,128)(2,1)}, bf16[896,1152]{1,0:T(8,128)(2,1)}, u32[]{:S(2)}, u32[]{:S(2)}) collective-permute-start(bf16[896,1152]{1,0:T(8,128)(2,1)} %get-tuple-element.90.refs_10_), channel_id=1, source_target_pairs={{0,1},{1,0},{2,3},{3,2},{4,5},{5,4},{6,7},{7,6}} | collective-permute-start | bytes 6193160 | tf_op jit(solution)/shard_map/ppermute | solution.py:33
  441.6 2.0 copy-start.5
  441.6 122.1 %collective-permute-start.9 = (bf16[1152,896]{1,0:T(8,128)(2,1)}, bf16[1152,896]{1,0:T(8,128)(2,1)}, u32[]{:S(2)}, u32[]{:S(2)}) collective-permute-start(bf16[1152,896]{1,0:T(8,128)(2,1)} %get-tuple-element.91.refs_11_), channel_id=1, source_target_pairs={{0,2},{1,3},{2,0},{3,1},{4,6},{5,7},{6,4},{7,5}} | collective-permute-start | bytes 6193160 | tf_op jit(solution)/shard_map/ppermute | solution.py:29
  443.6 121.2 %collective-permute-start.16 = (bf16[1152,896]{1,0:T(8,128)(2,1)}, bf16[1152,896]{1,0:T(8,128)(2,1)}, u32[]{:S(2)}, u32[]{:S(2)}) collective-permute-start(bf16[1152,896]{1,0:T(8,128)(2,1)} %get-tuple-element.91.refs_11_), channel_id=1, source_target_pairs={{0,1},{1,0},{2,3},{3,2},{4,5},{5,4},{6,7},{7,6}} | collective-permute-start | bytes 6193160 | tf_op jit(solution)/shard_map/ppermute | solution.py:33
  443.6 134.3 %copy-start.3 = (s32[8,102]{1,0:T(8,128)S(1)}, s32[8,102]{1,0:T(8,128)}, u32[]{:S(2)}) copy-start(s32[8,102]{1,0:T(8,128)} %constant.8.clone.table_ref) | copy-start | bytes 9796
  563.8 4.3 collective-permute-start.10
  563.9 7.2 collective-permute-start.6
  564.3 9.7 %collective-permute-start.8 = (bf16[896,1152]{1,0:T(8,128)(2,1)}, bf16[896,1152]{1,0:T(8,128)(2,1)S(1)}, u32[]{:S(2)}, u32[]{:S(2)}) collective-permute-start(bf16[896,1152]{1,0:T(8,128)(2,1)} %collective-permute-done.7.refs_16_), channel_id=1, source_target_pairs={{0,1},{1,0},{2,3},{3,2},{4,5},{5,4},{6,7},{7,6}} | collective-permute-start | bytes 6193160 | tf_op jit(solution)/shard_map/ppermute | solution.py:33
  564.4 12.5 %collective-permute-start.11 = (bf16[896,1152]{1,0:T(8,128)(2,1)}, bf16[896,1152]{1,0:T(8,128)(2,1)S(1)}, u32[]{:S(2)}, u32[]{:S(2)}) collective-permute-start(bf16[896,1152]{1,0:T(8,128)(2,1)} %get-tuple-element.92.refs_18_), channel_id=1, source_target_pairs={{0,1},{1,0},{2,3},{3,2},{4,5},{5,4},{6,7},{7,6}} | collective-permute-start | bytes 6193160 | tf_op jit(solution)/shard_map/ppermute | solution.py:33
  564.8 139.0 %collective-permute-start.13 = (bf16[1152,896]{1,0:T(8,128)(2,1)}, bf16[1152,896]{1,0:T(8,128)(2,1)S(1)}, u32[]{:S(2)}, u32[]{:S(2)}) collective-permute-start(bf16[1152,896]{1,0:T(8,128)(2,1)} %get-tuple-element.94.refs_20_), channel_id=1, source_target_pairs={{0,1},{1,0},{2,3},{3,2},{4,5},{5,4},{6,7},{7,6}} | collective-permute-start | bytes 6193160 | tf_op jit(solution)/shard_map/ppermute | solution.py:33
  568.1 179.0 %collective-permute-start.17 = (bf16[1152,896]{1,0:T(8,128)(2,1)}, bf16[1152,896]{1,0:T(8,128)(2,1)}, u32[]{:S(2)}, u32[]{:S(2)}) collective-permute-start(bf16[1152,896]{1,0:T(8,128)(2,1)} %get-tuple-element.94.refs_20_), channel_id=1, source_target_pairs={{0,2},{1,3},{2,0},{3,1},{4,6},{5,7},{6,4},{7,5}} | collective-permute-start | bytes 6193160 | tf_op jit(solution)/shard_map/ppermute | solution.py:29
  571.1 103.0 %collective-permute-start.19 = (bf16[896,1152]{1,0:T(8,128)(2,1)}, bf16[896,1152]{1,0:T(8,128)(2,1)S(1)}, u32[]{:S(2)}, u32[]{:S(2)}) collective-permute-start(bf16[896,1152]{1,0:T(8,128)(2,1)} %get-tuple-element.92.refs_18_), channel_id=1, source_target_pairs={{0,2},{1,3},{2,0},{3,1},{4,6},{5,7},{6,4},{7,5}} | collective-permute-start | bytes 6193160 | tf_op jit(solution)/shard_map/ppermute | solution.py:29
  574.0 129.8 %collective-permute-start.12 = (bf16[896,1152]{1,0:T(8,128)(2,1)}, bf16[896,1152]{1,0:T(8,128)(2,1)S(1)}, u32[]{:S(2)}, u32[]{:S(2)}) collective-permute-start(bf16[896,1152]{1,0:T(8,128)(2,1)} %get-tuple-element.93.refs_19_), channel_id=1, source_target_pairs={{0,1},{1,0},{2,3},{3,2},{4,5},{5,4},{6,7},{7,6}} | collective-permute-start | bytes 6193160 | tf_op jit(solution)/shard_map/ppermute | solution.py:33
  577.0 126.8 %collective-permute-start.20 = (bf16[896,1152]{1,0:T(8,128)(2,1)}, bf16[896,1152]{1,0:T(8,128)(2,1)S(1)}, u32[]{:S(2)}, u32[]{:S(2)}) collective-permute-start(bf16[896,1152]{1,0:T(8,128)(2,1)} %get-tuple-element.93.refs_19_), channel_id=1, source_target_pairs={{0,2},{1,3},{2,0},{3,1},{4,6},{5,7},{6,4},{7,5}} | collective-permute-start | bytes 6193160 | tf_op jit(solution)/shard_map/ppermute | solution.py:29
  577.9 0.7 copy-start
  578.6 125.2 %copy-start.2 = (s32[8,46]{1,0:T(8,128)S(1)}, s32[8,46]{1,0:T(8,128)}, u32[]{:S(2)}) copy-start(s32[8,46]{1,0:T(8,128)} %constant.9.clone.table_ref) | copy-start | bytes 4420
  674.0 73.7 %collective-permute-start.21 = (bf16[896,1152]{1,0:T(8,128)(2,1)S(1)}, bf16[896,1152]{1,0:T(8,128)(2,1)S(1)}, u32[]{:S(2)}, u32[]{:S(2)}) collective-permute-start(bf16[896,1152]{1,0:T(8,128)(2,1)S(1)} %collective-permute-done.19.refs_9_), channel_id=1, source_target_pairs={{0,1},{1,0},{2,3},{3,2},{4,5},{5,4},{6,7},{7,6}} | collective-permute-start | bytes 6193160 | tf_op jit(solution)/shard_map/ppermute | solution.py:33
  703.8 43.9 %collective-permute-start.22 = (bf16[896,1152]{1,0:T(8,128)(2,1)S(1)}, bf16[896,1152]{1,0:T(8,128)(2,1)S(1)}, u32[]{:S(2)}, u32[]{:S(2)}) collective-permute-start(bf16[896,1152]{1,0:T(8,128)(2,1)S(1)} %collective-permute-done.20.refs_10_), channel_id=1, source_target_pairs={{0,1},{1,0},{2,3},{3,2},{4,5},{5,4},{6,7},{7,6}} | collective-permute-start | bytes 6193160 | tf_op jit(solution)/shard_map/ppermute | solution.py:33
  703.8 43.9 %copy-start.1 = (s32[8,37]{1,0:T(8,128)S(1)}, s32[8,37]{1,0:T(8,128)}, u32[]{:S(2)}) copy-start(s32[8,37]{1,0:T(8,128)} %constant.10.clone.table_ref) | copy-start | bytes 3556
  747.1 36.8 %copy-start.4 = (s32[8,9]{1,0:T(8,128)S(1)}, s32[8,9]{1,0:T(8,128)}, u32[]{:S(2)}) copy-start(s32[8,9]{1,0:T(8,128)} %constant.11.clone.table_ref) | copy-start | bytes 868
  747.2 36.8 %collective-permute-start.18 = (bf16[1152,896]{1,0:T(8,128)(2,1)}, bf16[1152,896]{1,0:T(8,128)(2,1)S(1)}, u32[]{:S(2)}, u32[]{:S(2)}) collective-permute-start(bf16[1152,896]{1,0:T(8,128)(2,1)} %collective-permute-done.17.refs_11_), channel_id=1, source_target_pairs={{0,1},{1,0},{2,3},{3,2},{4,5},{5,4},{6,7},{7,6}} | collective-permute-start | bytes 6193160 | tf_op jit(solution)/shard_map/ppermute | solution.py:33
